TPU v7x, 32 devices: a 4x4x1 block of a 4x4x8 slice. The times are simulated.
32 devices in a mesh: dp: 1 (over z), tx: 4 (over y), ty: 8 (over x, core).
Axes of the slice: x: 4, y: 4, z: 1, core: 2. Of those that a mesh axis runs over, the one named last changes fastest.
The devices are a block of a 4x4x8 slice.
Arguments:
- x_act: bfloat16 [8, 1536, 2048], P('dp', None, 'tx')
- cot_out: bfloat16 [8, 1536, 2048], P('dp', None, 'tx')
- ln1_gain: bfloat16 [2048], P('tx')
- ln1_bias: bfloat16 [2048], P('tx')
- ln2_gain: bfloat16 [2048], P('tx')
- ln2_bias: bfloat16 [2048], P('tx')
- w_qkv: bfloat16 [2048, 8, 768], P('tx', 'ty')
- b_qkv: bfloat16 [8, 768], P('ty')
- w_dense: bfloat16 [2048, 2048], P('ty', 'tx')
- b_dense: bfloat16 [2048], P('tx')
- w_up: bfloat16 [2048, 8192], P('tx', 'ty')
- b_up: bfloat16 [8192], P('ty')
- w_down: bfloat16 [8192, 2048], P('ty', 'tx')
- b_down: bfloat16 [2048], P('tx')
Outputs:
- output 1: bfloat16 [8, 1536, 2048], P('dp', None, 'tx')
- output 2: bfloat16 [8, 1536, 2048], P('dp', None, 'tx')
- output 3: float32 [2048], P(('dp', 'tx'))
- output 4: float32 [2048], P(('dp', 'tx'))
- output 5: float32 [2048], P(('dp', 'tx'))
- output 6: float32 [2048], P(('dp', 'tx'))
- output 7: float32 [2048, 8, 768], P(('dp', 'tx'), 'ty')
- output 8: float32 [8, 768], P(('dp', 'ty'))
- output 9: float32 [2048, 2048], P(('dp', 'ty'), 'tx')
- output 10: float32 [2048], P(('dp', 'tx'))
- output 11: float32 [2048, 8192], P(('dp', 'tx'), 'ty')
- output 12: float32 [8192], P(('dp', 'ty'))
- output 13: float32 [8192, 2048], P(('dp', 'ty'), 'tx')
- output 14: float32 [2048], P(('dp', 'tx'))
All inputs are finite; a program needn't handle non-finite values.
Results may differ from a plain program's by a relative error of at most 0.02.
Values are sent between devices in bfloat16 or wider.
A program may use at most 768 MiB of HBM per device.

v0:
```python
import functools
import jax
import jax.numpy as jnp
from jax import lax
from jax.sharding import PartitionSpec as P

LN_EPS = 1e-5
ROPE_BASE = 10000.0
ROTARY_DIVISOR = 4


def rotary_tables(positions, rot_dim):
    inv_freq = ROPE_BASE ** (-jnp.arange(0, rot_dim, 2, dtype=jnp.float32) / rot_dim)
    angles = positions[:, None] * inv_freq[None, :]
    angles = jnp.concatenate([angles, angles], axis=-1)
    return jnp.cos(angles), jnp.sin(angles)


def apply_rotary(tensor, cos_tab, sin_tab, rot_dim):
    half_rot = rot_dim // 2
    rot_part = tensor[..., :rot_dim]
    turned = jnp.concatenate([-rot_part[..., half_rot:], rot_part[..., :half_rot]], axis=-1)
    mixed = rot_part * cos_tab[:, None, :] + turned * sin_tab[:, None, :]
    return jnp.concatenate([mixed, tensor[..., rot_dim:]], axis=-1)


def rotate_qkv(qkv_act, positions):
    head_dim = qkv_act.shape[-1] // 3
    rot_dim = head_dim // ROTARY_DIVISOR
    cos_tab, sin_tab = rotary_tables(positions, rot_dim)
    q_rot = apply_rotary(qkv_act[..., :head_dim].astype(jnp.float32), cos_tab, sin_tab, rot_dim).astype(jnp.bfloat16)
    k_rot = apply_rotary(qkv_act[..., head_dim:2 * head_dim].astype(jnp.float32), cos_tab, sin_tab, rot_dim).astype(jnp.bfloat16)
    return q_rot, k_rot, qkv_act[..., 2 * head_dim:]


def attend_rows(q_rot, k_rot, values, q_pos, key_pos):
    scores = jnp.einsum('bqhe,bkhe->bhqk', q_rot, k_rot, preferred_element_type=jnp.float32) * q_rot.shape[-1] ** -0.5
    scores = jnp.where(q_pos[:, None] >= key_pos[None, :], scores, -1e30)
    probs = jax.nn.softmax(scores, axis=-1).astype(jnp.bfloat16)
    return jnp.einsum('bhqk,bkhe->bqhe', probs, values, preferred_element_type=jnp.float32).astype(jnp.bfloat16)


def attend_seq(qkv_act, positions):
    q_rot, k_rot, values = rotate_qkv(qkv_act, positions)
    return attend_rows(q_rot, k_rot, values, positions, positions)


def gelu_bf16(pre_act):
    return jax.nn.gelu(pre_act.astype(jnp.float32), approximate=False).astype(jnp.bfloat16)


def solution(mesh):
    tx_size = mesh.shape['tx']
    act_spec = P('dp', None, 'tx')
    width_spec = P('tx')
    in_specs = (act_spec, act_spec, width_spec, width_spec, width_spec, width_spec, P('tx', 'ty', None), P('ty', None), P('ty', 'tx'), width_spec, P('tx', 'ty'), P('ty'), P('ty', 'tx'), width_spec)
    width_out = P(('dp', 'tx'))
    out_specs = (act_spec, act_spec, width_out, width_out, width_out, width_out, P(('dp', 'tx'), 'ty', None), P(('dp', 'ty'), None), P(('dp', 'ty'), 'tx'), width_out, P(('dp', 'tx'), 'ty'), P(('dp', 'ty')), P(('dp', 'ty'), 'tx'), width_out)

    def body(x_act, cot_out, ln1_gain, ln1_bias, ln2_gain, ln2_bias, w_qkv, b_qkv, w_dense, b_dense, w_up, b_up, w_down, b_down):
        batch, seq_len, d_local = x_act.shape
        d_model = d_local * tx_size
        x_float = x_act.astype(jnp.float32)
        moments = lax.psum(jnp.stack([x_float.sum(-1), (x_float * x_float).sum(-1)], axis=-1), 'tx')
        mean = moments[..., 0:1] / d_model
        inv_std = lax.rsqrt(moments[..., 1:2] / d_model - mean * mean + LN_EPS)
        x_hat = (x_float - mean) * inv_std
        gain_attn = ln1_gain.astype(jnp.float32)
        gain_mlp = ln2_gain.astype(jnp.float32)
        h_attn = (x_hat * gain_attn + ln1_bias.astype(jnp.float32)).astype(jnp.bfloat16)
        h_mlp = (x_hat * gain_mlp + ln2_bias.astype(jnp.float32)).astype(jnp.bfloat16)
        qkv_part = jnp.einsum('bsd,dhe->bshe', h_attn, w_qkv, preferred_element_type=jnp.float32).astype(jnp.bfloat16)
        qkv_act = (lax.psum(qkv_part, 'tx').astype(jnp.float32) + b_qkv.astype(jnp.float32)).astype(jnp.bfloat16)
        positions = jnp.arange(seq_len, dtype=jnp.float32)
        context, attn_pullback = jax.vjp(functools.partial(attend_seq, positions=positions), qkv_act)
        ctx_flat = context.reshape(batch, seq_len, -1)
        attn_part = jnp.einsum('bsk,kd->bsd', ctx_flat, w_dense, preferred_element_type=jnp.float32)
        up_part = jnp.einsum('bsd,df->bsf', h_mlp, w_up, preferred_element_type=jnp.float32).astype(jnp.bfloat16)
        pre_act = (lax.psum(up_part, 'tx').astype(jnp.float32) + b_up.astype(jnp.float32)).astype(jnp.bfloat16)
        gelu_out, gelu_pullback = jax.vjp(gelu_bf16, pre_act)
        down_part = jnp.einsum('bsf,fd->bsd', gelu_out, w_down, preferred_element_type=jnp.float32)
        mixed = lax.psum((attn_part + down_part).astype(jnp.bfloat16), 'ty')
        bias_out = b_dense.astype(jnp.float32) + b_down.astype(jnp.float32)
        y_out = (x_float + mixed.astype(jnp.float32) + bias_out).astype(jnp.bfloat16)

        cot_float = cot_out.astype(jnp.float32)
        d_b_out = cot_float.sum((0, 1))
        d_w_down = jnp.einsum('bsf,bsd->fd', gelu_out, cot_out, preferred_element_type=jnp.float32)
        d_gelu = lax.psum(jnp.einsum('bsd,fd->bsf', cot_out, w_down, preferred_element_type=jnp.float32).astype(jnp.bfloat16), 'tx')
        (d_pre,) = gelu_pullback(d_gelu)
        d_b_up = d_pre.astype(jnp.float32).sum((0, 1))
        d_w_up = jnp.einsum('bsd,bsf->df', h_mlp, d_pre, preferred_element_type=jnp.float32)
        d_h_mlp = lax.psum(jnp.einsum('bsf,df->bsd', d_pre, w_up, preferred_element_type=jnp.float32).astype(jnp.bfloat16), 'ty')
        d_w_dense = jnp.einsum('bsk,bsd->kd', ctx_flat, cot_out, preferred_element_type=jnp.float32)
        d_ctx = lax.psum(jnp.einsum('bsd,kd->bsk', cot_out, w_dense, preferred_element_type=jnp.float32).astype(jnp.bfloat16), 'tx')
        (d_qkv,) = attn_pullback(d_ctx.reshape(context.shape))
        d_b_qkv = d_qkv.astype(jnp.float32).sum((0, 1))
        d_w_qkv = jnp.einsum('bsd,bshe->dhe', h_attn, d_qkv, preferred_element_type=jnp.float32)
        d_h_attn = lax.psum(jnp.einsum('bshe,dhe->bsd', d_qkv, w_qkv, preferred_element_type=jnp.float32).astype(jnp.bfloat16), 'ty')
        d_attn_float = d_h_attn.astype(jnp.float32)
        d_mlp_float = d_h_mlp.astype(jnp.float32)
        d_ln1_gain = (d_attn_float * x_hat).sum((0, 1))
        d_ln1_bias = d_attn_float.sum((0, 1))
        d_ln2_gain = (d_mlp_float * x_hat).sum((0, 1))
        d_ln2_bias = d_mlp_float.sum((0, 1))
        value_a6 = d_attn_float * gain_attn + d_mlp_float * gain_mlp
        dx_moments = lax.psum(jnp.stack([value_a6.sum(-1), (value_a6 * x_hat).sum(-1)], axis=-1), 'tx')
        d_x = inv_std * (value_a6 - dx_moments[..., 0:1] / d_model - x_hat * dx_moments[..., 1:2] / d_model)
        dx_act = (cot_float + d_x).astype(jnp.bfloat16)
        return (y_out, dx_act, d_ln1_gain, d_ln1_bias, d_ln2_gain, d_ln2_bias, d_w_qkv, d_b_qkv, d_w_dense, d_b_out, d_w_up, d_b_up, d_w_down, d_b_out)

    return jax.shard_map(body, mesh=mesh, in_specs=in_specs, out_specs=out_specs, check_vma=False)
```

profile of v0, /device:TPU:98, one launch (start us, length us, event | category | flops | bytes accessed | tf_op | source)
XLA Modules:
  0.0 2428.6 jit_solution(3505539374090763514)
XLA Ops:
  16.0 20.5 convolution_convert_fusion.1
  36.4 10.8 convert_bitcast_fusion.2
  56.1 17.7 convert_bitcast_fusion
  73.9 20.8 convolution_convert_fusion.2
  102.3 1228.2 %all-reduce.24.cloned.1.call-done = (bf16[8,1536,1,768]{3,1,0,2:T(8,128)(2,1)}, bf16[8,1536,1024]{2,1,0:T(8,128)(2,1)}, bf16[8,1536,1024]{2,1,0:T(8,128)(2,1)}, bf16[8,256,1536]{1,2,0:T(8,128)(2,1)}) async-done(((bf16[8,1536,1,768]{3,1,0,2:T(8,128)(2,1)}, bf16[8,1536,1024]{2,1,0:T(8,128)(2,1)}, bf16[8,1536,1024]{2,1,0:T(8,128)(2,1)}, bf16[8,256,1536]{1,2,0:T(8,128)(2,1)}), ...) | async-done | bytes 75497488 | tf_op jit(solution)/shard_map/psum | solution.py:73
  1360.3 16.5 slice_negate_fusion.2
  1376.8 16.5 fusion.94
  1393.3 37.5 %fusion.131 = (f32[8,1536]{1,0:T(8,128)S(1)}, f32[8,1536,1536]{1,2,0:T(8,128)}) fusion(pred[1536,1536]{0,1:T(8,128)(4,1)} %iota_compare_fusion, bf16[8,1536,192]{2,1,0:T(8,128)(2,1)} %get-tuple-element.51, bf16[8,1536,64]{2,1,0:T(8,128)(2,1)} %get-tuple-element.64, bf16[8,1536,192]{2,1,0:T(8,128)(2,1)} %get-tuple-element.50, ...), kind=kOutput, calls=%fused_computation.184 | convolution fusion | flops 9764340736 | bytes 90488832 | tf_op jit(solution)/shard_map/jvp()/sub | solution.py:39
  1430.8 51.5 %fusion.6 = (f32[8,1536]{1,0:T(8,128)S(1)}, bf16[8,1536,1536]{1,2,0:T(8,128)(2,1)}, bf16[8,1536,1536]{1,2,0:T(8,128)(2,1)}) fusion(f32[8,1536,1536]{1,2,0:T(8,128)} %get-tuple-element.76, f32[8,1536]{1,0:T(8,128)S(1)} %multiply_divide_fusion, f32[8,1536]{1,0:T(8,128)S(1)} %get-tuple-element.75, bf16[8,256,1536]{1,2,0:T(8,128)(2,1)} %get-tuple-element.42, ...), kind=kOutput, calls=%fused_computation.9 | convolution fusion | flops 9795784704 | bytes 163725312 | tf_op jit(solution)/shard_map/transpose(jvp(bhqk,bkhe->bqhe))/dot_general | solution.py:40
  1482.4 21.0 fusion.93
  1503.4 20.9 convert_bitcast_fusion.1
  1524.2 47.3 %bitcast_convert_fusion = f32[8,1536,1,256]{3,1,0,2:T(8,128)} fusion(bf16[8,1536,192]{2,1,0:T(8,128)(2,1)} %get-tuple-element.51, bf16[8,1536,64]{2,1,0:T(8,128)(2,1)} %get-tuple-element.64, f32[8,1536,1536]{1,2,0:T(8,128)} %get-tuple-element.76, bf16[8,1536,1536]{1,2,0:T(8,128)(2,1)} %get-tuple-element.77, f32[8,1536]{1,0:T(8,128)S(1)} %neg.39, ...), kind=kOutput, calls=%fused_computation.136 | convolution fusion | flops 9795796992 | bytes 134578176 | tf_op jit(solution)/shard_map/transpose(jvp(bqhe,bkhe->bhqk))/dot_general | solution.py:37
  1571.6 45.8 %bitcast_convert_fusion.1 = f32[8,1536,1,256]{3,1,0,2:T(8,128)} fusion(bf16[8,1536,192]{2,1,0:T(8,128)(2,1)} %get-tuple-element.50, bf16[8,1536,64]{2,1,0:T(8,128)(2,1)} %get-tuple-element.63, f32[8,1536,1536]{1,2,0:T(8,128)} %get-tuple-element.76, bf16[8,1536,1536]{1,2,0:T(8,128)(2,1)} %get-tuple-element.77, f32[8,1536]{1,0:T(8,128)S(1)} %neg.39, ...), kind=kOutput, calls=%fused_computation.137 | convolution fusion | flops 9795796992 | bytes 134578176 | tf_op jit(solution)/shard_map/transpose(jvp(bqhe,bkhe->bhqk))/dot_general | solution.py:37
  1617.4 12.4 split.32
  1640.0 12.3 split.36
  1652.4 128.9 %convert_reduce_fusion = (f32[1024]{0:T(1024)}, bf16[8,1536,1024]{2,1,0:T(8,128)(2,1)}, f32[8,1536,1024]{2,1,0:T(8,128)}) fusion(bf16[8,1536,1024]{2,1,0:T(8,128)(2,1)} %get-tuple-element.41, f32[1024]{0:T(1024)S(1)} %copy-done.13, bf16[8,1536,1024]{2,1,0:T(8,128)(2,1)} %get-tuple-element.40), kind=kLoop, calls=%fused_computation.56 | loop fusion | flops 994049024 | bytes 125837312 | tf_op jit(solution)/shard_map/reduce_sum | solution.py:91
  1781.2 32.8 %fusion.9 = bf16[8,1536,1024]{2,1,0:T(8,128)(2,1)} fusion(f32[8,1536,1024]{2,1,0:T(8,128)} %get-tuple-element.45, f32[1024]{0:T(1024)S(1)} %copy-done.13, bf16[8,1536,1024]{2,1,0:T(8,128)(2,1)} %get-tuple-element.40), kind=kLoop, calls=%fused_computation.19 | loop fusion | flops 88080384 | bytes 100667392 | tf_op jit(solution)/shard_map/jvp()/convert_element_type | solution.py:49
  1814.0 24.8 %convolution_convert_fusion.3 = bf16[8,1536,512]{2,1,0:T(8,128)(2,1)} fusion(bf16[8,1536,1024]{2,1,0:T(8,128)(2,1)} %get-tuple-element.44, bf16[512,1024]{1,0:T(8,128)(2,1)S(1)} %copy-done), kind=kOutput, calls=%fused_computation.107 | convolution fusion | flops 12891193344 | bytes 38797312 | tf_op jit(solution)/shard_map/bsf,df->bsd/dot_general | solution.py:93
  1838.8 11.4 fusion.129
  1850.2 11.5 fusion.130
  1861.7 13.1 fusion.90
  1874.9 18.6 pad_add_fusion.2
  1893.5 12.1 add_convert_fusion.3
  1913.3 26.2 %add_convert_fusion.2 = bf16[8,1536,512]{2,1,0:T(8,128)(2,1)} fusion(f32[8,1536,512]{2,1,0:T(8,128)} %fusion.90, bf16[8,1536,1024]{2,1,0:T(8,128)(2,1)} %fusion.9, bf16[1024,512]{1,0:T(8,128)(2,1)S(1)} %copy-done.31), kind=kOutput, calls=%fused_computation.96 | convolution fusion | flops 12897484800 | bytes 63963136 | tf_op jit(solution)/shard_map/bsf,fd->bsd/dot_general | solution.py:81
  1939.5 16.2 fusion.74
  1964.5 21.3 convolution_bitcast_fusion
  1985.8 20.2 fusion.96
  2006.1 20.9 fusion.99
  2026.9 302.2 %all-reduce.22.cloned.1.call-done = (bf16[8,1536,512]{2,1,0:T(8,128)(2,1)}, bf16[8,1536,512]{2,1,0:T(8,128)(2,1)}, bf16[8,1536,512]{2,1,0:T(8,128)(2,1)}) async-done(((bf16[8,1536,512]{2,1,0:T(8,128)(2,1)}, bf16[8,1536,512]{2,1,0:T(8,128)(2,1)}, bf16[8,1536,512]{2,1,0:T(8,128)(2,1)}), (bf16[8,1536,512]{2,1,0:T(8,128)(2,1)}, bf16[8,1536,512]{2,1,0:T(8,128)(2,1)}, ...) | async-done | bytes 37748752 | tf_op jit(solution)/shard_map/psum | solution.py:82
  2329.2 22.0 fusion.52
  2365.8 24.7 %all-reduce.20.cloned.1.call-done = f32[8,1536,2]{1,0,2:T(8,128)} async-done(((f32[8,1536,2]{1,0,2:T(8,128)}), f32[8,1536,2]{1,0,2:T(8,128)}) %all-reduce.20.cloned.1.call-update) | async-done | bytes 98320 | tf_op jit(solution)/shard_map/psum | solution.py:107
  2391.3 29.7 %convert_reduce_fusion.5 = (f32[512]{0:T(512)S(1)}, bf16[8,1536,512]{2,1,0:T(8,128)(2,1)}, bf16[8,1536,512]{2,1,0:T(8,128)(2,1)}) fusion(bf16[8,1536,512]{2,1,0:T(8,128)(2,1)} %param.15, f32[8,1536]{1,0:T(8,128)S(1)} %get-tuple-element.72, f32[8,1536]{1,0:T(8,128)S(1)} %copy-done.8, bf16[8,1536,512]{2,1,0:T(8,128)(2,1)} %param.14, ...), kind=kLoop, calls=%fused_computation.74 | loop fusion | flops 132120064 | bytes 88285184 | tf_op jit(solution)/shard_map/reduce_sum | solution.py:87
  (124 shorter events, 97.7 us)
Async XLA Ops:
  7.2 66.7 %copy-start = (bf16[512,1024]{1,0:T(8,128)(2,1)S(1)}, bf16[512,1024]{1,0:T(8,128)(2,1)}, u32[]{:S(2)}) copy-start(bf16[512,1024]{1,0:T(8,128)(2,1)} %param.24) | copy-start | bytes 3145732
  7.2 48.0 %all-reduce.18.cloned.1.call-start = ((), (), s32[]{:S(2)}) async-start(), calls=%async_computation | async-start | bytes 196608 | tf_op jit(solution)/shard_map/psum | solution.py:64
  15.8 20.6 copy-start.11
  15.8 31.3 %copy-start.25 = (bf16[512]{0:T(512)(128)(2,1)S(1)}, bf16[512]{0:T(512)(128)(2,1)}, u32[]{:S(2)}) copy-start(bf16[512]{0:T(512)(128)(2,1)} %param.16) | copy-start | bytes 3076
  15.8 31.3 %copy-start.26 = (bf16[512]{0:T(512)(128)(2,1)S(1)}, bf16[512]{0:T(512)(128)(2,1)}, u32[]{:S(2)}) copy-start(bf16[512]{0:T(512)(128)(2,1)} %param.18) | copy-start | bytes 3076
  15.8 31.4 %copy-start.27 = (bf16[512]{0:T(512)(128)(2,1)S(1)}, bf16[512]{0:T(512)(128)(2,1)}, u32[]{:S(2)}) copy-start(bf16[512]{0:T(512)(128)(2,1)} %param.17) | copy-start | bytes 3076
  15.9 31.4 %copy-start.28 = (bf16[512]{0:T(512)(128)(2,1)S(1)}, bf16[512]{0:T(512)(128)(2,1)}, u32[]{:S(2)}) copy-start(bf16[512]{0:T(512)(128)(2,1)} %param.19) | copy-start | bytes 3076
  15.9 40.2 %copy-start.32 = (bf16[512,1,768]{2,0,1:T(8,128)(2,1)S(1)}, bf16[512,1,768]{2,0,1:T(8,128)(2,1)}, u32[]{:S(2)}) copy-start(bf16[512,1,768]{2,0,1:T(8,128)(2,1)} %param.20) | copy-start | bytes 2359300
  15.9 1314.6 %all-reduce.24.cloned.1.call-start = ((), (), s32[]{:S(2)}) async-start(), calls=%async_computation.3 | async-start | bytes 150994944 | tf_op jit(solution)/shard_map/psum | solution.py:73
  47.2 26.6 %copy-start.14 = (f32[512]{0:T(512)}, f32[512]{0:T(512)S(1)}, u32[]{:S(2)}) copy-start(f32[512]{0:T(512)S(1)} %convert_element_type.177) | copy-start | bytes 6148
  47.2 26.6 %copy-start.16 = (f32[512]{0:T(512)}, f32[512]{0:T(512)S(1)}, u32[]{:S(2)}) copy-start(f32[512]{0:T(512)S(1)} %convert_element_type.190) | copy-start | bytes 6148
  47.2 26.6 %copy-start.21 = (f32[512]{0:T(512)}, f32[512]{0:T(512)S(1)}, u32[]{:S(2)}) copy-start(f32[512]{0:T(512)S(1)} %convert_element_type.178) | copy-start | bytes 6148
  47.3 26.5 %copy-start.23 = (f32[512]{0:T(512)}, f32[512]{0:T(512)S(1)}, u32[]{:S(2)}) copy-start(f32[512]{0:T(512)S(1)} %convert_element_type.191) | copy-start | bytes 6148
  94.7 2234.4 %all-reduce.22.cloned.1.call-start = ((), (), s32[]{:S(2)}) async-start(), calls=%async_computation.2 | async-start | bytes 75497472 | tf_op jit(solution)/shard_map/psum | solution.py:82
  99.3 1277.5 %copy-start.2 = (f32[1536,64]{1,0:T(8,128)}, f32[1536,64]{1,0:T(8,128)S(1)}, u32[]{:S(2)}) copy-start(f32[1536,64]{1,0:T(8,128)S(1)} %get-tuple-element.70) | copy-start | bytes 1179652
  99.3 1277.5 %copy-start.4 = (f32[1536,64]{1,0:T(8,128)}, f32[1536,64]{1,0:T(8,128)S(1)}, u32[]{:S(2)}) copy-start(f32[1536,64]{1,0:T(8,128)S(1)} %get-tuple-element.69) | copy-start | bytes 1179652
  1341.0 19.4 copy-start.1
  1503.4 20.9 copy-start.6
  1629.9 22.5 copy-start.13
  1838.8 23.0 copy-start.12
  1893.5 19.7 copy-start.31
  1913.3 26.2 %copy-start.33 = (bf16[512,1,768]{2,0,1:T(8,128)(2,1)S(1)}, bf16[512,1,768]{2,0,1:T(8,128)(2,1)}, u32[]{:S(2)}) copy-start(bf16[512,1,768]{2,0,1:T(8,128)(2,1)} %param.20) | copy-start | bytes 2359300
  1955.7 434.8 %all-reduce.20.cloned.1.call-start = ((), (), s32[]{:S(2)}) async-start(), calls=%async_computation.1 | async-start | bytes 196608 | tf_op jit(solution)/shard_map/psum | solution.py:107
  1964.4 21.3 copy-start.8
  1964.4 21.3 copy-start.10
  1964.5 21.3 copy-start.17
  1964.5 21.3 copy-start.24
  1964.5 41.5 %slice-start = ((s8[12582912]{0:T(1024)(128)(4,1)}), s8[4194304]{0:T(1024)(128)(4,1)S(1)}, s32[]{:S(2)}) async-start(s8[12582912]{0:T(1024)(128)(4,1)} %bitcast.115), calls=%async_computation.4 | async-start | bytes 8388608
  1964.5 41.5 %slice-start.1 = ((s8[12582912]{0:T(1024)(128)(4,1)}), s8[4194304]{0:T(1024)(128)(4,1)S(1)}, s32[]{:S(2)}) async-start(s8[12582912]{0:T(1024)(128)(4,1)} %bitcast.115), calls=%async_computation.5 | async-start | bytes 8388608
  1985.8 20.2 slice-start.2
  1985.8 20.2 copy-start.15
  1985.8 20.2 copy-start.22
  (14 other events, 129.3 us)
Sparse Core Ops, SparseCore 0:
  15.9 39.2 all-reduce.17
  94.8 1235.5 all-reduce.23
  1955.8 373.2 all-reduce.21
  2352.0 38.4 all-reduce.19
where the time goes:
time: 2440 us; the launch traced here: 2430 us
  waiting for transfers between devices  1560 us (64%)
  matrix products  447 us (18%)
  other arithmetic  361 us (15%)
  local copies, waits for them, and re-layouts  42 us (2%)
    psum x1, waiting for transfers between devices, body(): lax.psum(qkv_part, 'tx').astype(jnp.float32) + b_qkv.astype(jnp.float32)  1230 us
    psum x1, waiting for transfers between devices, body(): mixed = lax.psum((attn_part + down_part).astype(jnp.bfloat16), 'ty')  302 us
    reduce_sum x1, other arithmetic, body(): d_b_up = d_pre.astype(jnp.float32).sum((0, 1))  129 us
    dot_general x3, matrix products, attend_rows(): jnp.einsum('bhqk,bkhe->bqhe', probs, values, preferred_element_type=jnp.f...  93.4 us
    dot_general x2, matrix products, attend_rows(): jnp.einsum('bqhe,bkhe->bhqk', q_rot, k_rot, preferred_element_type=jnp.fl...  93.2 us
  transfers between devices with their start and end apart: 4, of which 4 were waited for; matrix products, arithmetic and copies ran while one was open for 5% of the time, Pallas kernels for 0%

commit v1 on v0

v1 whole, which is shorter than its diff:
```python
import functools
import jax
import jax.numpy as jnp
from jax import lax
from jax.experimental import pallas as pl
from jax.experimental.pallas import tpu as pltpu
from jax.sharding import PartitionSpec as P


LN_EPS = 1e-5
ROPE_BASE = 10000.0
ROTARY_DIVISOR = 4
LANES = 128
Q_ROWS = 256

NT = (((1,), (1,)), ((), ()))
TN = (((0,), (0,)), ((), ()))
NN = (((1,), (0,)), ((), ()))


def dot(a, b, dims):
    return lax.dot_general(a, b, dims, preferred_element_type=jnp.float32)


def rotary_tables(seq_len, rot_dim):
    half = rot_dim // 2
    lane = jnp.arange(LANES)
    freq_index = jnp.where(lane < half, lane, lane - half)
    inv_freq = ROPE_BASE ** (-(2 * freq_index).astype(jnp.float32) / rot_dim)
    angles = jnp.arange(seq_len, dtype=jnp.float32)[:, None] * inv_freq[None, :]
    inside = (lane < rot_dim)[None, :]
    cos_tab = jnp.where(inside, jnp.cos(angles), 1.0)
    sin = jnp.where(inside, jnp.sin(angles), 0.0)
    first = (lane < half)[None, :]
    return cos_tab, jnp.where(first, -sin, 0.0), jnp.where(first, 0.0, sin)


def rotate(part, cos_tab, sin_lo, sin_hi, half, sign):
    head = part[:, :LANES]
    forward = pltpu.roll(head, half, 1)
    backward = pltpu.roll(head, LANES - half, 1)
    mixed = head * cos_tab + sign * (backward * sin_lo + forward * sin_hi)
    return jnp.concatenate([mixed, part[:, LANES:]], axis=1)


def causal_probs(q_rows, keys, row_start, scale):
    scores = dot(q_rows, keys, NT) * scale
    rows = row_start + lax.broadcasted_iota(jnp.int32, scores.shape, 0)
    cols = lax.broadcasted_iota(jnp.int32, scores.shape, 1)
    scores = jnp.where(rows >= cols, scores, -1e30)
    exps = jnp.exp(scores - jnp.max(scores, axis=1, keepdims=True))
    return exps * (1.0 / jnp.sum(exps, axis=1, keepdims=True))


def attn_fwd_kernel(qkv_ref, cos_ref, lo_ref, hi_ref, ctx_ref, q_ref, k_ref, *, half, scale, span):
    seq_len, width = ctx_ref.shape[1:]

    @pl.loop(0, seq_len // Q_ROWS)
    def _(step):
        rows = pl.ds(pl.multiple_of(step * Q_ROWS, Q_ROWS), Q_ROWS)
        for out, col in ((q_ref, 0), (k_ref, width)):
            part = qkv_ref[0, rows, col:col + width].astype(jnp.float32)
            out[rows, :] = rotate(part, cos_ref[rows, :], lo_ref[rows, :], hi_ref[rows, :], half, 1.0).astype(jnp.bfloat16)

    for end in range(span, seq_len + 1, span):
        @pl.loop(0, span // Q_ROWS)
        def _(step, end=end):
            start = pl.multiple_of(end - span + step * Q_ROWS, Q_ROWS)
            rows = pl.ds(start, Q_ROWS)
            probs = causal_probs(q_ref[rows, :], k_ref[:end, :], start, scale).astype(jnp.bfloat16)
            ctx_ref[0, rows, :] = dot(probs, qkv_ref[0, :end, 2 * width:], NN).astype(jnp.bfloat16)


def attn_bwd_kernel(qkv_ref, dctx_ref, cos_ref, lo_ref, hi_ref, dqkv_ref, db_ref, q_ref, k_ref, dk_ref, dv_ref, *, half, scale, span):
    seq_len, width = dctx_ref.shape[1:]

    @pl.loop(0, seq_len // Q_ROWS)
    def _(step):
        rows = pl.ds(pl.multiple_of(step * Q_ROWS, Q_ROWS), Q_ROWS)
        for out, col in ((q_ref, 0), (k_ref, width)):
            part = qkv_ref[0, rows, col:col + width].astype(jnp.float32)
            out[rows, :] = rotate(part, cos_ref[rows, :], lo_ref[rows, :], hi_ref[rows, :], half, 1.0).astype(jnp.bfloat16)
        dk_ref[rows, :] = jnp.zeros((Q_ROWS, width), jnp.float32)
        dv_ref[rows, :] = jnp.zeros((Q_ROWS, width), jnp.float32)

    db_ref[...] = jnp.zeros(db_ref.shape, jnp.float32)

    def store(rows, col, grad_rot, turn):
        grad = grad_rot.astype(jnp.bfloat16)
        if turn:
            wide = grad.astype(jnp.float32)
            grad = rotate(wide, cos_ref[rows, :], lo_ref[rows, :], hi_ref[rows, :], half, -1.0).astype(jnp.bfloat16)
        dqkv_ref[0, rows, col:col + width] = grad
        db_ref[0, :, col:col + width] += jnp.sum(grad.astype(jnp.float32), axis=0, keepdims=True)

    for end in range(span, seq_len + 1, span):
        @pl.loop(0, span // Q_ROWS)
        def _(step, end=end):
            start = pl.multiple_of(end - span + step * Q_ROWS, Q_ROWS)
            rows = pl.ds(start, Q_ROWS)
            q_rows = q_ref[rows, :]
            dctx = dctx_ref[0, rows, :]
            probs = causal_probs(q_rows, k_ref[:end, :], start, scale)
            dprobs = dot(dctx, qkv_ref[0, :end, 2 * width:], NT).astype(jnp.bfloat16).astype(jnp.float32)
            dv_ref[:end, :] += dot(probs.astype(jnp.bfloat16), dctx, TN)
            inner = jnp.sum(probs * dprobs, axis=1, keepdims=True)
            dscores = (probs * (dprobs - inner) * scale).astype(jnp.bfloat16)
            dk_ref[:end, :] += dot(dscores, q_rows, TN)
            store(rows, 0, dot(dscores, k_ref[:end, :], NN), True)

    @pl.loop(0, seq_len // Q_ROWS)
    def _(step):
        rows = pl.ds(pl.multiple_of(step * Q_ROWS, Q_ROWS), Q_ROWS)
        store(rows, width, dk_ref[rows, :], True)
        store(rows, 2 * width, dv_ref[rows, :], False)


def attention_calls(n_seq, seq_len, width):
    half = width // ROTARY_DIVISOR // 2
    scale = width ** -0.5
    span = 512 if seq_len % 512 == 0 else seq_len
    tables = rotary_tables(seq_len, 2 * half)
    seq_spec = lambda cols: pl.BlockSpec((1, seq_len, cols), lambda s: (s, 0, 0))
    tab_spec = pl.BlockSpec((seq_len, LANES), lambda s: (0, 0))
    rot_scratch = pltpu.VMEM((seq_len, width), jnp.bfloat16)
    acc_scratch = pltpu.VMEM((seq_len, width), jnp.float32)
    pairs = n_seq * seq_len * seq_len // 2
    params = pltpu.CompilerParams(dimension_semantics=("arbitrary",), vmem_limit_bytes=56 * 1024 * 1024)
    forward = pl.pallas_call(
        functools.partial(attn_fwd_kernel, half=half, scale=scale, span=span),
        grid=(n_seq,),
        in_specs=[seq_spec(3 * width), tab_spec, tab_spec, tab_spec],
        out_specs=seq_spec(width),
        out_shape=jax.ShapeDtypeStruct((n_seq, seq_len, width), jnp.bfloat16),
        scratch_shapes=[rot_scratch, rot_scratch],
        compiler_params=params,
        name="attn_fwd",
        cost_estimate=pl.CostEstimate(flops=8 * pairs * width, bytes_accessed=8 * n_seq * seq_len * width, transcendentals=pairs),
    )
    backward = pl.pallas_call(
        functools.partial(attn_bwd_kernel, half=half, scale=scale, span=span),
        grid=(n_seq,),
        in_specs=[seq_spec(3 * width), seq_spec(width), tab_spec, tab_spec, tab_spec],
        out_specs=[seq_spec(3 * width), pl.BlockSpec((1, 1, 3 * width), lambda s: (s, 0, 0))],
        out_shape=[jax.ShapeDtypeStruct((n_seq, seq_len, 3 * width), jnp.bfloat16), jax.ShapeDtypeStruct((n_seq, 1, 3 * width), jnp.float32)],
        scratch_shapes=[rot_scratch, rot_scratch, acc_scratch, acc_scratch],
        compiler_params=params,
        name="attn_bwd",
        cost_estimate=pl.CostEstimate(flops=20 * pairs * width, bytes_accessed=14 * n_seq * seq_len * width, transcendentals=pairs),
    )
    return (lambda qkv: forward(qkv, *tables)), (lambda qkv, dctx: backward(qkv, dctx, *tables))


def copy_kernel(row_ref, in_ref, out_ref):
    out_ref[...] = in_ref[...]


def place_groups(full, row):
    groups, tokens, width = full.shape
    rows = tokens // 4
    return pl.pallas_call(
        copy_kernel,
        grid_spec=pltpu.PrefetchScalarGridSpec(
            num_scalar_prefetch=1,
            grid=(groups, tokens // rows),
            in_specs=[pl.BlockSpec((1, rows, width), lambda t, c, row_ref: (lax.rem(row_ref[0] + groups - t, groups), c, 0))],
            out_specs=pl.BlockSpec((1, rows, width), lambda t, c, row_ref: (t, c, 0)),
        ),
        out_shape=jax.ShapeDtypeStruct(full.shape, full.dtype),
        name="place_groups",
        cost_estimate=pl.CostEstimate(flops=full.size, bytes_accessed=4 * full.size, transcendentals=0),
    )(row.reshape(1), full)


def split_width(value, out_refs):
    width = out_refs[0].shape[1]
    for index, out_ref in enumerate(out_refs):
        out_ref[...] = value[:, index * width:(index + 1) * width].astype(out_ref.dtype)


def finish_y_kernel(x_ref, mixed_ref, bias_ref, *out_refs):
    split_width(x_ref[...].astype(jnp.float32) + mixed_ref[...].astype(jnp.float32) + bias_ref[...], out_refs)


def normalize(act):
    act = act.astype(jnp.float32)
    mean = act.mean(-1, keepdims=True)
    inv_std = lax.rsqrt((act * act).mean(-1, keepdims=True) - mean * mean + LN_EPS)
    return (act - mean) * inv_std, inv_std


def finish_dx_kernel(x_ref, a6_ref, cot_ref, *out_refs):
    x_hat, inv_std = normalize(x_ref[...])
    value_a6 = a6_ref[...].astype(jnp.float32)
    mean_a6 = value_a6.mean(-1, keepdims=True)
    mean_a6x = (value_a6 * x_hat).mean(-1, keepdims=True)
    split_width(cot_ref[...].astype(jnp.float32) + inv_std * (value_a6 - mean_a6 - x_hat * mean_a6x), out_refs)


def row_call(kernel, parts, *operands):
    n_rows, width = operands[0].shape
    rows = 128 if n_rows % 128 == 0 else n_rows
    specs = [pl.BlockSpec((rows, width), lambda s: (s, 0)) if op.shape[0] == n_rows else pl.BlockSpec(op.shape, lambda s: (0, 0)) for op in operands]
    return pl.pallas_call(
        kernel,
        grid=(n_rows // rows,),
        in_specs=specs,
        out_specs=[pl.BlockSpec((rows, width // parts), lambda s: (s, 0))] * parts,
        out_shape=[jax.ShapeDtypeStruct((n_rows, width // parts), jnp.bfloat16)] * parts,
        cost_estimate=pl.CostEstimate(flops=16 * n_rows * width, bytes_accessed=8 * n_rows * width, transcendentals=0),
    )(*operands)


def gelu_bf16(pre_act):
    return jax.nn.gelu(pre_act.astype(jnp.float32), approximate=False).astype(jnp.bfloat16)


def solution(mesh):
    tx_size, ty_size = mesh.shape['tx'], mesh.shape['ty']
    act_spec = P('dp', None, 'tx')
    width_spec = P('tx')
    in_specs = (act_spec, act_spec, width_spec, width_spec, width_spec, width_spec, P('tx', 'ty', None), P('ty', None), P('ty', 'tx'), width_spec, P('tx', 'ty'), P('ty'), P('ty', 'tx'), width_spec)
    width_out = P(('dp', 'tx'))
    out_specs = (act_spec, act_spec, width_out, width_out, width_out, width_out, P(('dp', 'tx'), 'ty', None), P(('dp', 'ty'), None), P(('dp', 'ty'), 'tx'), width_out, P(('dp', 'tx'), 'ty'), P(('dp', 'ty')), P(('dp', 'ty'), 'tx'), width_out)
    antipode = tx_size // 2

    def shift(value, hops):
        return lax.ppermute(value, 'tx', [(s, (s - hops) % tx_size) for s in range(tx_size)])

    def small_sum(value, axis, size):
        step = 1
        while step < size:
            value = value + lax.ppermute(value, axis, [(s, s ^ step) for s in range(size)])
            step *= 2
        return value

    def ring_gather(block):
        blocks = {0: block}
        for hops in range(1, antipode):
            blocks[hops] = shift(blocks[hops - 1], 1)
            blocks[tx_size - hops] = shift(blocks[(tx_size - hops + 1) % tx_size], -1)
        rows = block.shape[0] // 2
        blocks[antipode] = jnp.concatenate([shift(blocks[antipode - 1][:rows], 1), shift(blocks[antipode + 1][rows:], -1)], axis=0)
        return [blocks[r] for r in range(tx_size)]

    def ring_scatter(make_part, rows):
        half = rows // 2
        far_low = make_part(antipode, 0, half).astype(jnp.bfloat16)
        far_high = make_part(antipode, half, rows).astype(jnp.bfloat16)
        moving_up, moving_down = shift(far_low, -1), shift(far_high, 1)
        moving_up = jnp.pad(moving_up, ((0, rows - half), (0, 0)))
        moving_down = jnp.pad(moving_down, ((half, 0), (0, 0)))
        for hops in range(antipode - 1, 0, -1):
            up = make_part(hops, 0, rows) + moving_up.astype(jnp.float32)
            down = make_part(tx_size - hops, 0, rows) + moving_down.astype(jnp.float32)
            up, down = up.astype(jnp.bfloat16), down.astype(jnp.bfloat16)
            moving_up, moving_down = shift(up, -1), shift(down, 1)
        return lambda own, low, high: own + moving_up[low:high].astype(jnp.float32) + moving_down[low:high].astype(jnp.float32)

    def body(x_act, cot_out, ln1_gain, ln1_bias, ln2_gain, ln2_bias, w_qkv, b_qkv, w_dense, b_dense, w_up, b_up, w_down, b_down):
        batch, seq_len, d_local = x_act.shape
        n_seq = batch // tx_size
        own = n_seq * seq_len // ty_size
        row, col = lax.axis_index('tx'), lax.axis_index('ty')
        qkv_width = w_qkv.shape[1] * w_qkv.shape[2]
        head = qkv_width // 3
        attn_fwd, attn_bwd = attention_calls(n_seq, seq_len, head)

        def to_tokens(act):
            parts = act.reshape(tx_size, ty_size, own, d_local)
            pick = lambda index: lax.dynamic_slice(parts, (index, col, 0, 0), (1, 1, own, d_local)).reshape(own, d_local)
            return jnp.concatenate([pick(row)] + [shift(pick((row - r) % tx_size), r) for r in range(1, tx_size)], axis=1)

        def to_width(parts):
            blocks = [parts[0]] + [shift(parts[r], -r) for r in range(1, tx_size)]
            stacked = jnp.stack(blocks)
            full = lax.all_gather(stacked, 'ty', axis=1, tiled=True)
            return place_groups(full, row).reshape(batch, seq_len, d_local)

        x_own = to_tokens(x_act)
        small = ring_gather(jnp.stack([ln1_gain, ln1_bias, ln2_gain, ln2_bias, b_dense, b_down]))
        small = jnp.concatenate(small, axis=1).astype(jnp.float32)
        gain_attn, bias_attn, gain_mlp, bias_mlp = small[0], small[1], small[2], small[3]
        bias_out = small[4] + small[5]
        x_group = lax.all_gather(x_own, 'ty', axis=0, tiled=True)
        w_in = jnp.concatenate([w_qkv.reshape(d_local, qkv_width), w_up], axis=1)
        w_in = jnp.concatenate(ring_gather(w_in), axis=0)
        wq, wu = w_in[:, :qkv_width], w_in[:, qkv_width:]
        cot_own = to_tokens(cot_out)
        cot_group = lax.all_gather(cot_own, 'ty', axis=0, tiled=True)
        w_back = jnp.concatenate(ring_gather(jnp.concatenate([w_dense, w_down], axis=0)), axis=1)

        x_hat, _ = normalize(x_group)
        h_attn = (x_hat * gain_attn + bias_attn).astype(jnp.bfloat16)
        h_mlp = (x_hat * gain_mlp + bias_mlp).astype(jnp.bfloat16)
        qkv_act = (dot(h_attn, wq, NN) + b_qkv.reshape(-1).astype(jnp.float32)).astype(jnp.bfloat16)
        qkv_seq = qkv_act.reshape(n_seq, seq_len, qkv_width)
        context = attn_fwd(qkv_seq).reshape(-1, head)
        pre_act = (dot(h_mlp, wu, NN) + b_up.astype(jnp.float32)).astype(jnp.bfloat16)
        gelu_out, gelu_pullback = jax.vjp(gelu_bf16, pre_act)
        inner = jnp.concatenate([context, gelu_out], axis=1)
        y_part = dot(inner, w_back, NN).astype(jnp.bfloat16)
        mixed = lax.psum_scatter(y_part, 'ty', scatter_dimension=0, tiled=True)
        y_out = to_width(row_call(finish_y_kernel, tx_size, x_own, mixed, bias_out.reshape(1, -1)))

        d_gelu = dot(cot_group, w_back[head:], NT).astype(jnp.bfloat16)
        (d_pre,) = gelu_pullback(d_gelu)
        d_ctx = dot(cot_group, w_back[:head], NT).astype(jnp.bfloat16)
        d_qkv_seq, d_b_qkv = attn_bwd(qkv_seq, d_ctx.reshape(n_seq, seq_len, head))
        d_qkv = d_qkv_seq.reshape(-1, qkv_width)
        d_b_up = d_pre.astype(jnp.float32).sum(0)
        d_h_mlp = dot(d_pre, wu, NT).astype(jnp.bfloat16).astype(jnp.float32)
        d_h_attn = dot(d_qkv, wq, NT).astype(jnp.bfloat16).astype(jnp.float32)
        a6_part = (d_h_attn * gain_attn + d_h_mlp * gain_mlp).astype(jnp.bfloat16)
        value_a6 = lax.psum_scatter(a6_part, 'ty', scatter_dimension=0, tiled=True)
        dx_act = to_width(row_call(finish_dx_kernel, tx_size, x_own, value_a6, cot_own))

        d_ln = jnp.stack([(d_h_attn * x_hat).sum(0), d_h_attn.sum(0), (d_h_mlp * x_hat).sum(0), d_h_mlp.sum(0)])
        d_ln = small_sum(d_ln, 'ty', ty_size).reshape(4, tx_size, d_local)
        d_ln = d_ln[:, 0] + sum(shift(d_ln[:, r], -r) for r in range(1, tx_size))
        d_bias = small_sum(jnp.concatenate([d_b_qkv.sum((0, 1)), d_b_up])[None], 'tx', tx_size)[0]
        d_b_out = cot_out.astype(jnp.float32).sum((0, 1))

        cols = lambda act, r: act[:, r * d_local:(r + 1) * d_local]
        add_back = ring_scatter(lambda r, low, high: dot(inner[:, low:high], cols(cot_group, r), TN), inner.shape[1])
        add_up = ring_scatter(lambda r, low, high: dot(cols(h_mlp, r)[:, low:high], d_pre, TN), d_local)
        add_qkv = ring_scatter(lambda r, low, high: dot(cols(h_attn, r)[:, low:high], d_qkv, TN), d_local)
        d_w_dense = add_back(dot(context, cols(cot_group, 0), TN), 0, head)
        d_w_down = add_back(dot(gelu_out, cols(cot_group, 0), TN), head, inner.shape[1])
        d_w_up = add_up(dot(cols(h_mlp, 0), d_pre, TN), 0, d_local)
        d_w_qkv = add_qkv(dot(cols(h_attn, 0), d_qkv, TN), 0, d_local)
        return (y_out, dx_act, d_ln[0], d_ln[1], d_ln[2], d_ln[3], d_w_qkv.reshape(w_qkv.shape), d_bias[:qkv_width].reshape(b_qkv.shape), d_w_dense, d_b_out, d_w_up, d_bias[qkv_width:], d_w_down, d_b_out)

    return jax.shard_map(body, mesh=mesh, in_specs=in_specs, out_specs=out_specs, check_vma=False)
```

time: 2440 us -> 729 us (0.30)
  waiting for transfers between devices: 1560 us -> 234 us
  other arithmetic: 361 us -> 45.8 us
  matrix products: 447 us -> 238 us
  Pallas kernels: 0 us -> 83.4 us
  starting transfers between devices: 0.25 us -> 76.6 us
    psum x4 -> x0, waiting for transfers between devices: 1560 us -> none  [the longest x1 1230 us: body(): lax.psum(qkv_part, 'tx').astype(jnp.float32) + b_qkv.astype(jnp.float32)]
    ppermute x0 -> x44, waiting for transfers between devices: none -> 193 us  [the longest x39 187 us: shift(): lax.ppermute(value, 'tx', [(s, (s - hops) % tx_size) for s in range(tx_si...]
    reduce_sum x5 -> x3, other arithmetic: 196 us -> 15 us  [the longest x1 8.3 us: normalize(): mean = act.mean(-1, keepdims=True)]
    dot_general x17 -> x23, matrix products: 410 us -> 238 us  [dot(): return lax.dot_general(a, b, dims, preferred_element_type=jnp.float32)]
    pallas_call x0 -> x6, Pallas kernels: none -> 83.4 us  [the longest x2 30.3 us: place_groups(): pl.pallas_call(copy_kernel, grid_spec=pltpu.PrefetchScalarGridSpec(num_sc...]
    ppermute x0 -> x44, starting transfers between devices: none -> 76.2 us  [the longest x39 71.7 us: shift(): lax.ppermute(value, 'tx', [(s, (s - hops) % tx_size) for s in range(tx_si...]
    convert_element_type x9 -> x1, other arithmetic: 70.4 us -> 14.3 us  [body(): h_attn = (x_hat * gain_attn + bias_attn).astype(jnp.bfloat16)]
    reduce_scatter x0 -> x2, waiting for transfers between devices: none -> 41.4 us  [the longest x1 41.4 us: body(): value_a6 = lax.psum_scatter(a6_part, 'ty', scatter_dimension=0, tiled=True)]
  transfers between devices with their start and end apart: 4 -> 50, of which waited for: 4 -> 17; matrix products, arithmetic and copies ran while one was open for 5% -> 42% of each run, Pallas kernels for 0% -> 9%
where the time goes in v1:
time: 729 us; the launch traced here: 721 us
  matrix products  238 us (33%)
  waiting for transfers between devices  234 us (32%)
  Pallas kernels  83.4 us (11%)
  starting transfers between devices  76.6 us (11%)
  other arithmetic  45.8 us (6%)
  local copies, waits for them, and re-layouts  27.2 us (4%)
  between operations  15.7 us (2%)
    dot_general x23, matrix products, dot(): return lax.dot_general(a, b, dims, preferred_element_type=jnp.float32)  238 us
    ppermute x39, waiting for transfers between devices, shift(): lax.ppermute(value, 'tx', [(s, (s - hops) % tx_size) for s in range(tx_si...  187 us
    ppermute x39, starting transfers between devices, shift(): lax.ppermute(value, 'tx', [(s, (s - hops) % tx_size) for s in range(tx_si...  71.7 us
    reduce_scatter x1, waiting for transfers between devices, body(): value_a6 = lax.psum_scatter(a6_part, 'ty', scatter_dimension=0, tiled=True)  41.4 us
    pallas_call x2, Pallas kernels, place_groups(): pl.pallas_call(copy_kernel, grid_spec=pltpu.PrefetchScalarGridSpec(num_sc...  30.3 us
    pallas_call x1, Pallas kernels, attention_calls(): backward(qkv, dctx, *tables)  25.9 us
    pallas_call x1, Pallas kernels, attention_calls(): forward(qkv, *tables)  18.6 us
  transfers between devices with their start and end apart: 50, of which 17 were waited for; matrix products, arithmetic and copies ran while one was open for 42% of the time, Pallas kernels for 9%

profile of v1, /device:TPU:98, one launch (start us, length us, event | category | flops | bytes accessed | tf_op | source)
XLA Modules:
  0.0 720.9 jit_solution(413543137214408254)
XLA Ops:
  16.1 6.9 collective-permute-done.2
  23.0 9.6 %collective-permute-done.1 = bf16[384,512]{1,0:T(8,128)(2,1)S(1)} collective-permute-done((bf16[384,512]{1,0:T(8,128)(2,1)S(1)}, bf16[384,512]{1,0:T(8,128)(2,1)S(1)}, u32[]{:S(2)}, u32[]{:S(2)}) %collective-permute-start.1) | collective-permute-done | bytes 393248 | tf_op jit(solution)/shard_map/ppermute | solution.py:228
  45.4 37.5 %collective-permute-done.5 = bf16[6,512]{1,0:T(8,128)(2,1)S(1)} collective-permute-done((bf16[6,512]{1,0:T(8,128)(2,1)S(1)}, bf16[6,512]{1,0:T(8,128)(2,1)S(1)}, u32[]{:S(2)}, u32[]{:S(2)}) %collective-permute-start.5) | collective-permute-done | bytes 6176 | tf_op jit(solution)/shard_map/ppermute | solution.py:228
  86.3 23.6 %collective-permute-done.6 = bf16[3,512]{1,0:T(4,128)(2,1)S(1)} collective-permute-done((bf16[3,512]{1,0:T(4,128)(2,1)S(1)}, bf16[3,512]{1,0:T(4,128)(2,1)S(1)}, u32[]{:S(2)}, u32[]{:S(2)}) %collective-permute-start.6) | collective-permute-done | bytes 3104 | tf_op jit(solution)/shard_map/ppermute | solution.py:228
  117.2 12.4 %collective-permute-done.20 = bf16[384,512]{1,0:T(8,128)(2,1)S(1)} collective-permute-done((bf16[384,512]{1,0:T(8,128)(2,1)S(1)}, bf16[384,512]{1,0:T(8,128)(2,1)S(1)}, u32[]{:S(2)}, u32[]{:S(2)}) %collective-permute-start.20) | collective-permute-done | bytes 393248 | tf_op jit(solution)/shard_map/ppermute | solution.py:228
  130.6 19.1 %collective-permute-start.10 = (bf16[256,1792]{1,0:T(8,128)(2,1)}, bf16[256,1792]{1,0:T(8,128)(2,1)}, u32[]{:S(2)}, u32[]{:S(2)}) collective-permute-start(bf16[256,1792]{1,0:T(8,128)(2,1)} %slice.202), channel_id=1, source_target_pairs={{0,8},{8,16},{16,24},{24,0},{1,9},{9,17},{17,25},{25,1},{2,10},{10... | collective-permute-start | bytes 2752520 | tf_op jit(solution)/shard_map/ppermute | solution.py:228
  149.7 8.9 %collective-permute-done.18 = bf16[384,512]{1,0:T(8,128)(2,1)S(1)} collective-permute-done((bf16[384,512]{1,0:T(8,128)(2,1)S(1)}, bf16[384,512]{1,0:T(8,128)(2,1)S(1)}, u32[]{:S(2)}, u32[]{:S(2)}) %collective-permute-start.18) | collective-permute-done | bytes 393248 | tf_op jit(solution)/shard_map/ppermute | solution.py:228
  169.7 8.7 %collective-permute-done.8 = bf16[256,1792]{1,0:T(8,128)(2,1)} collective-permute-done((bf16[256,1792]{1,0:T(8,128)(2,1)S(1)}, bf16[256,1792]{1,0:T(8,128)(2,1)}, u32[]{:S(2)}, u32[]{:S(2)}) %collective-permute-start.8) | collective-permute-done | bytes 917536 | tf_op jit(solution)/shard_map/ppermute | solution.py:228
  184.2 8.3 %convert_reduce_fusion.2 = (f32[3072]{0:T(1024)S(1)}, f32[3072]{0:T(1024)S(1)}) fusion(bf16[3072,2048]{1,0:T(8,128)(2,1)} %all-gather.5.cloned.1.call-done), kind=kLoop, calls=%fused_computation.8 | loop fusion | flops 25159680 | bytes 12607488 | tf_op jit(solution)/shard_map/reduce_sum | solution.py:187
  192.6 14.3 %fusion.4 = (bf16[3072,2048]{1,0:T(8,128)(2,1)}, bf16[3072,2048]{1,0:T(8,128)(2,1)S(1)}) fusion(bf16[3072,2048]{1,0:T(8,128)(2,1)} %all-gather.5.cloned.1.call-done, f32[2048]{0:T(1024)S(1)} %bitcast.119, f32[2048]{0:T(1024)S(1)} %bitcast.114, f32[3072]{0:T(1024)S(1)} %get-tuple-element.75, f32[3072]{0:T(1024)S(1)} %get-tuple-element.74, ...), kind=kLoop, calls=%fused_computation.13 | loop fusion | flops 56623104 | bytes 37806080 | tf_op jit(solution)/shard_map/convert_element_type | solution.py:294
  206.9 42.1 %fusion.13 = (bf16[3072,1024]{1,0:T(8,128)(2,1)}, f32[3072,1024]{1,0:T(8,128)}, bf16[3072,1024]{1,0:T(8,128)(2,1)}) fusion(f32[1024]{0:T(1024)S(1)} %convert_element_type.178, bf16[3072,2048]{1,0:T(8,128)(2,1)S(1)} %get-tuple-element.58, bf16[2048,1792]{1,0:T(8,128)(2,1)S(1)} %copy-done.6), kind=kOutput, calls=%fused_computation.28 | convolution fusion | flops 13098811392 | bytes 41947136 | tf_op jit(solution)/shard_map/dot_general | solution.py:22
  249.1 14.5 %add_convert_fusion.1 = bf16[3072,768]{1,0:T(8,128)(2,1)} fusion(bf16[3072,2048]{1,0:T(8,128)(2,1)} %get-tuple-element.57, f32[768]{0:T(1024)S(1)} %convert_reduce_fusion.5, bf16[2048,1792]{1,0:T(8,128)(2,1)S(1)} %copy-done.6), kind=kOutput, calls=%fused_computation.70 | convolution fusion | flops 9668395008 | bytes 20451328 | tf_op jit(solution)/shard_map/dot_general | solution.py:22
  263.6 18.6 %attn_fwd.1 = bf16[2,1536,256]{2,1,0:T(8,128)(2,1)} custom-call(bf16[2,1536,768]{2,1,0:T(8,128)(2,1)} %bitcast.140, f32[1536,128]{1,0:T(8,128)} %get-tuple-element.82.cos_ref, f32[1536,128]{1,0:T(8,128)} %get-tuple-element.81.lo_ref, f32[1536,128]{1,0:T(8,128)} %get-tuple-element.80.hi_ref), custom_call_target="tpu_custom_call" | custom-call | flops 4831838208 | bytes 6291456 | tf_op jit(solution)/shard_map/attn_fwd/pallas_call | solution.py:151
  282.1 23.0 %convolution_convert_fusion.2 = bf16[3072,2048]{1,0:T(8,128)(2,1)} fusion(bf16[1280,512]{1,0:T(8,128)(2,1)} %collective-permute-done.13, bf16[640,512]{1,0:T(8,128)(2,1)} %collective-permute-done.14, bf16[640,512]{1,0:T(8,128)(2,1)} %collective-permute-done.12, bf16[1280,512]{1,0:T(8,128)(2,1)} %collective-permute-done.11, ...), kind=kOutput, calls=%fused_computation.69 | convolution fusion | flops 16154361856 | bytes 25690112 | tf_op jit(solution)/shard_map/dot_general | solution.py:22
  305.3 9.4 %convolution_convert_fusion.3 = bf16[3072,256]{1,0:T(8,128)(2,1)} fusion(bf16[3072,2048]{1,0:T(8,128)(2,1)} %all-gather.9.cloned.1.call-done, bf16[1280,512]{1,0:T(8,128)(2,1)} %collective-permute-done.13, bf16[640,512]{1,0:T(8,128)(2,1)} %collective-permute-done.14, bf16[640,512]{1,0:T(8,128)(2,1)} %collective-permute-done.12, ...), kind=kOutput, calls=%fused_computation.96 | convolution fusion | flops 3227254784 | bytes 19398656 | tf_op jit(solution)/shard_map/dot_general | solution.py:22
  314.7 25.9 %attn_bwd.1 = (bf16[2,1536,768]{2,1,0:T(8,128)(2,1)}, f32[2,1,768]{2,1,0:T(1,128)}) custom-call(bf16[2,1536,768]{2,1,0:T(8,128)(2,1)} %bitcast.141, bf16[2,1536,256]{2,1,0:T(8,128)(2,1)} %bitcast.147, f32[1536,128]{1,0:T(8,128)} %get-tuple-element.82.cos_ref, f32[1536,128]{1,0:T(8,128)} %get-tuple-element.81.lo_ref, f32[1536,128]{1,0:T(8,128)} %get-tuple-element.80.hi_ref), custom_call_target="tpu_custom_call" | custom-call | flops 12079595520 | bytes 11010048 | tf_op jit(solution)/shard_map/attn_bwd/pallas_call | solution.py:151
  340.5 26.4 %convert_reduce_fusion.4 = (f32[1024]{0:T(1024)S(1)}, bf16[3072,1024]{1,0:T(8,128)(2,1)S(1)}) fusion(f32[3072,1024]{1,0:T(8,128)} %get-tuple-element.55, bf16[3072,2048]{1,0:T(8,128)(2,1)} %all-gather.9.cloned.1.call-done, bf16[1280,512]{1,0:T(8,128)(2,1)} %collective-permute-done.13, bf16[640,512]{1,0:T(8,128)(2,1)} %collective-permute-done.14, ...), kind=kOutput, calls=%fused_computation.65 | convolution fusion | flops 12965641216 | bytes 42995712 | tf_op jit(solution)/shard_map/dot_general | solution.py:22
  367.0 20.4 %convolution_convert_fusion = bf16[3072,2048]{1,0:T(8,128)(2,1)} fusion(bf16[3072,1024]{1,0:T(8,128)(2,1)S(1)} %get-tuple-element.85, bf16[2048,1792]{1,0:T(8,128)(2,1)} %constant_dynamic-update-slice_fusion), kind=kOutput, calls=%fused_computation.67 | convolution fusion | flops 12891193344 | bytes 23068672 | tf_op jit(solution)/shard_map/dot_general | solution.py:22
  387.4 22.1 %fusion.10 = (f32[2048]{0:T(1024)S(1)}, f32[2048]{0:T(1024)S(1)}, f32[2048]{0:T(1024)S(1)}, f32[2048]{0:T(1024)S(1)}, bf16[3072,2048]{1,0:T(8,128)(2,1)}) fusion(bf16[3072,2048]{1,0:T(8,128)(2,1)} %all-gather.5.cloned.1.call-done, f32[3072]{0:T(1024)S(1)} %copy-done.17, f32[3072]{0:T(1024)S(1)} %copy-done.15, ...), kind=kOutput, calls=%fused_computation.19 | convolution fusion | flops 9764331520 | bytes 45686784 | tf_op jit(solution)/shard_map/dot_general | solution.py:22
  417.9 14.5 %collective-permute-done.15 = bf16[384,512]{1,0:T(8,128)(2,1)S(1)} collective-permute-done((bf16[384,512]{1,0:T(8,128)(2,1)}, bf16[384,512]{1,0:T(8,128)(2,1)S(1)}, u32[]{:S(2)}, u32[]{:S(2)}) %collective-permute-start.15) | collective-permute-done | bytes 393248 | tf_op jit(solution)/shard_map/ppermute | solution.py:228
  435.4 41.4 %reduce-scatter.5.cloned.1.call-done.a6_ref = bf16[384,2048]{1,0:T(8,128)(2,1)} async-done(((bf16[3072,2048]{1,0:T(8,128)(2,1)}), bf16[384,2048]{1,0:T(8,128)(2,1)}) %reduce-scatter.5.cloned.1.call-update) | async-done | bytes 1572880 | tf_op jit(solution)/shard_map/reduce_scatter | solution.py:315
  487.7 7.1 collective-permute-done.21
  494.9 9.9 %collective-permute-done.22 = bf16[384,512]{1,0:T(8,128)(2,1)S(1)} collective-permute-done((bf16[384,512]{1,0:T(8,128)(2,1)}, bf16[384,512]{1,0:T(8,128)(2,1)S(1)}, u32[]{:S(2)}, u32[]{:S(2)}) %collective-permute-start.22) | collective-permute-done | bytes 393248 | tf_op jit(solution)/shard_map/ppermute | solution.py:228
  507.2 6.7 convert_reduce_fusion.3
  541.1 6.7 fusion.80
  592.6 7.8 %fusion.93 = bf16[1280,512]{1,0:T(8,128)(2,1)S(1)} fusion(bf16[3072,2048]{1,0:T(8,128)(2,1)S(1)} %bitcast.129, bf16[3072,1024]{1,0:T(8,128)(2,1)} %get-tuple-element.54, bf16[3072,256]{1,0:T(8,128)(2,1)} %bitcast.143, bf16[640,512]{1,0:T(8,128)(2,1)} %collective-permute-done.38), kind=kOutput, calls=%fused_computation.116 | convolution fusion | flops 4044226560 | bytes 12976128 | tf_op jit(solution)/shard_map/dot_general | solution.py:22
  602.2 7.0 fusion.90
  612.9 7.9 %collective-permute-done.33 = bf16[512,768]{1,0:T(8,128)(2,1)S(1)} collective-permute-done((bf16[512,768]{1,0:T(8,128)(2,1)S(1)}, bf16[512,768]{1,0:T(8,128)(2,1)S(1)}, u32[]{:S(2)}, u32[]{:S(2)}) %collective-permute-start.33) | collective-permute-done | bytes 786464 | tf_op jit(solution)/shard_map/ppermute | solution.py:228
  634.9 18.6 %collective-permute-done.41 = bf16[512,1024]{1,0:T(8,128)(2,1)S(1)} collective-permute-done((bf16[512,1024]{1,0:T(8,128)(2,1)}, bf16[512,1024]{1,0:T(8,128)(2,1)S(1)}, u32[]{:S(2)}, u32[]{:S(2)}) %collective-permute-start.41) | collective-permute-done | bytes 1048608 | tf_op jit(solution)/shard_map/ppermute | solution.py:228
  655.4 20.8 %collective-permute-done.37 = bf16[1280,512]{1,0:T(8,128)(2,1)S(1)} collective-permute-done((bf16[1280,512]{1,0:T(8,128)(2,1)S(1)}, bf16[1280,512]{1,0:T(8,128)(2,1)S(1)}, u32[]{:S(2)}, u32[]{:S(2)}) %collective-permute-start.37) | collective-permute-done | bytes 1310752 | tf_op jit(solution)/shard_map/ppermute | solution.py:228
  682.7 15.1 %place_groups.2 = bf16[4,3072,512]{2,1,0:T(8,128)(2,1)} custom-call(s32[1]{0:T(128)} %bitcast.row_ref, bf16[4,3072,512]{2,1,0:T(8,128)(2,1)} %all-gather.7.cloned.1.call-done.in_ref), custom_call_target="tpu_custom_call" | custom-call | flops 6291456 | bytes 25165824 | tf_op jit(solution)/shard_map/place_groups/pallas_call | solution.py:161
  697.9 15.1 %place_groups.3 = bf16[4,3072,512]{2,1,0:T(8,128)(2,1)} custom-call(s32[1]{0:T(128)} %bitcast.row_ref, bf16[4,3072,512]{2,1,0:T(8,128)(2,1)} %all-gather.11.cloned.1.call-done.in_ref), custom_call_target="tpu_custom_call" | custom-call | flops 6291456 | bytes 25165824 | tf_op jit(solution)/shard_map/place_groups/pallas_call | solution.py:161
  (293 shorter events, 175.1 us)
Async XLA Ops:
  7.3 176.9 %all-gather.5.cloned.1.call-start = ((), (), s32[]{:S(2)}) async-start(), calls=%async_computation.2 | async-start | bytes 14155776 | tf_op jit(solution)/shard_map/all_gather | solution.py:285
  34.0 271.3 %all-gather.9.cloned.1.call-start = ((), (), s32[]{:S(2)}) async-start(), calls=%async_computation.5 | async-start | bytes 14155776 | tf_op jit(solution)/shard_map/all_gather | solution.py:290
  36.2 75.7 %collective-permute-start.7 = (bf16[512,1792]{1,0:T(8,128)(2,1)}, bf16[512,1792]{1,0:T(8,128)(2,1)}, u32[]{:S(2)}, u32[]{:S(2)}) collective-permute-start(bf16[512,1792]{1,0:T(8,128)(2,1)} %get-tuple-element.67), channel_id=1, source_target_pairs={{0,24},{8,0},{16,8},{24,16},{1,25},{9,1},{17,9},{25,17},{2,26},{10... | collective-permute-start | bytes 5505032 | tf_op jit(solution)/shard_map/ppermute | solution.py:228
  38.4 91.2 %collective-permute-start.9 = (bf16[512,1792]{1,0:T(8,128)(2,1)}, bf16[512,1792]{1,0:T(8,128)(2,1)S(1)}, u32[]{:S(2)}, u32[]{:S(2)}) collective-permute-start(bf16[512,1792]{1,0:T(8,128)(2,1)} %get-tuple-element.67), channel_id=1, source_target_pairs={{0,8},{8,16},{16,24},{24,0},{1,9},{9,17},{17,25},{25,1},{2,10},{10... | collective-permute-start | bytes 5505032 | tf_op jit(solution)/shard_map/ppermute | solution.py:228
  38.5 44.3 %collective-permute-start.5 = (bf16[6,512]{1,0:T(8,128)(2,1)S(1)}, bf16[6,512]{1,0:T(8,128)(2,1)S(1)}, u32[]{:S(2)}, u32[]{:S(2)}) collective-permute-start(bf16[6,512]{1,0:T(8,128)(2,1)S(1)} %stack.72), channel_id=1, source_target_pairs={{0,8},{8,16},{16,24},{24,0},{1,9},{9,17},{17,25},{25,1},{2,10},{10... | collective-permute-start | bytes 18440 | tf_op jit(solution)/shard_map/ppermute | solution.py:228
  39.7 43.3 %collective-permute-start.3 = (bf16[6,512]{1,0:T(8,128)(2,1)S(1)}, bf16[6,512]{1,0:T(8,128)(2,1)S(1)}, u32[]{:S(2)}, u32[]{:S(2)}) collective-permute-start(bf16[6,512]{1,0:T(8,128)(2,1)S(1)} %stack.72), channel_id=1, source_target_pairs={{0,24},{8,0},{16,8},{24,16},{1,25},{9,1},{17,9},{25,17},{2,26},{10... | collective-permute-start | bytes 18440 | tf_op jit(solution)/shard_map/ppermute | solution.py:228
  43.7 116.4 %collective-permute-start.13 = (bf16[1280,512]{1,0:T(8,128)(2,1)}, bf16[1280,512]{1,0:T(8,128)(2,1)}, u32[]{:S(2)}, u32[]{:S(2)}) collective-permute-start(bf16[1280,512]{1,0:T(8,128)(2,1)} %constant_dynamic-update-slice_fusion.5), channel_id=1, source_target_pairs={{0,8},{8,16},{16,24},{24,0},{1,9},{9,17},{17,25},{25,1},{2,10},{10... | collective-permute-start | bytes 3932168 | tf_op jit(solution)/shard_map/ppermute | solution.py:228
  82.9 27.0 %collective-permute-start.6 = (bf16[3,512]{1,0:T(4,128)(2,1)S(1)}, bf16[3,512]{1,0:T(4,128)(2,1)S(1)}, u32[]{:S(2)}, u32[]{:S(2)}) collective-permute-start(bf16[3,512]{1,0:T(4,128)(2,1)S(1)} %slice.200), channel_id=1, source_target_pairs={{0,8},{8,16},{16,24},{24,0},{1,9},{9,17},{17,25},{25,1},{2,10},{10... | collective-permute-start | bytes 9224 | tf_op jit(solution)/shard_map/ppermute | solution.py:228
  83.0 26.9 %collective-permute-start.4 = (bf16[3,512]{1,0:T(4,128)(2,1)S(1)}, bf16[3,512]{1,0:T(4,128)(2,1)S(1)}, u32[]{:S(2)}, u32[]{:S(2)}) collective-permute-start(bf16[3,512]{1,0:T(4,128)(2,1)S(1)} %slice.199), channel_id=1, source_target_pairs={{0,24},{8,0},{16,8},{24,16},{1,25},{9,1},{17,9},{25,17},{2,26},{10... | collective-permute-start | bytes 9224 | tf_op jit(solution)/shard_map/ppermute | solution.py:228
  109.9 51.5 %collective-permute-start.11 = (bf16[1280,512]{1,0:T(8,128)(2,1)}, bf16[1280,512]{1,0:T(8,128)(2,1)}, u32[]{:S(2)}, u32[]{:S(2)}) collective-permute-start(bf16[1280,512]{1,0:T(8,128)(2,1)} %constant_dynamic-update-slice_fusion.5), channel_id=1, source_target_pairs={{0,24},{8,0},{16,8},{24,16},{1,25},{9,1},{17,9},{25,17},{2,26},{10... | collective-permute-start | bytes 3932168 | tf_op jit(solution)/shard_map/ppermute | solution.py:228
  129.5 29.1 %collective-permute-start.18 = (bf16[384,512]{1,0:T(8,128)(2,1)S(1)}, bf16[384,512]{1,0:T(8,128)(2,1)S(1)}, u32[]{:S(2)}, u32[]{:S(2)}) collective-permute-start(bf16[384,512]{1,0:T(8,128)(2,1)S(1)} %get-tuple-element.62), channel_id=1, source_target_pairs={{0,24},{8,0},{16,8},{24,16},{1,25},{9,1},{17,9},{25,17},{2,26},{10... | collective-permute-start | bytes 1179656 | tf_op jit(solution)/shard_map/ppermute | solution.py:228
  129.5 48.8 %collective-permute-start.8 = (bf16[256,1792]{1,0:T(8,128)(2,1)S(1)}, bf16[256,1792]{1,0:T(8,128)(2,1)}, u32[]{:S(2)}, u32[]{:S(2)}) collective-permute-start(bf16[256,1792]{1,0:T(8,128)(2,1)S(1)} %slice.201), channel_id=1, source_target_pairs={{0,24},{8,0},{16,8},{24,16},{1,25},{9,1},{17,9},{25,17},{2,26},{10... | collective-permute-start | bytes 2752520 | tf_op jit(solution)/shard_map/ppermute | solution.py:228
  130.6 50.0 %collective-permute-start.10 = (bf16[256,1792]{1,0:T(8,128)(2,1)}, bf16[256,1792]{1,0:T(8,128)(2,1)}, u32[]{:S(2)}, u32[]{:S(2)}) collective-permute-start(bf16[256,1792]{1,0:T(8,128)(2,1)} %slice.202), channel_id=1, source_target_pairs={{0,8},{8,16},{16,24},{24,0},{1,9},{9,17},{17,25},{25,1},{2,10},{10... | collective-permute-start | bytes 2752520 | tf_op jit(solution)/shard_map/ppermute | solution.py:228
  160.0 250.9 %reduce-scatter.3.cloned.1.call-start = ((), (), s32[]{:S(2)}) async-start(), calls=%async_computation.3 | async-start | bytes 14155776 | tf_op jit(solution)/shard_map/reduce_scatter | solution.py:303
  161.3 120.9 %collective-permute-start.14 = (bf16[640,512]{1,0:T(8,128)(2,1)S(1)}, bf16[640,512]{1,0:T(8,128)(2,1)}, u32[]{:S(2)}, u32[]{:S(2)}) collective-permute-start(bf16[640,512]{1,0:T(8,128)(2,1)S(1)} %slice.206), channel_id=1, source_target_pairs={{0,8},{8,16},{16,24},{24,0},{1,9},{9,17},{17,25},{25,1},{2,10},{10... | collective-permute-start | bytes 1966088 | tf_op jit(solution)/shard_map/ppermute | solution.py:228
  163.4 118.7 %collective-permute-start.12 = (bf16[640,512]{1,0:T(8,128)(2,1)}, bf16[640,512]{1,0:T(8,128)(2,1)}, u32[]{:S(2)}, u32[]{:S(2)}) collective-permute-start(bf16[640,512]{1,0:T(8,128)(2,1)} %slice.205), channel_id=1, source_target_pairs={{0,24},{8,0},{16,8},{24,16},{1,25},{9,1},{17,9},{25,17},{2,26},{10... | collective-permute-start | bytes 1966088 | tf_op jit(solution)/shard_map/ppermute | solution.py:228
  305.2 171.6 %reduce-scatter.5.cloned.1.call-start = ((), (), s32[]{:S(2)}) async-start(), calls=%async_computation.6 | async-start | bytes 14155776 | tf_op jit(solution)/shard_map/reduce_scatter | solution.py:315
  409.6 273.1 %all-gather.7.cloned.1.call-start = ((), (), s32[]{:S(2)}) async-start(), calls=%async_computation.4 | async-start | bytes 14155776 | tf_op jit(solution)/shard_map/all_gather | solution.py:277
  435.4 262.5 %all-gather.11.cloned.1.call-start = ((), (), s32[]{:S(2)}) async-start(), calls=%async_computation.7 | async-start | bytes 14155776 | tf_op jit(solution)/shard_map/all_gather | solution.py:277
  517.6 46.3 %collective-permute-start.30 = (bf16[256,768]{1,0:T(8,128)(2,1)}, bf16[256,768]{1,0:T(8,128)(2,1)}, u32[]{:S(2)}, u32[]{:S(2)}) collective-permute-start(bf16[256,768]{1,0:T(8,128)(2,1)} %fusion.136), channel_id=1, source_target_pairs={{0,8},{8,16},{16,24},{24,0},{1,9},{9,17},{17,25},{25,1},{2,10},{10... | collective-permute-start | bytes 1179656 | tf_op jit(solution)/shard_map/ppermute | solution.py:228
  524.9 45.8 %collective-permute-start.32 = (bf16[256,768]{1,0:T(8,128)(2,1)}, bf16[256,768]{1,0:T(8,128)(2,1)}, u32[]{:S(2)}, u32[]{:S(2)}) collective-permute-start(bf16[256,768]{1,0:T(8,128)(2,1)} %fusion.139), channel_id=1, source_target_pairs={{0,24},{8,0},{16,8},{24,16},{1,25},{9,1},{17,9},{25,17},{2,26},{10... | collective-permute-start | bytes 1179656 | tf_op jit(solution)/shard_map/ppermute | solution.py:228
  548.4 29.3 %collective-permute-start.42 = (bf16[256,1024]{1,0:T(8,128)(2,1)S(1)}, bf16[256,1024]{1,0:T(8,128)(2,1)S(1)}, u32[]{:S(2)}, u32[]{:S(2)}) collective-permute-start(bf16[256,1024]{1,0:T(8,128)(2,1)S(1)} %fusion.133), channel_id=1, source_target_pairs={{0,24},{8,0},{16,8},{24,16},{1,25},{9,1},{17,9},{25,17},{2,26},{10... | collective-permute-start | bytes 1572872 | tf_op jit(solution)/shard_map/ppermute | solution.py:228
  554.4 29.1 %collective-permute-start.40 = (bf16[256,1024]{1,0:T(8,128)(2,1)S(1)}, bf16[256,1024]{1,0:T(8,128)(2,1)}, u32[]{:S(2)}, u32[]{:S(2)}) collective-permute-start(bf16[256,1024]{1,0:T(8,128)(2,1)S(1)} %fusion.130), channel_id=1, source_target_pairs={{0,8},{8,16},{16,24},{24,0},{1,9},{9,17},{17,25},{25,1},{2,10},{10... | collective-permute-start | bytes 1572872 | tf_op jit(solution)/shard_map/ppermute | solution.py:228
  560.7 29.4 %collective-permute-start.38 = (bf16[640,512]{1,0:T(8,128)(2,1)S(1)}, bf16[640,512]{1,0:T(8,128)(2,1)}, u32[]{:S(2)}, u32[]{:S(2)}) collective-permute-start(bf16[640,512]{1,0:T(8,128)(2,1)S(1)} %fusion.125), channel_id=1, source_target_pairs={{0,24},{8,0},{16,8},{24,16},{1,25},{9,1},{17,9},{25,17},{2,26},{10... | collective-permute-start | bytes 1966088 | tf_op jit(solution)/shard_map/ppermute | solution.py:228
  563.9 36.5 %collective-permute-start.36 = (bf16[640,512]{1,0:T(8,128)(2,1)S(1)}, bf16[640,512]{1,0:T(8,128)(2,1)S(1)}, u32[]{:S(2)}, u32[]{:S(2)}) collective-permute-start(bf16[640,512]{1,0:T(8,128)(2,1)S(1)} %copy-done.36), channel_id=1, source_target_pairs={{0,8},{8,16},{16,24},{24,0},{1,9},{9,17},{17,25},{25,1},{2,10},{10... | collective-permute-start | bytes 1966088 | tf_op jit(solution)/shard_map/ppermute | solution.py:228
  570.6 38.6 %collective-permute-start.35 = (f32[1,1792]{1,0:T(1,128)S(1)}, f32[1,1792]{1,0:T(1,128)S(1)}, u32[]{:S(2)}, u32[]{:S(2)}) collective-permute-start(f32[1,1792]{1,0:T(1,128)S(1)} %reshape_add_fusion), channel_id=1, source_target_pairs={{0,16},{8,24},{16,0},{24,8},{1,17},{9,25},{17,1},{25,9},{2,18},{10... | collective-permute-start | bytes 21512 | tf_op jit(solution)/shard_map/ppermute | solution.py:233
  577.8 31.9 %collective-permute-start.28 = (f32[4,512]{1,0:T(4,128)S(1)}, f32[4,512]{1,0:T(4,128)S(1)}, u32[]{:S(2)}, u32[]{:S(2)}) collective-permute-start(f32[4,512]{1,0:T(4,128)S(1)} %get-tuple-element.69), channel_id=1, source_target_pairs={{0,16},{8,24},{16,0},{24,8},{1,17},{9,25},{17,1},{25,9},{2,18},{10... | collective-permute-start | bytes 24584 | tf_op jit(solution)/shard_map/ppermute | solution.py:228
  583.5 26.3 %collective-permute-start.27 = (f32[4,512]{1,0:T(4,128)S(1)}, f32[4,512]{1,0:T(4,128)S(1)}, u32[]{:S(2)}, u32[]{:S(2)}) collective-permute-start(f32[4,512]{1,0:T(4,128)S(1)} %get-tuple-element.70), channel_id=1, source_target_pairs={{0,8},{8,16},{16,24},{24,0},{1,9},{9,17},{17,25},{25,1},{2,10},{10... | collective-permute-start | bytes 24584 | tf_op jit(solution)/shard_map/ppermute | solution.py:228
  609.7 43.8 %collective-permute-start.41 = (bf16[512,1024]{1,0:T(8,128)(2,1)}, bf16[512,1024]{1,0:T(8,128)(2,1)S(1)}, u32[]{:S(2)}, u32[]{:S(2)}) collective-permute-start(bf16[512,1024]{1,0:T(8,128)(2,1)} %add_convert_fusion.3), channel_id=1, source_target_pairs={{0,8},{8,16},{16,24},{24,0},{1,9},{9,17},{17,25},{25,1},{2,10},{10... | collective-permute-start | bytes 3145736 | tf_op jit(solution)/shard_map/ppermute | solution.py:228
  609.8 43.7 %collective-permute-start.43 = (bf16[512,1024]{1,0:T(8,128)(2,1)}, bf16[512,1024]{1,0:T(8,128)(2,1)S(1)}, u32[]{:S(2)}, u32[]{:S(2)}) collective-permute-start(bf16[512,1024]{1,0:T(8,128)(2,1)} %add_convert_fusion.2), channel_id=1, source_target_pairs={{0,24},{8,0},{16,8},{24,16},{1,25},{9,1},{17,9},{25,17},{2,26},{10... | collective-permute-start | bytes 3145736 | tf_op jit(solution)/shard_map/ppermute | solution.py:228
  612.9 63.2 %collective-permute-start.37 = (bf16[1280,512]{1,0:T(8,128)(2,1)S(1)}, bf16[1280,512]{1,0:T(8,128)(2,1)S(1)}, u32[]{:S(2)}, u32[]{:S(2)}) collective-permute-start(bf16[1280,512]{1,0:T(8,128)(2,1)S(1)} %fusion.90), channel_id=1, source_target_pairs={{0,8},{8,16},{16,24},{24,0},{1,9},{9,17},{17,25},{25,1},{2,10},{10... | collective-permute-start | bytes 3932168 | tf_op jit(solution)/shard_map/ppermute | solution.py:228
  620.8 55.3 %collective-permute-start.39 = (bf16[1280,512]{1,0:T(8,128)(2,1)S(1)}, bf16[1280,512]{1,0:T(8,128)(2,1)S(1)}, u32[]{:S(2)}, u32[]{:S(2)}) collective-permute-start(bf16[1280,512]{1,0:T(8,128)(2,1)S(1)} %fusion.93), channel_id=1, source_target_pairs={{0,24},{8,0},{16,8},{24,16},{1,25},{9,1},{17,9},{25,17},{2,26},{10... | collective-permute-start | bytes 3932168 | tf_op jit(solution)/shard_map/ppermute | solution.py:228
  (79 other events, 2006.4 us)
Sparse Core Ops, SparseCore 0:
  34.1 64.6 all-gather.4
  160.1 63.6 all-gather.8
  305.3 67.1 reduce-scatter.2
  409.7 67.0 reduce-scatter.4
  478.3 66.1 all-gather.6
  545.9 65.4 all-gather.10

commit v2 on v1

--- a/solution.py
+++ b/solution.py
@@ -12,6 +12,10 @@
 ROTARY_DIVISOR = 4
 LANES = 128
 Q_ROWS = 256
+LN_ROWS = 64
+TILE = 256
+SQRT_HALF = 0.5 ** 0.5
+INV_SQRT_2PI = 0.3989422804014327
 
 NT = (((1,), (1,)), ((), ()))
 TN = (((0,), (0,)), ((), ()))
@@ -115,12 +119,13 @@
         store(rows, 2 * width, dv_ref[rows, :], False)
 
 
-def attention_calls(n_seq, seq_len, width):
+def attention_calls(seq_len, width, index):
+    n_seq = 1
     half = width // ROTARY_DIVISOR // 2
     scale = width ** -0.5
     span = 512 if seq_len % 512 == 0 else seq_len
     tables = rotary_tables(seq_len, 2 * half)
-    seq_spec = lambda cols: pl.BlockSpec((1, seq_len, cols), lambda s: (s, 0, 0))
+    seq_spec = lambda cols, first=0: pl.BlockSpec((1, seq_len, cols), lambda s: (s + first, 0, 0))
     tab_spec = pl.BlockSpec((seq_len, LANES), lambda s: (0, 0))
     rot_scratch = pltpu.VMEM((seq_len, width), jnp.bfloat16)
     acc_scratch = pltpu.VMEM((seq_len, width), jnp.float32)
@@ -129,7 +134,7 @@
     forward = pl.pallas_call(
         functools.partial(attn_fwd_kernel, half=half, scale=scale, span=span),
         grid=(n_seq,),
-        in_specs=[seq_spec(3 * width), tab_spec, tab_spec, tab_spec],
+        in_specs=[seq_spec(3 * width, index), tab_spec, tab_spec, tab_spec],
         out_specs=seq_spec(width),
         out_shape=jax.ShapeDtypeStruct((n_seq, seq_len, width), jnp.bfloat16),
         scratch_shapes=[rot_scratch, rot_scratch],
@@ -140,7 +145,7 @@
     backward = pl.pallas_call(
         functools.partial(attn_bwd_kernel, half=half, scale=scale, span=span),
         grid=(n_seq,),
-        in_specs=[seq_spec(3 * width), seq_spec(width), tab_spec, tab_spec, tab_spec],
+        in_specs=[seq_spec(3 * width, index), seq_spec(width, index), tab_spec, tab_spec, tab_spec],
         out_specs=[seq_spec(3 * width), pl.BlockSpec((1, 1, 3 * width), lambda s: (s, 0, 0))],
         out_shape=[jax.ShapeDtypeStruct((n_seq, seq_len, 3 * width), jnp.bfloat16), jax.ShapeDtypeStruct((n_seq, 1, 3 * width), jnp.float32)],
         scratch_shapes=[rot_scratch, rot_scratch, acc_scratch, acc_scratch],
@@ -151,25 +156,38 @@
     return (lambda qkv: forward(qkv, *tables)), (lambda qkv, dctx: backward(qkv, dctx, *tables))
 
 
-def copy_kernel(row_ref, in_ref, out_ref):
-    out_ref[...] = in_ref[...]
-
-
-def place_groups(full, row):
-    groups, tokens, width = full.shape
-    rows = tokens // 4
-    return pl.pallas_call(
-        copy_kernel,
-        grid_spec=pltpu.PrefetchScalarGridSpec(
-            num_scalar_prefetch=1,
-            grid=(groups, tokens // rows),
-            in_specs=[pl.BlockSpec((1, rows, width), lambda t, c, row_ref: (lax.rem(row_ref[0] + groups - t, groups), c, 0))],
-            out_specs=pl.BlockSpec((1, rows, width), lambda t, c, row_ref: (t, c, 0)),
-        ),
-        out_shape=jax.ShapeDtypeStruct(full.shape, full.dtype),
-        name="place_groups",
-        cost_estimate=pl.CostEstimate(flops=full.size, bytes_accessed=4 * full.size, transcendentals=0),
-    )(row.reshape(1), full)
+def place_kernel(row_ref, full_ref, *rest, chunk, n_seq):
+    out_ref, held_ref, in_sems, out_sems = rest[-4:]
+    groups = full_ref.shape[0]
+    fetch = [pltpu.make_async_copy(full_ref.at[lax.rem(row_ref[0] + groups - t, groups)], held_ref.at[t], in_sems.at[t]) for t in range(groups)]
+    store = [pltpu.make_async_copy(held_ref.at[t], out_ref.at[t * n_seq + chunk], out_sems.at[t]) for t in range(groups)]
+    for copy in fetch:
+        copy.start()
+    for t in range(groups):
+        fetch[t].wait()
+        store[t].start()
+    for copy in store:
+        copy.wait()
+
+
+def place_groups(fulls, row):
+    groups, tokens, width = fulls[0].shape
+    n_seq = len(fulls)
+    out = None
+    for chunk, full in enumerate(fulls):
+        operands = (row.reshape(1), full) + (() if out is None else (out,))
+        any_spec = pl.BlockSpec(memory_space=pl.ANY)
+        out = pl.pallas_call(
+            functools.partial(place_kernel, chunk=chunk, n_seq=n_seq),
+            in_specs=[pl.BlockSpec(memory_space=pltpu.SMEM)] + [any_spec] * (len(operands) - 1),
+            out_specs=any_spec,
+            out_shape=jax.ShapeDtypeStruct((groups * n_seq, tokens, width), full.dtype),
+            scratch_shapes=[pltpu.VMEM(full.shape, full.dtype), pltpu.SemaphoreType.DMA((groups,)), pltpu.SemaphoreType.DMA((groups,))],
+            input_output_aliases={} if chunk == 0 else {2: 0},
+            name="place_groups",
+            cost_estimate=pl.CostEstimate(flops=4 * full.size, bytes_accessed=4 * full.size, transcendentals=0),
+        )(*operands)
+    return out
 
 
 def split_width(value, out_refs):
@@ -211,8 +229,111 @@
     )(*operands)
 
 
-def gelu_bf16(pre_act):
-    return jax.nn.gelu(pre_act.astype(jnp.float32), approximate=False).astype(jnp.bfloat16)
+def sublane_sum(value):
+    return value.reshape(value.shape[0] // 8, 8, value.shape[1]).sum(0)
+
+
+def front_kernel(x_ref, small_ref, w_ref, b_qkv_ref, b_up_ref, h_attn_ref, h_mlp_ref, qkv_ref, pre_ref, gelu_ref):
+    rows = x_ref.shape[0]
+
+    @pl.loop(0, rows // LN_ROWS)
+    def _(step):
+        at = pl.ds(pl.multiple_of(step * LN_ROWS, LN_ROWS), LN_ROWS)
+        x_hat, _ = normalize(x_ref[at, :])
+        h_attn_ref[at, :] = (x_hat * small_ref[0:1, :] + small_ref[1:2, :]).astype(jnp.bfloat16)
+        h_mlp_ref[at, :] = (x_hat * small_ref[2:3, :] + small_ref[3:4, :]).astype(jnp.bfloat16)
+
+    qkv_width = qkv_ref.shape[1]
+    for low in range(0, qkv_width, TILE):
+        acc = dot(h_attn_ref[...], w_ref[:, low:low + TILE], NN) + b_qkv_ref[:, low:low + TILE]
+        qkv_ref[:, low:low + TILE] = acc.astype(jnp.bfloat16)
+    for low in range(0, pre_ref.shape[1], TILE):
+        acc = dot(h_mlp_ref[...], w_ref[:, qkv_width + low:qkv_width + low + TILE], NN) + b_up_ref[:, low:low + TILE]
+        pre = acc.astype(jnp.bfloat16)
+        pre_ref[:, low:low + TILE] = pre
+        wide = pre.astype(jnp.float32)
+        gelu_ref[:, low:low + TILE] = (0.5 * wide * (1.0 + lax.erf(wide * SQRT_HALF))).astype(jnp.bfloat16)
+
+
+def y_kernel(ctx_ref, gelu_ref, *refs):
+    w_refs, y_ref = refs[:-1], refs[-1]
+    head = ctx_ref.shape[1]
+    for index, w_ref in enumerate(w_refs):
+        width = w_ref.shape[1]
+        acc = dot(ctx_ref[...], w_ref[:head, :], NN) + dot(gelu_ref[...], w_ref[head:, :], NN)
+        y_ref[:, index * width:(index + 1) * width] = acc.astype(jnp.bfloat16)
+
+
+def d_pre_kernel(cot_ref, pre_ref, *refs):
+    w_refs, (d_ctx_ref, d_pre_ref, d_bias_ref) = refs[:-3], refs[-3:]
+    width = w_refs[0].shape[1]
+
+    def back(low, high):
+        return sum(dot(cot_ref[:, r * width:(r + 1) * width], w_ref[low:high, :], NT) for r, w_ref in enumerate(w_refs)).astype(jnp.bfloat16)
+
+    head = d_ctx_ref.shape[1]
+
+    @pl.when(pl.program_id(0) == 0)
+    def _():
+        d_bias_ref[...] = jnp.zeros(d_bias_ref.shape, jnp.float32)
+
+    d_ctx_ref[...] = back(0, head)
+    for low in range(0, d_pre_ref.shape[1], TILE):
+        at = slice(low, low + TILE)
+        d_gelu = back(head + low, head + low + TILE).astype(jnp.float32)
+        pre = pre_ref[:, at].astype(jnp.float32)
+        slope = 0.5 * (1.0 + lax.erf(pre * SQRT_HALF)) + pre * (jnp.exp(-0.5 * pre * pre) * INV_SQRT_2PI)
+        d_pre = (d_gelu * slope).astype(jnp.bfloat16)
+        d_pre_ref[:, at] = d_pre
+        d_bias_ref[:, at] += sublane_sum(d_pre.astype(jnp.float32))
+
+
+def d_h_kernel(d_qkv_ref, d_pre_ref, x_ref, small_ref, w_ref, a6_ref, sums_ref):
+    qkv_width = d_qkv_ref.shape[1]
+
+    @pl.when(pl.program_id(0) == 0)
+    def _():
+        sums_ref[...] = jnp.zeros(sums_ref.shape, jnp.float32)
+
+    x_float = x_ref[...].astype(jnp.float32)
+    mean = x_float.mean(-1, keepdims=True)
+    inv_std = lax.rsqrt((x_float * x_float).mean(-1, keepdims=True) - mean * mean + LN_EPS)
+    for low in range(0, a6_ref.shape[1], TILE):
+        at = slice(low, low + TILE)
+        d_attn = dot(d_qkv_ref[...], w_ref[at, :qkv_width], NT).astype(jnp.bfloat16).astype(jnp.float32)
+        d_mlp = dot(d_pre_ref[...], w_ref[at, qkv_width:], NT).astype(jnp.bfloat16).astype(jnp.float32)
+        a6_ref[:, at] = (d_attn * small_ref[0:1, at] + d_mlp * small_ref[2:3, at]).astype(jnp.bfloat16)
+        x_hat = (x_ref[:, at].astype(jnp.float32) - mean) * inv_std
+        sums_ref[0, :, at] += sublane_sum(d_attn * x_hat)
+        sums_ref[1, :, at] += sublane_sum(d_attn)
+        sums_ref[2, :, at] += sublane_sum(d_mlp * x_hat)
+        sums_ref[3, :, at] += sublane_sum(d_mlp)
+
+
+def tile_call(kernel, tiled, whole, outs, row_range, flops):
+    start, count = row_range
+    rows = next(r for r in (512, 256, 128, 64, count) if count % r == 0)
+    first = start // rows
+    in_specs = [pl.BlockSpec((rows, op.shape[1]), lambda s, f=(first if op.shape[0] != count else 0): (s + f, 0)) for op in tiled]
+    in_specs += [pl.BlockSpec(op.shape, lambda s, n=op.ndim: (0,) * n) for op in whole]
+    out_specs, out_shapes = [], []
+    for form, dtype in outs:
+        if isinstance(form, int):
+            out_specs.append(pl.BlockSpec((rows, form), lambda s: (s, 0)))
+            out_shapes.append(jax.ShapeDtypeStruct((count, form), dtype))
+        else:
+            out_specs.append(pl.BlockSpec(form, lambda s, n=len(form): (0,) * n))
+            out_shapes.append(jax.ShapeDtypeStruct(form, dtype))
+    moved = sum(op.size * 2 * count // op.shape[0] for op in tiled) + sum(op.size * 2 for op in whole) + sum(2 * shape.size for shape in out_shapes)
+    return pl.pallas_call(
+        kernel,
+        grid=(count // rows,),
+        in_specs=in_specs,
+        out_specs=out_specs,
+        out_shape=out_shapes,
+        compiler_params=pltpu.CompilerParams(dimension_semantics=("arbitrary",), vmem_limit_bytes=60 * 1024 * 1024),
+        cost_estimate=pl.CostEstimate(flops=flops, bytes_accessed=moved, transcendentals=0),
+    )(*tiled, *whole)
 
 
 def solution(mesh):
@@ -260,68 +381,82 @@
     def body(x_act, cot_out, ln1_gain, ln1_bias, ln2_gain, ln2_bias, w_qkv, b_qkv, w_dense, b_dense, w_up, b_up, w_down, b_down):
         batch, seq_len, d_local = x_act.shape
         n_seq = batch // tx_size
-        own = n_seq * seq_len // ty_size
+        own = seq_len // ty_size
         row, col = lax.axis_index('tx'), lax.axis_index('ty')
         qkv_width = w_qkv.shape[1] * w_qkv.shape[2]
         head = qkv_width // 3
-        attn_fwd, attn_bwd = attention_calls(n_seq, seq_len, head)
+        chunks = range(n_seq)
+        attention = [attention_calls(seq_len, head, s) for s in chunks]
 
         def to_tokens(act):
-            parts = act.reshape(tx_size, ty_size, own, d_local)
-            pick = lambda index: lax.dynamic_slice(parts, (index, col, 0, 0), (1, 1, own, d_local)).reshape(own, d_local)
-            return jnp.concatenate([pick(row)] + [shift(pick((row - r) % tx_size), r) for r in range(1, tx_size)], axis=1)
+            parts = act.reshape(tx_size, n_seq, ty_size, own, d_local)
+            pick = lambda index: lax.dynamic_slice(parts, (index, 0, col, 0, 0), (1, n_seq, 1, own, d_local)).reshape(n_seq, own, d_local)
+            blocks = [pick(row)] + [shift(pick((row - r) % tx_size), r) for r in range(1, tx_size)]
+            return jnp.concatenate(blocks, axis=2)
 
         def to_width(parts):
             blocks = [parts[0]] + [shift(parts[r], -r) for r in range(1, tx_size)]
-            stacked = jnp.stack(blocks)
-            full = lax.all_gather(stacked, 'ty', axis=1, tiled=True)
-            return place_groups(full, row).reshape(batch, seq_len, d_local)
-
+            return lax.all_gather(jnp.stack(blocks), 'ty', axis=1, tiled=True)
+
+        line = lax.broadcasted_iota(jnp.int32, (8, d_local), 0)
+        small = jnp.zeros((8, d_local), jnp.bfloat16)
+        for index, vector in enumerate((ln1_gain, ln1_bias, ln2_gain, ln2_bias, b_dense, b_down)):
+            small = jnp.where(line == index, vector[None, :], small)
+        small = [small] + [shift(small, r) for r in range(1, tx_size)]
+        small = jnp.concatenate(small, axis=1).astype(jnp.float32)
+        bias_out = small[4] + small[5]
         x_own = to_tokens(x_act)
-        small = ring_gather(jnp.stack([ln1_gain, ln1_bias, ln2_gain, ln2_bias, b_dense, b_down]))
-        small = jnp.concatenate(small, axis=1).astype(jnp.float32)
-        gain_attn, bias_attn, gain_mlp, bias_mlp = small[0], small[1], small[2], small[3]
-        bias_out = small[4] + small[5]
-        x_group = lax.all_gather(x_own, 'ty', axis=0, tiled=True)
+        cot_own = to_tokens(cot_out)
+        x_group = lax.all_gather(x_own, 'ty', axis=1, tiled=True)
+        cot_group = lax.all_gather(cot_own, 'ty', axis=1, tiled=True)
+        x_group, cot_group = x_group.reshape(n_seq * seq_len, -1), cot_group.reshape(n_seq * seq_len, -1)
         w_in = jnp.concatenate([w_qkv.reshape(d_local, qkv_width), w_up], axis=1)
-        w_in = jnp.concatenate(ring_gather(w_in), axis=0)
-        wq, wu = w_in[:, :qkv_width], w_in[:, qkv_width:]
-        cot_own = to_tokens(cot_out)
-        cot_group = lax.all_gather(cot_own, 'ty', axis=0, tiled=True)
-        w_back = jnp.concatenate(ring_gather(jnp.concatenate([w_dense, w_down], axis=0)), axis=1)
-
-        x_hat, _ = normalize(x_group)
-        h_attn = (x_hat * gain_attn + bias_attn).astype(jnp.bfloat16)
-        h_mlp = (x_hat * gain_mlp + bias_mlp).astype(jnp.bfloat16)
-        qkv_act = (dot(h_attn, wq, NN) + b_qkv.reshape(-1).astype(jnp.float32)).astype(jnp.bfloat16)
+        w_in = ring_gather(w_in)
+        w_in = jnp.concatenate(w_in, axis=0)
+        w_back = ring_gather(jnp.concatenate([w_dense, w_down], axis=0))
+        back_size = tx_size * w_back[0].size
+
+        n_tok, d_model = x_group.shape
+        ff_width = w_up.shape[1]
+        h_attn, h_mlp, qkv_act, pre_act, gelu_out = tile_call(
+            front_kernel, [x_group], [small, w_in, b_qkv.reshape(1, -1).astype(jnp.float32), b_up.reshape(1, -1).astype(jnp.float32)],
+            [(d_model, jnp.bfloat16), (d_model, jnp.bfloat16), (qkv_width, jnp.bfloat16), (ff_width, jnp.bfloat16), (ff_width, jnp.bfloat16)],
+            (0, n_tok), 2 * n_tok * w_in.size)
         qkv_seq = qkv_act.reshape(n_seq, seq_len, qkv_width)
-        context = attn_fwd(qkv_seq).reshape(-1, head)
-        pre_act = (dot(h_mlp, wu, NN) + b_up.astype(jnp.float32)).astype(jnp.bfloat16)
-        gelu_out, gelu_pullback = jax.vjp(gelu_bf16, pre_act)
+        context, y_full = [], []
+        for s in chunks:
+            context.append(attention[s][0](qkv_seq).reshape(seq_len, head))
+            (y_part,) = tile_call(y_kernel, [context[s], gelu_out], w_back, [(d_model, jnp.bfloat16)], (s * seq_len, seq_len), 2 * seq_len * back_size)
+            mixed = lax.psum_scatter(y_part, 'ty', scatter_dimension=0, tiled=True)
+            y_full.append(to_width(row_call(finish_y_kernel, tx_size, x_own[s], mixed, bias_out.reshape(1, -1))))
+        y_out = place_groups(y_full, row)
+        context = jnp.concatenate(context, axis=0)
+
+        d_ctx, d_pre, d_b_up = tile_call(
+            d_pre_kernel, [cot_group, pre_act], w_back,
+            [(head, jnp.bfloat16), (ff_width, jnp.bfloat16), ((8, ff_width), jnp.float32)], (0, n_tok), 2 * n_tok * back_size)
+        d_ctx, d_b_up = d_ctx.reshape(n_seq, seq_len, head), d_b_up.sum(0)
+        d_qkv, d_b_qkv, d_ln, dx_full = [], [], [], []
+        for s in chunks:
+            d_qkv_seq, d_b_seq = attention[s][1](qkv_seq, d_ctx)
+            d_qkv.append(d_qkv_seq.reshape(seq_len, qkv_width))
+            d_b_qkv.append(d_b_seq.reshape(-1))
+            a6_part, sums = tile_call(
+                d_h_kernel, [d_qkv[s], d_pre, x_group], [small, w_in],
+                [(d_model, jnp.bfloat16), ((4, 8, d_model), jnp.float32)], (s * seq_len, seq_len), 2 * seq_len * w_in.size)
+            d_ln.append(sums)
+            value_a6 = lax.psum_scatter(a6_part, 'ty', scatter_dimension=0, tiled=True)
+            dx_full.append(to_width(row_call(finish_dx_kernel, tx_size, x_own[s], value_a6, cot_own[s])))
+        dx_act = place_groups(dx_full, row)
+        d_qkv = jnp.concatenate(d_qkv, axis=0)
+
+        d_ln = small_sum(sum(d_ln).sum(1), 'ty', ty_size).reshape(4, tx_size, d_local)
+        d_ln = d_ln[:, 0] + sum(shift(d_ln[:, r], -r) for r in range(1, tx_size))
+        d_bias = small_sum(jnp.concatenate([sum(d_b_qkv), d_b_up])[None], 'tx', tx_size)[0]
+        d_b_out = cot_out.astype(jnp.float32).sum((0, 1))
+
+        cols = lambda act, r: act[:, r * d_local:(r + 1) * d_local]
         inner = jnp.concatenate([context, gelu_out], axis=1)
-        y_part = dot(inner, w_back, NN).astype(jnp.bfloat16)
-        mixed = lax.psum_scatter(y_part, 'ty', scatter_dimension=0, tiled=True)
-        y_out = to_width(row_call(finish_y_kernel, tx_size, x_own, mixed, bias_out.reshape(1, -1)))
-
-        d_gelu = dot(cot_group, w_back[head:], NT).astype(jnp.bfloat16)
-        (d_pre,) = gelu_pullback(d_gelu)
-        d_ctx = dot(cot_group, w_back[:head], NT).astype(jnp.bfloat16)
-        d_qkv_seq, d_b_qkv = attn_bwd(qkv_seq, d_ctx.reshape(n_seq, seq_len, head))
-        d_qkv = d_qkv_seq.reshape(-1, qkv_width)
-        d_b_up = d_pre.astype(jnp.float32).sum(0)
-        d_h_mlp = dot(d_pre, wu, NT).astype(jnp.bfloat16).astype(jnp.float32)
-        d_h_attn = dot(d_qkv, wq, NT).astype(jnp.bfloat16).astype(jnp.float32)
-        a6_part = (d_h_attn * gain_attn + d_h_mlp * gain_mlp).astype(jnp.bfloat16)
-        value_a6 = lax.psum_scatter(a6_part, 'ty', scatter_dimension=0, tiled=True)
-        dx_act = to_width(row_call(finish_dx_kernel, tx_size, x_own, value_a6, cot_own))
-
-        d_ln = jnp.stack([(d_h_attn * x_hat).sum(0), d_h_attn.sum(0), (d_h_mlp * x_hat).sum(0), d_h_mlp.sum(0)])
-        d_ln = small_sum(d_ln, 'ty', ty_size).reshape(4, tx_size, d_local)
-        d_ln = d_ln[:, 0] + sum(shift(d_ln[:, r], -r) for r in range(1, tx_size))
-        d_bias = small_sum(jnp.concatenate([d_b_qkv.sum((0, 1)), d_b_up])[None], 'tx', tx_size)[0]
-        d_b_out = cot_out.astype(jnp.float32).sum((0, 1))
-
-        cols = lambda act, r: act[:, r * d_local:(r + 1) * d_local]
         add_back = ring_scatter(lambda r, low, high: dot(inner[:, low:high], cols(cot_group, r), TN), inner.shape[1])
         add_up = ring_scatter(lambda r, low, high: dot(cols(h_mlp, r)[:, low:high], d_pre, TN), d_local)
         add_qkv = ring_scatter(lambda r, low, high: dot(cols(h_attn, r)[:, low:high], d_qkv, TN), d_local)

time: 729 us -> 662 us (0.908)
  matrix products: 238 us -> 81.5 us
  Pallas kernels: 83.4 us -> 225 us
  other arithmetic: 45.8 us -> 27.5 us
  waiting for transfers between devices: 234 us -> 217 us
  local copies, waits for them, and re-layouts: 27.2 us -> 18.2 us
    dot_general x23 -> x16, matrix products: 238 us -> 81.5 us  [dot(): return lax.dot_general(a, b, dims, preferred_element_type=jnp.float32)]
    pallas_call x2 -> x10, Pallas kernels: 30.3 us -> 162 us  [the longest x6 142 us: tile_call(): pl.pallas_call(kernel, grid=(count // rows,), in_specs=in_specs, out_spec...]
    reduce_scatter x1 -> x2, waiting for transfers between devices: 41.4 us -> 0.01 us  [body(): value_a6 = lax.psum_scatter(a6_part, 'ty', scatter_dimension=0, tiled=True)]
    ppermute x39 -> x44, waiting for transfers between devices: 187 us -> 212 us  [shift(): lax.ppermute(value, 'tx', [(s, (s - hops) % tx_size) for s in range(tx_si...]
    convert_element_type x2 -> x3, other arithmetic: 14.3 us -> 1.8 us  [the longest x1 0.62 us: body(): small = jnp.concatenate(small, axis=1).astype(jnp.float32)]
    reduce_sum x2, other arithmetic: 8.32 us -> 0.11 us  [the longest x1 0.09 us: body(): sum(d_ln).sum(1)]
    ppermute x39 -> x44, starting transfers between devices: 71.7 us -> 65.9 us  [shift(): lax.ppermute(value, 'tx', [(s, (s - hops) % tx_size) for s in range(tx_si...]
    pallas_call x1 -> x2, Pallas kernels: 25.9 us -> 29.7 us  [attention_calls(): backward(qkv, dctx, *tables)]
  transfers between devices with their start and end apart: 50 -> 59, of which waited for: 17 -> 24; matrix products, arithmetic and copies ran while one was open for 42% -> 18% of each run, Pallas kernels for 9% -> 33%
where the time goes in v2:
time: 662 us; the launch traced here: 657 us
  Pallas kernels  225 us (34%)
  waiting for transfers between devices  217 us (33%)
  matrix products  81.5 us (12%)
  starting transfers between devices  72.9 us (11%)
  other arithmetic  27.5 us (4%)
  local copies, waits for them, and re-layouts  18.2 us (3%)
  between operations  15.5 us (2%)
    ppermute x44, waiting for transfers between devices, shift(): lax.ppermute(value, 'tx', [(s, (s - hops) % tx_size) for s in range(tx_si...  212 us
    pallas_call x6, Pallas kernels, tile_call(): pl.pallas_call(kernel, grid=(count // rows,), in_specs=in_specs, out_spec...  142 us
    dot_general x16, matrix products, dot(): return lax.dot_general(a, b, dims, preferred_element_type=jnp.float32)  81.5 us
    ppermute x44, starting transfers between devices, shift(): lax.ppermute(value, 'tx', [(s, (s - hops) % tx_size) for s in range(tx_si...  65.9 us
    pallas_call x2, Pallas kernels, attention_calls(): backward(qkv, dctx, *tables)  29.7 us
    pallas_call x2, Pallas kernels, attention_calls(): forward(qkv, *tables)  21.3 us
    pallas_call x4, Pallas kernels, place_groups(): pl.pallas_call(functools.partial(place_kernel, chunk=chunk, n_seq=n_seq),...  20.7 us
  transfers between devices with their start and end apart: 59, of which 24 were waited for; matrix products, arithmetic and copies ran while one was open for 18% of the time, Pallas kernels for 33%

profile of v2, /device:TPU:98, one launch (start us, length us, event | category | flops | bytes accessed | tf_op | source)
XLA Modules:
  0.0 657.5 jit_solution(17564728206828757070)
XLA Ops:
  15.2 8.0 %collective-permute-done.1 = bf16[2,192,512]{2,1,0:T(8,128)(2,1)S(1)} collective-permute-done((bf16[2,192,512]{2,1,0:T(8,128)(2,1)S(1)}, bf16[2,192,512]{2,1,0:T(8,128)(2,1)S(1)}, u32[]{:S(2)}, u32[]{:S(2)}) %collective-permute-start.1) | collective-permute-done | bytes 393248 | tf_op jit(solution)/shard_map/ppermute | solution.py:349
  23.2 8.6 %collective-permute-done = bf16[2,192,512]{2,1,0:T(8,128)(2,1)S(1)} collective-permute-done((bf16[2,192,512]{2,1,0:T(8,128)(2,1)S(1)}, bf16[2,192,512]{2,1,0:T(8,128)(2,1)S(1)}, u32[]{:S(2)}, u32[]{:S(2)}) %collective-permute-start) | collective-permute-done | bytes 393248 | tf_op jit(solution)/shard_map/ppermute | solution.py:349
  39.3 9.2 %collective-permute-done.21 = bf16[2,192,512]{2,1,0:T(8,128)(2,1)S(1)} collective-permute-done((bf16[2,192,512]{2,1,0:T(8,128)(2,1)S(1)}, bf16[2,192,512]{2,1,0:T(8,128)(2,1)S(1)}, u32[]{:S(2)}, u32[]{:S(2)}) %collective-permute-start.21) | collective-permute-done | bytes 393248 | tf_op jit(solution)/shard_map/ppermute | solution.py:349
  48.5 7.1 %collective-permute-done.20 = bf16[2,192,512]{2,1,0:T(8,128)(2,1)S(1)} collective-permute-done((bf16[2,192,512]{2,1,0:T(8,128)(2,1)S(1)}, bf16[2,192,512]{2,1,0:T(8,128)(2,1)S(1)}, u32[]{:S(2)}, u32[]{:S(2)}) %collective-permute-start.20) | collective-permute-done | bytes 393248 | tf_op jit(solution)/shard_map/ppermute | solution.py:349
  65.1 67.2 %collective-permute-done.12.refs_3_ = bf16[1280,512]{1,0:T(8,128)(2,1)S(1)} collective-permute-done((bf16[1280,512]{1,0:T(8,128)(2,1)S(1)}, bf16[1280,512]{1,0:T(8,128)(2,1)S(1)}, u32[]{:S(2)}, u32[]{:S(2)}) %collective-permute-start.12) | collective-permute-done | bytes 1310752 | tf_op jit(solution)/shard_map/ppermute | solution.py:349
  147.7 5.2 collective-permute-done.11
  153.2 16.7 %collective-permute-done.7 = bf16[256,1792]{1,0:T(8,128)(2,1)S(1)} collective-permute-done((bf16[256,1792]{1,0:T(8,128)(2,1)S(1)}, bf16[256,1792]{1,0:T(8,128)(2,1)S(1)}, u32[]{:S(2)}, u32[]{:S(2)}) %collective-permute-start.7) | collective-permute-done | bytes 917536 | tf_op jit(solution)/shard_map/ppermute | solution.py:349
  173.3 45.1 %shard_map.245 = (bf16[3072,2048]{1,0:T(8,128)(2,1)}, bf16[3072,2048]{1,0:T(8,128)(2,1)}, bf16[3072,768]{1,0:T(8,128)(2,1)}, bf16[3072,1024]{1,0:T(8,128)(2,1)}, bf16[3072,1024]{1,0:T(8,128)(2,1)}) custom-call(bf16[3072,2048]{1,0:T(8,128)(2,1)} %bitcast.141, f32[8,2048]{1,0:T(8,128)} %maximum_convert_fusion.small_ref, ...), custom_call_target="tpu_custom_call" | custom-call | flops 22548578304 | bytes 62426624 | tf_op jit(solution)/shard_map/pallas_call | solution.py:328
  218.4 10.7 %attn_fwd.3 = bf16[1,1536,256]{2,1,0:T(8,128)(2,1)} custom-call(bf16[2,1536,768]{2,1,0:T(8,128)(2,1)} %bitcast.144, f32[1536,128]{1,0:T(8,128)} %get-tuple-element.114.cos_ref, f32[1536,128]{1,0:T(8,128)} %get-tuple-element.113.lo_ref, f32[1536,128]{1,0:T(8,128)} %get-tuple-element.112.hi_ref), custom_call_target="tpu_custom_call" | custom-call | flops 2415919104 | bytes 3145728 | tf_op jit(solution)/shard_map/attn_fwd/pallas_call | solution.py:156
  229.1 12.9 %shard_map.248 = bf16[1536,2048]{1,0:T(8,128)(2,1)} custom-call(bf16[1536,256]{1,0:T(8,128)(2,1)} %bitcast.162, bf16[3072,1024]{1,0:T(8,128)(2,1)} %get-tuple-element.47.gelu_ref, bf16[1280,512]{1,0:T(8,128)(2,1)} %copy-done.13, bf16[1280,512]{1,0:T(8,128)(2,1)} %copy-done.7, bf16[1280,512]{1,0:T(8,128)(2,1)} %copy-done.8, bf16[1280,512]{1,0:T(8,128)(2,1)} %copy-done.6), custom_call_target="tpu_custom_call" | custom-call | flops 8053063680 | bytes 15466496 | tf_op jit(solution)/shard_map/pallas_call | solution.py:328
  242.4 27.0 %shard_map.250 = (bf16[3072,256]{1,0:T(8,128)(2,1)}, bf16[3072,1024]{1,0:T(8,128)(2,1)}, f32[8,1024]{1,0:T(8,128)}) custom-call(bf16[3072,2048]{1,0:T(8,128)(2,1)} %bitcast.130, bf16[3072,1024]{1,0:T(8,128)(2,1)} %get-tuple-element.56.pre_ref, bf16[1280,512]{1,0:T(8,128)(2,1)} %copy-done.13, bf16[1280,512]{1,0:T(8,128)(2,1)} %copy-done.7, ...), custom_call_target="tpu_custom_call" | custom-call | flops 16106127360 | bytes 31997952 | tf_op jit(solution)/shard_map/pallas_call | solution.py:328
  269.3 14.9 %attn_bwd.3 = (bf16[1,1536,768]{2,1,0:T(8,128)(2,1)}, f32[1,1,768]{2,1,0:T(1,128)}) custom-call(bf16[2,1536,768]{2,1,0:T(8,128)(2,1)} %bitcast.145, bf16[2,1536,256]{2,1,0:T(8,128)(2,1)} %bitcast.160, f32[1536,128]{1,0:T(8,128)} %get-tuple-element.114.cos_ref, f32[1536,128]{1,0:T(8,128)} %get-tuple-element.113.lo_ref, f32[1536,128]{1,0:T(8,128)} %get-tuple-element.112.hi_ref), custom_call_target="tpu_custom_call" | custom-call | flops 6039797760 | bytes 5505024 | tf_op jit(solution)/shard_map/attn_bwd/pallas_call | solution.py:156
  284.2 21.8 %shard_map.253 = (bf16[1536,2048]{1,0:T(8,128)(2,1)}, f32[4,8,2048]{2,1,0:T(8,128)}) custom-call(bf16[1536,768]{1,0:T(8,128)(2,1)} %bitcast.148, bf16[3072,1024]{1,0:T(8,128)(2,1)} %get-tuple-element.59.d_pre_ref, bf16[3072,2048]{1,0:T(8,128)(2,1)} %bitcast.142, f32[8,2048]{1,0:T(8,128)} %maximum_convert_fusion.small_ref, ...), custom_call_target="tpu_custom_call" | custom-call | flops 11274289152 | bytes 25591808 | tf_op jit(solution)/shard_map/pallas_call | solution.py:328
  306.2 10.7 %attn_fwd.2 = bf16[1,1536,256]{2,1,0:T(8,128)(2,1)} custom-call(bf16[2,1536,768]{2,1,0:T(8,128)(2,1)} %bitcast.146, f32[1536,128]{1,0:T(8,128)} %get-tuple-element.114.cos_ref, f32[1536,128]{1,0:T(8,128)} %get-tuple-element.113.lo_ref, f32[1536,128]{1,0:T(8,128)} %get-tuple-element.112.hi_ref), custom_call_target="tpu_custom_call" | custom-call | flops 2415919104 | bytes 3145728 | tf_op jit(solution)/shard_map/attn_fwd/pallas_call | solution.py:156
  316.9 13.1 %shard_map.246 = bf16[1536,2048]{1,0:T(8,128)(2,1)} custom-call(bf16[1536,256]{1,0:T(8,128)(2,1)} %bitcast.167, bf16[3072,1024]{1,0:T(8,128)(2,1)} %get-tuple-element.47.gelu_ref, bf16[1280,512]{1,0:T(8,128)(2,1)} %copy-done.13, bf16[1280,512]{1,0:T(8,128)(2,1)} %copy-done.7, bf16[1280,512]{1,0:T(8,128)(2,1)} %copy-done.8, bf16[1280,512]{1,0:T(8,128)(2,1)} %copy-done.6), custom_call_target="tpu_custom_call" | custom-call | flops 8053063680 | bytes 15466496 | tf_op jit(solution)/shard_map/pallas_call | solution.py:328
  330.5 14.9 %attn_bwd.2 = (bf16[1,1536,768]{2,1,0:T(8,128)(2,1)}, f32[1,1,768]{2,1,0:T(1,128)}) custom-call(bf16[2,1536,768]{2,1,0:T(8,128)(2,1)} %bitcast.147, bf16[2,1536,256]{2,1,0:T(8,128)(2,1)} %bitcast.161, f32[1536,128]{1,0:T(8,128)} %get-tuple-element.114.cos_ref, f32[1536,128]{1,0:T(8,128)} %get-tuple-element.113.lo_ref, f32[1536,128]{1,0:T(8,128)} %get-tuple-element.112.hi_ref), custom_call_target="tpu_custom_call" | custom-call | flops 6039797760 | bytes 5505024 | tf_op jit(solution)/shard_map/attn_bwd/pallas_call | solution.py:156
  345.3 21.7 %shard_map.251 = (bf16[1536,2048]{1,0:T(8,128)(2,1)}, f32[4,8,2048]{2,1,0:T(8,128)}) custom-call(bf16[1536,768]{1,0:T(8,128)(2,1)} %bitcast.154, bf16[3072,1024]{1,0:T(8,128)(2,1)} %get-tuple-element.59.d_pre_ref, bf16[3072,2048]{1,0:T(8,128)(2,1)} %bitcast.143, f32[8,2048]{1,0:T(8,128)} %maximum_convert_fusion.small_ref, ...), custom_call_target="tpu_custom_call" | custom-call | flops 11274289152 | bytes 25591808 | tf_op jit(solution)/shard_map/pallas_call | solution.py:328
  419.1 6.7 %convert_reduce_fusion = f32[512]{0:T(512)S(1)} fusion(bf16[8,1536,512]{2,1,0:T(8,128)(2,1)} %param.15), kind=kLoop, calls=%fused_computation | loop fusion | flops 12582400 | bytes 12584960 | tf_op jit(solution)/shard_map/reduce_sum | solution.py:456
  428.3 5.4 fusion.70
  445.2 6.7 %fusion.18 = f32[512,1024]{1,0:T(8,128)} fusion(bf16[3072,1024]{1,0:T(8,128)(2,1)S(1)} %bitcast.97, bf16[3072,2048]{1,0:T(8,128)(2,1)} %get-tuple-element.77), kind=kOutput, calls=%fused_computation.21 | convolution fusion | flops 3221225472 | bytes 11534336 | tf_op jit(solution)/shard_map/dot_general | solution.py:26
  460.1 5.2 fusion.73
  489.3 12.2 %collective-permute-done.37 = bf16[256,768]{1,0:T(8,128)(2,1)} collective-permute-done((bf16[256,768]{1,0:T(8,128)(2,1)}, bf16[256,768]{1,0:T(8,128)(2,1)}, u32[]{:S(2)}, u32[]{:S(2)}) %collective-permute-start.37) | collective-permute-done | bytes 393248 | tf_op jit(solution)/shard_map/ppermute | solution.py:349
  502.6 7.1 %add_convert_fusion.2 = bf16[512,768]{1,0:T(8,128)(2,1)} fusion(bf16[3072,2048]{1,0:T(8,128)(2,1)} %get-tuple-element.73, bf16[256,768]{1,0:T(8,128)(2,1)} %collective-permute-done.37, bf16[1536,768]{1,0:T(8,128)(2,1)} %bitcast.157, bf16[1536,768]{1,0:T(8,128)(2,1)} %bitcast.151), kind=kOutput, calls=%fused_computation.52 | convolution fusion | flops 2426535936 | bytes 9043968 | tf_op jit(solution)/shard_map/dot_general | solution.py:26
  509.8 5.4 collective-permute-done.35
  515.1 5.5 add_convert_fusion.3
  524.2 5.6 add_convert_fusion.1
  538.9 7.6 %fusion.26 = bf16[1280,512]{1,0:T(8,128)(2,1)S(1)} fusion(bf16[3072,2048]{1,0:T(8,128)(2,1)S(1)} %bitcast.137, bf16[3072,1024]{1,0:T(8,128)(2,1)} %get-tuple-element.47.gelu_ref, bf16[1536,256]{1,0:T(8,128)(2,1)} %bitcast.168, bf16[1536,256]{1,0:T(8,128)(2,1)S(1)} %bitcast.164, bf16[640,512]{1,0:T(8,128)(2,1)} %copy-done.32), kind=kOutput, calls=%fused_computation.29 | convolution fusion | flops 4052090880 | bytes 12976128 | tf_op jit(solution)/shard_map/dot_general | solution.py:26
  546.7 7.4 %fusion.29 = bf16[1280,512]{1,0:T(8,128)(2,1)S(1)} fusion(bf16[3072,2048]{1,0:T(8,128)(2,1)S(1)} %bitcast.138, bf16[3072,1024]{1,0:T(8,128)(2,1)} %get-tuple-element.47.gelu_ref, bf16[1536,256]{1,0:T(8,128)(2,1)S(1)} %bitcast.170, bf16[1536,256]{1,0:T(8,128)(2,1)S(1)} %bitcast.165, bf16[640,512]{1,0:T(8,128)(2,1)} %collective-permute-done.41), kind=kOutput, calls=%fused_computation.30 | convolution fusion | flops 4052090880 | bytes 12976128 | tf_op jit(solution)/shard_map/dot_general | solution.py:26
  559.4 8.8 %collective-permute-done.36 = bf16[512,768]{1,0:T(8,128)(2,1)S(1)} collective-permute-done((bf16[512,768]{1,0:T(8,128)(2,1)S(1)}, bf16[512,768]{1,0:T(8,128)(2,1)S(1)}, u32[]{:S(2)}, u32[]{:S(2)}) %collective-permute-start.36) | collective-permute-done | bytes 786464 | tf_op jit(solution)/shard_map/ppermute | solution.py:349
  578.2 19.5 %collective-permute-done.48 = bf16[512,1024]{1,0:T(8,128)(2,1)S(1)} collective-permute-done((bf16[512,1024]{1,0:T(8,128)(2,1)S(1)}, bf16[512,1024]{1,0:T(8,128)(2,1)S(1)}, u32[]{:S(2)}, u32[]{:S(2)}) %collective-permute-start.48) | collective-permute-done | bytes 1048608 | tf_op jit(solution)/shard_map/ppermute | solution.py:349
  599.6 16.2 %collective-permute-done.42 = bf16[1280,512]{1,0:T(8,128)(2,1)S(1)} collective-permute-done((bf16[1280,512]{1,0:T(8,128)(2,1)S(1)}, bf16[1280,512]{1,0:T(8,128)(2,1)S(1)}, u32[]{:S(2)}, u32[]{:S(2)}) %collective-permute-start.42) | collective-permute-done | bytes 1310752 | tf_op jit(solution)/shard_map/ppermute | solution.py:349
  615.8 6.6 %collective-permute-done.44 = bf16[1280,512]{1,0:T(8,128)(2,1)S(1)} collective-permute-done((bf16[1280,512]{1,0:T(8,128)(2,1)S(1)}, bf16[1280,512]{1,0:T(8,128)(2,1)S(1)}, u32[]{:S(2)}, u32[]{:S(2)}) %collective-permute-start.44) | collective-permute-done | bytes 1310752 | tf_op jit(solution)/shard_map/ppermute | solution.py:349
  (312 shorter events, 201.5 us)
Async XLA Ops:
  7.2 166.1 %all-gather.7.cloned.1.call-start = ((), (), s32[]{:S(2)}) async-start(), calls=%async_computation.4 | async-start | bytes 14155776 | tf_op jit(solution)/shard_map/all_gather | solution.py:410
  33.2 209.2 %all-gather.13.cloned.1.call-start = ((), (), s32[]{:S(2)}) async-start(), calls=%async_computation.9 | async-start | bytes 14155776 | tf_op jit(solution)/shard_map/all_gather | solution.py:411
  57.0 313.1 %reduce-scatter.7.cloned.1.call-start = ((), (), s32[]{:S(2)}) async-start(), calls=%async_computation.7 | async-start | bytes 7077888 | tf_op jit(solution)/shard_map/reduce_scatter | solution.py:430
  58.6 75.6 %collective-permute-start.6 = (bf16[512,1792]{1,0:T(8,128)(2,1)S(1)}, bf16[512,1792]{1,0:T(8,128)(2,1)S(1)}, u32[]{:S(2)}, u32[]{:S(2)}) collective-permute-start(bf16[512,1792]{1,0:T(8,128)(2,1)S(1)} %get-tuple-element.100), channel_id=1, source_target_pairs={{0,24},{8,0},{16,8},{24,16},{1,25},{9,1},{17,9},{25,17},{2,26},{10... | collective-permute-start | bytes 5505032 | tf_op jit(solution)/shard_map/ppermute | solution.py:349
  61.3 76.5 %collective-permute-start.8 = (bf16[512,1792]{1,0:T(8,128)(2,1)S(1)}, bf16[512,1792]{1,0:T(8,128)(2,1)S(1)}, u32[]{:S(2)}, u32[]{:S(2)}) collective-permute-start(bf16[512,1792]{1,0:T(8,128)(2,1)S(1)} %get-tuple-element.100), channel_id=1, source_target_pairs={{0,8},{8,16},{16,24},{24,0},{1,9},{9,17},{17,25},{25,1},{2,10},{10... | collective-permute-start | bytes 5505032 | tf_op jit(solution)/shard_map/ppermute | solution.py:349
  61.4 70.9 %collective-permute-start.12 = (bf16[1280,512]{1,0:T(8,128)(2,1)S(1)}, bf16[1280,512]{1,0:T(8,128)(2,1)S(1)}, u32[]{:S(2)}, u32[]{:S(2)}) collective-permute-start(bf16[1280,512]{1,0:T(8,128)(2,1)S(1)} %constant_dynamic-update-slice_fusion.5.refs_0_), channel_id=1, source_target_pairs={{0,8},{8,16},{16,24},{24,0},{1,9},{9,17},{17,25},{25,1},{2,10},{10... | collective-permute-start | bytes 3932168 | tf_op jit(solution)/shard_map/ppermute | solution.py:349
  62.1 70.3 %collective-permute-start.10 = (bf16[1280,512]{1,0:T(8,128)(2,1)S(1)}, bf16[1280,512]{1,0:T(8,128)(2,1)S(1)}, u32[]{:S(2)}, u32[]{:S(2)}) collective-permute-start(bf16[1280,512]{1,0:T(8,128)(2,1)S(1)} %constant_dynamic-update-slice_fusion.5.refs_0_), channel_id=1, source_target_pairs={{0,24},{8,0},{16,8},{24,16},{1,25},{9,1},{17,9},{25,17},{2,26},{10... | collective-permute-start | bytes 3932168 | tf_op jit(solution)/shard_map/ppermute | solution.py:349
  65.0 69.7 %collective-permute-start.5 = (bf16[8,512]{1,0:T(8,128)(2,1)S(1)}, bf16[8,512]{1,0:T(8,128)(2,1)S(1)}, u32[]{:S(2)}, u32[]{:S(2)}) collective-permute-start(bf16[8,512]{1,0:T(8,128)(2,1)S(1)} %select_select_fusion), channel_id=1, source_target_pairs={{0,8},{8,16},{16,24},{24,0},{1,9},{9,17},{17,25},{25,1},{2,10},{10... | collective-permute-start | bytes 24584 | tf_op jit(solution)/shard_map/ppermute | solution.py:349
  137.8 32.2 %collective-permute-start.7 = (bf16[256,1792]{1,0:T(8,128)(2,1)S(1)}, bf16[256,1792]{1,0:T(8,128)(2,1)S(1)}, u32[]{:S(2)}, u32[]{:S(2)}) collective-permute-start(bf16[256,1792]{1,0:T(8,128)(2,1)S(1)} %slice.178), channel_id=1, source_target_pairs={{0,24},{8,0},{16,8},{24,16},{1,25},{9,1},{17,9},{25,17},{2,26},{10... | collective-permute-start | bytes 2752520 | tf_op jit(solution)/shard_map/ppermute | solution.py:349
  144.2 26.8 %collective-permute-start.9 = (bf16[256,1792]{1,0:T(8,128)(2,1)S(1)}, bf16[256,1792]{1,0:T(8,128)(2,1)S(1)}, u32[]{:S(2)}, u32[]{:S(2)}) collective-permute-start(bf16[256,1792]{1,0:T(8,128)(2,1)S(1)} %slice.179), channel_id=1, source_target_pairs={{0,8},{8,16},{16,24},{24,0},{1,9},{9,17},{17,25},{25,1},{2,10},{10... | collective-permute-start | bytes 2752520 | tf_op jit(solution)/shard_map/ppermute | solution.py:349
  242.1 145.6 %reduce-scatter.11.cloned.1.call-start = ((), (), s32[]{:S(2)}) async-start(), calls=%async_computation.12 | async-start | bytes 7077888 | tf_op jit(solution)/shard_map/reduce_scatter | solution.py:448
  306.1 98.0 %reduce-scatter.5.cloned.1.call-start = ((), (), s32[]{:S(2)}) async-start(), calls=%async_computation.5 | async-start | bytes 7077888 | tf_op jit(solution)/shard_map/reduce_scatter | solution.py:430
  330.0 121.9 %reduce-scatter.9.cloned.1.call-start = ((), (), s32[]{:S(2)}) async-start(), calls=%async_computation.10 | async-start | bytes 7077888 | tf_op jit(solution)/shard_map/reduce_scatter | solution.py:448
  367.2 261.9 %all-gather.11.cloned.1.call-start = ((), (), s32[]{:S(2)}) async-start(), calls=%async_computation.8 | async-start | bytes 7077888 | tf_op jit(solution)/shard_map/all_gather | solution.py:399
  386.4 247.9 %all-gather.17.cloned.1.call-start = ((), (), s32[]{:S(2)}) async-start(), calls=%async_computation.13 | async-start | bytes 7077888 | tf_op jit(solution)/shard_map/all_gather | solution.py:399
  404.1 235.4 %all-gather.9.cloned.1.call-start = ((), (), s32[]{:S(2)}) async-start(), calls=%async_computation.6 | async-start | bytes 7077888 | tf_op jit(solution)/shard_map/all_gather | solution.py:399
  418.8 225.8 %all-gather.15.cloned.1.call-start = ((), (), s32[]{:S(2)}) async-start(), calls=%async_computation.11 | async-start | bytes 7077888 | tf_op jit(solution)/shard_map/all_gather | solution.py:399
  425.9 55.3 %collective-permute-start.39 = (f32[1,1792]{1,0:T(1,128)S(1)}, f32[1,1792]{1,0:T(1,128)S(1)}, u32[]{:S(2)}, u32[]{:S(2)}) collective-permute-start(f32[1,1792]{1,0:T(1,128)S(1)} %broadcast_in_dim.148), channel_id=1, source_target_pairs={{0,8},{8,0},{16,24},{24,16},{1,9},{9,1},{17,25},{25,17},{2,10},{10... | collective-permute-start | bytes 21512 | tf_op jit(solution)/shard_map/ppermute | solution.py:354
  428.1 37.2 %collective-permute-start.29 = (f32[4,2048]{1,0:T(4,128)S(1)}, f32[4,2048]{1,0:T(4,128)S(1)}, u32[]{:S(2)}, u32[]{:S(2)}) collective-permute-start(f32[4,2048]{1,0:T(4,128)S(1)} %add_reduce_fusion), channel_id=1, source_target_pairs={{0,1},{1,0},{2,3},{3,2},{4,5},{5,4},{6,7},{7,6},{8,9},{9,8},{10,11... | collective-permute-start | bytes 98312 | tf_op jit(solution)/shard_map/ppermute | solution.py:354
  475.2 59.6 %collective-permute-start.43 = (bf16[640,512]{1,0:T(8,128)(2,1)S(1)}, bf16[640,512]{1,0:T(8,128)(2,1)S(1)}, u32[]{:S(2)}, u32[]{:S(2)}) collective-permute-start(bf16[640,512]{1,0:T(8,128)(2,1)S(1)} %copy-done.31), channel_id=1, source_target_pairs={{0,24},{8,0},{16,8},{24,16},{1,25},{9,1},{17,9},{25,17},{2,26},{10... | collective-permute-start | bytes 1966088 | tf_op jit(solution)/shard_map/ppermute | solution.py:349
  477.9 68.7 %collective-permute-start.41 = (bf16[640,512]{1,0:T(8,128)(2,1)S(1)}, bf16[640,512]{1,0:T(8,128)(2,1)}, u32[]{:S(2)}, u32[]{:S(2)}) collective-permute-start(bf16[640,512]{1,0:T(8,128)(2,1)S(1)} %copy-done.30), channel_id=1, source_target_pairs={{0,8},{8,16},{16,24},{24,0},{1,9},{9,17},{17,25},{25,1},{2,10},{10... | collective-permute-start | bytes 1966088 | tf_op jit(solution)/shard_map/ppermute | solution.py:349
  477.9 42.7 %collective-permute-start.45 = (bf16[256,1024]{1,0:T(8,128)(2,1)S(1)}, bf16[256,1024]{1,0:T(8,128)(2,1)}, u32[]{:S(2)}, u32[]{:S(2)}) collective-permute-start(bf16[256,1024]{1,0:T(8,128)(2,1)S(1)} %fusion.67), channel_id=1, source_target_pairs={{0,8},{8,16},{16,24},{24,0},{1,9},{9,17},{17,25},{25,1},{2,10},{10... | collective-permute-start | bytes 1572872 | tf_op jit(solution)/shard_map/ppermute | solution.py:349
  478.5 23.0 %collective-permute-start.37 = (bf16[256,768]{1,0:T(8,128)(2,1)}, bf16[256,768]{1,0:T(8,128)(2,1)}, u32[]{:S(2)}, u32[]{:S(2)}) collective-permute-start(bf16[256,768]{1,0:T(8,128)(2,1)} %fusion.76), channel_id=1, source_target_pairs={{0,24},{8,0},{16,8},{24,16},{1,25},{9,1},{17,9},{25,17},{2,26},{10... | collective-permute-start | bytes 1179656 | tf_op jit(solution)/shard_map/ppermute | solution.py:349
  487.2 42.6 %collective-permute-start.47 = (bf16[256,1024]{1,0:T(8,128)(2,1)S(1)}, bf16[256,1024]{1,0:T(8,128)(2,1)}, u32[]{:S(2)}, u32[]{:S(2)}) collective-permute-start(bf16[256,1024]{1,0:T(8,128)(2,1)S(1)} %fusion.70), channel_id=1, source_target_pairs={{0,24},{8,0},{16,8},{24,16},{1,25},{9,1},{17,9},{25,17},{2,26},{10... | collective-permute-start | bytes 1572872 | tf_op jit(solution)/shard_map/ppermute | solution.py:349
  515.1 39.0 %collective-permute-start.40 = (f32[1,1792]{1,0:T(1,128)S(1)}, f32[1,1792]{1,0:T(1,128)S(1)}, u32[]{:S(2)}, u32[]{:S(2)}) collective-permute-start(f32[1,1792]{1,0:T(1,128)S(1)} %reshape_add_fusion), channel_id=1, source_target_pairs={{0,16},{8,24},{16,0},{24,8},{1,17},{9,25},{17,1},{25,9},{2,18},{10... | collective-permute-start | bytes 21512 | tf_op jit(solution)/shard_map/ppermute | solution.py:354
  520.6 36.7 %collective-permute-start.33 = (f32[4,512]{1,0:T(4,128)S(1)}, f32[4,512]{1,0:T(4,128)S(1)}, u32[]{:S(2)}, u32[]{:S(2)}) collective-permute-start(f32[4,512]{1,0:T(4,128)S(1)} %get-tuple-element.106), channel_id=1, source_target_pairs={{0,16},{8,24},{16,0},{24,8},{1,17},{9,25},{17,1},{25,9},{2,18},{10... | collective-permute-start | bytes 24584 | tf_op jit(solution)/shard_map/ppermute | solution.py:349
  529.8 27.6 %collective-permute-start.32 = (f32[4,512]{1,0:T(4,128)S(1)}, f32[4,512]{1,0:T(4,128)S(1)}, u32[]{:S(2)}, u32[]{:S(2)}) collective-permute-start(f32[4,512]{1,0:T(4,128)S(1)} %get-tuple-element.107), channel_id=1, source_target_pairs={{0,8},{8,16},{16,24},{24,0},{1,9},{9,17},{17,25},{25,1},{2,10},{10... | collective-permute-start | bytes 24584 | tf_op jit(solution)/shard_map/ppermute | solution.py:349
  535.7 23.6 %collective-permute-start.34 = (f32[4,512]{1,0:T(4,128)S(1)}, f32[4,512]{1,0:T(4,128)S(1)}, u32[]{:S(2)}, u32[]{:S(2)}) collective-permute-start(f32[4,512]{1,0:T(4,128)S(1)} %bitcast.123), channel_id=1, source_target_pairs={{0,24},{8,0},{16,8},{24,16},{1,25},{9,1},{17,9},{25,17},{2,26},{10... | collective-permute-start | bytes 24584 | tf_op jit(solution)/shard_map/ppermute | solution.py:349
  557.3 40.4 %collective-permute-start.48 = (bf16[512,1024]{1,0:T(8,128)(2,1)S(1)}, bf16[512,1024]{1,0:T(8,128)(2,1)S(1)}, u32[]{:S(2)}, u32[]{:S(2)}) collective-permute-start(bf16[512,1024]{1,0:T(8,128)(2,1)S(1)} %copy-done.27), channel_id=1, source_target_pairs={{0,24},{8,0},{16,8},{24,16},{1,25},{9,1},{17,9},{25,17},{2,26},{10... | collective-permute-start | bytes 3145736 | tf_op jit(solution)/shard_map/ppermute | solution.py:349
  557.4 40.3 %collective-permute-start.46 = (bf16[512,1024]{1,0:T(8,128)(2,1)S(1)}, bf16[512,1024]{1,0:T(8,128)(2,1)S(1)}, u32[]{:S(2)}, u32[]{:S(2)}) collective-permute-start(bf16[512,1024]{1,0:T(8,128)(2,1)S(1)} %copy-done.26), channel_id=1, source_target_pairs={{0,8},{8,16},{16,24},{24,0},{1,9},{9,17},{17,25},{25,1},{2,10},{10... | collective-permute-start | bytes 3145736 | tf_op jit(solution)/shard_map/ppermute | solution.py:349
  559.3 56.5 %collective-permute-start.42 = (bf16[1280,512]{1,0:T(8,128)(2,1)S(1)}, bf16[1280,512]{1,0:T(8,128)(2,1)S(1)}, u32[]{:S(2)}, u32[]{:S(2)}) collective-permute-start(bf16[1280,512]{1,0:T(8,128)(2,1)S(1)} %fusion.29), channel_id=1, source_target_pairs={{0,8},{8,16},{16,24},{24,0},{1,9},{9,17},{17,25},{25,1},{2,10},{10... | collective-permute-start | bytes 3932168 | tf_op jit(solution)/shard_map/ppermute | solution.py:349
  568.3 54.2 %collective-permute-start.44 = (bf16[1280,512]{1,0:T(8,128)(2,1)S(1)}, bf16[1280,512]{1,0:T(8,128)(2,1)S(1)}, u32[]{:S(2)}, u32[]{:S(2)}) collective-permute-start(bf16[1280,512]{1,0:T(8,128)(2,1)S(1)} %fusion.26), channel_id=1, source_target_pairs={{0,24},{8,0},{16,8},{24,16},{1,25},{9,1},{17,9},{25,17},{2,26},{10... | collective-permute-start | bytes 3932168 | tf_op jit(solution)/shard_map/ppermute | solution.py:349
  (86 other events, 1479.7 us)
Sparse Core Ops, SparseCore 0:
  33.3 64.9 all-gather.6
  100.5 65.0 all-gather.12
  242.2 40.0 reduce-scatter.6
  306.2 40.0 reduce-scatter.10
  348.5 39.6 reduce-scatter.4
  390.4 39.6 reduce-scatter.8
  431.7 39.1 all-gather.10
  472.5 39.5 all-gather.16
  513.7 37.9 all-gather.8
  553.1 38.3 all-gather.14

commit v3 on v2

--- a/solution.py
+++ b/solution.py
@@ -13,6 +13,7 @@
 LANES = 128
 Q_ROWS = 256
 LN_ROWS = 64
+MIB = 1024 * 1024
 TILE = 256
 SQRT_HALF = 0.5 ** 0.5
 INV_SQRT_2PI = 0.3989422804014327
@@ -130,7 +131,7 @@
     rot_scratch = pltpu.VMEM((seq_len, width), jnp.bfloat16)
     acc_scratch = pltpu.VMEM((seq_len, width), jnp.float32)
     pairs = n_seq * seq_len * seq_len // 2
-    params = pltpu.CompilerParams(dimension_semantics=("arbitrary",), vmem_limit_bytes=56 * 1024 * 1024)
+    params = pltpu.CompilerParams(dimension_semantics=("arbitrary",), vmem_limit_bytes=32 * MIB)
     forward = pl.pallas_call(
         functools.partial(attn_fwd_kernel, half=half, scale=scale, span=span),
         grid=(n_seq,),
@@ -170,24 +171,45 @@
         copy.wait()
 
 
-def place_groups(fulls, row):
-    groups, tokens, width = fulls[0].shape
-    n_seq = len(fulls)
-    out = None
-    for chunk, full in enumerate(fulls):
-        operands = (row.reshape(1), full) + (() if out is None else (out,))
-        any_spec = pl.BlockSpec(memory_space=pl.ANY)
-        out = pl.pallas_call(
-            functools.partial(place_kernel, chunk=chunk, n_seq=n_seq),
-            in_specs=[pl.BlockSpec(memory_space=pltpu.SMEM)] + [any_spec] * (len(operands) - 1),
-            out_specs=any_spec,
-            out_shape=jax.ShapeDtypeStruct((groups * n_seq, tokens, width), full.dtype),
-            scratch_shapes=[pltpu.VMEM(full.shape, full.dtype), pltpu.SemaphoreType.DMA((groups,)), pltpu.SemaphoreType.DMA((groups,))],
-            input_output_aliases={} if chunk == 0 else {2: 0},
-            name="place_groups",
-            cost_estimate=pl.CostEstimate(flops=4 * full.size, bytes_accessed=4 * full.size, transcendentals=0),
-        )(*operands)
-    return out
+def place_pieces_kernel(place_ref, *refs, chunk, n_seq):
+    out_ref, held_ref, in_sems, out_sems = refs[-4:]
+    groups, own, _ = refs[0].shape
+    columns = held_ref.shape[0] // 2
+    row, column, core = place_ref[0], place_ref[1], place_ref[2]
+    fetch, store = [], []
+    for index in range(2 * columns):
+        source = 2 * lax.rem(column + index % columns, columns) + (core if index < columns else 1 - core)
+        at = pl.ds(pl.multiple_of(source * own, own), own)
+        fetch.append(pltpu.make_async_copy(refs[index], held_ref.at[index], in_sems.at[index]))
+        for t in range(groups):
+            piece = held_ref.at[index, lax.rem(row + groups - t, groups)]
+            store.append(pltpu.make_async_copy(piece, out_ref.at[t * n_seq + chunk, at], out_sems.at[index]))
+    for copy in fetch:
+        copy.start()
+    for index in range(2 * columns):
+        fetch[index].wait()
+        for copy in store[index * groups:(index + 1) * groups]:
+            copy.start()
+    for copy in store:
+        copy.wait()
+
+
+def place_call(kernel, place, operands, out, chunk, n_seq, tokens):
+    groups, _, width = operands[0].shape
+    operands = [place, *operands] + ([] if out is None else [out])
+    any_spec = pl.BlockSpec(memory_space=pl.ANY)
+    pieces = len(operands) - 1 - (out is not None)
+    held = operands[1].shape if pieces == 1 else (pieces,) + operands[1].shape
+    sems = pltpu.SemaphoreType.DMA((groups if pieces == 1 else pieces,))
+    return pl.pallas_call(
+        functools.partial(kernel, chunk=chunk, n_seq=n_seq),
+        in_specs=[pl.BlockSpec(memory_space=pltpu.SMEM)] + [any_spec] * (len(operands) - 1),
+        out_specs=any_spec,
+        out_shape=jax.ShapeDtypeStruct((groups * n_seq, tokens, width), jnp.bfloat16),
+        scratch_shapes=[pltpu.VMEM(held, jnp.bfloat16), sems, sems],
+        input_output_aliases={} if out is None else {len(operands) - 1: 0},
+        cost_estimate=pl.CostEstimate(flops=groups * tokens * width, bytes_accessed=4 * groups * tokens * width, transcendentals=0),
+    )(*operands)
 
 
 def split_width(value, out_refs):
@@ -215,17 +237,17 @@
     split_width(cot_ref[...].astype(jnp.float32) + inv_std * (value_a6 - mean_a6 - x_hat * mean_a6x), out_refs)
 
 
-def row_call(kernel, parts, *operands):
-    n_rows, width = operands[0].shape
-    rows = 128 if n_rows % 128 == 0 else n_rows
-    specs = [pl.BlockSpec((rows, width), lambda s: (s, 0)) if op.shape[0] == n_rows else pl.BlockSpec(op.shape, lambda s: (0, 0)) for op in operands]
+def row_call(kernel, parts, index, rows, *operands):
+    width = operands[0].shape[1]
+    specs = [pl.BlockSpec((min(rows, op.shape[0]), width), lambda s, i=(index if op.shape[0] > rows else 0): (i, 0)) for op in operands]
     return pl.pallas_call(
         kernel,
-        grid=(n_rows // rows,),
+        grid=(1,),
         in_specs=specs,
-        out_specs=[pl.BlockSpec((rows, width // parts), lambda s: (s, 0))] * parts,
-        out_shape=[jax.ShapeDtypeStruct((n_rows, width // parts), jnp.bfloat16)] * parts,
-        cost_estimate=pl.CostEstimate(flops=16 * n_rows * width, bytes_accessed=8 * n_rows * width, transcendentals=0),
+        out_specs=[pl.BlockSpec((rows, width // parts), lambda s: (0, 0))] * parts,
+        out_shape=[jax.ShapeDtypeStruct((rows, width // parts), jnp.bfloat16)] * parts,
+        compiler_params=pltpu.CompilerParams(vmem_limit_bytes=16 * MIB),
+        cost_estimate=pl.CostEstimate(flops=16 * rows * width, bytes_accessed=8 * rows * width, transcendentals=0),
     )(*operands)
 
 
@@ -233,26 +255,41 @@
     return value.reshape(value.shape[0] // 8, 8, value.shape[1]).sum(0)
 
 
-def front_kernel(x_ref, small_ref, w_ref, b_qkv_ref, b_up_ref, h_attn_ref, h_mlp_ref, qkv_ref, pre_ref, gelu_ref):
+def front_kernel(x_ref, next_ref, small_ref, w_ref, b_qkv_ref, b_up_ref, h_attn_ref, h_mlp_ref, qkv_ref, pre_ref, gelu_ref, norm_ref):
     rows = x_ref.shape[0]
-
-    @pl.loop(0, rows // LN_ROWS)
-    def _(step):
-        at = pl.ds(pl.multiple_of(step * LN_ROWS, LN_ROWS), LN_ROWS)
-        x_hat, _ = normalize(x_ref[at, :])
-        h_attn_ref[at, :] = (x_hat * small_ref[0:1, :] + small_ref[1:2, :]).astype(jnp.bfloat16)
-        h_mlp_ref[at, :] = (x_hat * small_ref[2:3, :] + small_ref[3:4, :]).astype(jnp.bfloat16)
+    step = pl.program_id(0)
+    now = lax.rem(step, 2)
+
+    def norm(from_ref, slot, at):
+        x_hat, _ = normalize(from_ref[at, :])
+        norm_ref[slot, 0, at, :] = (x_hat * small_ref[0:1, :] + small_ref[1:2, :]).astype(jnp.bfloat16)
+        norm_ref[slot, 1, at, :] = (x_hat * small_ref[2:3, :] + small_ref[3:4, :]).astype(jnp.bfloat16)
+
+    @pl.when(step == 0)
+    def _():
+        @pl.loop(0, rows // LN_ROWS)
+        def _(part):
+            norm(x_ref, 0, pl.ds(pl.multiple_of(part * LN_ROWS, LN_ROWS), LN_ROWS))
 
     qkv_width = qkv_ref.shape[1]
-    for low in range(0, qkv_width, TILE):
-        acc = dot(h_attn_ref[...], w_ref[:, low:low + TILE], NN) + b_qkv_ref[:, low:low + TILE]
-        qkv_ref[:, low:low + TILE] = acc.astype(jnp.bfloat16)
-    for low in range(0, pre_ref.shape[1], TILE):
-        acc = dot(h_mlp_ref[...], w_ref[:, qkv_width + low:qkv_width + low + TILE], NN) + b_up_ref[:, low:low + TILE]
-        pre = acc.astype(jnp.bfloat16)
-        pre_ref[:, low:low + TILE] = pre
-        wide = pre.astype(jnp.float32)
-        gelu_ref[:, low:low + TILE] = (0.5 * wide * (1.0 + lax.erf(wide * SQRT_HALF))).astype(jnp.bfloat16)
+    tiles = [(0, low) for low in range(0, qkv_width, TILE)] + [(1, low) for low in range(0, pre_ref.shape[1], TILE)]
+    ahead = -(-rows // (len(tiles) * 16)) * 16
+    for index, (which, low) in enumerate(tiles):
+        at = slice(low, low + TILE)
+        if which == 0:
+            qkv_ref[:, at] = (dot(norm_ref[now, 0], w_ref[:, at], NN) + b_qkv_ref[:, at]).astype(jnp.bfloat16)
+        else:
+            acc = dot(norm_ref[now, 1], w_ref[:, qkv_width + low:qkv_width + low + TILE], NN) + b_up_ref[:, at]
+            pre = acc.astype(jnp.bfloat16)
+            pre_ref[:, at] = pre
+            wide = pre.astype(jnp.float32)
+            gelu_ref[:, at] = (0.5 * wide * (1.0 + lax.erf(wide * SQRT_HALF))).astype(jnp.bfloat16)
+        start, stop = index * ahead, min(rows, (index + 1) * ahead)
+        if start < stop:
+            rows_at = slice(start, stop)
+            norm(next_ref, 1 - now, rows_at)
+            h_attn_ref[rows_at, :] = norm_ref[now, 0, rows_at, :]
+            h_mlp_ref[rows_at, :] = norm_ref[now, 1, rows_at, :]
 
 
 def y_kernel(ctx_ref, gelu_ref, *refs):
@@ -310,12 +347,15 @@
         sums_ref[3, :, at] += sublane_sum(d_mlp)
 
 
-def tile_call(kernel, tiled, whole, outs, row_range, flops):
+def tile_call(kernel, tiled, whole, outs, row_range, flops, limit, ahead=False):
     start, count = row_range
     rows = next(r for r in (512, 256, 128, 64, count) if count % r == 0)
     first = start // rows
     in_specs = [pl.BlockSpec((rows, op.shape[1]), lambda s, f=(first if op.shape[0] != count else 0): (s + f, 0)) for op in tiled]
-    in_specs += [pl.BlockSpec(op.shape, lambda s, n=op.ndim: (0,) * n) for op in whole]
+    if ahead:
+        in_specs.append(pl.BlockSpec((rows, tiled[0].shape[1]), lambda s: (jnp.minimum(s + 1, count // rows - 1), 0)))
+        tiled = [*tiled, tiled[0]]
+    in_specs += [pl.BlockSpec(op.shape, lambda s, n=op.ndim: (0,) * n, pipeline_mode=pl.Buffered(1)) for op in whole]
     out_specs, out_shapes = [], []
     for form, dtype in outs:
         if isinstance(form, int):
@@ -331,7 +371,8 @@
         in_specs=in_specs,
         out_specs=out_specs,
         out_shape=out_shapes,
-        compiler_params=pltpu.CompilerParams(dimension_semantics=("arbitrary",), vmem_limit_bytes=60 * 1024 * 1024),
+        compiler_params=pltpu.CompilerParams(dimension_semantics=("arbitrary",), vmem_limit_bytes=limit * MIB),
+        scratch_shapes=[pltpu.VMEM((2, 2, rows, tiled[0].shape[1]), jnp.bfloat16)] if ahead else [],
         cost_estimate=pl.CostEstimate(flops=flops, bytes_accessed=moved, transcendentals=0),
     )(*tiled, *whole)
 
@@ -355,14 +396,21 @@
             step *= 2
         return value
 
-    def ring_gather(block):
+    def along(value, hops):
+        return lax.ppermute(value, 'ty', [(s, (s - 2 * hops) % ty_size) for s in range(ty_size)])
+
+    def partner(value):
+        return lax.ppermute(value, 'ty', [(s, s ^ 1) for s in range(ty_size)])
+
+    def ring_gather(block, move, size):
+        far = size // 2
         blocks = {0: block}
-        for hops in range(1, antipode):
-            blocks[hops] = shift(blocks[hops - 1], 1)
-            blocks[tx_size - hops] = shift(blocks[(tx_size - hops + 1) % tx_size], -1)
-        rows = block.shape[0] // 2
-        blocks[antipode] = jnp.concatenate([shift(blocks[antipode - 1][:rows], 1), shift(blocks[antipode + 1][rows:], -1)], axis=0)
-        return [blocks[r] for r in range(tx_size)]
+        for hops in range(1, far):
+            blocks[hops] = move(blocks[hops - 1], 1)
+            blocks[size - hops] = move(blocks[(size - hops + 1) % size], -1)
+        half = block.shape[0] // 2
+        blocks[far] = jnp.concatenate([move(blocks[far - 1][:half], 1), move(blocks[far + 1][half:], -1)], axis=0)
+        return [blocks[r] for r in range(size)]
 
     def ring_scatter(make_part, rows):
         half = rows // 2
@@ -394,9 +442,10 @@
             blocks = [pick(row)] + [shift(pick((row - r) % tx_size), r) for r in range(1, tx_size)]
             return jnp.concatenate(blocks, axis=2)
 
+        place = jnp.stack([row, col // 2, col % 2])
+
         def to_width(parts):
-            blocks = [parts[0]] + [shift(parts[r], -r) for r in range(1, tx_size)]
-            return lax.all_gather(jnp.stack(blocks), 'ty', axis=1, tiled=True)
+            return jnp.stack([parts[0]] + [shift(parts[r], -r) for r in range(1, tx_size)])
 
         line = lax.broadcasted_iota(jnp.int32, (8, d_local), 0)
         small = jnp.zeros((8, d_local), jnp.bfloat16)
@@ -411,43 +460,47 @@
         cot_group = lax.all_gather(cot_own, 'ty', axis=1, tiled=True)
         x_group, cot_group = x_group.reshape(n_seq * seq_len, -1), cot_group.reshape(n_seq * seq_len, -1)
         w_in = jnp.concatenate([w_qkv.reshape(d_local, qkv_width), w_up], axis=1)
-        w_in = ring_gather(w_in)
+        w_in = ring_gather(w_in, shift, tx_size)
         w_in = jnp.concatenate(w_in, axis=0)
-        w_back = ring_gather(jnp.concatenate([w_dense, w_down], axis=0))
+        w_back = ring_gather(jnp.concatenate([w_dense, w_down], axis=0), shift, tx_size)
         back_size = tx_size * w_back[0].size
 
         n_tok, d_model = x_group.shape
+        x_rows, cot_rows = x_own.reshape(-1, d_model), cot_own.reshape(-1, d_model)
         ff_width = w_up.shape[1]
         h_attn, h_mlp, qkv_act, pre_act, gelu_out = tile_call(
             front_kernel, [x_group], [small, w_in, b_qkv.reshape(1, -1).astype(jnp.float32), b_up.reshape(1, -1).astype(jnp.float32)],
             [(d_model, jnp.bfloat16), (d_model, jnp.bfloat16), (qkv_width, jnp.bfloat16), (ff_width, jnp.bfloat16), (ff_width, jnp.bfloat16)],
-            (0, n_tok), 2 * n_tok * w_in.size)
+            (0, n_tok), 2 * n_tok * w_in.size, 48, True)
         qkv_seq = qkv_act.reshape(n_seq, seq_len, qkv_width)
-        context, y_full = [], []
+        context, y_out = [], None
         for s in chunks:
             context.append(attention[s][0](qkv_seq).reshape(seq_len, head))
-            (y_part,) = tile_call(y_kernel, [context[s], gelu_out], w_back, [(d_model, jnp.bfloat16)], (s * seq_len, seq_len), 2 * seq_len * back_size)
+            (y_part,) = tile_call(y_kernel, [context[s], gelu_out], w_back, [(d_model, jnp.bfloat16)], (s * seq_len, seq_len), 2 * seq_len * back_size, 24)
             mixed = lax.psum_scatter(y_part, 'ty', scatter_dimension=0, tiled=True)
-            y_full.append(to_width(row_call(finish_y_kernel, tx_size, x_own[s], mixed, bias_out.reshape(1, -1))))
-        y_out = place_groups(y_full, row)
+            blocks = to_width(row_call(finish_y_kernel, tx_size, s, own, x_rows, mixed, bias_out.reshape(1, -1)))
+            full = lax.all_gather(blocks, 'ty', axis=1, tiled=True)
+            y_out = place_call(place_kernel, place, [full], y_out, s, n_seq, seq_len)
         context = jnp.concatenate(context, axis=0)
 
         d_ctx, d_pre, d_b_up = tile_call(
             d_pre_kernel, [cot_group, pre_act], w_back,
-            [(head, jnp.bfloat16), (ff_width, jnp.bfloat16), ((8, ff_width), jnp.float32)], (0, n_tok), 2 * n_tok * back_size)
+            [(head, jnp.bfloat16), (ff_width, jnp.bfloat16), ((8, ff_width), jnp.float32)], (0, n_tok), 2 * n_tok * back_size, 32)
         d_ctx, d_b_up = d_ctx.reshape(n_seq, seq_len, head), d_b_up.sum(0)
-        d_qkv, d_b_qkv, d_ln, dx_full = [], [], [], []
+        d_qkv, d_b_qkv, d_ln, dx_act = [], [], [], None
         for s in chunks:
             d_qkv_seq, d_b_seq = attention[s][1](qkv_seq, d_ctx)
             d_qkv.append(d_qkv_seq.reshape(seq_len, qkv_width))
             d_b_qkv.append(d_b_seq.reshape(-1))
             a6_part, sums = tile_call(
                 d_h_kernel, [d_qkv[s], d_pre, x_group], [small, w_in],
-                [(d_model, jnp.bfloat16), ((4, 8, d_model), jnp.float32)], (s * seq_len, seq_len), 2 * seq_len * w_in.size)
+                [(d_model, jnp.bfloat16), ((4, 8, d_model), jnp.float32)], (s * seq_len, seq_len), 2 * seq_len * w_in.size, 32)
             d_ln.append(sums)
             value_a6 = lax.psum_scatter(a6_part, 'ty', scatter_dimension=0, tiled=True)
-            dx_full.append(to_width(row_call(finish_dx_kernel, tx_size, x_own[s], value_a6, cot_own[s])))
-        dx_act = place_groups(dx_full, row)
+            parts = row_call(finish_dx_kernel, tx_size, s, own, x_rows, value_a6, cot_rows)
+            blocks = ring_gather(to_width(parts), along, ty_size // 2)
+            blocks = blocks + [partner(block) for block in blocks]
+            dx_act = place_call(place_pieces_kernel, place, blocks, dx_act, s, n_seq, seq_len)
         d_qkv = jnp.concatenate(d_qkv, axis=0)
 
         d_ln = small_sum(sum(d_ln).sum(1), 'ty', ty_size).reshape(4, tx_size, d_local)

time: 662 us -> 717 us (1.083)
  local copies, waits for them, and re-layouts: 18.2 us -> 68.2 us
  Pallas kernels: 225 us -> 193 us
  matrix products: 81.5 us -> 96.5 us
  waiting for transfers between devices: 217 us -> 226 us
    unnamed x126 -> x218, local copies, waits for them, and re-layouts: 9.15 us -> 58.2 us
    dot_general x16, matrix products: 81.5 us -> 96.5 us  [dot(): return lax.dot_general(a, b, dims, preferred_element_type=jnp.float32)]
    ppermute x0 -> x16, waiting for transfers between devices: none -> 14.7 us  [the longest x8 14.7 us: along(): lax.ppermute(value, 'ty', [(s, (s - 2 * hops) % ty_size) for s in range(t...]
    ppermute x0 -> x16, starting transfers between devices: none -> 12.9 us  [the longest x8 11.3 us: along(): lax.ppermute(value, 'ty', [(s, (s - 2 * hops) % ty_size) for s in range(t...]
    pallas_call x6, Pallas kernels: 142 us -> 130 us  [tile_call(): pl.pallas_call(kernel, grid=(count // rows,), in_specs=in_specs, out_spec...]
    pallas_call x2, Pallas kernels: 29.7 us -> 21.6 us  [attention_calls(): backward(qkv, dctx, *tables)]
  transfers between devices with their start and end apart: 59 -> 73, of which waited for: 24 -> 23; matrix products, arithmetic and copies ran while one was open for 18% -> 19% of each run, Pallas kernels for 33% -> 27%
where the time goes in v3:
time: 717 us; the launch traced here: 706 us
  waiting for transfers between devices  226 us (32%)
  Pallas kernels  193 us (27%)
  matrix products  96.5 us (13%)
  starting transfers between devices  79.7 us (11%)
  local copies, waits for them, and re-layouts  68.2 us (10%)
  other arithmetic  26.1 us (4%)
  between operations  15.9 us (2%)
    ppermute x44, waiting for transfers between devices, shift(): lax.ppermute(value, 'tx', [(s, (s - hops) % tx_size) for s in range(tx_si...  211 us
    pallas_call x6, Pallas kernels, tile_call(): pl.pallas_call(kernel, grid=(count // rows,), in_specs=in_specs, out_spec...  130 us
    dot_general x16, matrix products, dot(): return lax.dot_general(a, b, dims, preferred_element_type=jnp.float32)  96.5 us
    ppermute x44, starting transfers between devices, shift(): lax.ppermute(value, 'tx', [(s, (s - hops) % tx_size) for s in range(tx_si...  60.6 us
    unnamed x218, local copies, waits for them, and re-layouts  58.2 us
    pallas_call x4, Pallas kernels, place_call(): pl.pallas_call(functools.partial(kernel, chunk=chunk, n_seq=n_seq), in_sp...  23.9 us
    pallas_call x2, Pallas kernels, attention_calls(): backward(qkv, dctx, *tables)  21.6 us
    pallas_call x2, Pallas kernels, attention_calls(): forward(qkv, *tables)  14.9 us
  transfers between devices with their start and end apart: 73, of which 23 were waited for; matrix products, arithmetic and copies ran while one was open for 19% of the time, Pallas kernels for 27%

profile of v3, /device:TPU:98, one launch (start us, length us, event | category | flops | bytes accessed | tf_op | source)
XLA Modules:
  0.0 706.0 jit_solution(5213715223959426963)
XLA Ops:
  15.8 6.9 collective-permute-done.2
  22.7 9.6 %collective-permute-done.1 = bf16[2,192,512]{2,1,0:T(8,128)(2,1)S(1)} collective-permute-done((bf16[2,192,512]{2,1,0:T(8,128)(2,1)S(1)}, bf16[2,192,512]{2,1,0:T(8,128)(2,1)S(1)}, u32[]{:S(2)}, u32[]{:S(2)}) %collective-permute-start.1) | collective-permute-done | bytes 393248 | tf_op jit(solution)/shard_map/ppermute | solution.py:390
  40.9 6.8 collective-permute-done.22
  47.7 9.6 %collective-permute-done.21 = bf16[2,192,512]{2,1,0:T(8,128)(2,1)S(1)} collective-permute-done((bf16[2,192,512]{2,1,0:T(8,128)(2,1)S(1)}, bf16[2,192,512]{2,1,0:T(8,128)(2,1)S(1)}, u32[]{:S(2)}, u32[]{:S(2)}) %collective-permute-start.21) | collective-permute-done | bytes 393248 | tf_op jit(solution)/shard_map/ppermute | solution.py:390
  67.3 67.2 %collective-permute-done.12.refs_3_ = bf16[1280,512]{1,0:T(8,128)(2,1)S(1)} collective-permute-done((bf16[1280,512]{1,0:T(8,128)(2,1)S(1)}, bf16[1280,512]{1,0:T(8,128)(2,1)S(1)}, u32[]{:S(2)}, u32[]{:S(2)}) %collective-permute-start.12) | collective-permute-done | bytes 1310752 | tf_op jit(solution)/shard_map/ppermute | solution.py:390
  148.7 8.3 %collective-permute-done.11 = bf16[640,512]{1,0:T(8,128)(2,1)S(1)} collective-permute-done((bf16[640,512]{1,0:T(8,128)(2,1)S(1)}, bf16[640,512]{1,0:T(8,128)(2,1)S(1)}, u32[]{:S(2)}, u32[]{:S(2)}) %collective-permute-start.11) | collective-permute-done | bytes 655392 | tf_op jit(solution)/shard_map/ppermute | solution.py:390
  158.4 15.6 %collective-permute-done.7 = bf16[256,1792]{1,0:T(8,128)(2,1)S(1)} collective-permute-done((bf16[256,1792]{1,0:T(8,128)(2,1)S(1)}, bf16[256,1792]{1,0:T(8,128)(2,1)S(1)}, u32[]{:S(2)}, u32[]{:S(2)}) %collective-permute-start.7) | collective-permute-done | bytes 917536 | tf_op jit(solution)/shard_map/ppermute | solution.py:390
  177.4 47.7 %shard_map.245 = (bf16[3072,2048]{1,0:T(8,128)(2,1)}, bf16[3072,2048]{1,0:T(8,128)(2,1)}, bf16[3072,768]{1,0:T(8,128)(2,1)S(1)}, bf16[3072,1024]{1,0:T(8,128)(2,1)}, bf16[3072,1024]{1,0:T(8,128)(2,1)}) custom-call(bf16[3072,2048]{1,0:T(8,128)(2,1)} %bitcast.168, bf16[3072,2048]{1,0:T(8,128)(2,1)} %bitcast.169, f32[8,2048]{1,0:T(8,128)S(1)} %maximum_convert_fusion.small_ref, ...), custom_call_target="tpu_custom_call" | custom-call | flops 22548578304 | bytes 75009536 | tf_op jit(solution)/shard_map/pallas_call | solution.py:368
  225.2 7.5 %attn_fwd.3 = bf16[1,1536,256]{2,1,0:T(8,128)(2,1)S(1)} custom-call(bf16[2,1536,768]{2,1,0:T(8,128)(2,1)S(1)} %bitcast.95, f32[1536,128]{1,0:T(8,128)S(1)} %get-tuple-element.110.cos_ref, f32[1536,128]{1,0:T(8,128)S(1)} %get-tuple-element.109.lo_ref, f32[1536,128]{1,0:T(8,128)S(1)} %get-tuple-element.108.hi_ref), custom_call_target="tpu_custom_call" | custom-call | flops 2415919104 | bytes 3145728 | tf_op jit(solution)/shard_map/attn_fwd/pallas_call | solution.py:157
  235.8 8.6 %shard_map.248 = bf16[1536,2048]{1,0:T(8,128)(2,1)S(1)} custom-call(bf16[1536,256]{1,0:T(8,128)(2,1)S(1)} %bitcast.113, bf16[3072,1024]{1,0:T(8,128)(2,1)S(1)} %copy-done.50, bf16[1280,512]{1,0:T(8,128)(2,1)S(1)} %copy-done.26, bf16[1280,512]{1,0:T(8,128)(2,1)S(1)} %copy-done.18, bf16[1280,512]{1,0:T(8,128)(2,1)S(1)} %copy-done.22, ...), custom_call_target="tpu_custom_call" | custom-call | flops 8053063680 | bytes 15466496 | tf_op jit(solution)/shard_map/pallas_call | solution.py:368
  249.5 7.5 %attn_fwd.2 = bf16[1,1536,256]{2,1,0:T(8,128)(2,1)S(1)} custom-call(bf16[2,1536,768]{2,1,0:T(8,128)(2,1)S(1)} %bitcast.96, f32[1536,128]{1,0:T(8,128)S(1)} %get-tuple-element.110.cos_ref, f32[1536,128]{1,0:T(8,128)S(1)} %get-tuple-element.109.lo_ref, f32[1536,128]{1,0:T(8,128)S(1)} %get-tuple-element.108.hi_ref), custom_call_target="tpu_custom_call" | custom-call | flops 2415919104 | bytes 3145728 | tf_op jit(solution)/shard_map/attn_fwd/pallas_call | solution.py:157
  259.9 8.6 %shard_map.246 = bf16[1536,2048]{1,0:T(8,128)(2,1)S(1)} custom-call(bf16[1536,256]{1,0:T(8,128)(2,1)S(1)} %bitcast.118, bf16[3072,1024]{1,0:T(8,128)(2,1)S(1)} %copy-done.51, bf16[1280,512]{1,0:T(8,128)(2,1)S(1)} %copy-done.27, bf16[1280,512]{1,0:T(8,128)(2,1)S(1)} %copy-done.19, bf16[1280,512]{1,0:T(8,128)(2,1)S(1)} %copy-done.23, ...), custom_call_target="tpu_custom_call" | custom-call | flops 8053063680 | bytes 15466496 | tf_op jit(solution)/shard_map/pallas_call | solution.py:368
  281.0 24.0 %shard_map.252 = (bf16[3072,256]{1,0:T(8,128)(2,1)S(1)}, bf16[3072,1024]{1,0:T(8,128)(2,1)S(1)}, f32[8,1024]{1,0:T(8,128)S(1)}) custom-call(bf16[3072,2048]{1,0:T(8,128)(2,1)} %bitcast.159, bf16[3072,1024]{1,0:T(8,128)(2,1)S(1)} %copy-done.52, bf16[1280,512]{1,0:T(8,128)(2,1)S(1)} %copy-done.28, bf16[1280,512]{1,0:T(8,128)(2,1)S(1)} %copy-done.20, ...), custom_call_target="tpu_custom_call" | custom-call | flops 16106127360 | bytes 31997952 | tf_op jit(solution)/shard_map/pallas_call | solution.py:368
  310.2 10.8 %attn_bwd.3 = (bf16[1,1536,768]{2,1,0:T(8,128)(2,1)S(1)}, f32[1,1,768]{2,1,0:T(1,128)S(1)}) custom-call(bf16[2,1536,768]{2,1,0:T(8,128)(2,1)S(1)} %bitcast.97, bf16[2,1536,256]{2,1,0:T(8,128)(2,1)S(1)} %bitcast.111, f32[1536,128]{1,0:T(8,128)S(1)} %get-tuple-element.110.cos_ref, f32[1536,128]{1,0:T(8,128)S(1)} %get-tuple-element.109.lo_ref, ...), custom_call_target="tpu_custom_call" | custom-call | flops 6039797760 | bytes 5505024 | tf_op jit(solution)/shard_map/attn_bwd/pallas_call | solution.py:157
  321.0 20.4 %shard_map.255 = (bf16[1536,2048]{1,0:T(8,128)(2,1)S(1)}, f32[4,8,2048]{2,1,0:T(8,128)S(1)}) custom-call(bf16[1536,768]{1,0:T(8,128)(2,1)S(1)} %bitcast.99, bf16[3072,1024]{1,0:T(8,128)(2,1)S(1)} %get-tuple-element.59.d_pre_ref, bf16[3072,2048]{1,0:T(8,128)(2,1)} %bitcast.170, f32[8,2048]{1,0:T(8,128)S(1)} %maximum_convert_fusion.small_ref, ...), custom_call_target="tpu_custom_call" | custom-call | flops 11274289152 | bytes 25591808 | tf_op jit(solution)/shard_map/pallas_call | solution.py:368
  348.1 10.8 %attn_bwd.2 = (bf16[1,1536,768]{2,1,0:T(8,128)(2,1)S(1)}, f32[1,1,768]{2,1,0:T(1,128)S(1)}) custom-call(bf16[2,1536,768]{2,1,0:T(8,128)(2,1)S(1)} %bitcast.98, bf16[2,1536,256]{2,1,0:T(8,128)(2,1)S(1)} %bitcast.112, f32[1536,128]{1,0:T(8,128)S(1)} %get-tuple-element.110.cos_ref, f32[1536,128]{1,0:T(8,128)S(1)} %get-tuple-element.109.lo_ref, ...), custom_call_target="tpu_custom_call" | custom-call | flops 6039797760 | bytes 5505024 | tf_op jit(solution)/shard_map/attn_bwd/pallas_call | solution.py:157
  359.0 20.4 %shard_map.253 = (bf16[1536,2048]{1,0:T(8,128)(2,1)S(1)}, f32[4,8,2048]{2,1,0:T(8,128)S(1)}) custom-call(bf16[1536,768]{1,0:T(8,128)(2,1)S(1)} %bitcast.105, bf16[3072,1024]{1,0:T(8,128)(2,1)S(1)} %copy-done.1, bf16[3072,2048]{1,0:T(8,128)(2,1)} %bitcast.171, f32[8,2048]{1,0:T(8,128)S(1)} %maximum_convert_fusion.small_ref, ...), custom_call_target="tpu_custom_call" | custom-call | flops 11274289152 | bytes 25591808 | tf_op jit(solution)/shard_map/pallas_call | solution.py:368
  399.8 7.1 %convert_reduce_fusion = f32[512]{0:T(512)} fusion(bf16[8,1536,512]{2,1,0:T(8,128)(2,1)} %param.15), kind=kLoop, calls=%fused_computation | loop fusion | flops 12582400 | bytes 12584960 | tf_op jit(solution)/shard_map/reduce_sum | solution.py:509
  411.3 6.2 fusion.70
  421.7 6.3 fusion.57
  433.0 6.8 fusion.18
  472.7 7.0 add_convert_fusion.2
  479.8 19.2 %collective-permute-done.51 = bf16[256,768]{1,0:T(8,128)(2,1)S(1)} collective-permute-done((bf16[256,768]{1,0:T(8,128)(2,1)S(1)}, bf16[256,768]{1,0:T(8,128)(2,1)S(1)}, u32[]{:S(2)}, u32[]{:S(2)}) %collective-permute-start.51) | collective-permute-done | bytes 393248 | tf_op jit(solution)/shard_map/ppermute | solution.py:390
  505.3 6.7 add_convert_fusion.1
  516.2 8.2 %add_convert_fusion = bf16[512,1024]{1,0:T(8,128)(2,1)} fusion(bf16[3072,1024]{1,0:T(8,128)(2,1)} %copy-done, bf16[3072,2048]{1,0:T(8,128)(2,1)} %get-tuple-element.77, bf16[256,1024]{1,0:T(8,128)(2,1)} %collective-permute-done.63), kind=kOutput, calls=%fused_computation.39 | convolution fusion | flops 3222798336 | bytes 11010048 | tf_op jit(solution)/shard_map/dot_general | solution.py:27
  533.6 12.9 %fusion.26 = bf16[1280,512]{1,0:T(8,128)(2,1)} fusion(bf16[3072,2048]{1,0:T(8,128)(2,1)} %bitcast.162, bf16[3072,1024]{1,0:T(8,128)(2,1)} %get-tuple-element.47.gelu_ref, bf16[1536,256]{1,0:T(8,128)(2,1)S(1)} %bitcast.120, bf16[1536,256]{1,0:T(8,128)(2,1)S(1)} %bitcast.115, bf16[640,512]{1,0:T(8,128)(2,1)} %collective-permute-done.59), kind=kOutput, calls=%fused_computation.29 | convolution fusion | flops 4052090880 | bytes 12976128 | tf_op jit(solution)/shard_map/dot_general | solution.py:27
  557.9 7.4 %fusion.29 = bf16[1280,512]{1,0:T(8,128)(2,1)} fusion(bf16[3072,2048]{1,0:T(8,128)(2,1)} %bitcast.163, bf16[3072,1024]{1,0:T(8,128)(2,1)S(1)} %bitcast.126, bf16[1536,256]{1,0:T(8,128)(2,1)S(1)} %bitcast.121, bf16[1536,256]{1,0:T(8,128)(2,1)S(1)} %bitcast.116, bf16[640,512]{1,0:T(8,128)(2,1)} %collective-permute-done.57), kind=kOutput, calls=%fused_computation.30 | convolution fusion | flops 4052090880 | bytes 12976128 | tf_op jit(solution)/shard_map/dot_general | solution.py:27
  565.4 29.7 %collective-permute-done.25 = bf16[192,512]{1,0:T(8,128)(2,1)S(1)} collective-permute-done((bf16[192,512]{1,0:T(8,128)(2,1)S(1)}, bf16[192,512]{1,0:T(8,128)(2,1)S(1)}, u32[]{:S(2)}, u32[]{:S(2)}) %collective-permute-start.25) | collective-permute-done | bytes 196640 | tf_op jit(solution)/shard_map/ppermute | solution.py:390
  636.7 13.0 %collective-permute-done.58 = bf16[1280,512]{1,0:T(8,128)(2,1)} collective-permute-done((bf16[1280,512]{1,0:T(8,128)(2,1)}, bf16[1280,512]{1,0:T(8,128)(2,1)}, u32[]{:S(2)}, u32[]{:S(2)}) %collective-permute-start.58) | collective-permute-done | bytes 1310752 | tf_op jit(solution)/shard_map/ppermute | solution.py:390
  666.5 5.9 convert_add_fusion
  673.3 6.1 shard_map.257.refs_8_
  680.4 6.1 shard_map.258
  (435 shorter events, 251.2 us)
Async XLA Ops:
  7.2 170.3 %all-gather.5.cloned.1.call-start = ((), (), s32[]{:S(2)}) async-start(), calls=%async_computation.4 | async-start | bytes 14155776 | tf_op jit(solution)/shard_map/all_gather | solution.py:459
  34.7 238.0 %all-gather.11.cloned.1.call-start = ((), (), s32[]{:S(2)}) async-start(), calls=%async_computation.9 | async-start | bytes 14155776 | tf_op jit(solution)/shard_map/all_gather | solution.py:460
  59.6 324.9 %reduce-scatter.7.cloned.1.call-start = ((), (), s32[]{:S(2)}) async-start(), calls=%async_computation.7 | async-start | bytes 7077888 | tf_op jit(solution)/shard_map/reduce_scatter | solution.py:480
  61.4 77.1 %collective-permute-start.6 = (bf16[512,1792]{1,0:T(8,128)(2,1)S(1)}, bf16[512,1792]{1,0:T(8,128)(2,1)S(1)}, u32[]{:S(2)}, u32[]{:S(2)}) collective-permute-start(bf16[512,1792]{1,0:T(8,128)(2,1)S(1)} %get-tuple-element.100), channel_id=1, source_target_pairs={{0,24},{8,0},{16,8},{24,16},{1,25},{9,1},{17,9},{25,17},{2,26},{10... | collective-permute-start | bytes 5505032 | tf_op jit(solution)/shard_map/ppermute | solution.py:390
  63.4 78.5 %collective-permute-start.8 = (bf16[512,1792]{1,0:T(8,128)(2,1)S(1)}, bf16[512,1792]{1,0:T(8,128)(2,1)S(1)}, u32[]{:S(2)}, u32[]{:S(2)}) collective-permute-start(bf16[512,1792]{1,0:T(8,128)(2,1)S(1)} %get-tuple-element.100), channel_id=1, source_target_pairs={{0,8},{8,16},{16,24},{24,0},{1,9},{9,17},{17,25},{25,1},{2,10},{10... | collective-permute-start | bytes 5505032 | tf_op jit(solution)/shard_map/ppermute | solution.py:390
  63.5 70.9 %collective-permute-start.12 = (bf16[1280,512]{1,0:T(8,128)(2,1)S(1)}, bf16[1280,512]{1,0:T(8,128)(2,1)S(1)}, u32[]{:S(2)}, u32[]{:S(2)}) collective-permute-start(bf16[1280,512]{1,0:T(8,128)(2,1)S(1)} %constant_dynamic-update-slice_fusion.5.refs_0_), channel_id=1, source_target_pairs={{0,8},{8,16},{16,24},{24,0},{1,9},{9,17},{17,25},{25,1},{2,10},{10... | collective-permute-start | bytes 3932168 | tf_op jit(solution)/shard_map/ppermute | solution.py:390
  64.6 71.0 %collective-permute-start.10 = (bf16[1280,512]{1,0:T(8,128)(2,1)S(1)}, bf16[1280,512]{1,0:T(8,128)(2,1)S(1)}, u32[]{:S(2)}, u32[]{:S(2)}) collective-permute-start(bf16[1280,512]{1,0:T(8,128)(2,1)S(1)} %constant_dynamic-update-slice_fusion.5.refs_0_), channel_id=1, source_target_pairs={{0,24},{8,0},{16,8},{24,16},{1,25},{9,1},{17,9},{25,17},{2,26},{10... | collective-permute-start | bytes 3932168 | tf_op jit(solution)/shard_map/ppermute | solution.py:390
  67.2 71.7 %collective-permute-start.5 = (bf16[8,512]{1,0:T(8,128)(2,1)S(1)}, bf16[8,512]{1,0:T(8,128)(2,1)S(1)}, u32[]{:S(2)}, u32[]{:S(2)}) collective-permute-start(bf16[8,512]{1,0:T(8,128)(2,1)S(1)} %select_select_fusion), channel_id=1, source_target_pairs={{0,8},{8,16},{16,24},{24,0},{1,9},{9,17},{17,25},{25,1},{2,10},{10... | collective-permute-start | bytes 24584 | tf_op jit(solution)/shard_map/ppermute | solution.py:390
  141.9 32.2 %collective-permute-start.7 = (bf16[256,1792]{1,0:T(8,128)(2,1)S(1)}, bf16[256,1792]{1,0:T(8,128)(2,1)S(1)}, u32[]{:S(2)}, u32[]{:S(2)}) collective-permute-start(bf16[256,1792]{1,0:T(8,128)(2,1)S(1)} %slice.175), channel_id=1, source_target_pairs={{0,24},{8,0},{16,8},{24,16},{1,25},{9,1},{17,9},{25,17},{2,26},{10... | collective-permute-start | bytes 2752520 | tf_op jit(solution)/shard_map/ppermute | solution.py:390
  146.2 28.9 %collective-permute-start.9 = (bf16[256,1792]{1,0:T(8,128)(2,1)S(1)}, bf16[256,1792]{1,0:T(8,128)(2,1)S(1)}, u32[]{:S(2)}, u32[]{:S(2)}) collective-permute-start(bf16[256,1792]{1,0:T(8,128)(2,1)S(1)} %slice.176), channel_id=1, source_target_pairs={{0,8},{8,16},{16,24},{24,0},{1,9},{9,17},{17,25},{25,1},{2,10},{10... | collective-permute-start | bytes 2752520 | tf_op jit(solution)/shard_map/ppermute | solution.py:390
  247.0 204.5 %reduce-scatter.5.cloned.1.call-start = ((), (), s32[]{:S(2)}) async-start(), calls=%async_computation.5 | async-start | bytes 7077888 | tf_op jit(solution)/shard_map/reduce_scatter | solution.py:480
  272.1 239.8 %reduce-scatter.11.cloned.1.call-start = ((), (), s32[]{:S(2)}) async-start(), calls=%async_computation.11 | async-start | bytes 7077888 | tf_op jit(solution)/shard_map/reduce_scatter | solution.py:499
  344.1 180.3 %reduce-scatter.9.cloned.1.call-start = ((), (), s32[]{:S(2)}) async-start(), calls=%async_computation.10 | async-start | bytes 7077888 | tf_op jit(solution)/shard_map/reduce_scatter | solution.py:499
  382.1 304.5 %all-gather.9.cloned.1.call-start = ((), (), s32[]{:S(2)}) async-start(), calls=%async_computation.8 | async-start | bytes 7077888 | tf_op jit(solution)/shard_map/all_gather | solution.py:482
  399.5 292.9 %all-gather.7.cloned.1.call-start = ((), (), s32[]{:S(2)}) async-start(), calls=%async_computation.6 | async-start | bytes 7077888 | tf_op jit(solution)/shard_map/all_gather | solution.py:482
  410.4 46.2 %collective-permute-start.55 = (f32[1,1792]{1,0:T(1,128)S(1)}, f32[1,1792]{1,0:T(1,128)S(1)}, u32[]{:S(2)}, u32[]{:S(2)}) collective-permute-start(f32[1,1792]{1,0:T(1,128)S(1)} %broadcast_in_dim.148), channel_id=1, source_target_pairs={{0,8},{8,0},{16,24},{24,16},{1,9},{9,1},{17,25},{25,17},{2,10},{10... | collective-permute-start | bytes 21512 | tf_op jit(solution)/shard_map/ppermute | solution.py:395
  411.1 31.5 %collective-permute-start.45 = (f32[4,2048]{1,0:T(4,128)S(1)}, f32[4,2048]{1,0:T(4,128)S(1)}, u32[]{:S(2)}, u32[]{:S(2)}) collective-permute-start(f32[4,2048]{1,0:T(4,128)S(1)} %add_reduce_fusion), channel_id=1, source_target_pairs={{0,1},{1,0},{2,3},{3,2},{4,5},{5,4},{6,7},{7,6},{8,9},{9,8},{10,11... | collective-permute-start | bytes 98312 | tf_op jit(solution)/shard_map/ppermute | solution.py:395
  457.7 73.0 %collective-permute-start.59 = (bf16[640,512]{1,0:T(8,128)(2,1)}, bf16[640,512]{1,0:T(8,128)(2,1)}, u32[]{:S(2)}, u32[]{:S(2)}) collective-permute-start(bf16[640,512]{1,0:T(8,128)(2,1)} %fusion.57), channel_id=1, source_target_pairs={{0,24},{8,0},{16,8},{24,16},{1,25},{9,1},{17,9},{25,17},{2,26},{10... | collective-permute-start | bytes 1966088 | tf_op jit(solution)/shard_map/ppermute | solution.py:390
  461.8 93.2 %collective-permute-start.57 = (bf16[640,512]{1,0:T(8,128)(2,1)}, bf16[640,512]{1,0:T(8,128)(2,1)}, u32[]{:S(2)}, u32[]{:S(2)}) collective-permute-start(bf16[640,512]{1,0:T(8,128)(2,1)} %fusion.62), channel_id=1, source_target_pairs={{0,8},{8,16},{16,24},{24,0},{1,9},{9,17},{17,25},{25,1},{2,10},{10... | collective-permute-start | bytes 1966088 | tf_op jit(solution)/shard_map/ppermute | solution.py:390
  466.5 38.8 %collective-permute-start.61 = (bf16[256,1024]{1,0:T(8,128)(2,1)}, bf16[256,1024]{1,0:T(8,128)(2,1)}, u32[]{:S(2)}, u32[]{:S(2)}) collective-permute-start(bf16[256,1024]{1,0:T(8,128)(2,1)} %fusion.67), channel_id=1, source_target_pairs={{0,8},{8,16},{16,24},{24,0},{1,9},{9,17},{17,25},{25,1},{2,10},{10... | collective-permute-start | bytes 1572872 | tf_op jit(solution)/shard_map/ppermute | solution.py:390
  468.4 47.8 %collective-permute-start.63 = (bf16[256,1024]{1,0:T(8,128)(2,1)}, bf16[256,1024]{1,0:T(8,128)(2,1)}, u32[]{:S(2)}, u32[]{:S(2)}) collective-permute-start(bf16[256,1024]{1,0:T(8,128)(2,1)} %fusion.70), channel_id=1, source_target_pairs={{0,24},{8,0},{16,8},{24,16},{1,25},{9,1},{17,9},{25,17},{2,26},{10... | collective-permute-start | bytes 1572872 | tf_op jit(solution)/shard_map/ppermute | solution.py:390
  499.0 29.8 %collective-permute-start.56 = (f32[1,1792]{1,0:T(1,128)S(1)}, f32[1,1792]{1,0:T(1,128)}, u32[]{:S(2)}, u32[]{:S(2)}) collective-permute-start(f32[1,1792]{1,0:T(1,128)S(1)} %reshape_add_fusion), channel_id=1, source_target_pairs={{0,16},{8,24},{16,0},{24,8},{1,17},{9,25},{17,1},{25,9},{2,18},{10... | collective-permute-start | bytes 21512 | tf_op jit(solution)/shard_map/ppermute | solution.py:395
  526.6 28.8 %collective-permute-start.23 = (bf16[192,512]{1,0:T(8,128)(2,1)S(1)}, bf16[192,512]{1,0:T(8,128)(2,1)S(1)}, u32[]{:S(2)}, u32[]{:S(2)}) collective-permute-start(bf16[192,512]{1,0:T(8,128)(2,1)S(1)} %get-tuple-element.62), channel_id=1, source_target_pairs={{0,8},{8,16},{16,24},{24,0},{1,9},{9,17},{17,25},{25,1},{2,10},{10... | collective-permute-start | bytes 589832 | tf_op jit(solution)/shard_map/ppermute | solution.py:390
  551.8 48.4 %collective-permute-start.52 = (bf16[512,768]{1,0:T(8,128)(2,1)S(1)}, bf16[512,768]{1,0:T(8,128)(2,1)S(1)}, u32[]{:S(2)}, u32[]{:S(2)}) collective-permute-start(bf16[512,768]{1,0:T(8,128)(2,1)S(1)} %copy-done.92), channel_id=1, source_target_pairs={{0,8},{8,16},{16,24},{24,0},{1,9},{9,17},{17,25},{25,1},{2,10},{10... | collective-permute-start | bytes 2359304 | tf_op jit(solution)/shard_map/ppermute | solution.py:390
  552.7 49.1 %collective-permute-start.54 = (bf16[512,768]{1,0:T(8,128)(2,1)S(1)}, bf16[512,768]{1,0:T(8,128)(2,1)S(1)}, u32[]{:S(2)}, u32[]{:S(2)}) collective-permute-start(bf16[512,768]{1,0:T(8,128)(2,1)S(1)} %copy-done.91), channel_id=1, source_target_pairs={{0,24},{8,0},{16,8},{24,16},{1,25},{9,1},{17,9},{25,17},{2,26},{10... | collective-permute-start | bytes 2359304 | tf_op jit(solution)/shard_map/ppermute | solution.py:390
  555.0 48.9 %collective-permute-start.64 = (bf16[512,1024]{1,0:T(8,128)(2,1)S(1)}, bf16[512,1024]{1,0:T(8,128)(2,1)S(1)}, u32[]{:S(2)}, u32[]{:S(2)}) collective-permute-start(bf16[512,1024]{1,0:T(8,128)(2,1)S(1)} %copy-done.90), channel_id=1, source_target_pairs={{0,24},{8,0},{16,8},{24,16},{1,25},{9,1},{17,9},{25,17},{2,26},{10... | collective-permute-start | bytes 3145736 | tf_op jit(solution)/shard_map/ppermute | solution.py:390
  555.3 39.7 %collective-permute-start.25 = (bf16[192,512]{1,0:T(8,128)(2,1)S(1)}, bf16[192,512]{1,0:T(8,128)(2,1)S(1)}, u32[]{:S(2)}, u32[]{:S(2)}) collective-permute-start(bf16[192,512]{1,0:T(8,128)(2,1)S(1)} %get-tuple-element.64), channel_id=1, source_target_pairs={{0,24},{8,0},{16,8},{24,16},{1,25},{9,1},{17,9},{25,17},{2,26},{10... | collective-permute-start | bytes 589832 | tf_op jit(solution)/shard_map/ppermute | solution.py:390
  555.5 49.3 %collective-permute-start.37 = (bf16[4,192,512]{2,1,0:T(8,128)(2,1)S(1)}, bf16[4,192,512]{2,1,0:T(8,128)(2,1)S(1)}, u32[]{:S(2)}, u32[]{:S(2)}) collective-permute-start(bf16[4,192,512]{2,1,0:T(8,128)(2,1)S(1)} %pad_maximum_fusion.20.refs_0_), channel_id=1, source_target_pairs={{0,6},{1,7},{2,0},{3,1},{4,2},{5,3},{6,4},{7,5},{8,14},{9,15},{10,... | collective-permute-start | bytes 2359304 | tf_op jit(solution)/shard_map/ppermute | solution.py:400
  600.1 27.6 %collective-permute-start.62 = (bf16[512,1024]{1,0:T(8,128)(2,1)S(1)}, bf16[512,1024]{1,0:T(8,128)(2,1)S(1)}, u32[]{:S(2)}, u32[]{:S(2)}) collective-permute-start(bf16[512,1024]{1,0:T(8,128)(2,1)S(1)} %copy-done.89), channel_id=1, source_target_pairs={{0,8},{8,16},{16,24},{24,0},{1,9},{9,17},{17,25},{25,1},{2,10},{10... | collective-permute-start | bytes 3145736 | tf_op jit(solution)/shard_map/ppermute | solution.py:390
  600.1 49.6 %collective-permute-start.58 = (bf16[1280,512]{1,0:T(8,128)(2,1)}, bf16[1280,512]{1,0:T(8,128)(2,1)}, u32[]{:S(2)}, u32[]{:S(2)}) collective-permute-start(bf16[1280,512]{1,0:T(8,128)(2,1)} %fusion.29), channel_id=1, source_target_pairs={{0,8},{8,16},{16,24},{24,0},{1,9},{9,17},{17,25},{25,1},{2,10},{10... | collective-permute-start | bytes 3932168 | tf_op jit(solution)/shard_map/ppermute | solution.py:390
  601.8 49.4 %collective-permute-start.60 = (bf16[1280,512]{1,0:T(8,128)(2,1)}, bf16[1280,512]{1,0:T(8,128)(2,1)}, u32[]{:S(2)}, u32[]{:S(2)}) collective-permute-start(bf16[1280,512]{1,0:T(8,128)(2,1)} %fusion.26), channel_id=1, source_target_pairs={{0,24},{8,0},{16,8},{24,16},{1,25},{9,1},{17,9},{25,17},{2,26},{10... | collective-permute-start | bytes 3932168 | tf_op jit(solution)/shard_map/ppermute | solution.py:390
  635.6 29.8 %collective-permute-start.41 = (bf16[4,192,512]{2,1,0:T(8,128)(2,1)S(1)}, bf16[4,192,512]{2,1,0:T(8,128)(2,1)S(1)}, u32[]{:S(2)}, u32[]{:S(2)}) collective-permute-start(bf16[4,192,512]{2,1,0:T(8,128)(2,1)S(1)} %pad_maximum_fusion.20.refs_0_), channel_id=1, source_target_pairs={{0,1},{1,0},{2,3},{3,2},{4,5},{5,4},{6,7},{7,6},{8,9},{9,8},{10,11... | collective-permute-start | bytes 2359304 | tf_op jit(solution)/shard_map/ppermute | solution.py:403
  (145 other events, 2333.7 us)
Sparse Core Ops, SparseCore 0:
  34.8 64.5 all-gather.4
  101.6 65.0 all-gather.10
  247.2 40.0 reduce-scatter.6
  289.5 39.6 reduce-scatter.4
  344.3 40.0 reduce-scatter.10
  386.6 39.6 reduce-scatter.8
  427.9 39.7 all-gather.8
  472.1 37.2 all-gather.6

commit v4 on v3

--- a/solution.py
+++ b/solution.py
@@ -57,37 +57,21 @@
     return exps * (1.0 / jnp.sum(exps, axis=1, keepdims=True))
 
 
-def attn_fwd_kernel(qkv_ref, cos_ref, lo_ref, hi_ref, ctx_ref, q_ref, k_ref, *, half, scale, span):
+def attn_fwd_kernel(qkv_ref, ctx_ref, *, scale, span):
     seq_len, width = ctx_ref.shape[1:]
-
-    @pl.loop(0, seq_len // Q_ROWS)
-    def _(step):
-        rows = pl.ds(pl.multiple_of(step * Q_ROWS, Q_ROWS), Q_ROWS)
-        for out, col in ((q_ref, 0), (k_ref, width)):
-            part = qkv_ref[0, rows, col:col + width].astype(jnp.float32)
-            out[rows, :] = rotate(part, cos_ref[rows, :], lo_ref[rows, :], hi_ref[rows, :], half, 1.0).astype(jnp.bfloat16)
-
     for end in range(span, seq_len + 1, span):
         @pl.loop(0, span // Q_ROWS)
         def _(step, end=end):
             start = pl.multiple_of(end - span + step * Q_ROWS, Q_ROWS)
             rows = pl.ds(start, Q_ROWS)
-            probs = causal_probs(q_ref[rows, :], k_ref[:end, :], start, scale).astype(jnp.bfloat16)
+            probs = causal_probs(qkv_ref[0, rows, :width], qkv_ref[0, :end, width:2 * width], start, scale).astype(jnp.bfloat16)
             ctx_ref[0, rows, :] = dot(probs, qkv_ref[0, :end, 2 * width:], NN).astype(jnp.bfloat16)
 
 
-def attn_bwd_kernel(qkv_ref, dctx_ref, cos_ref, lo_ref, hi_ref, dqkv_ref, db_ref, q_ref, k_ref, dk_ref, dv_ref, *, half, scale, span):
+def attn_bwd_kernel(qkv_ref, dctx_ref, cos_ref, lo_ref, hi_ref, dqkv_ref, db_ref, dk_ref, dv_ref, *, half, scale, span):
     seq_len, width = dctx_ref.shape[1:]
-
-    @pl.loop(0, seq_len // Q_ROWS)
-    def _(step):
-        rows = pl.ds(pl.multiple_of(step * Q_ROWS, Q_ROWS), Q_ROWS)
-        for out, col in ((q_ref, 0), (k_ref, width)):
-            part = qkv_ref[0, rows, col:col + width].astype(jnp.float32)
-            out[rows, :] = rotate(part, cos_ref[rows, :], lo_ref[rows, :], hi_ref[rows, :], half, 1.0).astype(jnp.bfloat16)
-        dk_ref[rows, :] = jnp.zeros((Q_ROWS, width), jnp.float32)
-        dv_ref[rows, :] = jnp.zeros((Q_ROWS, width), jnp.float32)
-
+    dk_ref[...] = jnp.zeros(dk_ref.shape, jnp.float32)
+    dv_ref[...] = jnp.zeros(dv_ref.shape, jnp.float32)
     db_ref[...] = jnp.zeros(db_ref.shape, jnp.float32)
 
     def store(rows, col, grad_rot, turn):
@@ -96,22 +80,22 @@
             wide = grad.astype(jnp.float32)
             grad = rotate(wide, cos_ref[rows, :], lo_ref[rows, :], hi_ref[rows, :], half, -1.0).astype(jnp.bfloat16)
         dqkv_ref[0, rows, col:col + width] = grad
-        db_ref[0, :, col:col + width] += jnp.sum(grad.astype(jnp.float32), axis=0, keepdims=True)
+        db_ref[0, :, col:col + width] += sublane_sum(grad.astype(jnp.float32))
 
     for end in range(span, seq_len + 1, span):
         @pl.loop(0, span // Q_ROWS)
         def _(step, end=end):
             start = pl.multiple_of(end - span + step * Q_ROWS, Q_ROWS)
             rows = pl.ds(start, Q_ROWS)
-            q_rows = q_ref[rows, :]
+            q_rows, keys = qkv_ref[0, rows, :width], qkv_ref[0, :end, width:2 * width]
             dctx = dctx_ref[0, rows, :]
-            probs = causal_probs(q_rows, k_ref[:end, :], start, scale)
+            probs = causal_probs(q_rows, keys, start, scale)
             dprobs = dot(dctx, qkv_ref[0, :end, 2 * width:], NT).astype(jnp.bfloat16).astype(jnp.float32)
             dv_ref[:end, :] += dot(probs.astype(jnp.bfloat16), dctx, TN)
             inner = jnp.sum(probs * dprobs, axis=1, keepdims=True)
             dscores = (probs * (dprobs - inner) * scale).astype(jnp.bfloat16)
             dk_ref[:end, :] += dot(dscores, q_rows, TN)
-            store(rows, 0, dot(dscores, k_ref[:end, :], NN), True)
+            store(rows, 0, dot(dscores, keys, NN), True)
 
     @pl.loop(0, seq_len // Q_ROWS)
     def _(step):
@@ -120,48 +104,48 @@
         store(rows, 2 * width, dv_ref[rows, :], False)
 
 
-def attention_calls(seq_len, width, index):
-    n_seq = 1
+def attention_calls(n_seq, seq_len, width, tables):
     half = width // ROTARY_DIVISOR // 2
     scale = width ** -0.5
     span = 512 if seq_len % 512 == 0 else seq_len
-    tables = rotary_tables(seq_len, 2 * half)
     seq_spec = lambda cols, first=0: pl.BlockSpec((1, seq_len, cols), lambda s: (s + first, 0, 0))
     tab_spec = pl.BlockSpec((seq_len, LANES), lambda s: (0, 0))
-    rot_scratch = pltpu.VMEM((seq_len, width), jnp.bfloat16)
     acc_scratch = pltpu.VMEM((seq_len, width), jnp.float32)
-    pairs = n_seq * seq_len * seq_len // 2
-    params = pltpu.CompilerParams(dimension_semantics=("arbitrary",), vmem_limit_bytes=32 * MIB)
-    forward = pl.pallas_call(
-        functools.partial(attn_fwd_kernel, half=half, scale=scale, span=span),
-        grid=(n_seq,),
-        in_specs=[seq_spec(3 * width, index), tab_spec, tab_spec, tab_spec],
-        out_specs=seq_spec(width),
-        out_shape=jax.ShapeDtypeStruct((n_seq, seq_len, width), jnp.bfloat16),
-        scratch_shapes=[rot_scratch, rot_scratch],
-        compiler_params=params,
-        name="attn_fwd",
-        cost_estimate=pl.CostEstimate(flops=8 * pairs * width, bytes_accessed=8 * n_seq * seq_len * width, transcendentals=pairs),
-    )
-    backward = pl.pallas_call(
-        functools.partial(attn_bwd_kernel, half=half, scale=scale, span=span),
-        grid=(n_seq,),
-        in_specs=[seq_spec(3 * width, index), seq_spec(width, index), tab_spec, tab_spec, tab_spec],
-        out_specs=[seq_spec(3 * width), pl.BlockSpec((1, 1, 3 * width), lambda s: (s, 0, 0))],
-        out_shape=[jax.ShapeDtypeStruct((n_seq, seq_len, 3 * width), jnp.bfloat16), jax.ShapeDtypeStruct((n_seq, 1, 3 * width), jnp.float32)],
-        scratch_shapes=[rot_scratch, rot_scratch, acc_scratch, acc_scratch],
-        compiler_params=params,
-        name="attn_bwd",
-        cost_estimate=pl.CostEstimate(flops=20 * pairs * width, bytes_accessed=14 * n_seq * seq_len * width, transcendentals=pairs),
-    )
-    return (lambda qkv: forward(qkv, *tables)), (lambda qkv, dctx: backward(qkv, dctx, *tables))
-
-
-def place_kernel(row_ref, full_ref, *rest, chunk, n_seq):
-    out_ref, held_ref, in_sems, out_sems = rest[-4:]
+    pairs = seq_len * seq_len // 2
+    params = pltpu.CompilerParams(dimension_semantics=("arbitrary",), vmem_limit_bytes=60 * MIB)
+
+    def forward(qkv):
+        return pl.pallas_call(
+            functools.partial(attn_fwd_kernel, scale=scale, span=span),
+            grid=(n_seq,),
+            in_specs=[seq_spec(3 * width)],
+            out_specs=seq_spec(width),
+            out_shape=jax.ShapeDtypeStruct((n_seq, seq_len, width), jnp.bfloat16),
+            compiler_params=params,
+            name="af",
+            cost_estimate=pl.CostEstimate(flops=8 * n_seq * pairs * width, bytes_accessed=8 * n_seq * seq_len * width, transcendentals=n_seq * pairs),
+        )(qkv)
+
+    def backward(qkv, dctx, index):
+        return pl.pallas_call(
+            functools.partial(attn_bwd_kernel, half=half, scale=scale, span=span),
+            grid=(1,),
+            in_specs=[seq_spec(3 * width, index), seq_spec(width, index), tab_spec, tab_spec, tab_spec],
+            out_specs=[seq_spec(3 * width), pl.BlockSpec((1, 8, 3 * width), lambda s: (s, 0, 0))],
+            out_shape=[jax.ShapeDtypeStruct((1, seq_len, 3 * width), jnp.bfloat16), jax.ShapeDtypeStruct((1, 8, 3 * width), jnp.float32)],
+            scratch_shapes=[acc_scratch, acc_scratch],
+            compiler_params=params,
+            name="ab",
+            cost_estimate=pl.CostEstimate(flops=20 * pairs * width, bytes_accessed=14 * seq_len * width, transcendentals=pairs),
+        )(qkv, dctx, *tables)
+
+    return forward, backward
+
+
+def place_kernel(place_ref, full_ref, out_ref, held_ref, in_sems, out_sems, *, chunk, n_seq):
     groups = full_ref.shape[0]
-    fetch = [pltpu.make_async_copy(full_ref.at[lax.rem(row_ref[0] + groups - t, groups)], held_ref.at[t], in_sems.at[t]) for t in range(groups)]
-    store = [pltpu.make_async_copy(held_ref.at[t], out_ref.at[t * n_seq + chunk], out_sems.at[t]) for t in range(groups)]
+    fetch = [pltpu.make_async_copy(full_ref.at[lax.rem(place_ref[0] + groups - t, groups)], held_ref.at[t], in_sems.at[t]) for t in range(groups)]
+    store = [pltpu.make_async_copy(held_ref.at[t], out_ref.at[t], out_sems.at[t]) for t in range(groups)]
     for copy in fetch:
         copy.start()
     for t in range(groups):
@@ -255,50 +239,41 @@
     return value.reshape(value.shape[0] // 8, 8, value.shape[1]).sum(0)
 
 
-def front_kernel(x_ref, next_ref, small_ref, w_ref, b_qkv_ref, b_up_ref, h_attn_ref, h_mlp_ref, qkv_ref, pre_ref, gelu_ref, norm_ref):
-    rows = x_ref.shape[0]
-    step = pl.program_id(0)
-    now = lax.rem(step, 2)
-
-    def norm(from_ref, slot, at):
-        x_hat, _ = normalize(from_ref[at, :])
-        norm_ref[slot, 0, at, :] = (x_hat * small_ref[0:1, :] + small_ref[1:2, :]).astype(jnp.bfloat16)
-        norm_ref[slot, 1, at, :] = (x_hat * small_ref[2:3, :] + small_ref[3:4, :]).astype(jnp.bfloat16)
-
-    @pl.when(step == 0)
-    def _():
-        @pl.loop(0, rows // LN_ROWS)
-        def _(part):
-            norm(x_ref, 0, pl.ds(pl.multiple_of(part * LN_ROWS, LN_ROWS), LN_ROWS))
-
+def norm_kernel(x_ref, small_ref, h_attn_ref, h_mlp_ref):
+    @pl.loop(0, x_ref.shape[0] // LN_ROWS)
+    def _(step):
+        at = pl.ds(pl.multiple_of(step * LN_ROWS, LN_ROWS), LN_ROWS)
+        x_hat, _ = normalize(x_ref[at, :])
+        h_attn_ref[at, :] = (x_hat * small_ref[0:1, :] + small_ref[1:2, :]).astype(jnp.bfloat16)
+        h_mlp_ref[at, :] = (x_hat * small_ref[2:3, :] + small_ref[3:4, :]).astype(jnp.bfloat16)
+
+
+def front_kernel(h_attn_ref, h_mlp_ref, cos_ref, lo_ref, hi_ref, w_ref, b_qkv_ref, b_up_ref, qkv_ref, pre_ref, gelu_ref):
     qkv_width = qkv_ref.shape[1]
-    tiles = [(0, low) for low in range(0, qkv_width, TILE)] + [(1, low) for low in range(0, pre_ref.shape[1], TILE)]
-    ahead = -(-rows // (len(tiles) * 16)) * 16
-    for index, (which, low) in enumerate(tiles):
+    head = qkv_width // 3
+    for low in range(0, qkv_width, head):
+        at = slice(low, low + head)
+        part = (dot(h_attn_ref[...], w_ref[:, at], NN) + b_qkv_ref[:, at]).astype(jnp.bfloat16)
+        if low < 2 * head:
+            part = rotate(part.astype(jnp.float32), cos_ref[...], lo_ref[...], hi_ref[...], head // ROTARY_DIVISOR // 2, 1.0).astype(jnp.bfloat16)
+        qkv_ref[:, at] = part
+    for low in range(0, pre_ref.shape[1], TILE):
         at = slice(low, low + TILE)
-        if which == 0:
-            qkv_ref[:, at] = (dot(norm_ref[now, 0], w_ref[:, at], NN) + b_qkv_ref[:, at]).astype(jnp.bfloat16)
-        else:
-            acc = dot(norm_ref[now, 1], w_ref[:, qkv_width + low:qkv_width + low + TILE], NN) + b_up_ref[:, at]
-            pre = acc.astype(jnp.bfloat16)
-            pre_ref[:, at] = pre
-            wide = pre.astype(jnp.float32)
-            gelu_ref[:, at] = (0.5 * wide * (1.0 + lax.erf(wide * SQRT_HALF))).astype(jnp.bfloat16)
-        start, stop = index * ahead, min(rows, (index + 1) * ahead)
-        if start < stop:
-            rows_at = slice(start, stop)
-            norm(next_ref, 1 - now, rows_at)
-            h_attn_ref[rows_at, :] = norm_ref[now, 0, rows_at, :]
-            h_mlp_ref[rows_at, :] = norm_ref[now, 1, rows_at, :]
+        acc = dot(h_mlp_ref[...], w_ref[:, qkv_width + low:qkv_width + low + TILE], NN) + b_up_ref[:, at]
+        pre = acc.astype(jnp.bfloat16)
+        pre_ref[:, at] = pre
+        wide = pre.astype(jnp.float32)
+        gelu_ref[:, at] = (0.5 * wide * (1.0 + lax.erf(wide * SQRT_HALF))).astype(jnp.bfloat16)
 
 
 def y_kernel(ctx_ref, gelu_ref, *refs):
     w_refs, y_ref = refs[:-1], refs[-1]
     head = ctx_ref.shape[1]
+    places, _, own, _ = y_ref.shape
     for index, w_ref in enumerate(w_refs):
         width = w_ref.shape[1]
         acc = dot(ctx_ref[...], w_ref[:head, :], NN) + dot(gelu_ref[...], w_ref[head:, :], NN)
-        y_ref[:, index * width:(index + 1) * width] = acc.astype(jnp.bfloat16)
+        y_ref[:, 0, :, index * width:(index + 1) * width] = acc.astype(jnp.bfloat16).reshape(places, own, width)
 
 
 def d_pre_kernel(cot_ref, pre_ref, *refs):
@@ -347,32 +322,38 @@
         sums_ref[3, :, at] += sublane_sum(d_mlp)
 
 
-def tile_call(kernel, tiled, whole, outs, row_range, flops, limit, ahead=False):
+def tile_call(kernel, tiled, whole, outs, row_range, flops, rows=512):
     start, count = row_range
-    rows = next(r for r in (512, 256, 128, 64, count) if count % r == 0)
+    rows = next(r for r in (rows, 256, 128, 64, count) if count % r == 0 and all(op.shape[0] % r == 0 for op in tiled))
     first = start // rows
-    in_specs = [pl.BlockSpec((rows, op.shape[1]), lambda s, f=(first if op.shape[0] != count else 0): (s + f, 0)) for op in tiled]
-    if ahead:
-        in_specs.append(pl.BlockSpec((rows, tiled[0].shape[1]), lambda s: (jnp.minimum(s + 1, count // rows - 1), 0)))
-        tiled = [*tiled, tiled[0]]
+
+    def tile_spec(op):
+        blocks = op.shape[0] // rows
+        if blocks * rows < count:
+            return pl.BlockSpec((rows, op.shape[1]), lambda s: (lax.rem(s, blocks), 0))
+        return pl.BlockSpec((rows, op.shape[1]), lambda s, f=(first if op.shape[0] != count else 0): (s + f, 0))
+
+    in_specs = [tile_spec(op) for op in tiled]
     in_specs += [pl.BlockSpec(op.shape, lambda s, n=op.ndim: (0,) * n, pipeline_mode=pl.Buffered(1)) for op in whole]
     out_specs, out_shapes = [], []
     for form, dtype in outs:
         if isinstance(form, int):
             out_specs.append(pl.BlockSpec((rows, form), lambda s: (s, 0)))
             out_shapes.append(jax.ShapeDtypeStruct((count, form), dtype))
+        elif isinstance(form[0], tuple):
+            out_specs.append(pl.BlockSpec(form[1], form[2]))
+            out_shapes.append(jax.ShapeDtypeStruct(form[0], dtype))
         else:
             out_specs.append(pl.BlockSpec(form, lambda s, n=len(form): (0,) * n))
             out_shapes.append(jax.ShapeDtypeStruct(form, dtype))
-    moved = sum(op.size * 2 * count // op.shape[0] for op in tiled) + sum(op.size * 2 for op in whole) + sum(2 * shape.size for shape in out_shapes)
+    moved = sum(2 * op.shape[1] * count for op in tiled) + sum(2 * op.size for op in whole) + sum(2 * shape.size for shape in out_shapes)
     return pl.pallas_call(
         kernel,
         grid=(count // rows,),
         in_specs=in_specs,
         out_specs=out_specs,
         out_shape=out_shapes,
-        compiler_params=pltpu.CompilerParams(dimension_semantics=("arbitrary",), vmem_limit_bytes=limit * MIB),
-        scratch_shapes=[pltpu.VMEM((2, 2, rows, tiled[0].shape[1]), jnp.bfloat16)] if ahead else [],
+        compiler_params=pltpu.CompilerParams(dimension_semantics=("arbitrary",), vmem_limit_bytes=60 * MIB),
         cost_estimate=pl.CostEstimate(flops=flops, bytes_accessed=moved, transcendentals=0),
     )(*tiled, *whole)
 
@@ -414,14 +395,13 @@
 
     def ring_scatter(make_part, rows):
         half = rows // 2
-        far_low = make_part(antipode, 0, half).astype(jnp.bfloat16)
-        far_high = make_part(antipode, half, rows).astype(jnp.bfloat16)
-        moving_up, moving_down = shift(far_low, -1), shift(far_high, 1)
+        far = make_part(antipode).astype(jnp.bfloat16)
+        moving_up, moving_down = shift(far[:half], -1), shift(far[half:], 1)
         moving_up = jnp.pad(moving_up, ((0, rows - half), (0, 0)))
         moving_down = jnp.pad(moving_down, ((half, 0), (0, 0)))
         for hops in range(antipode - 1, 0, -1):
-            up = make_part(hops, 0, rows) + moving_up.astype(jnp.float32)
-            down = make_part(tx_size - hops, 0, rows) + moving_down.astype(jnp.float32)
+            up = make_part(hops) + moving_up.astype(jnp.float32)
+            down = make_part(tx_size - hops) + moving_down.astype(jnp.float32)
             up, down = up.astype(jnp.bfloat16), down.astype(jnp.bfloat16)
             moving_up, moving_down = shift(up, -1), shift(down, 1)
         return lambda own, low, high: own + moving_up[low:high].astype(jnp.float32) + moving_down[low:high].astype(jnp.float32)
@@ -434,7 +414,8 @@
         qkv_width = w_qkv.shape[1] * w_qkv.shape[2]
         head = qkv_width // 3
         chunks = range(n_seq)
-        attention = [attention_calls(seq_len, head, s) for s in chunks]
+        tables = rotary_tables(seq_len, head // ROTARY_DIVISOR)
+        attn_fwd, attn_bwd = attention_calls(n_seq, seq_len, head, tables)
 
         def to_tokens(act):
             parts = act.reshape(tx_size, n_seq, ty_size, own, d_local)
@@ -468,33 +449,32 @@
         n_tok, d_model = x_group.shape
         x_rows, cot_rows = x_own.reshape(-1, d_model), cot_own.reshape(-1, d_model)
         ff_width = w_up.shape[1]
-        h_attn, h_mlp, qkv_act, pre_act, gelu_out = tile_call(
-            front_kernel, [x_group], [small, w_in, b_qkv.reshape(1, -1).astype(jnp.float32), b_up.reshape(1, -1).astype(jnp.float32)],
-            [(d_model, jnp.bfloat16), (d_model, jnp.bfloat16), (qkv_width, jnp.bfloat16), (ff_width, jnp.bfloat16), (ff_width, jnp.bfloat16)],
-            (0, n_tok), 2 * n_tok * w_in.size, 48, True)
+        h_attn, h_mlp = tile_call(norm_kernel, [x_group], [small], [(d_model, jnp.bfloat16), (d_model, jnp.bfloat16)], (0, n_tok), 16 * x_group.size)
+        qkv_act, pre_act, gelu_out = tile_call(
+            front_kernel, [h_attn, h_mlp, *tables], [w_in, b_qkv.reshape(1, -1).astype(jnp.float32), b_up.reshape(1, -1).astype(jnp.float32)],
+            [(qkv_width, jnp.bfloat16), (ff_width, jnp.bfloat16), (ff_width, jnp.bfloat16)], (0, n_tok), 2 * n_tok * w_in.size)
         qkv_seq = qkv_act.reshape(n_seq, seq_len, qkv_width)
-        context, y_out = [], None
-        for s in chunks:
-            context.append(attention[s][0](qkv_seq).reshape(seq_len, head))
-            (y_part,) = tile_call(y_kernel, [context[s], gelu_out], w_back, [(d_model, jnp.bfloat16)], (s * seq_len, seq_len), 2 * seq_len * back_size, 24)
-            mixed = lax.psum_scatter(y_part, 'ty', scatter_dimension=0, tiled=True)
-            blocks = to_width(row_call(finish_y_kernel, tx_size, s, own, x_rows, mixed, bias_out.reshape(1, -1)))
-            full = lax.all_gather(blocks, 'ty', axis=1, tiled=True)
-            y_out = place_call(place_kernel, place, [full], y_out, s, n_seq, seq_len)
-        context = jnp.concatenate(context, axis=0)
+        context = attn_fwd(qkv_seq).reshape(n_tok, head)
+        blocks_per_seq = ty_size // 2
+        y_form = ((ty_size, n_seq, own, d_model), (2, 1, own, d_model), lambda s: (lax.rem(s, blocks_per_seq), s // blocks_per_seq, 0, 0))
+        (y_part,) = tile_call(y_kernel, [context, gelu_out], w_back, [(y_form, jnp.bfloat16)], (0, n_tok), 2 * n_tok * back_size, 2 * own)
+        mixed = lax.psum_scatter(y_part.reshape(n_tok, d_model), 'ty', scatter_dimension=0, tiled=True)
+        blocks = to_width(row_call(finish_y_kernel, tx_size, 0, n_seq * own, x_rows, mixed, bias_out.reshape(1, -1)))
+        full = lax.all_gather(blocks.reshape(tx_size * n_seq, own, d_local), 'ty', axis=1, tiled=True)
+        y_out = place_call(place_kernel, place, [full.reshape(tx_size, n_seq * seq_len, d_local)], None, 0, 1, n_seq * seq_len)
 
         d_ctx, d_pre, d_b_up = tile_call(
             d_pre_kernel, [cot_group, pre_act], w_back,
-            [(head, jnp.bfloat16), (ff_width, jnp.bfloat16), ((8, ff_width), jnp.float32)], (0, n_tok), 2 * n_tok * back_size, 32)
+            [(head, jnp.bfloat16), (ff_width, jnp.bfloat16), ((8, ff_width), jnp.float32)], (0, n_tok), 2 * n_tok * back_size)
         d_ctx, d_b_up = d_ctx.reshape(n_seq, seq_len, head), d_b_up.sum(0)
         d_qkv, d_b_qkv, d_ln, dx_act = [], [], [], None
         for s in chunks:
-            d_qkv_seq, d_b_seq = attention[s][1](qkv_seq, d_ctx)
+            d_qkv_seq, d_b_seq = attn_bwd(qkv_seq, d_ctx, s)
             d_qkv.append(d_qkv_seq.reshape(seq_len, qkv_width))
-            d_b_qkv.append(d_b_seq.reshape(-1))
+            d_b_qkv.append(d_b_seq.sum((0, 1)))
             a6_part, sums = tile_call(
                 d_h_kernel, [d_qkv[s], d_pre, x_group], [small, w_in],
-                [(d_model, jnp.bfloat16), ((4, 8, d_model), jnp.float32)], (s * seq_len, seq_len), 2 * seq_len * w_in.size, 32)
+                [(d_model, jnp.bfloat16), ((4, 8, d_model), jnp.float32)], (s * seq_len, seq_len), 2 * seq_len * w_in.size)
             d_ln.append(sums)
             value_a6 = lax.psum_scatter(a6_part, 'ty', scatter_dimension=0, tiled=True)
             parts = row_call(finish_dx_kernel, tx_size, s, own, x_rows, value_a6, cot_rows)
@@ -510,13 +490,14 @@
 
         cols = lambda act, r: act[:, r * d_local:(r + 1) * d_local]
         inner = jnp.concatenate([context, gelu_out], axis=1)
-        add_back = ring_scatter(lambda r, low, high: dot(inner[:, low:high], cols(cot_group, r), TN), inner.shape[1])
-        add_up = ring_scatter(lambda r, low, high: dot(cols(h_mlp, r)[:, low:high], d_pre, TN), d_local)
-        add_qkv = ring_scatter(lambda r, low, high: dot(cols(h_attn, r)[:, low:high], d_qkv, TN), d_local)
+        add_back = ring_scatter(lambda r: dot(inner, cols(cot_group, r), TN), inner.shape[1])
+        add_up = ring_scatter(lambda r: dot(cols(h_mlp, r), d_pre, TN), d_local)
+        add_qkv = ring_scatter(lambda r: dot(cols(h_attn, r), d_qkv, TN), d_local)
         d_w_dense = add_back(dot(context, cols(cot_group, 0), TN), 0, head)
         d_w_down = add_back(dot(gelu_out, cols(cot_group, 0), TN), head, inner.shape[1])
         d_w_up = add_up(dot(cols(h_mlp, 0), d_pre, TN), 0, d_local)
         d_w_qkv = add_qkv(dot(cols(h_attn, 0), d_qkv, TN), 0, d_local)
+        y_out = y_out.reshape(batch, seq_len, d_local)
         return (y_out, dx_act, d_ln[0], d_ln[1], d_ln[2], d_ln[3], d_w_qkv.reshape(w_qkv.shape), d_bias[:qkv_width].reshape(b_qkv.shape), d_w_dense, d_b_out, d_w_up, d_bias[qkv_width:], d_w_down, d_b_out)
 
     return jax.shard_map(body, mesh=mesh, in_specs=in_specs, out_specs=out_specs, check_vma=False)

time: 717 us -> 676 us (0.943)
  local copies, waits for them, and re-layouts: 68.2 us -> 31.7 us
  Pallas kernels: 193 us -> 213 us
  waiting for transfers between devices: 226 us -> 211 us
  matrix products: 96.5 us -> 88.2 us
    unnamed x218 -> x126, local copies, waits for them, and re-layouts: 58.2 us -> 15.8 us
    ppermute x44 -> x41, waiting for transfers between devices: 211 us -> 195 us  [shift(): lax.ppermute(value, 'tx', [(s, (s - hops) % tx_size) for s in range(tx_si...]
    pallas_call x6, Pallas kernels: 130 us -> 144 us  [tile_call(): pl.pallas_call(kernel, grid=(count // rows,), in_specs=in_specs, out_spec...]
    dot_general x16 -> x13, matrix products: 96.5 us -> 88.2 us  [dot(): return lax.dot_general(a, b, dims, preferred_element_type=jnp.float32)]
    ppermute x5, waiting for transfers between devices: 0.01 us -> 8.07 us  [small_sum(): lax.ppermute(value, axis, [(s, s ^ step) for s in range(size)])]
    pallas_call x4 -> x3, Pallas kernels: 36.5 us -> 43.3 us  [the longest x2 27.7 us: backward(): pl.pallas_call(functools.partial(attn_bwd_kernel, half=half, scale=scale,...]
    pallas_call x4 -> x3, Pallas kernels: 23.9 us -> 21.8 us  [place_call(): pl.pallas_call(functools.partial(kernel, chunk=chunk, n_seq=n_seq), in_sp...]
    ppermute x44 -> x41, starting transfers between devices: 60.6 us -> 60.1 us  [shift(): lax.ppermute(value, 'tx', [(s, (s - hops) % tx_size) for s in range(tx_si...]
  transfers between devices with their start and end apart: 73 -> 68, of which waited for: 23 -> 21; matrix products, arithmetic and copies ran while one was open for 19% -> 21% of each run, Pallas kernels for 27% -> 30%
where the time goes in v4:
time: 676 us; the launch traced here: 668 us
  Pallas kernels  213 us (32%)
  waiting for transfers between devices  211 us (31%)
  matrix products  88.2 us (13%)
  starting transfers between devices  76.5 us (11%)
  other arithmetic  32 us (5%)
  local copies, waits for them, and re-layouts  31.7 us (5%)
  between operations  15.6 us (2%)
    ppermute x41, waiting for transfers between devices, shift(): lax.ppermute(value, 'tx', [(s, (s - hops) % tx_size) for s in range(tx_si...  195 us
    pallas_call x6, Pallas kernels, tile_call(): pl.pallas_call(kernel, grid=(count // rows,), in_specs=in_specs, out_spec...  144 us
    dot_general x13, matrix products, dot(): return lax.dot_general(a, b, dims, preferred_element_type=jnp.float32)  88.2 us
    ppermute x41, starting transfers between devices, shift(): lax.ppermute(value, 'tx', [(s, (s - hops) % tx_size) for s in range(tx_si...  60.1 us
    pallas_call x2, Pallas kernels, backward(): pl.pallas_call(functools.partial(attn_bwd_kernel, half=half, scale=scale,...  27.7 us
    pallas_call x3, Pallas kernels, place_call(): pl.pallas_call(functools.partial(kernel, chunk=chunk, n_seq=n_seq), in_sp...  21.8 us
    unnamed x126, local copies, waits for them, and re-layouts  15.8 us
    pallas_call x1, Pallas kernels, forward(): pl.pallas_call(functools.partial(attn_fwd_kernel, scale=scale, span=span)...  15.6 us
  transfers between devices with their start and end apart: 68, of which 21 were waited for; matrix products, arithmetic and copies ran while one was open for 21% of the time, Pallas kernels for 30%

profile of v4, /device:TPU:98, one launch (start us, length us, event | category | flops | bytes accessed | tf_op | source)
XLA Modules:
  0.0 667.7 jit_solution(1852826113587448512)
XLA Ops:
  15.8 6.9 %collective-permute-done.2 = bf16[2,192,512]{2,1,0:T(8,128)(2,1)S(1)} collective-permute-done((bf16[2,192,512]{2,1,0:T(8,128)(2,1)S(1)}, bf16[2,192,512]{2,1,0:T(8,128)(2,1)S(1)}, u32[]{:S(2)}, u32[]{:S(2)}) %collective-permute-start.2) | collective-permute-done | bytes 393248 | tf_op jit(solution)/shard_map/ppermute | solution.py:371
  22.8 9.6 %collective-permute-done.1 = bf16[2,192,512]{2,1,0:T(8,128)(2,1)S(1)} collective-permute-done((bf16[2,192,512]{2,1,0:T(8,128)(2,1)S(1)}, bf16[2,192,512]{2,1,0:T(8,128)(2,1)S(1)}, u32[]{:S(2)}, u32[]{:S(2)}) %collective-permute-start.1) | collective-permute-done | bytes 393248 | tf_op jit(solution)/shard_map/ppermute | solution.py:371
  40.1 6.8 %collective-permute-done.19 = bf16[2,192,512]{2,1,0:T(8,128)(2,1)S(1)} collective-permute-done((bf16[2,192,512]{2,1,0:T(8,128)(2,1)S(1)}, bf16[2,192,512]{2,1,0:T(8,128)(2,1)S(1)}, u32[]{:S(2)}, u32[]{:S(2)}) %collective-permute-start.19) | collective-permute-done | bytes 393248 | tf_op jit(solution)/shard_map/ppermute | solution.py:371
  46.9 9.6 %collective-permute-done.18 = bf16[2,192,512]{2,1,0:T(8,128)(2,1)S(1)} collective-permute-done((bf16[2,192,512]{2,1,0:T(8,128)(2,1)S(1)}, bf16[2,192,512]{2,1,0:T(8,128)(2,1)S(1)}, u32[]{:S(2)}, u32[]{:S(2)}) %collective-permute-start.18) | collective-permute-done | bytes 393248 | tf_op jit(solution)/shard_map/ppermute | solution.py:371
  68.3 67.2 %collective-permute-done.12.refs_3_ = bf16[1280,512]{1,0:T(8,128)(2,1)S(1)} collective-permute-done((bf16[1280,512]{1,0:T(8,128)(2,1)S(1)}, bf16[1280,512]{1,0:T(8,128)(2,1)S(1)}, u32[]{:S(2)}, u32[]{:S(2)}) %collective-permute-start.12) | collective-permute-done | bytes 1310752 | tf_op jit(solution)/shard_map/ppermute | solution.py:371
  156.5 16.8 %collective-permute-done.7 = bf16[256,1792]{1,0:T(8,128)(2,1)S(1)} collective-permute-done((bf16[256,1792]{1,0:T(8,128)(2,1)S(1)}, bf16[256,1792]{1,0:T(8,128)(2,1)S(1)}, u32[]{:S(2)}, u32[]{:S(2)}) %collective-permute-start.7) | collective-permute-done | bytes 917536 | tf_op jit(solution)/shard_map/ppermute | solution.py:371
  176.6 18.7 %shard_map.245 = (bf16[3072,2048]{1,0:T(8,128)(2,1)}, bf16[3072,2048]{1,0:T(8,128)(2,1)}) custom-call(bf16[3072,2048]{1,0:T(8,128)(2,1)} %bitcast.89, f32[8,2048]{1,0:T(8,128)} %maximum_convert_fusion.small_ref), custom_call_target="tpu_custom_call" | custom-call | flops 100663296 | bytes 37781504 | tf_op jit(solution)/shard_map/pallas_call | solution.py:350
  195.3 32.8 %shard_map.246 = (bf16[3072,768]{1,0:T(8,128)(2,1)}, bf16[3072,1024]{1,0:T(8,128)(2,1)}, bf16[3072,1024]{1,0:T(8,128)(2,1)}) custom-call(bf16[3072,2048]{1,0:T(8,128)(2,1)} %get-tuple-element.42.h_attn_ref, bf16[3072,2048]{1,0:T(8,128)(2,1)} %get-tuple-element.43.h_mlp_ref, f32[1536,128]{1,0:T(8,128)} %get-tuple-element.108.cos_ref, ...), custom_call_target="tpu_custom_call" | custom-call | flops 22548578304 | bytes 52170240 | tf_op jit(solution)/shard_map/pallas_call | solution.py:350
  228.1 15.6 %af.1 = bf16[2,1536,256]{2,1,0:T(8,128)(2,1)} custom-call(bf16[2,1536,768]{2,1,0:T(8,128)(2,1)} %bitcast.132), custom_call_target="tpu_custom_call" | custom-call | flops 4831838208 | bytes 6291456 | tf_op jit(solution)/shard_map/af/pallas_call | solution.py:118
  243.6 22.0 %shard_map.247 = bf16[8,2,192,2048]{3,2,1,0:T(8,128)(2,1)} custom-call(bf16[3072,256]{1,0:T(8,128)(2,1)} %bitcast.145, bf16[3072,1024]{1,0:T(8,128)(2,1)} %get-tuple-element.45.gelu_ref, bf16[1280,512]{1,0:T(8,128)(2,1)} %copy-done.29, bf16[1280,512]{1,0:T(8,128)(2,1)} %copy-done.25, bf16[1280,512]{1,0:T(8,128)(2,1)} %copy-done.26, bf16[1280,512]{1,0:T(8,128)(2,1)} %copy-done.24), custom_call_target="tpu_custom_call" | custom-call | flops 16106127360 | bytes 25690112 | tf_op jit(solution)/shard_map/pallas_call | solution.py:350
  266.0 26.9 %shard_map.250 = (bf16[3072,256]{1,0:T(8,128)(2,1)}, bf16[3072,1024]{1,0:T(8,128)(2,1)}, f32[8,1024]{1,0:T(8,128)}) custom-call(bf16[3072,2048]{1,0:T(8,128)(2,1)} %bitcast.124, bf16[3072,1024]{1,0:T(8,128)(2,1)} %get-tuple-element.50.pre_ref, bf16[1280,512]{1,0:T(8,128)(2,1)} %copy-done.29, bf16[1280,512]{1,0:T(8,128)(2,1)} %copy-done.25, ...), custom_call_target="tpu_custom_call" | custom-call | flops 16106127360 | bytes 31997952 | tf_op jit(solution)/shard_map/pallas_call | solution.py:350
  292.8 13.8 %ab.3 = (bf16[1,1536,768]{2,1,0:T(8,128)(2,1)}, f32[1,8,768]{2,1,0:T(8,128)}) custom-call(bf16[2,1536,768]{2,1,0:T(8,128)(2,1)} %bitcast.133, bf16[2,1536,256]{2,1,0:T(8,128)(2,1)} %bitcast.150, f32[1536,128]{1,0:T(8,128)} %get-tuple-element.108.cos_ref, f32[1536,128]{1,0:T(8,128)} %get-tuple-element.107.lo_ref, f32[1536,128]{1,0:T(8,128)} %get-tuple-element.106.hi_ref), custom_call_target="tpu_custom_call" | custom-call | flops 6039797760 | bytes 5505024 | tf_op jit(solution)/shard_map/ab/pallas_call | solution.py:130
  306.7 21.8 %shard_map.253 = (bf16[1536,2048]{1,0:T(8,128)(2,1)}, f32[4,8,2048]{2,1,0:T(8,128)}) custom-call(bf16[1536,768]{1,0:T(8,128)(2,1)} %bitcast.135, bf16[3072,1024]{1,0:T(8,128)(2,1)} %get-tuple-element.53.d_pre_ref, bf16[3072,2048]{1,0:T(8,128)(2,1)} %bitcast.90, f32[8,2048]{1,0:T(8,128)} %maximum_convert_fusion.small_ref, ...), custom_call_target="tpu_custom_call" | custom-call | flops 11274289152 | bytes 25591808 | tf_op jit(solution)/shard_map/pallas_call | solution.py:350
  328.8 13.9 %ab.2 = (bf16[1,1536,768]{2,1,0:T(8,128)(2,1)}, f32[1,8,768]{2,1,0:T(8,128)}) custom-call(bf16[2,1536,768]{2,1,0:T(8,128)(2,1)} %bitcast.134, bf16[2,1536,256]{2,1,0:T(8,128)(2,1)} %bitcast.151, f32[1536,128]{1,0:T(8,128)} %get-tuple-element.108.cos_ref, f32[1536,128]{1,0:T(8,128)} %get-tuple-element.107.lo_ref, f32[1536,128]{1,0:T(8,128)} %get-tuple-element.106.hi_ref), custom_call_target="tpu_custom_call" | custom-call | flops 6039797760 | bytes 5505024 | tf_op jit(solution)/shard_map/ab/pallas_call | solution.py:130
  342.7 22.2 %shard_map.251 = (bf16[1536,2048]{1,0:T(8,128)(2,1)}, f32[4,8,2048]{2,1,0:T(8,128)}) custom-call(bf16[1536,768]{1,0:T(8,128)(2,1)} %bitcast.140, bf16[3072,1024]{1,0:T(8,128)(2,1)} %get-tuple-element.53.d_pre_ref, bf16[3072,2048]{1,0:T(8,128)(2,1)} %bitcast.91, f32[8,2048]{1,0:T(8,128)} %maximum_convert_fusion.small_ref, ...), custom_call_target="tpu_custom_call" | custom-call | flops 11274289152 | bytes 25591808 | tf_op jit(solution)/shard_map/pallas_call | solution.py:350
  375.2 7.1 %collective-permute-done.14 = bf16[384,512]{1,0:T(8,128)(2,1)S(1)} collective-permute-done((bf16[384,512]{1,0:T(8,128)(2,1)S(1)}, bf16[384,512]{1,0:T(8,128)(2,1)S(1)}, u32[]{:S(2)}, u32[]{:S(2)}) %collective-permute-start.14) | collective-permute-done | bytes 393248 | tf_op jit(solution)/shard_map/ppermute | solution.py:371
  382.3 6.7 collective-permute-done.15
  390.3 7.1 %convert_reduce_fusion = f32[512]{0:T(512)} fusion(bf16[8,1536,512]{2,1,0:T(8,128)(2,1)} %param.15), kind=kLoop, calls=%fused_computation | loop fusion | flops 12582400 | bytes 12584960 | tf_op jit(solution)/shard_map/reduce_sum | solution.py:489
  399.6 8.8 %fusion.28 = bf16[1280,512]{1,0:T(8,128)(2,1)S(1)} fusion(bf16[3072,2048]{1,0:T(8,128)(2,1)} %bitcast.125, bf16[3072,1024]{1,0:T(8,128)(2,1)} %get-tuple-element.45.gelu_ref, bf16[3072,256]{1,0:T(8,128)(2,1)} %bitcast.146), kind=kOutput, calls=%fused_computation.27 | convolution fusion | flops 4042915840 | bytes 12320768 | tf_op jit(solution)/shard_map/dot_general | solution.py:27
  426.7 9.0 %fusion.18 = f32[512,1024]{1,0:T(8,128)} fusion(bf16[3072,1024]{1,0:T(8,128)(2,1)} %get-tuple-element.53.d_pre_ref, bf16[3072,2048]{1,0:T(8,128)(2,1)} %get-tuple-element.43.h_mlp_ref), kind=kOutput, calls=%fused_computation.17 | convolution fusion | flops 3221225472 | bytes 11534336 | tf_op jit(solution)/shard_map/dot_general | solution.py:27
  457.1 7.2 %add_convert_fusion.3 = bf16[512,768]{1,0:T(8,128)(2,1)} fusion(bf16[256,768]{1,0:T(8,128)(2,1)} %collective-permute-done.48, bf16[1536,768]{1,0:T(8,128)(2,1)} %bitcast.142, bf16[1536,768]{1,0:T(8,128)(2,1)} %bitcast.137, bf16[3072,2048]{1,0:T(8,128)(2,1)} %get-tuple-element.42.h_attn_ref), kind=kOutput, calls=%fused_computation.46 | convolution fusion | flops 2426535936 | bytes 9043968 | tf_op jit(solution)/shard_map/dot_general | solution.py:27
  464.3 6.8 %collective-permute-done.50 = bf16[256,768]{1,0:T(8,128)(2,1)S(1)} collective-permute-done((bf16[256,768]{1,0:T(8,128)(2,1)S(1)}, bf16[256,768]{1,0:T(8,128)(2,1)S(1)}, u32[]{:S(2)}, u32[]{:S(2)}) %collective-permute-start.50) | collective-permute-done | bytes 393248 | tf_op jit(solution)/shard_map/ppermute | solution.py:371
  478.8 6.5 add_convert_fusion.1
  490.1 8.2 %add_convert_fusion = bf16[512,1024]{1,0:T(8,128)(2,1)} fusion(bf16[3072,1024]{1,0:T(8,128)(2,1)} %get-tuple-element.53.d_pre_ref, bf16[3072,2048]{1,0:T(8,128)(2,1)} %get-tuple-element.43.h_mlp_ref, bf16[256,1024]{1,0:T(8,128)(2,1)} %collective-permute-done.60), kind=kOutput, calls=%fused_computation.36 | convolution fusion | flops 3222798336 | bytes 11010048 | tf_op jit(solution)/shard_map/dot_general | solution.py:27
  507.6 8.9 %fusion.31 = bf16[1280,512]{1,0:T(8,128)(2,1)S(1)} fusion(bf16[3072,2048]{1,0:T(8,128)(2,1)} %bitcast.126, bf16[3072,1024]{1,0:T(8,128)(2,1)} %get-tuple-element.45.gelu_ref, bf16[3072,256]{1,0:T(8,128)(2,1)S(1)} %bitcast.147, bf16[640,512]{1,0:T(8,128)(2,1)} %collective-permute-done.54), kind=kOutput, calls=%fused_computation.28 | convolution fusion | flops 4044226560 | bytes 12976128 | tf_op jit(solution)/shard_map/dot_general | solution.py:27
  526.6 7.2 %fusion.34 = bf16[1280,512]{1,0:T(8,128)(2,1)S(1)} fusion(bf16[3072,2048]{1,0:T(8,128)(2,1)S(1)} %bitcast.129, bf16[3072,1024]{1,0:T(8,128)(2,1)} %get-tuple-element.45.gelu_ref, bf16[3072,256]{1,0:T(8,128)(2,1)S(1)} %bitcast.148, bf16[640,512]{1,0:T(8,128)(2,1)} %collective-permute-done.56), kind=kOutput, calls=%fused_computation.29 | convolution fusion | flops 4044226560 | bytes 12976128 | tf_op jit(solution)/shard_map/dot_general | solution.py:27
  533.9 29.8 %collective-permute-done.22 = bf16[192,512]{1,0:T(8,128)(2,1)S(1)} collective-permute-done((bf16[192,512]{1,0:T(8,128)(2,1)S(1)}, bf16[192,512]{1,0:T(8,128)(2,1)S(1)}, u32[]{:S(2)}, u32[]{:S(2)}) %collective-permute-start.22) | collective-permute-done | bytes 196640 | tf_op jit(solution)/shard_map/ppermute | solution.py:371
  605.1 12.1 %collective-permute-done.55 = bf16[1280,512]{1,0:T(8,128)(2,1)S(1)} collective-permute-done((bf16[1280,512]{1,0:T(8,128)(2,1)S(1)}, bf16[1280,512]{1,0:T(8,128)(2,1)S(1)}, u32[]{:S(2)}, u32[]{:S(2)}) %collective-permute-start.55) | collective-permute-done | bytes 1310752 | tf_op jit(solution)/shard_map/ppermute | solution.py:371
  628.5 7.6 %convert_add_fusion = f32[1024,512]{1,0:T(8,128)} fusion(bf16[1280,512]{1,0:T(8,128)(2,1)S(1)} %collective-permute-done.57, bf16[1280,512]{1,0:T(8,128)(2,1)S(1)} %collective-permute-done.55, bf16[3072,1024]{1,0:T(8,128)(2,1)} %get-tuple-element.45.gelu_ref, bf16[3072,2048]{1,0:T(8,128)(2,1)S(1)} %bitcast.131), kind=kOutput, calls=%fused_computation.34 | convolution fusion | flops 3223322624 | bytes 13631488 | tf_op jit(solution)/shard_map/dot_general | solution.py:27
  637.0 6.1 shard_map.255.refs_8_
  644.1 6.1 shard_map.256
  650.3 9.6 %shard_map.249 = bf16[4,3072,512]{2,1,0:T(8,128)(2,1)} custom-call(s32[3]{0:T(128)} %pad_add_fusion.place_ref, bf16[4,3072,512]{2,1,0:T(8,128)(2,1)} %bitcast.93), custom_call_target="tpu_custom_call" | custom-call | flops 6291456 | bytes 25165824 | tf_op jit(solution)/shard_map/pallas_call | solution.py:188
  (327 shorter events, 192.8 us)
Async XLA Ops:
  7.2 169.4 %all-gather.4.cloned.1.call-start = ((), (), s32[]{:S(2)}) async-start(), calls=%async_computation.3 | async-start | bytes 14155776 | tf_op jit(solution)/shard_map/all_gather | solution.py:440
  33.8 232.1 %all-gather.8.cloned.1.call-start = ((), (), s32[]{:S(2)}) async-start(), calls=%async_computation.6 | async-start | bytes 14155776 | tf_op jit(solution)/shard_map/all_gather | solution.py:441
  59.1 308.2 %reduce-scatter.4.cloned.1.call-start = ((), (), s32[]{:S(2)}) async-start(), calls=%async_computation.4 | async-start | bytes 14155776 | tf_op jit(solution)/shard_map/reduce_scatter | solution.py:461
  62.3 75.2 %collective-permute-start.6 = (bf16[512,1792]{1,0:T(8,128)(2,1)S(1)}, bf16[512,1792]{1,0:T(8,128)(2,1)S(1)}, u32[]{:S(2)}, u32[]{:S(2)}) collective-permute-start(bf16[512,1792]{1,0:T(8,128)(2,1)S(1)} %get-tuple-element.92), channel_id=1, source_target_pairs={{0,24},{8,0},{16,8},{24,16},{1,25},{9,1},{17,9},{25,17},{2,26},{10... | collective-permute-start | bytes 5505032 | tf_op jit(solution)/shard_map/ppermute | solution.py:371
  64.4 76.6 %collective-permute-start.8 = (bf16[512,1792]{1,0:T(8,128)(2,1)S(1)}, bf16[512,1792]{1,0:T(8,128)(2,1)S(1)}, u32[]{:S(2)}, u32[]{:S(2)}) collective-permute-start(bf16[512,1792]{1,0:T(8,128)(2,1)S(1)} %get-tuple-element.92), channel_id=1, source_target_pairs={{0,8},{8,16},{16,24},{24,0},{1,9},{9,17},{17,25},{25,1},{2,10},{10... | collective-permute-start | bytes 5505032 | tf_op jit(solution)/shard_map/ppermute | solution.py:371
  64.5 71.0 %collective-permute-start.12 = (bf16[1280,512]{1,0:T(8,128)(2,1)S(1)}, bf16[1280,512]{1,0:T(8,128)(2,1)S(1)}, u32[]{:S(2)}, u32[]{:S(2)}) collective-permute-start(bf16[1280,512]{1,0:T(8,128)(2,1)S(1)} %constant_dynamic-update-slice_fusion.5.refs_0_), channel_id=1, source_target_pairs={{0,8},{8,16},{16,24},{24,0},{1,9},{9,17},{17,25},{25,1},{2,10},{10... | collective-permute-start | bytes 3932168 | tf_op jit(solution)/shard_map/ppermute | solution.py:371
  65.6 70.0 %collective-permute-start.10 = (bf16[1280,512]{1,0:T(8,128)(2,1)S(1)}, bf16[1280,512]{1,0:T(8,128)(2,1)S(1)}, u32[]{:S(2)}, u32[]{:S(2)}) collective-permute-start(bf16[1280,512]{1,0:T(8,128)(2,1)S(1)} %constant_dynamic-update-slice_fusion.5.refs_0_), channel_id=1, source_target_pairs={{0,24},{8,0},{16,8},{24,16},{1,25},{9,1},{17,9},{25,17},{2,26},{10... | collective-permute-start | bytes 3932168 | tf_op jit(solution)/shard_map/ppermute | solution.py:371
  68.2 69.8 %collective-permute-start.5 = (bf16[8,512]{1,0:T(8,128)(2,1)S(1)}, bf16[8,512]{1,0:T(8,128)(2,1)S(1)}, u32[]{:S(2)}, u32[]{:S(2)}) collective-permute-start(bf16[8,512]{1,0:T(8,128)(2,1)S(1)} %select_select_fusion), channel_id=1, source_target_pairs={{0,8},{8,16},{16,24},{24,0},{1,9},{9,17},{17,25},{25,1},{2,10},{10... | collective-permute-start | bytes 24584 | tf_op jit(solution)/shard_map/ppermute | solution.py:371
  141.0 32.2 %collective-permute-start.7 = (bf16[256,1792]{1,0:T(8,128)(2,1)S(1)}, bf16[256,1792]{1,0:T(8,128)(2,1)S(1)}, u32[]{:S(2)}, u32[]{:S(2)}) collective-permute-start(bf16[256,1792]{1,0:T(8,128)(2,1)S(1)} %slice.174), channel_id=1, source_target_pairs={{0,24},{8,0},{16,8},{24,16},{1,25},{9,1},{17,9},{25,17},{2,26},{10... | collective-permute-start | bytes 2752520 | tf_op jit(solution)/shard_map/ppermute | solution.py:371
  147.4 26.8 %collective-permute-start.9 = (bf16[256,1792]{1,0:T(8,128)(2,1)S(1)}, bf16[256,1792]{1,0:T(8,128)(2,1)S(1)}, u32[]{:S(2)}, u32[]{:S(2)}) collective-permute-start(bf16[256,1792]{1,0:T(8,128)(2,1)S(1)} %slice.175), channel_id=1, source_target_pairs={{0,8},{8,16},{16,24},{24,0},{1,9},{9,17},{17,25},{25,1},{2,10},{10... | collective-permute-start | bytes 2752520 | tf_op jit(solution)/shard_map/ppermute | solution.py:371
  265.7 219.7 %reduce-scatter.8.cloned.1.call-start = ((), (), s32[]{:S(2)}) async-start(), calls=%async_computation.8 | async-start | bytes 7077888 | tf_op jit(solution)/shard_map/reduce_scatter | solution.py:479
  328.6 169.7 %reduce-scatter.6.cloned.1.call-start = ((), (), s32[]{:S(2)}) async-start(), calls=%async_computation.7 | async-start | bytes 7077888 | tf_op jit(solution)/shard_map/reduce_scatter | solution.py:479
  365.0 285.2 %all-gather.6.cloned.1.call-start = ((), (), s32[]{:S(2)}) async-start(), calls=%async_computation.5 | async-start | bytes 14155776 | tf_op jit(solution)/shard_map/all_gather | solution.py:463
  409.6 94.6 %collective-permute-start.54 = (bf16[640,512]{1,0:T(8,128)(2,1)}, bf16[640,512]{1,0:T(8,128)(2,1)}, u32[]{:S(2)}, u32[]{:S(2)}) collective-permute-start(bf16[640,512]{1,0:T(8,128)(2,1)} %get-tuple-element.94), channel_id=1, source_target_pairs={{0,8},{8,16},{16,24},{24,0},{1,9},{9,17},{17,25},{25,1},{2,10},{10... | collective-permute-start | bytes 1966088 | tf_op jit(solution)/shard_map/ppermute | solution.py:371
  410.2 113.6 %collective-permute-start.56 = (bf16[640,512]{1,0:T(8,128)(2,1)}, bf16[640,512]{1,0:T(8,128)(2,1)}, u32[]{:S(2)}, u32[]{:S(2)}) collective-permute-start(bf16[640,512]{1,0:T(8,128)(2,1)} %get-tuple-element.95), channel_id=1, source_target_pairs={{0,24},{8,0},{16,8},{24,16},{1,25},{9,1},{17,9},{25,17},{2,26},{10... | collective-permute-start | bytes 1966088 | tf_op jit(solution)/shard_map/ppermute | solution.py:371
  419.4 59.4 %collective-permute-start.58 = (bf16[256,1024]{1,0:T(8,128)(2,1)}, bf16[256,1024]{1,0:T(8,128)(2,1)}, u32[]{:S(2)}, u32[]{:S(2)}) collective-permute-start(bf16[256,1024]{1,0:T(8,128)(2,1)} %get-tuple-element.96), channel_id=1, source_target_pairs={{0,8},{8,16},{16,24},{24,0},{1,9},{9,17},{17,25},{25,1},{2,10},{10... | collective-permute-start | bytes 1572872 | tf_op jit(solution)/shard_map/ppermute | solution.py:371
  449.2 40.9 %collective-permute-start.60 = (bf16[256,1024]{1,0:T(8,128)(2,1)}, bf16[256,1024]{1,0:T(8,128)(2,1)}, u32[]{:S(2)}, u32[]{:S(2)}) collective-permute-start(bf16[256,1024]{1,0:T(8,128)(2,1)} %get-tuple-element.97), channel_id=1, source_target_pairs={{0,24},{8,0},{16,8},{24,16},{1,25},{9,1},{17,9},{25,17},{2,26},{10... | collective-permute-start | bytes 1572872 | tf_op jit(solution)/shard_map/ppermute | solution.py:371
  471.1 29.8 %collective-permute-start.53 = (f32[1,1792]{1,0:T(1,128)S(1)}, f32[1,1792]{1,0:T(1,128)}, u32[]{:S(2)}, u32[]{:S(2)}) collective-permute-start(f32[1,1792]{1,0:T(1,128)S(1)} %reshape_add_fusion), channel_id=1, source_target_pairs={{0,16},{8,24},{16,0},{24,8},{1,17},{9,25},{17,1},{25,9},{2,18},{10... | collective-permute-start | bytes 21512 | tf_op jit(solution)/shard_map/ppermute | solution.py:376
  500.4 25.6 %collective-permute-start.20 = (bf16[192,512]{1,0:T(8,128)(2,1)S(1)}, bf16[192,512]{1,0:T(8,128)(2,1)S(1)}, u32[]{:S(2)}, u32[]{:S(2)}) collective-permute-start(bf16[192,512]{1,0:T(8,128)(2,1)S(1)} %get-tuple-element.56), channel_id=1, source_target_pairs={{0,8},{8,16},{16,24},{24,0},{1,9},{9,17},{17,25},{25,1},{2,10},{10... | collective-permute-start | bytes 589832 | tf_op jit(solution)/shard_map/ppermute | solution.py:371
  500.8 25.3 %collective-permute-start.21 = (bf16[192,512]{1,0:T(8,128)(2,1)S(1)}, bf16[192,512]{1,0:T(8,128)(2,1)S(1)}, u32[]{:S(2)}, u32[]{:S(2)}) collective-permute-start(bf16[192,512]{1,0:T(8,128)(2,1)S(1)} %get-tuple-element.57), channel_id=1, source_target_pairs={{0,16},{8,24},{16,0},{24,8},{1,17},{9,25},{17,1},{25,9},{2,18},{10... | collective-permute-start | bytes 589832 | tf_op jit(solution)/shard_map/ppermute | solution.py:371
  521.8 46.4 %collective-permute-start.51 = (bf16[512,768]{1,0:T(8,128)(2,1)S(1)}, bf16[512,768]{1,0:T(8,128)(2,1)S(1)}, u32[]{:S(2)}, u32[]{:S(2)}) collective-permute-start(bf16[512,768]{1,0:T(8,128)(2,1)S(1)} %copy-done.47), channel_id=1, source_target_pairs={{0,24},{8,0},{16,8},{24,16},{1,25},{9,1},{17,9},{25,17},{2,26},{10... | collective-permute-start | bytes 2359304 | tf_op jit(solution)/shard_map/ppermute | solution.py:371
  522.8 48.5 %collective-permute-start.49 = (bf16[512,768]{1,0:T(8,128)(2,1)S(1)}, bf16[512,768]{1,0:T(8,128)(2,1)S(1)}, u32[]{:S(2)}, u32[]{:S(2)}) collective-permute-start(bf16[512,768]{1,0:T(8,128)(2,1)S(1)} %copy-done.46), channel_id=1, source_target_pairs={{0,8},{8,16},{16,24},{24,0},{1,9},{9,17},{17,25},{25,1},{2,10},{10... | collective-permute-start | bytes 2359304 | tf_op jit(solution)/shard_map/ppermute | solution.py:371
  523.9 47.4 %collective-permute-start.61 = (bf16[512,1024]{1,0:T(8,128)(2,1)S(1)}, bf16[512,1024]{1,0:T(8,128)(2,1)S(1)}, u32[]{:S(2)}, u32[]{:S(2)}) collective-permute-start(bf16[512,1024]{1,0:T(8,128)(2,1)S(1)} %copy-done.45), channel_id=1, source_target_pairs={{0,24},{8,0},{16,8},{24,16},{1,25},{9,1},{17,9},{25,17},{2,26},{10... | collective-permute-start | bytes 3145736 | tf_op jit(solution)/shard_map/ppermute | solution.py:371
  526.0 37.6 %collective-permute-start.22 = (bf16[192,512]{1,0:T(8,128)(2,1)S(1)}, bf16[192,512]{1,0:T(8,128)(2,1)S(1)}, u32[]{:S(2)}, u32[]{:S(2)}) collective-permute-start(bf16[192,512]{1,0:T(8,128)(2,1)S(1)} %get-tuple-element.58), channel_id=1, source_target_pairs={{0,24},{8,0},{16,8},{24,16},{1,25},{9,1},{17,9},{25,17},{2,26},{10... | collective-permute-start | bytes 589832 | tf_op jit(solution)/shard_map/ppermute | solution.py:371
  526.1 46.7 %collective-permute-start.34 = (bf16[4,192,512]{2,1,0:T(8,128)(2,1)S(1)}, bf16[4,192,512]{2,1,0:T(8,128)(2,1)S(1)}, u32[]{:S(2)}, u32[]{:S(2)}) collective-permute-start(bf16[4,192,512]{2,1,0:T(8,128)(2,1)S(1)} %pad_maximum_fusion.12.refs_0_), channel_id=1, source_target_pairs={{0,6},{1,7},{2,0},{3,1},{4,2},{5,3},{6,4},{7,5},{8,14},{9,15},{10,... | collective-permute-start | bytes 2359304 | tf_op jit(solution)/shard_map/ppermute | solution.py:381
  567.6 27.6 %collective-permute-start.59 = (bf16[512,1024]{1,0:T(8,128)(2,1)S(1)}, bf16[512,1024]{1,0:T(8,128)(2,1)S(1)}, u32[]{:S(2)}, u32[]{:S(2)}) collective-permute-start(bf16[512,1024]{1,0:T(8,128)(2,1)S(1)} %copy-done.44), channel_id=1, source_target_pairs={{0,8},{8,16},{16,24},{24,0},{1,9},{9,17},{17,25},{25,1},{2,10},{10... | collective-permute-start | bytes 3145736 | tf_op jit(solution)/shard_map/ppermute | solution.py:371
  568.2 36.8 %collective-permute-start.57 = (bf16[1280,512]{1,0:T(8,128)(2,1)S(1)}, bf16[1280,512]{1,0:T(8,128)(2,1)S(1)}, u32[]{:S(2)}, u32[]{:S(2)}) collective-permute-start(bf16[1280,512]{1,0:T(8,128)(2,1)S(1)} %fusion.34), channel_id=1, source_target_pairs={{0,24},{8,0},{16,8},{24,16},{1,25},{9,1},{17,9},{25,17},{2,26},{10... | collective-permute-start | bytes 3932168 | tf_op jit(solution)/shard_map/ppermute | solution.py:371
  571.3 46.0 %collective-permute-start.55 = (bf16[1280,512]{1,0:T(8,128)(2,1)S(1)}, bf16[1280,512]{1,0:T(8,128)(2,1)S(1)}, u32[]{:S(2)}, u32[]{:S(2)}) collective-permute-start(bf16[1280,512]{1,0:T(8,128)(2,1)S(1)} %fusion.31), channel_id=1, source_target_pairs={{0,8},{8,16},{16,24},{24,0},{1,9},{9,17},{17,25},{25,1},{2,10},{10... | collective-permute-start | bytes 3932168 | tf_op jit(solution)/shard_map/ppermute | solution.py:371
  571.3 25.0 %collective-permute-start.36 = (bf16[4,192,512]{2,1,0:T(8,128)(2,1)S(1)}, bf16[4,192,512]{2,1,0:T(8,128)(2,1)S(1)}, u32[]{:S(2)}, u32[]{:S(2)}) collective-permute-start(bf16[4,192,512]{2,1,0:T(8,128)(2,1)S(1)} %pad_maximum_fusion.12.refs_0_), channel_id=1, source_target_pairs={{0,2},{1,3},{2,4},{3,5},{4,6},{5,7},{6,0},{7,1},{8,10},{9,11},{10,... | collective-permute-start | bytes 2359304 | tf_op jit(solution)/shard_map/ppermute | solution.py:381
  595.2 23.4 %collective-permute-start.35 = (bf16[2,192,512]{2,1,0:T(8,128)(2,1)S(1)}, bf16[2,192,512]{2,1,0:T(8,128)(2,1)S(1)}, u32[]{:S(2)}, u32[]{:S(2)}) collective-permute-start(bf16[2,192,512]{2,1,0:T(8,128)(2,1)S(1)} %slice.182), channel_id=1, source_target_pairs={{0,6},{1,7},{2,0},{3,1},{4,2},{5,3},{6,4},{7,5},{8,14},{9,15},{10,... | collective-permute-start | bytes 1179656 | tf_op jit(solution)/shard_map/ppermute | solution.py:381
  596.3 22.3 %collective-permute-start.24 = (bf16[2,192,512]{2,1,0:T(8,128)(2,1)S(1)}, bf16[2,192,512]{2,1,0:T(8,128)(2,1)S(1)}, u32[]{:S(2)}, u32[]{:S(2)}) collective-permute-start(bf16[2,192,512]{2,1,0:T(8,128)(2,1)S(1)} %slice.180), channel_id=1, source_target_pairs={{0,6},{1,7},{2,0},{3,1},{4,2},{5,3},{6,4},{7,5},{8,14},{9,15},{10,... | collective-permute-start | bytes 1179656 | tf_op jit(solution)/shard_map/ppermute | solution.py:381
  603.8 22.0 %collective-permute-start.38 = (bf16[4,192,512]{2,1,0:T(8,128)(2,1)S(1)}, bf16[4,192,512]{2,1,0:T(8,128)(2,1)S(1)}, u32[]{:S(2)}, u32[]{:S(2)}) collective-permute-start(bf16[4,192,512]{2,1,0:T(8,128)(2,1)S(1)} %pad_maximum_fusion.12.refs_0_), channel_id=1, source_target_pairs={{0,1},{1,0},{2,3},{3,2},{4,5},{5,4},{6,7},{7,6},{8,9},{9,8},{10,11... | collective-permute-start | bytes 2359304 | tf_op jit(solution)/shard_map/ppermute | solution.py:384
  (94 other events, 1613.1 us)
Sparse Core Ops, SparseCore 0:
  33.9 64.6 all-gather.3
  100.8 65.0 all-gather.7
  265.8 69.5 reduce-scatter.3
  337.6 39.9 reduce-scatter.7
  379.7 39.7 reduce-scatter.5
  420.9 66.7 all-gather.5

commit v5 on v4

--- a/solution.py
+++ b/solution.py
@@ -142,10 +142,11 @@
     return forward, backward
 
 
-def place_kernel(place_ref, full_ref, out_ref, held_ref, in_sems, out_sems, *, chunk, n_seq):
+def place_kernel(place_ref, full_ref, *rest, chunk, n_seq):
+    out_ref, held_ref, in_sems, out_sems = rest[-4:]
     groups = full_ref.shape[0]
     fetch = [pltpu.make_async_copy(full_ref.at[lax.rem(place_ref[0] + groups - t, groups)], held_ref.at[t], in_sems.at[t]) for t in range(groups)]
-    store = [pltpu.make_async_copy(held_ref.at[t], out_ref.at[t], out_sems.at[t]) for t in range(groups)]
+    store = [pltpu.make_async_copy(held_ref.at[t], out_ref.at[t * n_seq + chunk], out_sems.at[t]) for t in range(groups)]
     for copy in fetch:
         copy.start()
     for t in range(groups):
@@ -248,19 +249,30 @@
         h_mlp_ref[at, :] = (x_hat * small_ref[2:3, :] + small_ref[3:4, :]).astype(jnp.bfloat16)
 
 
-def front_kernel(h_attn_ref, h_mlp_ref, cos_ref, lo_ref, hi_ref, w_ref, b_qkv_ref, b_up_ref, qkv_ref, pre_ref, gelu_ref):
+def offsets(refs, axis):
+    starts = [0]
+    for ref in refs:
+        starts.append(starts[-1] + ref.shape[axis])
+    return list(zip(refs, starts, starts[1:]))
+
+
+def front_kernel(h_attn_ref, h_mlp_ref, cos_ref, lo_ref, hi_ref, b_qkv_ref, b_up_ref, *refs):
+    w_refs, (qkv_ref, pre_ref, gelu_ref) = refs[:-3], refs[-3:]
     qkv_width = qkv_ref.shape[1]
     head = qkv_width // 3
+
+    def project(h_ref, cols):
+        return sum(dot(h_ref[:, start:stop], w_ref[:, cols], NN) for w_ref, start, stop in offsets(w_refs, 0))
+
     for low in range(0, qkv_width, head):
         at = slice(low, low + head)
-        part = (dot(h_attn_ref[...], w_ref[:, at], NN) + b_qkv_ref[:, at]).astype(jnp.bfloat16)
+        part = (project(h_attn_ref, at) + b_qkv_ref[:, at]).astype(jnp.bfloat16)
         if low < 2 * head:
             part = rotate(part.astype(jnp.float32), cos_ref[...], lo_ref[...], hi_ref[...], head // ROTARY_DIVISOR // 2, 1.0).astype(jnp.bfloat16)
         qkv_ref[:, at] = part
     for low in range(0, pre_ref.shape[1], TILE):
         at = slice(low, low + TILE)
-        acc = dot(h_mlp_ref[...], w_ref[:, qkv_width + low:qkv_width + low + TILE], NN) + b_up_ref[:, at]
-        pre = acc.astype(jnp.bfloat16)
+        pre = (project(h_mlp_ref, slice(qkv_width + low, qkv_width + low + TILE)) + b_up_ref[:, at]).astype(jnp.bfloat16)
         pre_ref[:, at] = pre
         wide = pre.astype(jnp.float32)
         gelu_ref[:, at] = (0.5 * wide * (1.0 + lax.erf(wide * SQRT_HALF))).astype(jnp.bfloat16)
@@ -270,18 +282,16 @@
     w_refs, y_ref = refs[:-1], refs[-1]
     head = ctx_ref.shape[1]
     places, _, own, _ = y_ref.shape
-    for index, w_ref in enumerate(w_refs):
-        width = w_ref.shape[1]
+    for w_ref, start, stop in offsets(w_refs, 1):
         acc = dot(ctx_ref[...], w_ref[:head, :], NN) + dot(gelu_ref[...], w_ref[head:, :], NN)
-        y_ref[:, 0, :, index * width:(index + 1) * width] = acc.astype(jnp.bfloat16).reshape(places, own, width)
+        y_ref[:, 0, :, start:stop] = acc.astype(jnp.bfloat16).reshape(places, own, stop - start)
 
 
 def d_pre_kernel(cot_ref, pre_ref, *refs):
     w_refs, (d_ctx_ref, d_pre_ref, d_bias_ref) = refs[:-3], refs[-3:]
-    width = w_refs[0].shape[1]
 
     def back(low, high):
-        return sum(dot(cot_ref[:, r * width:(r + 1) * width], w_ref[low:high, :], NT) for r, w_ref in enumerate(w_refs)).astype(jnp.bfloat16)
+        return sum(dot(cot_ref[:, start:stop], w_ref[low:high, :], NT) for w_ref, start, stop in offsets(w_refs, 1)).astype(jnp.bfloat16)
 
     head = d_ctx_ref.shape[1]
 
@@ -300,7 +310,8 @@
         d_bias_ref[:, at] += sublane_sum(d_pre.astype(jnp.float32))
 
 
-def d_h_kernel(d_qkv_ref, d_pre_ref, x_ref, small_ref, w_ref, a6_ref, sums_ref):
+def d_h_kernel(d_qkv_ref, d_pre_ref, x_ref, small_ref, *refs):
+    w_refs, (a6_ref, sums_ref) = refs[:-2], refs[-2:]
     qkv_width = d_qkv_ref.shape[1]
 
     @pl.when(pl.program_id(0) == 0)
@@ -310,16 +321,18 @@
     x_float = x_ref[...].astype(jnp.float32)
     mean = x_float.mean(-1, keepdims=True)
     inv_std = lax.rsqrt((x_float * x_float).mean(-1, keepdims=True) - mean * mean + LN_EPS)
-    for low in range(0, a6_ref.shape[1], TILE):
-        at = slice(low, low + TILE)
-        d_attn = dot(d_qkv_ref[...], w_ref[at, :qkv_width], NT).astype(jnp.bfloat16).astype(jnp.float32)
-        d_mlp = dot(d_pre_ref[...], w_ref[at, qkv_width:], NT).astype(jnp.bfloat16).astype(jnp.float32)
-        a6_ref[:, at] = (d_attn * small_ref[0:1, at] + d_mlp * small_ref[2:3, at]).astype(jnp.bfloat16)
-        x_hat = (x_ref[:, at].astype(jnp.float32) - mean) * inv_std
-        sums_ref[0, :, at] += sublane_sum(d_attn * x_hat)
-        sums_ref[1, :, at] += sublane_sum(d_attn)
-        sums_ref[2, :, at] += sublane_sum(d_mlp * x_hat)
-        sums_ref[3, :, at] += sublane_sum(d_mlp)
+    for w_ref, start, stop in offsets(w_refs, 0):
+        for low in range(0, stop - start, TILE):
+            part = slice(low, min(low + TILE, stop - start))
+            at = slice(start + part.start, start + part.stop)
+            d_attn = dot(d_qkv_ref[...], w_ref[part, :qkv_width], NT).astype(jnp.bfloat16).astype(jnp.float32)
+            d_mlp = dot(d_pre_ref[...], w_ref[part, qkv_width:], NT).astype(jnp.bfloat16).astype(jnp.float32)
+            a6_ref[:, at] = (d_attn * small_ref[0:1, at] + d_mlp * small_ref[2:3, at]).astype(jnp.bfloat16)
+            x_hat = (x_ref[:, at].astype(jnp.float32) - mean) * inv_std
+            sums_ref[0, :, at] += sublane_sum(d_attn * x_hat)
+            sums_ref[1, :, at] += sublane_sum(d_attn)
+            sums_ref[2, :, at] += sublane_sum(d_mlp * x_hat)
+            sums_ref[3, :, at] += sublane_sum(d_mlp)
 
 
 def tile_call(kernel, tiled, whole, outs, row_range, flops, rows=512):
@@ -383,15 +396,16 @@
     def partner(value):
         return lax.ppermute(value, 'ty', [(s, s ^ 1) for s in range(ty_size)])
 
-    def ring_gather(block, move, size):
-        far = size // 2
-        blocks = {0: block}
-        for hops in range(1, far):
-            blocks[hops] = move(blocks[hops - 1], 1)
-            blocks[size - hops] = move(blocks[(size - hops + 1) % size], -1)
-        half = block.shape[0] // 2
-        blocks[far] = jnp.concatenate([move(blocks[far - 1][:half], 1), move(blocks[far + 1][half:], -1)], axis=0)
-        return [blocks[r] for r in range(size)]
+    def ring_gather(block, axis):
+        blocks = {0: [block]}
+        for hops in range(1, antipode):
+            blocks[hops] = [shift(blocks[hops - 1][0], 1)]
+            blocks[tx_size - hops] = [shift(blocks[(tx_size - hops + 1) % tx_size][0], -1)]
+        half = block.shape[axis] // 2
+        low = lax.slice_in_dim(blocks[antipode - 1][0], 0, half, axis=axis)
+        high = lax.slice_in_dim(blocks[antipode + 1][0], half, 2 * half, axis=axis)
+        blocks[antipode] = [shift(low, 1), shift(high, -1)]
+        return [piece for r in range(tx_size) for piece in blocks[r]]
 
     def ring_scatter(make_part, rows):
         half = rows // 2
@@ -441,18 +455,18 @@
         cot_group = lax.all_gather(cot_own, 'ty', axis=1, tiled=True)
         x_group, cot_group = x_group.reshape(n_seq * seq_len, -1), cot_group.reshape(n_seq * seq_len, -1)
         w_in = jnp.concatenate([w_qkv.reshape(d_local, qkv_width), w_up], axis=1)
-        w_in = ring_gather(w_in, shift, tx_size)
-        w_in = jnp.concatenate(w_in, axis=0)
-        w_back = ring_gather(jnp.concatenate([w_dense, w_down], axis=0), shift, tx_size)
-        back_size = tx_size * w_back[0].size
+        w_in = ring_gather(w_in, 0)
+        w_back = jnp.concatenate([w_dense, w_down], axis=0)
+        w_back = ring_gather(w_back, 1)
+        in_size, back_size = sum(w.size for w in w_in), sum(w.size for w in w_back)
 
         n_tok, d_model = x_group.shape
         x_rows, cot_rows = x_own.reshape(-1, d_model), cot_own.reshape(-1, d_model)
         ff_width = w_up.shape[1]
         h_attn, h_mlp = tile_call(norm_kernel, [x_group], [small], [(d_model, jnp.bfloat16), (d_model, jnp.bfloat16)], (0, n_tok), 16 * x_group.size)
         qkv_act, pre_act, gelu_out = tile_call(
-            front_kernel, [h_attn, h_mlp, *tables], [w_in, b_qkv.reshape(1, -1).astype(jnp.float32), b_up.reshape(1, -1).astype(jnp.float32)],
-            [(qkv_width, jnp.bfloat16), (ff_width, jnp.bfloat16), (ff_width, jnp.bfloat16)], (0, n_tok), 2 * n_tok * w_in.size)
+            front_kernel, [h_attn, h_mlp, *tables], [b_qkv.reshape(1, -1).astype(jnp.float32), b_up.reshape(1, -1).astype(jnp.float32), *w_in],
+            [(qkv_width, jnp.bfloat16), (ff_width, jnp.bfloat16), (ff_width, jnp.bfloat16)], (0, n_tok), 2 * n_tok * in_size)
         qkv_seq = qkv_act.reshape(n_seq, seq_len, qkv_width)
         context = attn_fwd(qkv_seq).reshape(n_tok, head)
         blocks_per_seq = ty_size // 2
@@ -473,19 +487,28 @@
             d_qkv.append(d_qkv_seq.reshape(seq_len, qkv_width))
             d_b_qkv.append(d_b_seq.sum((0, 1)))
             a6_part, sums = tile_call(
-                d_h_kernel, [d_qkv[s], d_pre, x_group], [small, w_in],
-                [(d_model, jnp.bfloat16), ((4, 8, d_model), jnp.float32)], (s * seq_len, seq_len), 2 * seq_len * w_in.size)
+                d_h_kernel, [d_qkv[s], d_pre, x_group], [small, *w_in],
+                [(d_model, jnp.bfloat16), ((4, 8, d_model), jnp.float32)], (s * seq_len, seq_len), 2 * seq_len * in_size)
             d_ln.append(sums)
             value_a6 = lax.psum_scatter(a6_part, 'ty', scatter_dimension=0, tiled=True)
             parts = row_call(finish_dx_kernel, tx_size, s, own, x_rows, value_a6, cot_rows)
-            blocks = ring_gather(to_width(parts), along, ty_size // 2)
-            blocks = blocks + [partner(block) for block in blocks]
-            dx_act = place_call(place_pieces_kernel, place, blocks, dx_act, s, n_seq, seq_len)
+            block = to_width(parts)
+            if s < n_seq - 1:
+                blocks = [block] + [along(block, hops) for hops in range(1, ty_size // 2)]
+                blocks = blocks + [partner(piece) for piece in blocks]
+                dx_act = place_call(place_pieces_kernel, place, blocks, dx_act, s, n_seq, seq_len)
+            else:
+                full = lax.all_gather(block, 'ty', axis=1, tiled=True)
+                dx_act = place_call(place_kernel, place, [full], dx_act, s, n_seq, seq_len)
         d_qkv = jnp.concatenate(d_qkv, axis=0)
 
-        d_ln = small_sum(sum(d_ln).sum(1), 'ty', ty_size).reshape(4, tx_size, d_local)
-        d_ln = d_ln[:, 0] + sum(shift(d_ln[:, r], -r) for r in range(1, tx_size))
-        d_bias = small_sum(jnp.concatenate([sum(d_b_qkv), d_b_up])[None], 'tx', tx_size)[0]
+        d_ln = sum(d_ln).sum(1).reshape(4, tx_size, d_local)
+        d_bias = jnp.concatenate([sum(d_b_qkv), d_b_up]).reshape(4, -1)
+        sent = [jnp.concatenate([d_ln[:, r], d_bias], axis=1) for r in range(tx_size)]
+        got = [sent[0]] + [shift(sent[r], -r) for r in range(1, tx_size)]
+        got = sum(got[r] + got[r + antipode] for r in range(antipode))
+        d_bias = got[:, d_local:].reshape(-1)
+        d_ln = small_sum(got[:, :d_local], 'ty', ty_size)
         d_b_out = cot_out.astype(jnp.float32).sum((0, 1))
 
         cols = lambda act, r: act[:, r * d_local:(r + 1) * d_local]

time: 676 us -> 676 us (level)
  waiting for transfers between devices: 211 us -> 236 us
  local copies, waits for them, and re-layouts: 31.7 us -> 20.4 us
  starting transfers between devices: 76.5 us -> 68.6 us
    reduce_scatter x1, waiting for transfers between devices: 0.02 us -> 18.2 us  [body(): lax.psum_scatter(y_part.reshape(n_tok, d_model), 'ty', scatter_dimension=...]
    ppermute x8 -> x3, waiting for transfers between devices: 7.97 us -> 18.5 us  [along(): lax.ppermute(value, 'ty', [(s, (s - 2 * hops) % ty_size) for s in range(t...]
    unnamed x126 -> x110, local copies, waits for them, and re-layouts: 15.8 us -> 13 us
  transfers between devices with their start and end apart: 68 -> 58, of which waited for: 21 -> 22; matrix products, arithmetic and copies ran while one was open for 21% -> 18% of each run, Pallas kernels for 30% -> 21%
where the time goes in v5:
time: 676 us; the launch traced here: 669 us
  waiting for transfers between devices  236 us (35%)
  Pallas kernels  213 us (32%)
  matrix products  87.2 us (13%)
  starting transfers between devices  68.6 us (10%)
  other arithmetic  29 us (4%)
  local copies, waits for them, and re-layouts  20.4 us (3%)
  between operations  15.4 us (2%)
    ppermute x41, waiting for transfers between devices, shift(): lax.ppermute(value, 'tx', [(s, (s - hops) % tx_size) for s in range(tx_si...  196 us
    pallas_call x6, Pallas kernels, tile_call(): pl.pallas_call(kernel, grid=(count // rows,), in_specs=in_specs, out_spec...  145 us
    dot_general x13, matrix products, dot(): return lax.dot_general(a, b, dims, preferred_element_type=jnp.float32)  87.2 us
    ppermute x41, starting transfers between devices, shift(): lax.ppermute(value, 'tx', [(s, (s - hops) % tx_size) for s in range(tx_si...  58.4 us
    pallas_call x2, Pallas kernels, backward(): pl.pallas_call(functools.partial(attn_bwd_kernel, half=half, scale=scale,...  27.7 us
    pallas_call x3, Pallas kernels, place_call(): pl.pallas_call(functools.partial(kernel, chunk=chunk, n_seq=n_seq), in_sp...  21.5 us
    ppermute x3, waiting for transfers between devices, along(): lax.ppermute(value, 'ty', [(s, (s - 2 * hops) % ty_size) for s in range(t...  18.5 us
    reduce_scatter x1, waiting for transfers between devices, body(): lax.psum_scatter(y_part.reshape(n_tok, d_model), 'ty', scatter_dimension=...  18.2 us
  transfers between devices with their start and end apart: 58, of which 22 were waited for; matrix products, arithmetic and copies ran while one was open for 18% of the time, Pallas kernels for 21%

profile of v5, /device:TPU:98, one launch (start us, length us, event | category | flops | bytes accessed | tf_op | source)
XLA Modules:
  0.0 669.1 jit_solution(5436956114164537291)
XLA Ops:
  15.8 6.9 %collective-permute-done.2 = bf16[2,192,512]{2,1,0:T(8,128)(2,1)S(1)} collective-permute-done((bf16[2,192,512]{2,1,0:T(8,128)(2,1)S(1)}, bf16[2,192,512]{2,1,0:T(8,128)(2,1)S(1)}, u32[]{:S(2)}, u32[]{:S(2)}) %collective-permute-start.2) | collective-permute-done | bytes 393248 | tf_op jit(solution)/shard_map/ppermute | solution.py:384
  22.7 9.6 %collective-permute-done.1 = bf16[2,192,512]{2,1,0:T(8,128)(2,1)S(1)} collective-permute-done((bf16[2,192,512]{2,1,0:T(8,128)(2,1)S(1)}, bf16[2,192,512]{2,1,0:T(8,128)(2,1)S(1)}, u32[]{:S(2)}, u32[]{:S(2)}) %collective-permute-start.1) | collective-permute-done | bytes 393248 | tf_op jit(solution)/shard_map/ppermute | solution.py:384
  40.1 6.8 %collective-permute-done.19 = bf16[2,192,512]{2,1,0:T(8,128)(2,1)S(1)} collective-permute-done((bf16[2,192,512]{2,1,0:T(8,128)(2,1)S(1)}, bf16[2,192,512]{2,1,0:T(8,128)(2,1)S(1)}, u32[]{:S(2)}, u32[]{:S(2)}) %collective-permute-start.19) | collective-permute-done | bytes 393248 | tf_op jit(solution)/shard_map/ppermute | solution.py:384
  46.9 9.6 %collective-permute-done.18 = bf16[2,192,512]{2,1,0:T(8,128)(2,1)S(1)} collective-permute-done((bf16[2,192,512]{2,1,0:T(8,128)(2,1)S(1)}, bf16[2,192,512]{2,1,0:T(8,128)(2,1)S(1)}, u32[]{:S(2)}, u32[]{:S(2)}) %collective-permute-start.18) | collective-permute-done | bytes 393248 | tf_op jit(solution)/shard_map/ppermute | solution.py:384
  67.3 37.1 %collective-permute-done.8.refs_4_ = bf16[512,1792]{1,0:T(8,128)(2,1)S(1)} collective-permute-done((bf16[512,1792]{1,0:T(8,128)(2,1)S(1)}, bf16[512,1792]{1,0:T(8,128)(2,1)S(1)}, u32[]{:S(2)}, u32[]{:S(2)}) %collective-permute-start.8) | collective-permute-done | bytes 1835040 | tf_op jit(solution)/shard_map/ppermute | solution.py:384
  109.0 23.8 %collective-permute-done.5 = bf16[8,512]{1,0:T(8,128)(2,1)S(1)} collective-permute-done((bf16[8,512]{1,0:T(8,128)(2,1)S(1)}, bf16[8,512]{1,0:T(8,128)(2,1)S(1)}, u32[]{:S(2)}, u32[]{:S(2)}) %collective-permute-start.5) | collective-permute-done | bytes 8224 | tf_op jit(solution)/shard_map/ppermute | solution.py:384
  133.2 18.7 %collective-permute-done.4 = bf16[8,512]{1,0:T(8,128)(2,1)S(1)} collective-permute-done((bf16[8,512]{1,0:T(8,128)(2,1)S(1)}, bf16[8,512]{1,0:T(8,128)(2,1)S(1)}, u32[]{:S(2)}, u32[]{:S(2)}) %collective-permute-start.4) | collective-permute-done | bytes 8224 | tf_op jit(solution)/shard_map/ppermute | solution.py:384
  165.2 18.7 %shard_map.245 = (bf16[3072,2048]{1,0:T(8,128)(2,1)}, bf16[3072,2048]{1,0:T(8,128)(2,1)}) custom-call(bf16[3072,2048]{1,0:T(8,128)(2,1)} %bitcast.86, f32[8,2048]{1,0:T(8,128)} %maximum_convert_fusion.small_ref), custom_call_target="tpu_custom_call" | custom-call | flops 100663296 | bytes 37781504 | tf_op jit(solution)/shard_map/pallas_call | solution.py:363
  183.9 32.8 %shard_map.246 = (bf16[3072,768]{1,0:T(8,128)(2,1)}, bf16[3072,1024]{1,0:T(8,128)(2,1)}, bf16[3072,1024]{1,0:T(8,128)(2,1)}) custom-call(bf16[3072,2048]{1,0:T(8,128)(2,1)} %get-tuple-element.42.h_attn_ref, bf16[3072,2048]{1,0:T(8,128)(2,1)} %get-tuple-element.43.h_mlp_ref, f32[1536,128]{1,0:T(8,128)} %get-tuple-element.110.cos_ref, ...), custom_call_target="tpu_custom_call" | custom-call | flops 22548578304 | bytes 52170240 | tf_op jit(solution)/shard_map/pallas_call | solution.py:363
  216.8 27.0 %shard_map.250 = (bf16[3072,256]{1,0:T(8,128)(2,1)}, bf16[3072,1024]{1,0:T(8,128)(2,1)}, f32[8,1024]{1,0:T(8,128)}) custom-call(bf16[3072,2048]{1,0:T(8,128)(2,1)} %bitcast.121, bf16[3072,1024]{1,0:T(8,128)(2,1)} %get-tuple-element.50.pre_ref, bf16[1280,512]{1,0:T(8,128)(2,1)} %copy-done.28, bf16[1280,512]{1,0:T(8,128)(2,1)} %copy-done.25, ...), custom_call_target="tpu_custom_call" | custom-call | flops 16106127360 | bytes 31997952 | tf_op jit(solution)/shard_map/pallas_call | solution.py:363
  243.7 13.7 %ab.2 = (bf16[1,1536,768]{2,1,0:T(8,128)(2,1)}, f32[1,8,768]{2,1,0:T(8,128)}) custom-call(bf16[2,1536,768]{2,1,0:T(8,128)(2,1)} %bitcast.129, bf16[2,1536,256]{2,1,0:T(8,128)(2,1)} %bitcast.147, f32[1536,128]{1,0:T(8,128)} %get-tuple-element.110.cos_ref, f32[1536,128]{1,0:T(8,128)} %get-tuple-element.109.lo_ref, f32[1536,128]{1,0:T(8,128)} %get-tuple-element.108.hi_ref), custom_call_target="tpu_custom_call" | custom-call | flops 6039797760 | bytes 5505024 | tf_op jit(solution)/shard_map/ab/pallas_call | solution.py:130
  257.5 22.3 %shard_map.251 = (bf16[1536,2048]{1,0:T(8,128)(2,1)}, f32[4,8,2048]{2,1,0:T(8,128)}) custom-call(bf16[1536,768]{1,0:T(8,128)(2,1)} %bitcast.132, bf16[3072,1024]{1,0:T(8,128)(2,1)} %get-tuple-element.53.d_pre_ref, bf16[3072,2048]{1,0:T(8,128)(2,1)} %bitcast.87, f32[8,2048]{1,0:T(8,128)} %maximum_convert_fusion.small_ref, bf16[512,1792]{1,0:T(8,128)(2,1)} %copy-done.7, ...), custom_call_target="tpu_custom_call" | custom-call | flops 11274289152 | bytes 25591808 | tf_op jit(solution)/shard_map/pallas_call | solution.py:363
  279.9 15.6 %af.1 = bf16[2,1536,256]{2,1,0:T(8,128)(2,1)} custom-call(bf16[2,1536,768]{2,1,0:T(8,128)(2,1)} %bitcast.130), custom_call_target="tpu_custom_call" | custom-call | flops 4831838208 | bytes 6291456 | tf_op jit(solution)/shard_map/af/pallas_call | solution.py:118
  295.5 22.1 %shard_map.247 = bf16[8,2,192,2048]{3,2,1,0:T(8,128)(2,1)} custom-call(bf16[3072,256]{1,0:T(8,128)(2,1)} %bitcast.142, bf16[3072,1024]{1,0:T(8,128)(2,1)} %get-tuple-element.45.gelu_ref, bf16[1280,512]{1,0:T(8,128)(2,1)} %copy-done.28, bf16[1280,512]{1,0:T(8,128)(2,1)} %copy-done.25, bf16[1280,256]{1,0:T(8,128)(2,1)} %collective-permute-done.11.refs_2_, ...), custom_call_target="tpu_custom_call" | custom-call | flops 16106127360 | bytes 25690112 | tf_op jit(solution)/shard_map/pallas_call | solution.py:363
  317.7 13.9 %ab.3 = (bf16[1,1536,768]{2,1,0:T(8,128)(2,1)}, f32[1,8,768]{2,1,0:T(8,128)}) custom-call(bf16[2,1536,768]{2,1,0:T(8,128)(2,1)} %bitcast.131, bf16[2,1536,256]{2,1,0:T(8,128)(2,1)} %bitcast.148, f32[1536,128]{1,0:T(8,128)} %get-tuple-element.110.cos_ref, f32[1536,128]{1,0:T(8,128)} %get-tuple-element.109.lo_ref, f32[1536,128]{1,0:T(8,128)} %get-tuple-element.108.hi_ref), custom_call_target="tpu_custom_call" | custom-call | flops 6039797760 | bytes 5505024 | tf_op jit(solution)/shard_map/ab/pallas_call | solution.py:130
  331.6 21.8 %shard_map.253 = (bf16[1536,2048]{1,0:T(8,128)(2,1)}, f32[4,8,2048]{2,1,0:T(8,128)}) custom-call(bf16[1536,768]{1,0:T(8,128)(2,1)} %bitcast.137, bf16[3072,1024]{1,0:T(8,128)(2,1)} %get-tuple-element.53.d_pre_ref, bf16[3072,2048]{1,0:T(8,128)(2,1)} %bitcast.88, f32[8,2048]{1,0:T(8,128)} %maximum_convert_fusion.small_ref, bf16[512,1792]{1,0:T(8,128)(2,1)} %copy-done.7, ...), custom_call_target="tpu_custom_call" | custom-call | flops 11274289152 | bytes 25591808 | tf_op jit(solution)/shard_map/pallas_call | solution.py:363
  360.5 6.9 %collective-permute-done.20 = bf16[192,512]{1,0:T(8,128)(2,1)S(1)} collective-permute-done((bf16[192,512]{1,0:T(8,128)(2,1)S(1)}, bf16[192,512]{1,0:T(8,128)(2,1)S(1)}, u32[]{:S(2)}, u32[]{:S(2)}) %collective-permute-start.20) | collective-permute-done | bytes 196640 | tf_op jit(solution)/shard_map/ppermute | solution.py:384
  370.2 18.2 %reduce-scatter.4.cloned.1.call-done.mixed_ref = bf16[384,2048]{1,0:T(8,128)(2,1)} async-done(((bf16[3072,2048]{1,0:T(8,128)(2,1)}), bf16[384,2048]{1,0:T(8,128)(2,1)}) %reduce-scatter.4.cloned.1.call-update) | async-done | bytes 1572880 | tf_op jit(solution)/shard_map/reduce_scatter | solution.py:475
  403.1 9.8 %collective-permute-done.15 = bf16[384,512]{1,0:T(8,128)(2,1)S(1)} collective-permute-done((bf16[384,512]{1,0:T(8,128)(2,1)S(1)}, bf16[384,512]{1,0:T(8,128)(2,1)S(1)}, u32[]{:S(2)}, u32[]{:S(2)}) %collective-permute-start.15) | collective-permute-done | bytes 393248 | tf_op jit(solution)/shard_map/ppermute | solution.py:384
  414.4 7.2 %convert_reduce_fusion = f32[512]{0:T(512)} fusion(bf16[8,1536,512]{2,1,0:T(8,128)(2,1)} %param.15), kind=kLoop, calls=%fused_computation | loop fusion | flops 12582400 | bytes 12584960 | tf_op jit(solution)/shard_map/reduce_sum | solution.py:512
  440.1 7.1 %fusion.10 = f32[512,1024]{1,0:T(8,128)} fusion(bf16[3072,1024]{1,0:T(8,128)(2,1)S(1)} %bitcast.152, bf16[3072,2048]{1,0:T(8,128)(2,1)} %get-tuple-element.43.h_mlp_ref), kind=kOutput, calls=%fused_computation.15 | convolution fusion | flops 3221225472 | bytes 11534336 | tf_op jit(solution)/shard_map/dot_general | solution.py:27
  447.3 7.2 %fusion.20 = bf16[1280,512]{1,0:T(8,128)(2,1)S(1)} fusion(bf16[3072,2048]{1,0:T(8,128)(2,1)S(1)} %bitcast.126, bf16[3072,1024]{1,0:T(8,128)(2,1)} %get-tuple-element.45.gelu_ref, bf16[3072,256]{1,0:T(8,128)(2,1)S(1)} %bitcast.143), kind=kOutput, calls=%fused_computation.25 | convolution fusion | flops 4042915840 | bytes 12320768 | tf_op jit(solution)/shard_map/dot_general | solution.py:27
  466.1 15.8 %collective-permute-done.39 = bf16[256,768]{1,0:T(8,128)(2,1)S(1)} collective-permute-done((bf16[256,768]{1,0:T(8,128)(2,1)S(1)}, bf16[256,768]{1,0:T(8,128)(2,1)S(1)}, u32[]{:S(2)}, u32[]{:S(2)}) %collective-permute-start.39) | collective-permute-done | bytes 393248 | tf_op jit(solution)/shard_map/ppermute | solution.py:384
  499.9 8.3 %add_convert_fusion.1 = bf16[512,1024]{1,0:T(8,128)(2,1)} fusion(bf16[3072,1024]{1,0:T(8,128)(2,1)} %get-tuple-element.53.d_pre_ref, bf16[3072,2048]{1,0:T(8,128)(2,1)} %get-tuple-element.43.h_mlp_ref, bf16[256,1024]{1,0:T(8,128)(2,1)S(1)} %collective-permute-done.47), kind=kOutput, calls=%fused_computation.35 | convolution fusion | flops 3222798336 | bytes 11010048 | tf_op jit(solution)/shard_map/dot_general | solution.py:27
  508.2 8.3 %add_convert_fusion = bf16[512,1024]{1,0:T(8,128)(2,1)} fusion(bf16[3072,1024]{1,0:T(8,128)(2,1)} %get-tuple-element.53.d_pre_ref, bf16[3072,2048]{1,0:T(8,128)(2,1)} %get-tuple-element.43.h_mlp_ref, bf16[256,1024]{1,0:T(8,128)(2,1)S(1)} %collective-permute-done.49), kind=kOutput, calls=%fused_computation.34 | convolution fusion | flops 3222798336 | bytes 11010048 | tf_op jit(solution)/shard_map/dot_general | solution.py:27
  520.0 8.3 %fusion.23 = bf16[1280,512]{1,0:T(8,128)(2,1)} fusion(bf16[3072,2048]{1,0:T(8,128)(2,1)S(1)} %bitcast.127, bf16[3072,1024]{1,0:T(8,128)(2,1)} %get-tuple-element.45.gelu_ref, bf16[3072,256]{1,0:T(8,128)(2,1)S(1)} %bitcast.144, bf16[640,512]{1,0:T(8,128)(2,1)S(1)} %collective-permute-done.43), kind=kOutput, calls=%fused_computation.26 | convolution fusion | flops 4044226560 | bytes 12976128 | tf_op jit(solution)/shard_map/dot_general | solution.py:27
  528.2 8.2 %fusion.26 = bf16[1280,512]{1,0:T(8,128)(2,1)} fusion(bf16[3072,2048]{1,0:T(8,128)(2,1)S(1)} %bitcast.128, bf16[3072,1024]{1,0:T(8,128)(2,1)} %get-tuple-element.45.gelu_ref, bf16[3072,256]{1,0:T(8,128)(2,1)S(1)} %bitcast.145, bf16[640,512]{1,0:T(8,128)(2,1)S(1)} %collective-permute-done.45), kind=kOutput, calls=%fused_computation.27 | convolution fusion | flops 4044226560 | bytes 12976128 | tf_op jit(solution)/shard_map/dot_general | solution.py:27
  550.7 33.1 %collective-permute-done.23 = bf16[192,512]{1,0:T(8,128)(2,1)S(1)} collective-permute-done((bf16[192,512]{1,0:T(8,128)(2,1)}, bf16[192,512]{1,0:T(8,128)(2,1)S(1)}, u32[]{:S(2)}, u32[]{:S(2)}) %collective-permute-start.23) | collective-permute-done | bytes 196640 | tf_op jit(solution)/shard_map/ppermute | solution.py:384
  612.7 7.5 %collective-permute-done.28.refs_3_ = bf16[4,192,512]{2,1,0:T(8,128)(2,1)S(1)} collective-permute-done((bf16[4,192,512]{2,1,0:T(8,128)(2,1)S(1)}, bf16[4,192,512]{2,1,0:T(8,128)(2,1)S(1)}, u32[]{:S(2)}, u32[]{:S(2)}) %collective-permute-start.28) | collective-permute-done | bytes 786464 | tf_op jit(solution)/shard_map/ppermute | solution.py:394
  622.4 8.8 %collective-permute-done.26.refs_1_ = bf16[4,192,512]{2,1,0:T(8,128)(2,1)S(1)} collective-permute-done((bf16[4,192,512]{2,1,0:T(8,128)(2,1)S(1)}, bf16[4,192,512]{2,1,0:T(8,128)(2,1)S(1)}, u32[]{:S(2)}, u32[]{:S(2)}) %collective-permute-start.26) | collective-permute-done | bytes 786464 | tf_op jit(solution)/shard_map/ppermute | solution.py:394
  631.2 7.1 %convert_add_fusion = f32[1024,512]{1,0:T(8,128)} fusion(bf16[1280,512]{1,0:T(8,128)(2,1)} %collective-permute-done.46, bf16[1280,512]{1,0:T(8,128)(2,1)} %collective-permute-done.44, bf16[3072,1024]{1,0:T(8,128)(2,1)S(1)} %bitcast.150, bf16[3072,2048]{1,0:T(8,128)(2,1)} %bitcast.123), kind=kOutput, calls=%fused_computation.32 | convolution fusion | flops 3223322624 | bytes 13631488 | tf_op jit(solution)/shard_map/dot_general | solution.py:27
  651.8 9.6 %shard_map.249 = bf16[4,3072,512]{2,1,0:T(8,128)(2,1)} custom-call(s32[3]{0:T(128)} %pad_add_fusion.place_ref, bf16[4,3072,512]{2,1,0:T(8,128)(2,1)} %bitcast.90), custom_call_target="tpu_custom_call" | custom-call | flops 6291456 | bytes 25165824 | tf_op jit(solution)/shard_map/pallas_call | solution.py:189
  (287 shorter events, 181.9 us)
Async XLA Ops:
  7.2 158.0 %all-gather.5.cloned.1.call-start = ((), (), s32[]{:S(2)}) async-start(), calls=%async_computation.3 | async-start | bytes 14155776 | tf_op jit(solution)/shard_map/all_gather | solution.py:454
  33.8 183.0 %all-gather.9.cloned.1.call-start = ((), (), s32[]{:S(2)}) async-start(), calls=%async_computation.6 | async-start | bytes 14155776 | tf_op jit(solution)/shard_map/all_gather | solution.py:455
  58.8 296.3 %reduce-scatter.6.cloned.1.call-start = ((), (), s32[]{:S(2)}) async-start(), calls=%async_computation.7 | async-start | bytes 7077888 | tf_op jit(solution)/shard_map/reduce_scatter | solution.py:493
  60.3 44.2 %collective-permute-start.8 = (bf16[512,1792]{1,0:T(8,128)(2,1)S(1)}, bf16[512,1792]{1,0:T(8,128)(2,1)S(1)}, u32[]{:S(2)}, u32[]{:S(2)}) collective-permute-start(bf16[512,1792]{1,0:T(8,128)(2,1)S(1)} %pad_maximum_fusion.5.refs_0_), channel_id=1, source_target_pairs={{0,8},{8,16},{16,24},{24,0},{1,9},{9,17},{17,25},{25,1},{2,10},{10... | collective-permute-start | bytes 5505032 | tf_op jit(solution)/shard_map/ppermute | solution.py:384
  61.4 43.3 %collective-permute-start.6 = (bf16[512,1792]{1,0:T(8,128)(2,1)S(1)}, bf16[512,1792]{1,0:T(8,128)(2,1)S(1)}, u32[]{:S(2)}, u32[]{:S(2)}) collective-permute-start(bf16[512,1792]{1,0:T(8,128)(2,1)S(1)} %pad_maximum_fusion.5.refs_0_), channel_id=1, source_target_pairs={{0,24},{8,0},{16,8},{24,16},{1,25},{9,1},{17,9},{25,17},{2,26},{10... | collective-permute-start | bytes 5505032 | tf_op jit(solution)/shard_map/ppermute | solution.py:384
  63.8 95.8 %collective-permute-start.12 = (bf16[1280,512]{1,0:T(8,128)(2,1)S(1)}, bf16[1280,512]{1,0:T(8,128)(2,1)S(1)}, u32[]{:S(2)}, u32[]{:S(2)}) collective-permute-start(bf16[1280,512]{1,0:T(8,128)(2,1)S(1)} %constant_dynamic-update-slice_fusion.refs_0_), channel_id=1, source_target_pairs={{0,8},{8,16},{16,24},{24,0},{1,9},{9,17},{17,25},{25,1},{2,10},{10... | collective-permute-start | bytes 3932168 | tf_op jit(solution)/shard_map/ppermute | solution.py:384
  63.9 96.7 %collective-permute-start.10 = (bf16[1280,512]{1,0:T(8,128)(2,1)S(1)}, bf16[1280,512]{1,0:T(8,128)(2,1)S(1)}, u32[]{:S(2)}, u32[]{:S(2)}) collective-permute-start(bf16[1280,512]{1,0:T(8,128)(2,1)S(1)} %constant_dynamic-update-slice_fusion.refs_0_), channel_id=1, source_target_pairs={{0,24},{8,0},{16,8},{24,16},{1,25},{9,1},{17,9},{25,17},{2,26},{10... | collective-permute-start | bytes 3932168 | tf_op jit(solution)/shard_map/ppermute | solution.py:384
  67.3 65.5 %collective-permute-start.5 = (bf16[8,512]{1,0:T(8,128)(2,1)S(1)}, bf16[8,512]{1,0:T(8,128)(2,1)S(1)}, u32[]{:S(2)}, u32[]{:S(2)}) collective-permute-start(bf16[8,512]{1,0:T(8,128)(2,1)S(1)} %select_select_fusion), channel_id=1, source_target_pairs={{0,8},{8,16},{16,24},{24,0},{1,9},{9,17},{17,25},{25,1},{2,10},{10... | collective-permute-start | bytes 24584 | tf_op jit(solution)/shard_map/ppermute | solution.py:384
  104.5 79.4 %collective-permute-start.9 = (bf16[256,1792]{1,0:T(8,128)(2,1)S(1)}, bf16[256,1792]{1,0:T(8,128)(2,1)}, u32[]{:S(2)}, u32[]{:S(2)}) collective-permute-start(bf16[256,1792]{1,0:T(8,128)(2,1)S(1)} %slice.162), channel_id=1, source_target_pairs={{0,8},{8,16},{16,24},{24,0},{1,9},{9,17},{17,25},{25,1},{2,10},{10... | collective-permute-start | bytes 2752520 | tf_op jit(solution)/shard_map/ppermute | solution.py:384
  105.9 78.0 %collective-permute-start.7 = (bf16[256,1792]{1,0:T(8,128)(2,1)}, bf16[256,1792]{1,0:T(8,128)(2,1)}, u32[]{:S(2)}, u32[]{:S(2)}) collective-permute-start(bf16[256,1792]{1,0:T(8,128)(2,1)} %slice.161), channel_id=1, source_target_pairs={{0,24},{8,0},{16,8},{24,16},{1,25},{9,1},{17,9},{25,17},{2,26},{10... | collective-permute-start | bytes 2752520 | tf_op jit(solution)/shard_map/ppermute | solution.py:384
  159.6 57.1 %collective-permute-start.13 = (bf16[1280,256]{1,0:T(8,128)(2,1)S(1)}, bf16[1280,256]{1,0:T(8,128)(2,1)}, u32[]{:S(2)}, u32[]{:S(2)}) collective-permute-start(bf16[1280,256]{1,0:T(8,128)(2,1)S(1)} %slice.164), channel_id=1, source_target_pairs={{0,8},{8,16},{16,24},{24,0},{1,9},{9,17},{17,25},{25,1},{2,10},{10... | collective-permute-start | bytes 1966088 | tf_op jit(solution)/shard_map/ppermute | solution.py:384
  162.6 54.1 %collective-permute-start.11 = (bf16[1280,256]{1,0:T(8,128)(2,1)}, bf16[1280,256]{1,0:T(8,128)(2,1)}, u32[]{:S(2)}, u32[]{:S(2)}) collective-permute-start(bf16[1280,256]{1,0:T(8,128)(2,1)} %slice.163), channel_id=1, source_target_pairs={{0,24},{8,0},{16,8},{24,16},{1,25},{9,1},{17,9},{25,17},{2,26},{10... | collective-permute-start | bytes 1966088 | tf_op jit(solution)/shard_map/ppermute | solution.py:384
  279.8 108.5 %reduce-scatter.4.cloned.1.call-start = ((), (), s32[]{:S(2)}) async-start(), calls=%async_computation.4 | async-start | bytes 14155776 | tf_op jit(solution)/shard_map/reduce_scatter | solution.py:475
  317.6 218.8 %reduce-scatter.8.cloned.1.call-start = ((), (), s32[]{:S(2)}) async-start(), calls=%async_computation.9 | async-start | bytes 7077888 | tf_op jit(solution)/shard_map/reduce_scatter | solution.py:493
  353.5 292.4 %all-gather.11.cloned.1.call-start = ((), (), s32[]{:S(2)}) async-start(), calls=%async_computation.8 | async-start | bytes 7077888 | tf_op jit(solution)/shard_map/all_gather | solution.py:501
  369.2 282.6 %all-gather.7.cloned.1.call-start = ((), (), s32[]{:S(2)}) async-start(), calls=%async_computation.5 | async-start | bytes 14155776 | tf_op jit(solution)/shard_map/all_gather | solution.py:477
  423.6 34.3 %collective-permute-start.35 = (f32[4,960]{1,0:T(4,128)S(1)}, f32[4,960]{1,0:T(4,128)S(1)}, u32[]{:S(2)}, u32[]{:S(2)}) collective-permute-start(f32[4,960]{1,0:T(4,128)S(1)} %get-tuple-element.105), channel_id=1, source_target_pairs={{0,24},{8,0},{16,8},{24,16},{1,25},{9,1},{17,9},{25,17},{2,26},{10... | collective-permute-start | bytes 46088 | tf_op jit(solution)/shard_map/ppermute | solution.py:384
  426.2 31.7 %collective-permute-start.33 = (f32[4,960]{1,0:T(4,128)S(1)}, f32[4,960]{1,0:T(4,128)S(1)}, u32[]{:S(2)}, u32[]{:S(2)}) collective-permute-start(f32[4,960]{1,0:T(4,128)S(1)} %get-tuple-element.106), channel_id=1, source_target_pairs={{0,16},{8,24},{16,0},{24,8},{1,17},{9,25},{17,1},{25,9},{2,18},{10... | collective-permute-start | bytes 46088 | tf_op jit(solution)/shard_map/ppermute | solution.py:384
  427.7 30.2 %collective-permute-start.34 = (f32[4,960]{1,0:T(4,128)S(1)}, f32[4,960]{1,0:T(4,128)S(1)}, u32[]{:S(2)}, u32[]{:S(2)}) collective-permute-start(f32[4,960]{1,0:T(4,128)S(1)} %get-tuple-element.107), channel_id=1, source_target_pairs={{0,8},{8,16},{16,24},{24,0},{1,9},{9,17},{17,25},{25,1},{2,10},{10... | collective-permute-start | bytes 46088 | tf_op jit(solution)/shard_map/ppermute | solution.py:384
  454.6 62.0 %collective-permute-start.43 = (bf16[640,512]{1,0:T(8,128)(2,1)S(1)}, bf16[640,512]{1,0:T(8,128)(2,1)S(1)}, u32[]{:S(2)}, u32[]{:S(2)}) collective-permute-start(bf16[640,512]{1,0:T(8,128)(2,1)S(1)} %get-tuple-element.92), channel_id=1, source_target_pairs={{0,8},{8,16},{16,24},{24,0},{1,9},{9,17},{17,25},{25,1},{2,10},{10... | collective-permute-start | bytes 1966088 | tf_op jit(solution)/shard_map/ppermute | solution.py:384
  456.3 71.9 %collective-permute-start.45 = (bf16[640,512]{1,0:T(8,128)(2,1)S(1)}, bf16[640,512]{1,0:T(8,128)(2,1)S(1)}, u32[]{:S(2)}, u32[]{:S(2)}) collective-permute-start(bf16[640,512]{1,0:T(8,128)(2,1)S(1)} %get-tuple-element.93), channel_id=1, source_target_pairs={{0,24},{8,0},{16,8},{24,16},{1,25},{9,1},{17,9},{25,17},{2,26},{10... | collective-permute-start | bytes 1966088 | tf_op jit(solution)/shard_map/ppermute | solution.py:384
  460.4 37.4 %collective-permute-start.47 = (bf16[256,1024]{1,0:T(8,128)(2,1)S(1)}, bf16[256,1024]{1,0:T(8,128)(2,1)S(1)}, u32[]{:S(2)}, u32[]{:S(2)}) collective-permute-start(bf16[256,1024]{1,0:T(8,128)(2,1)S(1)} %get-tuple-element.94), channel_id=1, source_target_pairs={{0,8},{8,16},{16,24},{24,0},{1,9},{9,17},{17,25},{25,1},{2,10},{10... | collective-permute-start | bytes 1572872 | tf_op jit(solution)/shard_map/ppermute | solution.py:384
  463.2 45.1 %collective-permute-start.49 = (bf16[256,1024]{1,0:T(8,128)(2,1)S(1)}, bf16[256,1024]{1,0:T(8,128)(2,1)S(1)}, u32[]{:S(2)}, u32[]{:S(2)}) collective-permute-start(bf16[256,1024]{1,0:T(8,128)(2,1)S(1)} %get-tuple-element.95), channel_id=1, source_target_pairs={{0,24},{8,0},{16,8},{24,16},{1,25},{9,1},{17,9},{25,17},{2,26},{10... | collective-permute-start | bytes 1572872 | tf_op jit(solution)/shard_map/ppermute | solution.py:384
  491.9 48.0 %collective-permute-start.38 = (f32[4,512]{1,0:T(4,128)}, f32[4,512]{1,0:T(4,128)}, u32[]{:S(2)}, u32[]{:S(2)}) collective-permute-start(f32[4,512]{1,0:T(4,128)} %add.155), channel_id=1, source_target_pairs={{0,4},{1,5},{2,6},{3,7},{4,0},{5,1},{6,2},{7,3},{8,12},{9,13},{10,... | collective-permute-start | bytes 24584 | tf_op jit(solution)/shard_map/ppermute | solution.py:389
  497.7 45.5 %collective-permute-start.42 = (bf16[512,768]{1,0:T(8,128)(2,1)}, bf16[512,768]{1,0:T(8,128)(2,1)}, u32[]{:S(2)}, u32[]{:S(2)}) collective-permute-start(bf16[512,768]{1,0:T(8,128)(2,1)} %add_convert_fusion.2), channel_id=1, source_target_pairs={{0,24},{8,0},{16,8},{24,16},{1,25},{9,1},{17,9},{25,17},{2,26},{10... | collective-permute-start | bytes 2359304 | tf_op jit(solution)/shard_map/ppermute | solution.py:384
  508.2 35.0 %collective-permute-start.40 = (bf16[512,768]{1,0:T(8,128)(2,1)}, bf16[512,768]{1,0:T(8,128)(2,1)}, u32[]{:S(2)}, u32[]{:S(2)}) collective-permute-start(bf16[512,768]{1,0:T(8,128)(2,1)} %add_convert_fusion.3), channel_id=1, source_target_pairs={{0,8},{8,16},{16,24},{24,0},{1,9},{9,17},{17,25},{25,1},{2,10},{10... | collective-permute-start | bytes 2359304 | tf_op jit(solution)/shard_map/ppermute | solution.py:384
  516.6 83.9 %collective-permute-start.50 = (bf16[512,1024]{1,0:T(8,128)(2,1)}, bf16[512,1024]{1,0:T(8,128)(2,1)}, u32[]{:S(2)}, u32[]{:S(2)}) collective-permute-start(bf16[512,1024]{1,0:T(8,128)(2,1)} %add_convert_fusion), channel_id=1, source_target_pairs={{0,24},{8,0},{16,8},{24,16},{1,25},{9,1},{17,9},{25,17},{2,26},{10... | collective-permute-start | bytes 3145736 | tf_op jit(solution)/shard_map/ppermute | solution.py:384
  528.2 75.6 %collective-permute-start.48 = (bf16[512,1024]{1,0:T(8,128)(2,1)}, bf16[512,1024]{1,0:T(8,128)(2,1)}, u32[]{:S(2)}, u32[]{:S(2)}) collective-permute-start(bf16[512,1024]{1,0:T(8,128)(2,1)} %add_convert_fusion.1), channel_id=1, source_target_pairs={{0,8},{8,16},{16,24},{24,0},{1,9},{9,17},{17,25},{25,1},{2,10},{10... | collective-permute-start | bytes 3145736 | tf_op jit(solution)/shard_map/ppermute | solution.py:384
  539.9 68.8 %collective-permute-start.46 = (bf16[1280,512]{1,0:T(8,128)(2,1)}, bf16[1280,512]{1,0:T(8,128)(2,1)}, u32[]{:S(2)}, u32[]{:S(2)}) collective-permute-start(bf16[1280,512]{1,0:T(8,128)(2,1)} %fusion.26), channel_id=1, source_target_pairs={{0,24},{8,0},{16,8},{24,16},{1,25},{9,1},{17,9},{25,17},{2,26},{10... | collective-permute-start | bytes 3932168 | tf_op jit(solution)/shard_map/ppermute | solution.py:384
  543.2 65.5 %collective-permute-start.44 = (bf16[1280,512]{1,0:T(8,128)(2,1)}, bf16[1280,512]{1,0:T(8,128)(2,1)}, u32[]{:S(2)}, u32[]{:S(2)}) collective-permute-start(bf16[1280,512]{1,0:T(8,128)(2,1)} %fusion.23), channel_id=1, source_target_pairs={{0,8},{8,16},{16,24},{24,0},{1,9},{9,17},{17,25},{25,1},{2,10},{10... | collective-permute-start | bytes 3932168 | tf_op jit(solution)/shard_map/ppermute | solution.py:384
  543.2 40.5 %collective-permute-start.23 = (bf16[192,512]{1,0:T(8,128)(2,1)}, bf16[192,512]{1,0:T(8,128)(2,1)S(1)}, u32[]{:S(2)}, u32[]{:S(2)}) collective-permute-start(bf16[192,512]{1,0:T(8,128)(2,1)} %get-tuple-element.62), channel_id=1, source_target_pairs={{0,8},{8,16},{16,24},{24,0},{1,9},{9,17},{17,25},{25,1},{2,10},{10... | collective-permute-start | bytes 589832 | tf_op jit(solution)/shard_map/ppermute | solution.py:384
  603.8 27.4 %collective-permute-start.26 = (bf16[4,192,512]{2,1,0:T(8,128)(2,1)S(1)}, bf16[4,192,512]{2,1,0:T(8,128)(2,1)S(1)}, u32[]{:S(2)}, u32[]{:S(2)}) collective-permute-start(bf16[4,192,512]{2,1,0:T(8,128)(2,1)S(1)} %pad_maximum_fusion.12.refs_0_), channel_id=1, source_target_pairs={{0,6},{1,7},{2,0},{3,1},{4,2},{5,3},{6,4},{7,5},{8,14},{9,15},{10,... | collective-permute-start | bytes 2359304 | tf_op jit(solution)/shard_map/ppermute | solution.py:394
  (79 other events, 1252.6 us)
Sparse Core Ops, SparseCore 0:
  33.9 64.6 all-gather.4
  100.2 65.0 all-gather.8
  279.9 37.0 reduce-scatter.5
  319.2 69.1 reduce-scatter.3
  390.5 39.8 reduce-scatter.7
  431.9 39.1 all-gather.10
  472.7 65.4 all-gather.6

commit v6 on v5

--- a/solution.py
+++ b/solution.py
@@ -156,44 +156,47 @@
         copy.wait()
 
 
-def place_pieces_kernel(place_ref, *refs, chunk, n_seq):
+def place_pieces_kernel(place_ref, *refs, spans, n_seq):
     out_ref, held_ref, in_sems, out_sems = refs[-4:]
-    groups, own, _ = refs[0].shape
-    columns = held_ref.shape[0] // 2
     row, column, core = place_ref[0], place_ref[1], place_ref[2]
-    fetch, store = [], []
-    for index in range(2 * columns):
-        source = 2 * lax.rem(column + index % columns, columns) + (core if index < columns else 1 - core)
+    groups, columns = out_ref.shape[0] // n_seq, out_ref.shape[1] // refs[0].shape[1] // 2
+    own = refs[0].shape[1]
+    fetch, store, low = [], [], 0
+    for index, (distance, other, first) in enumerate(spans):
+        count = refs[index].shape[0]
+        source = 2 * lax.rem(column + distance, columns) + (1 - core if other else core)
         at = pl.ds(pl.multiple_of(source * own, own), own)
-        fetch.append(pltpu.make_async_copy(refs[index], held_ref.at[index], in_sems.at[index]))
-        for t in range(groups):
-            piece = held_ref.at[index, lax.rem(row + groups - t, groups)]
-            store.append(pltpu.make_async_copy(piece, out_ref.at[t * n_seq + chunk, at], out_sems.at[index]))
+        fetch.append(pltpu.make_async_copy(refs[index], held_ref.at[pl.ds(low, count)], in_sems.at[index]))
+        stores = []
+        for place in range(count // n_seq):
+            to = lax.rem(row + groups - first - place, groups) * n_seq
+            stores.append(pltpu.make_async_copy(held_ref.at[pl.ds(low + place * n_seq, n_seq)], out_ref.at[pl.ds(to, n_seq), at], out_sems.at[index]))
+        store.append(stores)
+        low += count
     for copy in fetch:
         copy.start()
-    for index in range(2 * columns):
+    for index, stores in enumerate(store):
         fetch[index].wait()
-        for copy in store[index * groups:(index + 1) * groups]:
+        for copy in stores:
             copy.start()
-    for copy in store:
-        copy.wait()
-
-
-def place_call(kernel, place, operands, out, chunk, n_seq, tokens):
-    groups, _, width = operands[0].shape
+    for stores in store:
+        for copy in stores:
+            copy.wait()
+
+
+def place_call(kernel, place, operands, out, shape, held, n_sems):
     operands = [place, *operands] + ([] if out is None else [out])
     any_spec = pl.BlockSpec(memory_space=pl.ANY)
-    pieces = len(operands) - 1 - (out is not None)
-    held = operands[1].shape if pieces == 1 else (pieces,) + operands[1].shape
-    sems = pltpu.SemaphoreType.DMA((groups if pieces == 1 else pieces,))
+    size = held[0] * held[1] * held[2]
+    sems = pltpu.SemaphoreType.DMA((n_sems,))
     return pl.pallas_call(
-        functools.partial(kernel, chunk=chunk, n_seq=n_seq),
+        kernel,
         in_specs=[pl.BlockSpec(memory_space=pltpu.SMEM)] + [any_spec] * (len(operands) - 1),
         out_specs=any_spec,
-        out_shape=jax.ShapeDtypeStruct((groups * n_seq, tokens, width), jnp.bfloat16),
+        out_shape=jax.ShapeDtypeStruct(shape, jnp.bfloat16),
         scratch_shapes=[pltpu.VMEM(held, jnp.bfloat16), sems, sems],
         input_output_aliases={} if out is None else {len(operands) - 1: 0},
-        cost_estimate=pl.CostEstimate(flops=groups * tokens * width, bytes_accessed=4 * groups * tokens * width, transcendentals=0),
+        cost_estimate=pl.CostEstimate(flops=size, bytes_accessed=4 * size, transcendentals=0),
     )(*operands)
 
 
@@ -335,24 +338,27 @@
             sums_ref[3, :, at] += sublane_sum(d_mlp)
 
 
-def tile_call(kernel, tiled, whole, outs, row_range, flops, rows=512):
+def tile_call(kernel, tiled, whole, outs, row_range, flops, rows=512, total=None, into=()):
     start, count = row_range
     rows = next(r for r in (rows, 256, 128, 64, count) if count % r == 0 and all(op.shape[0] % r == 0 for op in tiled))
     first = start // rows
 
     def tile_spec(op):
         blocks = op.shape[0] // rows
-        if blocks * rows < count:
+        if blocks * rows < count or (total and op.shape[0] < total):
             return pl.BlockSpec((rows, op.shape[1]), lambda s: (lax.rem(s, blocks), 0))
         return pl.BlockSpec((rows, op.shape[1]), lambda s, f=(first if op.shape[0] != count else 0): (s + f, 0))
 
     in_specs = [tile_spec(op) for op in tiled]
     in_specs += [pl.BlockSpec(op.shape, lambda s, n=op.ndim: (0,) * n, pipeline_mode=pl.Buffered(1)) for op in whole]
+    in_specs += [pl.BlockSpec(memory_space=pl.ANY)] * len(into)
+    before = len(tiled) + len(whole)
+    body = kernel if not into else lambda *refs: kernel(*refs[:before], *refs[before + len(into):])
     out_specs, out_shapes = [], []
     for form, dtype in outs:
         if isinstance(form, int):
-            out_specs.append(pl.BlockSpec((rows, form), lambda s: (s, 0)))
-            out_shapes.append(jax.ShapeDtypeStruct((count, form), dtype))
+            out_specs.append(pl.BlockSpec((rows, form), lambda s: (s + (first if total else 0), 0)))
+            out_shapes.append(jax.ShapeDtypeStruct((total or count, form), dtype))
         elif isinstance(form[0], tuple):
             out_specs.append(pl.BlockSpec(form[1], form[2]))
             out_shapes.append(jax.ShapeDtypeStruct(form[0], dtype))
@@ -361,14 +367,15 @@
             out_shapes.append(jax.ShapeDtypeStruct(form, dtype))
     moved = sum(2 * op.shape[1] * count for op in tiled) + sum(2 * op.size for op in whole) + sum(2 * shape.size for shape in out_shapes)
     return pl.pallas_call(
-        kernel,
+        body,
         grid=(count // rows,),
         in_specs=in_specs,
         out_specs=out_specs,
         out_shape=out_shapes,
+        input_output_aliases={before + k: k for k in range(min(len(into), len(outs)))},
         compiler_params=pltpu.CompilerParams(dimension_semantics=("arbitrary",), vmem_limit_bytes=60 * MIB),
         cost_estimate=pl.CostEstimate(flops=flops, bytes_accessed=moved, transcendentals=0),
-    )(*tiled, *whole)
+    )(*tiled, *whole, *into)
 
 
 def solution(mesh):
@@ -396,16 +403,17 @@
     def partner(value):
         return lax.ppermute(value, 'ty', [(s, s ^ 1) for s in range(ty_size)])
 
-    def ring_gather(block, axis):
+    def ring_gather(block, axis, move, size):
+        far = size // 2
         blocks = {0: [block]}
-        for hops in range(1, antipode):
-            blocks[hops] = [shift(blocks[hops - 1][0], 1)]
-            blocks[tx_size - hops] = [shift(blocks[(tx_size - hops + 1) % tx_size][0], -1)]
+        for hops in range(1, far):
+            blocks[hops] = [move(blocks[hops - 1][0], 1)]
+            blocks[size - hops] = [move(blocks[(size - hops + 1) % size][0], -1)]
         half = block.shape[axis] // 2
-        low = lax.slice_in_dim(blocks[antipode - 1][0], 0, half, axis=axis)
-        high = lax.slice_in_dim(blocks[antipode + 1][0], half, 2 * half, axis=axis)
-        blocks[antipode] = [shift(low, 1), shift(high, -1)]
-        return [piece for r in range(tx_size) for piece in blocks[r]]
+        low = lax.slice_in_dim(blocks[far - 1][0], 0, half, axis=axis)
+        high = lax.slice_in_dim(blocks[far + 1][0], half, 2 * half, axis=axis)
+        blocks[far] = [move(low, 1), move(high, -1)]
+        return [blocks[r] for r in range(size)]
 
     def ring_scatter(make_part, rows):
         half = rows // 2
@@ -451,31 +459,48 @@
         bias_out = small[4] + small[5]
         x_own = to_tokens(x_act)
         cot_own = to_tokens(cot_out)
-        x_group = lax.all_gather(x_own, 'ty', axis=1, tiled=True)
+        x_seqs = []
+        for s in chunks:
+            x_seqs.append(lax.all_gather(x_own[s], 'ty', axis=0, tiled=True))
         cot_group = lax.all_gather(cot_own, 'ty', axis=1, tiled=True)
-        x_group, cot_group = x_group.reshape(n_seq * seq_len, -1), cot_group.reshape(n_seq * seq_len, -1)
+        cot_group = cot_group.reshape(n_seq * seq_len, -1)
         w_in = jnp.concatenate([w_qkv.reshape(d_local, qkv_width), w_up], axis=1)
-        w_in = ring_gather(w_in, 0)
+        w_in = sum(ring_gather(w_in, 0, shift, tx_size), [])
         w_back = jnp.concatenate([w_dense, w_down], axis=0)
-        w_back = ring_gather(w_back, 1)
+        w_back = sum(ring_gather(w_back, 1, shift, tx_size), [])
         in_size, back_size = sum(w.size for w in w_in), sum(w.size for w in w_back)
 
-        n_tok, d_model = x_group.shape
+        n_tok, d_model = cot_group.shape
         x_rows, cot_rows = x_own.reshape(-1, d_model), cot_own.reshape(-1, d_model)
         ff_width = w_up.shape[1]
-        h_attn, h_mlp = tile_call(norm_kernel, [x_group], [small], [(d_model, jnp.bfloat16), (d_model, jnp.bfloat16)], (0, n_tok), 16 * x_group.size)
-        qkv_act, pre_act, gelu_out = tile_call(
-            front_kernel, [h_attn, h_mlp, *tables], [b_qkv.reshape(1, -1).astype(jnp.float32), b_up.reshape(1, -1).astype(jnp.float32), *w_in],
-            [(qkv_width, jnp.bfloat16), (ff_width, jnp.bfloat16), (ff_width, jnp.bfloat16)], (0, n_tok), 2 * n_tok * in_size)
+        bias_rows = [b_qkv.reshape(1, -1).astype(jnp.float32), b_up.reshape(1, -1).astype(jnp.float32)]
+        normed, front = (), ()
+        for s in chunks:
+            at = (s * seq_len, seq_len)
+            normed = tile_call(
+                norm_kernel, [x_seqs[s]], [small], [(d_model, jnp.bfloat16), (d_model, jnp.bfloat16)],
+                at, 16 * x_seqs[s].size, total=n_tok, into=(*normed, *front[:1]))
+            front = tile_call(
+                front_kernel, [*normed, *tables], [*bias_rows, *w_in], [(qkv_width, jnp.bfloat16), (ff_width, jnp.bfloat16), (ff_width, jnp.bfloat16)],
+                at, 2 * seq_len * in_size, total=n_tok, into=front)
+        h_attn, h_mlp = normed
+        qkv_act, pre_act, gelu_out = front
         qkv_seq = qkv_act.reshape(n_seq, seq_len, qkv_width)
         context = attn_fwd(qkv_seq).reshape(n_tok, head)
         blocks_per_seq = ty_size // 2
         y_form = ((ty_size, n_seq, own, d_model), (2, 1, own, d_model), lambda s: (lax.rem(s, blocks_per_seq), s // blocks_per_seq, 0, 0))
         (y_part,) = tile_call(y_kernel, [context, gelu_out], w_back, [(y_form, jnp.bfloat16)], (0, n_tok), 2 * n_tok * back_size, 2 * own)
         mixed = lax.psum_scatter(y_part.reshape(n_tok, d_model), 'ty', scatter_dimension=0, tiled=True)
-        blocks = to_width(row_call(finish_y_kernel, tx_size, 0, n_seq * own, x_rows, mixed, bias_out.reshape(1, -1)))
-        full = lax.all_gather(blocks.reshape(tx_size * n_seq, own, d_local), 'ty', axis=1, tiled=True)
-        y_out = place_call(place_kernel, place, [full.reshape(tx_size, n_seq * seq_len, d_local)], None, 0, 1, n_seq * seq_len)
+        block = to_width(row_call(finish_y_kernel, tx_size, 0, n_seq * own, x_rows, mixed, bias_out.reshape(1, -1)))
+        block = block.reshape(tx_size * n_seq, own, d_local)
+        pieces, spans = [], []
+        for distance, found in enumerate(ring_gather(block, 0, along, ty_size // 2)):
+            for index, piece in enumerate(found):
+                pieces += [piece, partner(piece)]
+                spans += [(distance, other, index * (tx_size // 2)) for other in (0, 1)]
+        y_out = place_call(
+            functools.partial(place_pieces_kernel, spans=spans, n_seq=n_seq), place, pieces, None,
+            (batch, seq_len, d_local), (batch * ty_size, own, d_local), len(spans))
 
         d_ctx, d_pre, d_b_up = tile_call(
             d_pre_kernel, [cot_group, pre_act], w_back,
@@ -487,19 +512,16 @@
             d_qkv.append(d_qkv_seq.reshape(seq_len, qkv_width))
             d_b_qkv.append(d_b_seq.sum((0, 1)))
             a6_part, sums = tile_call(
-                d_h_kernel, [d_qkv[s], d_pre, x_group], [small, *w_in],
+                d_h_kernel, [d_qkv[s], d_pre, x_seqs[s]], [small, *w_in],
                 [(d_model, jnp.bfloat16), ((4, 8, d_model), jnp.float32)], (s * seq_len, seq_len), 2 * seq_len * in_size)
             d_ln.append(sums)
             value_a6 = lax.psum_scatter(a6_part, 'ty', scatter_dimension=0, tiled=True)
             parts = row_call(finish_dx_kernel, tx_size, s, own, x_rows, value_a6, cot_rows)
             block = to_width(parts)
-            if s < n_seq - 1:
-                blocks = [block] + [along(block, hops) for hops in range(1, ty_size // 2)]
-                blocks = blocks + [partner(piece) for piece in blocks]
-                dx_act = place_call(place_pieces_kernel, place, blocks, dx_act, s, n_seq, seq_len)
-            else:
-                full = lax.all_gather(block, 'ty', axis=1, tiled=True)
-                dx_act = place_call(place_kernel, place, [full], dx_act, s, n_seq, seq_len)
+            full = lax.all_gather(block, 'ty', axis=1, tiled=True)
+            dx_act = place_call(
+                functools.partial(place_kernel, chunk=s, n_seq=n_seq), place, [full], dx_act,
+                (batch, seq_len, d_local), full.shape, tx_size)
         d_qkv = jnp.concatenate(d_qkv, axis=0)
 
         d_ln = sum(d_ln).sum(1).reshape(4, tx_size, d_local)
@@ -520,7 +542,6 @@
         d_w_down = add_back(dot(gelu_out, cols(cot_group, 0), TN), head, inner.shape[1])
         d_w_up = add_up(dot(cols(h_mlp, 0), d_pre, TN), 0, d_local)
         d_w_qkv = add_qkv(dot(cols(h_attn, 0), d_qkv, TN), 0, d_local)
-        y_out = y_out.reshape(batch, seq_len, d_local)
         return (y_out, dx_act, d_ln[0], d_ln[1], d_ln[2], d_ln[3], d_w_qkv.reshape(w_qkv.shape), d_bias[:qkv_width].reshape(b_qkv.shape), d_w_dense, d_b_out, d_w_up, d_bias[qkv_width:], d_w_down, d_b_out)
 
     return jax.shard_map(body, mesh=mesh, in_specs=in_specs, out_specs=out_specs, check_vma=False)

time: 676 us -> 646 us (0.956)
  waiting for transfers between devices: 236 us -> 186 us
  Pallas kernels: 213 us -> 223 us
    ppermute x41, waiting for transfers between devices: 196 us -> 153 us  [shift(): lax.ppermute(value, 'tx', [(s, (s - hops) % tx_size) for s in range(tx_si...]
    reduce_scatter x1, waiting for transfers between devices: 18.2 us -> 0.01 us  [body(): lax.psum_scatter(y_part.reshape(n_tok, d_model), 'ty', scatter_dimension=...]
    ppermute x3 -> x4, waiting for transfers between devices: 18.5 us -> 29.5 us  [along(): lax.ppermute(value, 'ty', [(s, (s - 2 * hops) % ty_size) for s in range(t...]
    pallas_call x9 -> x11, Pallas kernels: 166 us -> 176 us  [the longest x8 154 us: tile_call(): pl.pallas_call(body, grid=(count // rows,), in_specs=in_specs, out_specs=...]
    unnamed x110 -> x162, local copies, waits for them, and re-layouts: 13 us -> 14.7 us
  transfers between devices with their start and end apart: 58 -> 61, of which waited for: 22 -> 23; matrix products, arithmetic and copies ran while one was open for 18% -> 21% of each run, Pallas kernels for 21% -> 24%
where the time goes in v6:
time: 646 us; the launch traced here: 637 us
  Pallas kernels  223 us (35%)
  waiting for transfers between devices  186 us (29%)
  matrix products  89.9 us (14%)
  starting transfers between devices  66.4 us (10%)
  other arithmetic  29.2 us (5%)
  local copies, waits for them, and re-layouts  26.8 us (4%)
  between operations  15.6 us (2%)
    pallas_call x8, Pallas kernels, tile_call(): pl.pallas_call(body, grid=(count // rows,), in_specs=in_specs, out_specs=...  154 us
    ppermute x41, waiting for transfers between devices, shift(): lax.ppermute(value, 'tx', [(s, (s - hops) % tx_size) for s in range(tx_si...  153 us
    dot_general x13, matrix products, dot(): return lax.dot_general(a, b, dims, preferred_element_type=jnp.float32)  89.9 us
    ppermute x41, starting transfers between devices, shift(): lax.ppermute(value, 'tx', [(s, (s - hops) % tx_size) for s in range(tx_si...  56 us
    ppermute x4, waiting for transfers between devices, along(): lax.ppermute(value, 'ty', [(s, (s - 2 * hops) % ty_size) for s in range(t...  29.5 us
    pallas_call x2, Pallas kernels, backward(): pl.pallas_call(functools.partial(attn_bwd_kernel, half=half, scale=scale,...  27.8 us
    pallas_call x3, Pallas kernels, place_call(): pl.pallas_call(kernel, in_specs=[pl.BlockSpec(memory_space=pltpu.SMEM)] +...  21.6 us
    pallas_call x1, Pallas kernels, forward(): pl.pallas_call(functools.partial(attn_fwd_kernel, scale=scale, span=span)...  15.9 us
  transfers between devices with their start and end apart: 61, of which 23 were waited for; matrix products, arithmetic and copies ran while one was open for 21% of the time, Pallas kernels for 24%

profile of v6, /device:TPU:98, one launch (start us, length us, event | category | flops | bytes accessed | tf_op | source)
XLA Modules:
  0.0 637.2 jit_solution(6930812158769588204)
XLA Ops:
  14.6 15.8 %collective-permute-done = bf16[2,192,512]{2,1,0:T(8,128)(2,1)S(1)} collective-permute-done((bf16[2,192,512]{2,1,0:T(8,128)(2,1)S(1)}, bf16[2,192,512]{2,1,0:T(8,128)(2,1)S(1)}, u32[]{:S(2)}, u32[]{:S(2)}) %collective-permute-start) | collective-permute-done | bytes 393248 | tf_op jit(solution)/shard_map/ppermute | solution.py:391
  40.0 10.0 %collective-permute-done.26 = bf16[2,192,512]{2,1,0:T(8,128)(2,1)S(1)} collective-permute-done((bf16[2,192,512]{2,1,0:T(8,128)(2,1)S(1)}, bf16[2,192,512]{2,1,0:T(8,128)(2,1)S(1)}, u32[]{:S(2)}, u32[]{:S(2)}) %collective-permute-start.26) | collective-permute-done | bytes 393248 | tf_op jit(solution)/shard_map/ppermute | solution.py:391
  52.4 6.4 collective-permute-done.28
  69.4 34.9 %collective-permute-done.6.refs_1_.refs_8_ = bf16[512,1792]{1,0:T(8,128)(2,1)S(1)} collective-permute-done((bf16[512,1792]{1,0:T(8,128)(2,1)S(1)}, bf16[512,1792]{1,0:T(8,128)(2,1)S(1)}, u32[]{:S(2)}, u32[]{:S(2)}) %collective-permute-start.6) | collective-permute-done | bytes 1835040 | tf_op jit(solution)/shard_map/ppermute | solution.py:391
  107.8 24.7 %collective-permute-done.3 = bf16[8,512]{1,0:T(8,128)(2,1)S(1)} collective-permute-done((bf16[8,512]{1,0:T(8,128)(2,1)S(1)}, bf16[8,512]{1,0:T(8,128)(2,1)S(1)}, u32[]{:S(2)}, u32[]{:S(2)}) %collective-permute-start.3) | collective-permute-done | bytes 8224 | tf_op jit(solution)/shard_map/ppermute | solution.py:391
  133.4 18.6 %collective-permute-done.4 = bf16[8,512]{1,0:T(8,128)(2,1)S(1)} collective-permute-done((bf16[8,512]{1,0:T(8,128)(2,1)S(1)}, bf16[8,512]{1,0:T(8,128)(2,1)S(1)}, u32[]{:S(2)}, u32[]{:S(2)}) %collective-permute-start.4) | collective-permute-done | bytes 8224 | tf_op jit(solution)/shard_map/ppermute | solution.py:391
  163.6 11.1 %shard_map.245 = (bf16[3072,2048]{1,0:T(8,128)(2,1)}, bf16[3072,2048]{1,0:T(8,128)(2,1)}) custom-call(bf16[1536,2048]{1,0:T(8,128)(2,1)} %bitcast.101, f32[8,2048]{1,0:T(8,128)} %maximum_convert_fusion.small_ref.refs_1_), custom_call_target="tpu_custom_call" | custom-call | flops 50331648 | bytes 31490048 | tf_op jit(solution)/shard_map/pallas_call | solution.py:369
  174.7 19.8 %shard_map.246 = (bf16[3072,768]{1,0:T(8,128)(2,1)}, bf16[3072,1024]{1,0:T(8,128)(2,1)}, bf16[3072,1024]{1,0:T(8,128)(2,1)}) custom-call(bf16[3072,2048]{1,0:T(8,128)(2,1)} %get-tuple-element.47.h_attn_ref.refs_2_, bf16[3072,2048]{1,0:T(8,128)(2,1)} %get-tuple-element.48.h_mlp_ref.refs_3_, f32[1536,128]{1,0:T(8,128)} %get-tuple-element.122.cos_ref.refs_2_, ...), custom_call_target="tpu_custom_call" | custom-call | flops 11274289152 | bytes 38407680 | tf_op jit(solution)/shard_map/pallas_call | solution.py:369
  194.6 11.0 %shard_map.247 = (bf16[3072,2048]{1,0:T(8,128)(2,1)}, bf16[3072,2048]{1,0:T(8,128)(2,1)}) custom-call(bf16[1536,2048]{1,0:T(8,128)(2,1)} %bitcast.103, f32[8,2048]{1,0:T(8,128)} %maximum_convert_fusion.small_ref.refs_1_, bf16[3072,2048]{1,0:T(8,128)(2,1)} %get-tuple-element.47.h_attn_ref.refs_2_, ...), custom_call_target="tpu_custom_call", output_to_operand_aliasing={{0}: (2, {}), {1}: (3, {})} | custom-call | flops 50331648 | bytes 31490048 | tf_op jit(solution)/shard_map/pallas_call | solution.py:369
  205.5 19.7 %shard_map.248 = (bf16[3072,768]{1,0:T(8,128)(2,1)}, bf16[3072,1024]{1,0:T(8,128)(2,1)}, bf16[3072,1024]{1,0:T(8,128)(2,1)}) custom-call(bf16[3072,2048]{1,0:T(8,128)(2,1)} %get-tuple-element.50.refs_0_, bf16[3072,2048]{1,0:T(8,128)(2,1)} %get-tuple-element.51.refs_1_, ...), custom_call_target="tpu_custom_call", output_to_operand_aliasing={{0}: (12, {}), {1}: (13, {}), {2}: (14, {})} | custom-call | flops 11274289152 | bytes 38407680 | tf_op jit(solution)/shard_map/pallas_call | solution.py:369
  226.1 26.9 %shard_map.252 = (bf16[3072,256]{1,0:T(8,128)(2,1)}, bf16[3072,1024]{1,0:T(8,128)(2,1)}, f32[8,1024]{1,0:T(8,128)}) custom-call(bf16[3072,2048]{1,0:T(8,128)(2,1)} %bitcast.136, bf16[3072,1024]{1,0:T(8,128)(2,1)} %get-tuple-element.60.pre_ref, bf16[1280,512]{1,0:T(8,128)(2,1)} %copy-done.42, bf16[1280,512]{1,0:T(8,128)(2,1)} %copy-done.37, ...), custom_call_target="tpu_custom_call" | custom-call | flops 16106127360 | bytes 31997952 | tf_op jit(solution)/shard_map/pallas_call | solution.py:369
  253.0 13.9 %ab.3 = (bf16[1,1536,768]{2,1,0:T(8,128)(2,1)}, f32[1,8,768]{2,1,0:T(8,128)}) custom-call(bf16[2,1536,768]{2,1,0:T(8,128)(2,1)} %bitcast.90, bf16[2,1536,256]{2,1,0:T(8,128)(2,1)} %bitcast.157, f32[1536,128]{1,0:T(8,128)} %get-tuple-element.122.cos_ref.refs_2_, f32[1536,128]{1,0:T(8,128)} %get-tuple-element.121.lo_ref.refs_3_, ...), custom_call_target="tpu_custom_call" | custom-call | flops 6039797760 | bytes 5505024 | tf_op jit(solution)/shard_map/ab/pallas_call | solution.py:130
  266.9 21.7 %shard_map.255 = (bf16[1536,2048]{1,0:T(8,128)(2,1)}, f32[4,8,2048]{2,1,0:T(8,128)}) custom-call(bf16[1536,768]{1,0:T(8,128)(2,1)} %bitcast.142, bf16[3072,1024]{1,0:T(8,128)(2,1)} %get-tuple-element.63.d_pre_ref, bf16[1536,2048]{1,0:T(8,128)(2,1)} %bitcast.102, f32[8,2048]{1,0:T(8,128)} %maximum_convert_fusion.small_ref.refs_1_, ...), custom_call_target="tpu_custom_call" | custom-call | flops 11274289152 | bytes 25591808 | tf_op jit(solution)/shard_map/pallas_call | solution.py:369
  288.8 13.9 %ab.2 = (bf16[1,1536,768]{2,1,0:T(8,128)(2,1)}, f32[1,8,768]{2,1,0:T(8,128)}) custom-call(bf16[2,1536,768]{2,1,0:T(8,128)(2,1)} %bitcast.91, bf16[2,1536,256]{2,1,0:T(8,128)(2,1)} %bitcast.158, f32[1536,128]{1,0:T(8,128)} %get-tuple-element.122.cos_ref.refs_2_, f32[1536,128]{1,0:T(8,128)} %get-tuple-element.121.lo_ref.refs_3_, ...), custom_call_target="tpu_custom_call" | custom-call | flops 6039797760 | bytes 5505024 | tf_op jit(solution)/shard_map/ab/pallas_call | solution.py:130
  302.7 21.9 %shard_map.253 = (bf16[1536,2048]{1,0:T(8,128)(2,1)}, f32[4,8,2048]{2,1,0:T(8,128)}) custom-call(bf16[1536,768]{1,0:T(8,128)(2,1)} %bitcast.147, bf16[3072,1024]{1,0:T(8,128)(2,1)} %get-tuple-element.63.d_pre_ref, bf16[1536,2048]{1,0:T(8,128)(2,1)} %bitcast.104, f32[8,2048]{1,0:T(8,128)} %maximum_convert_fusion.small_ref.refs_1_, ...), custom_call_target="tpu_custom_call" | custom-call | flops 11274289152 | bytes 25591808 | tf_op jit(solution)/shard_map/pallas_call | solution.py:369
  324.7 15.9 %af.1 = bf16[2,1536,256]{2,1,0:T(8,128)(2,1)} custom-call(bf16[2,1536,768]{2,1,0:T(8,128)(2,1)} %bitcast.92), custom_call_target="tpu_custom_call" | custom-call | flops 4831838208 | bytes 6291456 | tf_op jit(solution)/shard_map/af/pallas_call | solution.py:118
  340.6 22.2 %shard_map.249 = bf16[8,2,192,2048]{3,2,1,0:T(8,128)(2,1)} custom-call(bf16[3072,256]{1,0:T(8,128)(2,1)} %bitcast.152, bf16[3072,1024]{1,0:T(8,128)(2,1)} %get-tuple-element.55.gelu_ref, bf16[1280,512]{1,0:T(8,128)(2,1)} %copy-done.42, bf16[1280,512]{1,0:T(8,128)(2,1)} %copy-done.37, bf16[1280,256]{1,0:T(8,128)(2,1)} %collective-permute-done.11.refs_2_, ...), custom_call_target="tpu_custom_call" | custom-call | flops 16106127360 | bytes 25690112 | tf_op jit(solution)/shard_map/pallas_call | solution.py:369
  380.2 7.5 %convert_reduce_fusion = f32[512]{0:T(512)} fusion(bf16[8,1536,512]{2,1,0:T(8,128)(2,1)} %param.15), kind=kLoop, calls=%fused_computation | loop fusion | flops 12582400 | bytes 12584960 | tf_op jit(solution)/shard_map/reduce_sum | solution.py:534
  391.6 7.2 %fusion.44 = bf16[512,768]{1,0:T(8,128)(2,1)} fusion(bf16[3072,2048]{1,0:T(8,128)(2,1)} %get-tuple-element.50.refs_0_, bf16[1536,768]{1,0:T(8,128)(2,1)} %bitcast.148, bf16[1536,768]{1,0:T(8,128)(2,1)} %bitcast.143), kind=kOutput, calls=%fused_computation.46 | convolution fusion | flops 2425749504 | bytes 8650752 | tf_op jit(solution)/shard_map/dot_general | solution.py:27
  398.9 8.5 %fusion.37 = bf16[512,1024]{1,0:T(8,128)(2,1)} fusion(bf16[3072,1024]{1,0:T(8,128)(2,1)} %get-tuple-element.63.d_pre_ref, bf16[3072,2048]{1,0:T(8,128)(2,1)} %get-tuple-element.51.refs_1_), kind=kOutput, calls=%fused_computation.45 | convolution fusion | flops 3221749760 | bytes 10485760 | tf_op jit(solution)/shard_map/dot_general | solution.py:27
  407.4 6.8 %fusion.10 = f32[512,1024]{1,0:T(8,128)} fusion(bf16[3072,1024]{1,0:T(8,128)(2,1)S(1)} %bitcast.160, bf16[3072,2048]{1,0:T(8,128)(2,1)} %get-tuple-element.51.refs_1_), kind=kOutput, calls=%fused_computation.15 | convolution fusion | flops 3221225472 | bytes 11534336 | tf_op jit(solution)/shard_map/dot_general | solution.py:27
  414.2 7.6 %fusion.20 = bf16[1280,512]{1,0:T(8,128)(2,1)} fusion(bf16[3072,2048]{1,0:T(8,128)(2,1)} %bitcast.137, bf16[3072,1024]{1,0:T(8,128)(2,1)S(1)} %bitcast.96, bf16[3072,256]{1,0:T(8,128)(2,1)S(1)} %bitcast.153), kind=kOutput, calls=%fused_computation.25 | convolution fusion | flops 4042915840 | bytes 12320768 | tf_op jit(solution)/shard_map/dot_general | solution.py:27
  451.3 16.1 %collective-permute-done.41 = bf16[256,768]{1,0:T(8,128)(2,1)S(1)} collective-permute-done((bf16[256,768]{1,0:T(8,128)(2,1)S(1)}, bf16[256,768]{1,0:T(8,128)(2,1)S(1)}, u32[]{:S(2)}, u32[]{:S(2)}) %collective-permute-start.41) | collective-permute-done | bytes 393248 | tf_op jit(solution)/shard_map/ppermute | solution.py:391
  468.2 6.5 %add_convert_fusion.3 = bf16[512,768]{1,0:T(8,128)(2,1)} fusion(bf16[3072,2048]{1,0:T(8,128)(2,1)} %get-tuple-element.50.refs_0_, bf16[256,768]{1,0:T(8,128)(2,1)S(1)} %collective-permute-done.41, bf16[1536,768]{1,0:T(8,128)(2,1)} %bitcast.149, bf16[1536,768]{1,0:T(8,128)(2,1)S(1)} %bitcast.144), kind=kOutput, calls=%fused_computation.44 | convolution fusion | flops 2426535936 | bytes 9043968 | tf_op jit(solution)/shard_map/dot_general | solution.py:27
  481.4 6.4 %add_convert_fusion.1 = bf16[512,1024]{1,0:T(8,128)(2,1)} fusion(bf16[3072,1024]{1,0:T(8,128)(2,1)S(1)} %bitcast.162, bf16[3072,2048]{1,0:T(8,128)(2,1)} %get-tuple-element.51.refs_1_, bf16[256,1024]{1,0:T(8,128)(2,1)S(1)} %collective-permute-done.49), kind=kOutput, calls=%fused_computation.35 | convolution fusion | flops 3222798336 | bytes 11010048 | tf_op jit(solution)/shard_map/dot_general | solution.py:27
  494.3 10.1 %fusion.23 = bf16[1280,512]{1,0:T(8,128)(2,1)} fusion(bf16[3072,2048]{1,0:T(8,128)(2,1)} %bitcast.138, bf16[3072,1024]{1,0:T(8,128)(2,1)} %get-tuple-element.55.gelu_ref, bf16[3072,256]{1,0:T(8,128)(2,1)S(1)} %bitcast.154, bf16[640,512]{1,0:T(8,128)(2,1)} %collective-permute-done.45), kind=kOutput, calls=%fused_computation.26 | convolution fusion | flops 4044226560 | bytes 12976128 | tf_op jit(solution)/shard_map/dot_general | solution.py:27
  512.8 8.1 %fusion.26 = bf16[1280,512]{1,0:T(8,128)(2,1)} fusion(bf16[3072,2048]{1,0:T(8,128)(2,1)} %bitcast.139, bf16[3072,1024]{1,0:T(8,128)(2,1)S(1)} %bitcast.98, bf16[3072,256]{1,0:T(8,128)(2,1)S(1)} %bitcast.155, bf16[640,512]{1,0:T(8,128)(2,1)} %collective-permute-done.47), kind=kOutput, calls=%fused_computation.27 | convolution fusion | flops 4044226560 | bytes 12976128 | tf_op jit(solution)/shard_map/dot_general | solution.py:27
  527.5 6.5 %add_convert_fusion = bf16[512,1024]{1,0:T(8,128)(2,1)} fusion(bf16[3072,1024]{1,0:T(8,128)(2,1)S(1)} %bitcast.164, bf16[3072,2048]{1,0:T(8,128)(2,1)} %get-tuple-element.51.refs_1_, bf16[256,1024]{1,0:T(8,128)(2,1)} %collective-permute-done.51), kind=kOutput, calls=%fused_computation.34 | convolution fusion | flops 3222798336 | bytes 11010048 | tf_op jit(solution)/shard_map/dot_general | solution.py:27
  534.1 20.7 %collective-permute-done.18.refs_2_ = bf16[8,192,512]{2,1,0:T(8,128)(2,1)S(1)} collective-permute-done((bf16[8,192,512]{2,1,0:T(8,128)(2,1)S(1)}, bf16[8,192,512]{2,1,0:T(8,128)(2,1)S(1)}, u32[]{:S(2)}, u32[]{:S(2)}) %collective-permute-start.18) | collective-permute-done | bytes 1572896 | tf_op jit(solution)/shard_map/ppermute | solution.py:401
  597.8 7.1 %convert_add_fusion = f32[1024,512]{1,0:T(8,128)} fusion(bf16[1280,512]{1,0:T(8,128)(2,1)} %collective-permute-done.48, bf16[1280,512]{1,0:T(8,128)(2,1)} %collective-permute-done.46, bf16[3072,1024]{1,0:T(8,128)(2,1)S(1)} %bitcast.100, bf16[3072,2048]{1,0:T(8,128)(2,1)} %bitcast.141), kind=kOutput, calls=%fused_computation.32 | convolution fusion | flops 3223322624 | bytes 13631488 | tf_op jit(solution)/shard_map/dot_general | solution.py:27
  607.8 10.0 %shard_map.251 = bf16[8,1536,512]{2,1,0:T(8,128)(2,1)} custom-call(s32[3]{0:T(128)} %pad_add_fusion.place_ref, bf16[8,192,512]{2,1,0:T(8,128)(2,1)} %bitcast.108, bf16[8,192,512]{2,1,0:T(8,128)(2,1)} %copy-done.23, bf16[8,192,512]{2,1,0:T(8,128)(2,1)} %copy-done.9, bf16[8,192,512]{2,1,0:T(8,128)(2,1)} %copy-done.24, bf16[4,192,512]{2,1,0:T(8,128)(2,1)} %copy-done.29, ...), custom_call_target="tpu_custom_call" | custom-call | flops 6291456 | bytes 25165824 | tf_op jit(solution)/shard_map/pallas_call | solution.py:192
  623.6 5.8 shard_map.258
  (355 shorter events, 178.3 us)
Async XLA Ops:
  7.2 156.4 %all-gather.16.cloned.1.call-start = ((), (), s32[]{:S(2)}) async-start(), calls=%async_computation.10 | async-start | bytes 7077888 | tf_op jit(solution)/shard_map/all_gather | solution.py:464
  35.5 159.1 %all-gather.14.cloned.1.call-start = ((), (), s32[]{:S(2)}) async-start(), calls=%async_computation.9 | async-start | bytes 7077888 | tf_op jit(solution)/shard_map/all_gather | solution.py:464
  36.3 189.0 %all-gather.8.cloned.1.call-start = ((), (), s32[]{:S(2)}) async-start(), calls=%async_computation.4 | async-start | bytes 14155776 | tf_op jit(solution)/shard_map/all_gather | solution.py:465
  60.9 303.9 %reduce-scatter.8.cloned.1.call-start = ((), (), s32[]{:S(2)}) async-start(), calls=%async_computation.7 | async-start | bytes 7077888 | tf_op jit(solution)/shard_map/reduce_scatter | solution.py:518
  61.3 43.0 %collective-permute-start.6 = (bf16[512,1792]{1,0:T(8,128)(2,1)S(1)}, bf16[512,1792]{1,0:T(8,128)(2,1)S(1)}, u32[]{:S(2)}, u32[]{:S(2)}) collective-permute-start(bf16[512,1792]{1,0:T(8,128)(2,1)S(1)} %pad_maximum_fusion.5.refs_0_.refs_7_), channel_id=1, source_target_pairs={{0,24},{8,0},{16,8},{24,16},{1,25},{9,1},{17,9},{25,17},{2,26},{10... | collective-permute-start | bytes 5505032 | tf_op jit(solution)/shard_map/ppermute | solution.py:391
  62.4 44.3 %collective-permute-start.8 = (bf16[512,1792]{1,0:T(8,128)(2,1)S(1)}, bf16[512,1792]{1,0:T(8,128)(2,1)S(1)}, u32[]{:S(2)}, u32[]{:S(2)}) collective-permute-start(bf16[512,1792]{1,0:T(8,128)(2,1)S(1)} %pad_maximum_fusion.5.refs_0_.refs_7_), channel_id=1, source_target_pairs={{0,8},{8,16},{16,24},{24,0},{1,9},{9,17},{17,25},{25,1},{2,10},{10... | collective-permute-start | bytes 5505032 | tf_op jit(solution)/shard_map/ppermute | solution.py:391
  63.5 94.3 %collective-permute-start.10 = (bf16[1280,512]{1,0:T(8,128)(2,1)S(1)}, bf16[1280,512]{1,0:T(8,128)(2,1)S(1)}, u32[]{:S(2)}, u32[]{:S(2)}) collective-permute-start(bf16[1280,512]{1,0:T(8,128)(2,1)S(1)} %constant_dynamic-update-slice_fusion.refs_0_), channel_id=1, source_target_pairs={{0,24},{8,0},{16,8},{24,16},{1,25},{9,1},{17,9},{25,17},{2,26},{10... | collective-permute-start | bytes 3932168 | tf_op jit(solution)/shard_map/ppermute | solution.py:391
  65.9 96.1 %collective-permute-start.12 = (bf16[1280,512]{1,0:T(8,128)(2,1)S(1)}, bf16[1280,512]{1,0:T(8,128)(2,1)S(1)}, u32[]{:S(2)}, u32[]{:S(2)}) collective-permute-start(bf16[1280,512]{1,0:T(8,128)(2,1)S(1)} %constant_dynamic-update-slice_fusion.refs_0_), channel_id=1, source_target_pairs={{0,8},{8,16},{16,24},{24,0},{1,9},{9,17},{17,25},{25,1},{2,10},{10... | collective-permute-start | bytes 3932168 | tf_op jit(solution)/shard_map/ppermute | solution.py:391
  66.1 66.4 %collective-permute-start.3 = (bf16[8,512]{1,0:T(8,128)(2,1)S(1)}, bf16[8,512]{1,0:T(8,128)(2,1)S(1)}, u32[]{:S(2)}, u32[]{:S(2)}) collective-permute-start(bf16[8,512]{1,0:T(8,128)(2,1)S(1)} %select_select_fusion), channel_id=1, source_target_pairs={{0,24},{8,0},{16,8},{24,16},{1,25},{9,1},{17,9},{25,17},{2,26},{10... | collective-permute-start | bytes 24584 | tf_op jit(solution)/shard_map/ppermute | solution.py:391
  104.3 70.4 %collective-permute-start.7 = (bf16[256,1792]{1,0:T(8,128)(2,1)S(1)}, bf16[256,1792]{1,0:T(8,128)(2,1)}, u32[]{:S(2)}, u32[]{:S(2)}) collective-permute-start(bf16[256,1792]{1,0:T(8,128)(2,1)S(1)} %slice.179), channel_id=1, source_target_pairs={{0,24},{8,0},{16,8},{24,16},{1,25},{9,1},{17,9},{25,17},{2,26},{10... | collective-permute-start | bytes 2752520 | tf_op jit(solution)/shard_map/ppermute | solution.py:391
  107.7 67.0 %collective-permute-start.9 = (bf16[256,1792]{1,0:T(8,128)(2,1)}, bf16[256,1792]{1,0:T(8,128)(2,1)}, u32[]{:S(2)}, u32[]{:S(2)}) collective-permute-start(bf16[256,1792]{1,0:T(8,128)(2,1)} %slice.180), channel_id=1, source_target_pairs={{0,8},{8,16},{16,24},{24,0},{1,9},{9,17},{17,25},{25,1},{2,10},{10... | collective-permute-start | bytes 2752520 | tf_op jit(solution)/shard_map/ppermute | solution.py:391
  158.7 66.5 %collective-permute-start.11 = (bf16[1280,256]{1,0:T(8,128)(2,1)}, bf16[1280,256]{1,0:T(8,128)(2,1)}, u32[]{:S(2)}, u32[]{:S(2)}) collective-permute-start(bf16[1280,256]{1,0:T(8,128)(2,1)} %slice.181), channel_id=1, source_target_pairs={{0,24},{8,0},{16,8},{24,16},{1,25},{9,1},{17,9},{25,17},{2,26},{10... | collective-permute-start | bytes 1966088 | tf_op jit(solution)/shard_map/ppermute | solution.py:391
  163.0 62.2 %collective-permute-start.13 = (bf16[1280,256]{1,0:T(8,128)(2,1)S(1)}, bf16[1280,256]{1,0:T(8,128)(2,1)S(1)}, u32[]{:S(2)}, u32[]{:S(2)}) collective-permute-start(bf16[1280,256]{1,0:T(8,128)(2,1)S(1)} %slice.182), channel_id=1, source_target_pairs={{0,8},{8,16},{16,24},{24,0},{1,9},{9,17},{17,25},{25,1},{2,10},{10... | collective-permute-start | bytes 1966088 | tf_op jit(solution)/shard_map/ppermute | solution.py:391
  288.7 133.2 %reduce-scatter.6.cloned.1.call-start = ((), (), s32[]{:S(2)}) async-start(), calls=%async_computation.5 | async-start | bytes 7077888 | tf_op jit(solution)/shard_map/reduce_scatter | solution.py:518
  324.7 163.1 %reduce-scatter.4.cloned.1.call-start = ((), (), s32[]{:S(2)}) async-start(), calls=%async_computation.3 | async-start | bytes 14155776 | tf_op jit(solution)/shard_map/reduce_scatter | solution.py:493
  362.9 254.9 %all-gather.12.cloned.1.call-start = ((), (), s32[]{:S(2)}) async-start(), calls=%async_computation.8 | async-start | bytes 7077888 | tf_op jit(solution)/shard_map/all_gather | solution.py:521
  379.6 244.1 %all-gather.10.cloned.1.call-start = ((), (), s32[]{:S(2)}) async-start(), calls=%async_computation.6 | async-start | bytes 7077888 | tf_op jit(solution)/shard_map/all_gather | solution.py:521
  439.9 52.9 %collective-permute-start.45 = (bf16[640,512]{1,0:T(8,128)(2,1)}, bf16[640,512]{1,0:T(8,128)(2,1)}, u32[]{:S(2)}, u32[]{:S(2)}) collective-permute-start(bf16[640,512]{1,0:T(8,128)(2,1)} %get-tuple-element.104), channel_id=1, source_target_pairs={{0,8},{8,16},{16,24},{24,0},{1,9},{9,17},{17,25},{25,1},{2,10},{10... | collective-permute-start | bytes 1966088 | tf_op jit(solution)/shard_map/ppermute | solution.py:391
  441.1 71.5 %collective-permute-start.47 = (bf16[640,512]{1,0:T(8,128)(2,1)S(1)}, bf16[640,512]{1,0:T(8,128)(2,1)}, u32[]{:S(2)}, u32[]{:S(2)}) collective-permute-start(bf16[640,512]{1,0:T(8,128)(2,1)S(1)} %get-tuple-element.105), channel_id=1, source_target_pairs={{0,24},{8,0},{16,8},{24,16},{1,25},{9,1},{17,9},{25,17},{2,26},{10... | collective-permute-start | bytes 1966088 | tf_op jit(solution)/shard_map/ppermute | solution.py:391
  444.2 23.2 %collective-permute-start.41 = (bf16[256,768]{1,0:T(8,128)(2,1)S(1)}, bf16[256,768]{1,0:T(8,128)(2,1)S(1)}, u32[]{:S(2)}, u32[]{:S(2)}) collective-permute-start(bf16[256,768]{1,0:T(8,128)(2,1)S(1)} %get-tuple-element.108), channel_id=1, source_target_pairs={{0,8},{8,16},{16,24},{24,0},{1,9},{9,17},{17,25},{25,1},{2,10},{10... | collective-permute-start | bytes 1179656 | tf_op jit(solution)/shard_map/ppermute | solution.py:391
  447.0 34.4 %collective-permute-start.49 = (bf16[256,1024]{1,0:T(8,128)(2,1)S(1)}, bf16[256,1024]{1,0:T(8,128)(2,1)S(1)}, u32[]{:S(2)}, u32[]{:S(2)}) collective-permute-start(bf16[256,1024]{1,0:T(8,128)(2,1)S(1)} %get-tuple-element.106), channel_id=1, source_target_pairs={{0,8},{8,16},{16,24},{24,0},{1,9},{9,17},{17,25},{25,1},{2,10},{10... | collective-permute-start | bytes 1572872 | tf_op jit(solution)/shard_map/ppermute | solution.py:391
  449.0 72.0 %collective-permute-start.51 = (bf16[256,1024]{1,0:T(8,128)(2,1)}, bf16[256,1024]{1,0:T(8,128)(2,1)}, u32[]{:S(2)}, u32[]{:S(2)}) collective-permute-start(bf16[256,1024]{1,0:T(8,128)(2,1)} %get-tuple-element.107), channel_id=1, source_target_pairs={{0,24},{8,0},{16,8},{24,16},{1,25},{9,1},{17,9},{25,17},{2,26},{10... | collective-permute-start | bytes 1572872 | tf_op jit(solution)/shard_map/ppermute | solution.py:391
  509.2 24.8 %collective-permute-start.44 = (bf16[512,768]{1,0:T(8,128)(2,1)S(1)}, bf16[512,768]{1,0:T(8,128)(2,1)S(1)}, u32[]{:S(2)}, u32[]{:S(2)}) collective-permute-start(bf16[512,768]{1,0:T(8,128)(2,1)S(1)} %copy-done.57), channel_id=1, source_target_pairs={{0,24},{8,0},{16,8},{24,16},{1,25},{9,1},{17,9},{25,17},{2,26},{10... | collective-permute-start | bytes 2359304 | tf_op jit(solution)/shard_map/ppermute | solution.py:391
  512.6 42.2 %collective-permute-start.18 = (bf16[8,192,512]{2,1,0:T(8,128)(2,1)S(1)}, bf16[8,192,512]{2,1,0:T(8,128)(2,1)S(1)}, u32[]{:S(2)}, u32[]{:S(2)}) collective-permute-start(bf16[8,192,512]{2,1,0:T(8,128)(2,1)S(1)} %bitcast.105), channel_id=1, source_target_pairs={{0,6},{1,7},{2,0},{3,1},{4,2},{5,3},{6,4},{7,5},{8,14},{9,15},{10,... | collective-permute-start | bytes 4718600 | tf_op jit(solution)/shard_map/ppermute | solution.py:401
  520.9 60.0 %collective-permute-start.46 = (bf16[1280,512]{1,0:T(8,128)(2,1)}, bf16[1280,512]{1,0:T(8,128)(2,1)}, u32[]{:S(2)}, u32[]{:S(2)}) collective-permute-start(bf16[1280,512]{1,0:T(8,128)(2,1)} %fusion.23), channel_id=1, source_target_pairs={{0,8},{8,16},{16,24},{24,0},{1,9},{9,17},{17,25},{25,1},{2,10},{10... | collective-permute-start | bytes 3932168 | tf_op jit(solution)/shard_map/ppermute | solution.py:391
  521.0 59.9 %collective-permute-start.48 = (bf16[1280,512]{1,0:T(8,128)(2,1)}, bf16[1280,512]{1,0:T(8,128)(2,1)}, u32[]{:S(2)}, u32[]{:S(2)}) collective-permute-start(bf16[1280,512]{1,0:T(8,128)(2,1)} %fusion.26), channel_id=1, source_target_pairs={{0,24},{8,0},{16,8},{24,16},{1,25},{9,1},{17,9},{25,17},{2,26},{10... | collective-permute-start | bytes 3932168 | tf_op jit(solution)/shard_map/ppermute | solution.py:391
  524.3 46.1 %collective-permute-start.22 = (bf16[8,192,512]{2,1,0:T(8,128)(2,1)S(1)}, bf16[8,192,512]{2,1,0:T(8,128)(2,1)}, u32[]{:S(2)}, u32[]{:S(2)}) collective-permute-start(bf16[8,192,512]{2,1,0:T(8,128)(2,1)S(1)} %bitcast.106), channel_id=1, source_target_pairs={{0,2},{1,3},{2,4},{3,5},{4,6},{5,7},{6,0},{7,1},{8,10},{9,11},{10,... | collective-permute-start | bytes 4718600 | tf_op jit(solution)/shard_map/ppermute | solution.py:401
  534.0 40.8 %collective-permute-start.50 = (bf16[512,1024]{1,0:T(8,128)(2,1)}, bf16[512,1024]{1,0:T(8,128)(2,1)}, u32[]{:S(2)}, u32[]{:S(2)}) collective-permute-start(bf16[512,1024]{1,0:T(8,128)(2,1)} %add_convert_fusion.1), channel_id=1, source_target_pairs={{0,8},{8,16},{16,24},{24,0},{1,9},{9,17},{17,25},{25,1},{2,10},{10... | collective-permute-start | bytes 3145736 | tf_op jit(solution)/shard_map/ppermute | solution.py:391
  554.9 25.1 %collective-permute-start.52 = (bf16[512,1024]{1,0:T(8,128)(2,1)}, bf16[512,1024]{1,0:T(8,128)(2,1)}, u32[]{:S(2)}, u32[]{:S(2)}) collective-permute-start(bf16[512,1024]{1,0:T(8,128)(2,1)} %add_convert_fusion), channel_id=1, source_target_pairs={{0,24},{8,0},{16,8},{24,16},{1,25},{9,1},{17,9},{25,17},{2,26},{10... | collective-permute-start | bytes 3145736 | tf_op jit(solution)/shard_map/ppermute | solution.py:391
  570.4 34.5 %collective-permute-start.17 = (bf16[8,192,512]{2,1,0:T(8,128)(2,1)S(1)}, bf16[8,192,512]{2,1,0:T(8,128)(2,1)S(1)}, u32[]{:S(2)}, u32[]{:S(2)}) collective-permute-start(bf16[8,192,512]{2,1,0:T(8,128)(2,1)S(1)} %bitcast.107), channel_id=1, source_target_pairs={{0,1},{1,0},{2,3},{3,2},{4,5},{5,4},{6,7},{7,6},{8,9},{9,8},{10,11... | collective-permute-start | bytes 4718600 | tf_op jit(solution)/shard_map/ppermute | solution.py:404
  580.9 24.0 %collective-permute-start.19 = (bf16[8,192,512]{2,1,0:T(8,128)(2,1)S(1)}, bf16[8,192,512]{2,1,0:T(8,128)(2,1)S(1)}, u32[]{:S(2)}, u32[]{:S(2)}) collective-permute-start(bf16[8,192,512]{2,1,0:T(8,128)(2,1)S(1)} %collective-permute-done.18.refs_2_), channel_id=1, source_target_pairs={{0,1},{1,0},{2,3},{3,2},{4,5},{5,4},{6,7},{7,6},{8,9},{9,8},{10,11... | collective-permute-start | bytes 4718600 | tf_op jit(solution)/shard_map/ppermute | solution.py:404
  580.9 26.8 %collective-permute-start.25 = (bf16[8,192,512]{2,1,0:T(8,128)(2,1)}, bf16[8,192,512]{2,1,0:T(8,128)(2,1)}, u32[]{:S(2)}, u32[]{:S(2)}) collective-permute-start(bf16[8,192,512]{2,1,0:T(8,128)(2,1)} %collective-permute-done.22.refs_8_), channel_id=1, source_target_pairs={{0,1},{1,0},{2,3},{3,2},{4,5},{5,4},{6,7},{7,6},{8,9},{9,8},{10,11... | collective-permute-start | bytes 4718600 | tf_op jit(solution)/shard_map/ppermute | solution.py:404
  (109 other events, 1618.4 us)
Sparse Core Ops, SparseCore 0:
  35.6 36.6 all-gather.15
  73.9 38.3 all-gather.13
  114.4 65.0 all-gather.7
  288.8 39.4 reduce-scatter.7
  330.5 39.6 reduce-scatter.5
  372.4 69.1 reduce-scatter.3
  443.2 39.3 all-gather.11
  484.2 46.0 all-gather.9

commit v7 on v5

--- a/solution.py
+++ b/solution.py
@@ -13,6 +13,7 @@
 LANES = 128
 Q_ROWS = 256
 LN_ROWS = 64
+PAIRS = 2
 MIB = 1024 * 1024
 TILE = 256
 SQRT_HALF = 0.5 ** 0.5
@@ -126,75 +127,123 @@
             cost_estimate=pl.CostEstimate(flops=8 * n_seq * pairs * width, bytes_accessed=8 * n_seq * seq_len * width, transcendentals=n_seq * pairs),
         )(qkv)
 
-    def backward(qkv, dctx, index):
+    def backward(qkv, dctx, index, into):
+        kernel = functools.partial(attn_bwd_kernel, half=half, scale=scale, span=span)
         return pl.pallas_call(
-            functools.partial(attn_bwd_kernel, half=half, scale=scale, span=span),
+            (lambda *refs: kernel(*refs[:5], *refs[5 + len(into):])),
             grid=(1,),
-            in_specs=[seq_spec(3 * width, index), seq_spec(width, index), tab_spec, tab_spec, tab_spec],
-            out_specs=[seq_spec(3 * width), pl.BlockSpec((1, 8, 3 * width), lambda s: (s, 0, 0))],
-            out_shape=[jax.ShapeDtypeStruct((1, seq_len, 3 * width), jnp.bfloat16), jax.ShapeDtypeStruct((1, 8, 3 * width), jnp.float32)],
+            in_specs=[seq_spec(3 * width, index), seq_spec(width, index), tab_spec, tab_spec, tab_spec] + [pl.BlockSpec(memory_space=pl.ANY)] * len(into),
+            out_specs=[seq_spec(3 * width, index), pl.BlockSpec((1, 8, 3 * width), lambda s: (s, 0, 0))],
+            input_output_aliases={5: 0} if into else {},
+            out_shape=[jax.ShapeDtypeStruct((n_seq, seq_len, 3 * width), jnp.bfloat16), jax.ShapeDtypeStruct((1, 8, 3 * width), jnp.float32)],
             scratch_shapes=[acc_scratch, acc_scratch],
             compiler_params=params,
             name="ab",
             cost_estimate=pl.CostEstimate(flops=20 * pairs * width, bytes_accessed=14 * seq_len * width, transcendentals=pairs),
-        )(qkv, dctx, *tables)
+        )(qkv, dctx, *tables, *into)
 
     return forward, backward
 
 
-def place_kernel(place_ref, full_ref, *rest, chunk, n_seq):
+def place_kernel(place_ref, same_ref, other_ref, *rest, per, chunk, n_seq):
     out_ref, held_ref, in_sems, out_sems = rest[-4:]
-    groups = full_ref.shape[0]
-    fetch = [pltpu.make_async_copy(full_ref.at[lax.rem(place_ref[0] + groups - t, groups)], held_ref.at[t], in_sems.at[t]) for t in range(groups)]
-    store = [pltpu.make_async_copy(held_ref.at[t], out_ref.at[t * n_seq + chunk], out_sems.at[t]) for t in range(groups)]
+    groups = same_ref.shape[0] // per
+    fetch, store = [], []
+    for which, ref in enumerate((same_ref, other_ref)):
+        core = place_ref[2] if which == 0 else 1 - place_ref[2]
+        for r in range(groups):
+            sem = which * groups + r
+            part = pl.ds(r * per, per)
+            to = lax.rem(place_ref[0] + groups - r, groups) * n_seq + chunk
+            fetch.append(pltpu.make_async_copy(ref.at[part], held_ref.at[which, part], in_sems.at[sem]))
+            store.append(pltpu.make_async_copy(held_ref.at[which, part], out_ref.at[pl.ds(to, per), :, core], out_sems.at[sem]))
     for copy in fetch:
         copy.start()
-    for t in range(groups):
-        fetch[t].wait()
-        store[t].start()
+    for copy_in, copy_out in zip(fetch, store):
+        copy_in.wait()
+        copy_out.start()
     for copy in store:
         copy.wait()
 
 
-def place_pieces_kernel(place_ref, *refs, chunk, n_seq):
-    out_ref, held_ref, in_sems, out_sems = refs[-4:]
-    groups, own, _ = refs[0].shape
-    columns = held_ref.shape[0] // 2
-    row, column, core = place_ref[0], place_ref[1], place_ref[2]
-    fetch, store = [], []
-    for index in range(2 * columns):
-        source = 2 * lax.rem(column + index % columns, columns) + (core if index < columns else 1 - core)
-        at = pl.ds(pl.multiple_of(source * own, own), own)
-        fetch.append(pltpu.make_async_copy(refs[index], held_ref.at[index], in_sems.at[index]))
-        for t in range(groups):
-            piece = held_ref.at[index, lax.rem(row + groups - t, groups)]
-            store.append(pltpu.make_async_copy(piece, out_ref.at[t * n_seq + chunk, at], out_sems.at[index]))
-    for copy in fetch:
-        copy.start()
-    for index in range(2 * columns):
-        fetch[index].wait()
-        for copy in store[index * groups:(index + 1) * groups]:
-            copy.start()
-    for copy in store:
-        copy.wait()
-
-
-def place_call(kernel, place, operands, out, chunk, n_seq, tokens):
-    groups, _, width = operands[0].shape
-    operands = [place, *operands] + ([] if out is None else [out])
+def place_call(place, same, other, out, chunk, n_seq):
+    total, columns, own, width = same.shape
+    per = n_seq if out is None and chunk is None else 1
+    groups = total // per
+    operands = [place, same, other] + ([] if out is None else [out])
     any_spec = pl.BlockSpec(memory_space=pl.ANY)
-    pieces = len(operands) - 1 - (out is not None)
-    held = operands[1].shape if pieces == 1 else (pieces,) + operands[1].shape
-    sems = pltpu.SemaphoreType.DMA((groups if pieces == 1 else pieces,))
+    sems = pltpu.SemaphoreType.DMA((2 * groups,))
     return pl.pallas_call(
-        functools.partial(kernel, chunk=chunk, n_seq=n_seq),
+        functools.partial(place_kernel, per=per, chunk=chunk or 0, n_seq=n_seq),
         in_specs=[pl.BlockSpec(memory_space=pltpu.SMEM)] + [any_spec] * (len(operands) - 1),
         out_specs=any_spec,
-        out_shape=jax.ShapeDtypeStruct((groups * n_seq, tokens, width), jnp.bfloat16),
-        scratch_shapes=[pltpu.VMEM(held, jnp.bfloat16), sems, sems],
-        input_output_aliases={} if out is None else {len(operands) - 1: 0},
-        cost_estimate=pl.CostEstimate(flops=groups * tokens * width, bytes_accessed=4 * groups * tokens * width, transcendentals=0),
+        out_shape=jax.ShapeDtypeStruct((groups * n_seq, columns, 2, own, width), jnp.bfloat16),
+        scratch_shapes=[pltpu.VMEM((2, *same.shape), jnp.bfloat16), sems, sems],
+        input_output_aliases={} if out is None else {3: 0},
+        cost_estimate=pl.CostEstimate(flops=2 * same.size, bytes_accessed=8 * same.size, transcendentals=0),
     )(*operands)
+
+
+def grad_kernel(*refs, blocks, moving, splits):
+    acc_ref = refs[-1]
+    n_out = sum(len(parts) for parts in splits)
+    ins, outs = refs[:-1 - n_out], list(refs[-1 - n_out:-1])
+    step = pl.program_id(0)
+
+    @pl.when(step == 0)
+    def _():
+        acc_ref[...] = jnp.zeros(acc_ref.shape, jnp.float32)
+
+    for index, terms in enumerate(blocks):
+        for lhs, rhs, row, column in terms:
+            part = dot(ins[lhs][...], ins[rhs][...], TN)
+            acc_ref[index, row:row + part.shape[0], column:column + part.shape[1]] += part
+
+    @pl.when(step == pl.num_programs(0) - 1)
+    def _():
+        for index, adds in enumerate(moving):
+            for ref, row in adds:
+                at = slice(row, row + ins[ref].shape[0])
+                acc_ref[index, at, :] += ins[ref][...].astype(jnp.float32)
+        for index, parts in enumerate(splits):
+            for rows, cols in parts:
+                out = outs.pop(0)
+                out[...] = acc_ref[index, rows, cols].astype(out.dtype)
+
+
+def grad_call(blocks, shape, moving, splits, dtype, rows=512):
+    ins, specs, keys = [], [], {}
+
+    def operand(array, block, width):
+        key = (id(array), block, width)
+        if key not in keys:
+            keys[key] = len(ins)
+            ins.append(array)
+            specs.append(pl.BlockSpec((rows, width), lambda s, b=block: (s, b)))
+        return keys[key]
+
+    count = blocks[0][0][0].shape[0]
+    terms = [[(operand(lhs, lb, lw), operand(rhs, rb, rw), row, col) for lhs, lb, lw, rhs, rb, rw, row, col in block] for block in blocks]
+    adds = []
+    for block in moving:
+        found = []
+        for array, row in block:
+            found.append((len(ins), row))
+            ins.append(array)
+            specs.append(pl.BlockSpec(array.shape, lambda s: (0, 0)))
+        adds.append(found)
+    span = lambda at, size: len(range(*at.indices(size)))
+    shapes = [(span(r, shape[0]), span(c, shape[1])) for parts in splits for r, c in parts]
+    return pl.pallas_call(
+        functools.partial(grad_kernel, blocks=terms, moving=adds, splits=splits),
+        grid=(count // rows,),
+        in_specs=specs,
+        out_specs=[pl.BlockSpec(one, lambda s: (0, 0)) for one in shapes],
+        out_shape=[jax.ShapeDtypeStruct(one, dtype) for one in shapes],
+        scratch_shapes=[pltpu.VMEM((len(blocks), *shape), jnp.float32)],
+        compiler_params=pltpu.CompilerParams(dimension_semantics=("arbitrary",), vmem_limit_bytes=60 * MIB),
+        cost_estimate=pl.CostEstimate(flops=2 * len(blocks) * count * shape[0] * shape[1], bytes_accessed=sum(2 * count * spec.block_shape[1] for spec in specs), transcendentals=0),
+    )(*ins)
 
 
 def split_width(value, out_refs):
@@ -278,13 +327,28 @@
         gelu_ref[:, at] = (0.5 * wide * (1.0 + lax.erf(wide * SQRT_HALF))).astype(jnp.bfloat16)
 
 
-def y_kernel(ctx_ref, gelu_ref, *refs):
-    w_refs, y_ref = refs[:-1], refs[-1]
+def split_places(rows_ref, place_ref, mine, other):
+    core = place_ref[2]
+    own = rows_ref.shape[0] // (2 * PAIRS)
+    for pair in range(PAIRS):
+        for store, which in ((mine, core), (other, 1 - core)):
+            store(pair, rows_ref[pl.ds(pl.multiple_of((2 * pair + which) * own, own), own), :])
+
+
+def y_kernel(ctx_ref, gelu_ref, place_ref, *refs):
+    w_refs, (mine_ref, other_ref, rows_ref) = refs[:-3], refs[-3:]
     head = ctx_ref.shape[1]
-    places, _, own, _ = y_ref.shape
     for w_ref, start, stop in offsets(w_refs, 1):
         acc = dot(ctx_ref[...], w_ref[:head, :], NN) + dot(gelu_ref[...], w_ref[head:, :], NN)
-        y_ref[:, 0, :, start:stop] = acc.astype(jnp.bfloat16).reshape(places, own, stop - start)
+        rows_ref[:, start:stop] = acc.astype(jnp.bfloat16)
+
+    def put(ref):
+        def store(pair, value):
+            ref[pair, 0] = value
+
+        return store
+
+    split_places(rows_ref, place_ref, put(mine_ref), put(other_ref))
 
 
 def d_pre_kernel(cot_ref, pre_ref, *refs):
@@ -310,8 +374,8 @@
         d_bias_ref[:, at] += sublane_sum(d_pre.astype(jnp.float32))
 
 
-def d_h_kernel(d_qkv_ref, d_pre_ref, x_ref, small_ref, *refs):
-    w_refs, (a6_ref, sums_ref) = refs[:-2], refs[-2:]
+def d_h_kernel(d_qkv_ref, d_pre_ref, x_ref, small_ref, place_ref, *refs):
+    w_refs, (mine_ref, other_ref, sums_ref, a6_ref) = refs[:-4], refs[-4:]
     qkv_width = d_qkv_ref.shape[1]
 
     @pl.when(pl.program_id(0) == 0)
@@ -334,8 +398,16 @@
             sums_ref[2, :, at] += sublane_sum(d_mlp * x_hat)
             sums_ref[3, :, at] += sublane_sum(d_mlp)
 
-
-def tile_call(kernel, tiled, whole, outs, row_range, flops, rows=512):
+    def put(ref):
+        def store(pair, value):
+            ref[pair, 0] = value
+
+        return store
+
+    split_places(a6_ref, place_ref, put(mine_ref), put(other_ref))
+
+
+def tile_call(kernel, tiled, whole, outs, row_range, flops, rows=512, scratch=()):
     start, count = row_range
     rows = next(r for r in (rows, 256, 128, 64, count) if count % r == 0 and all(op.shape[0] % r == 0 for op in tiled))
     first = start // rows
@@ -347,7 +419,11 @@
         return pl.BlockSpec((rows, op.shape[1]), lambda s, f=(first if op.shape[0] != count else 0): (s + f, 0))
 
     in_specs = [tile_spec(op) for op in tiled]
-    in_specs += [pl.BlockSpec(op.shape, lambda s, n=op.ndim: (0,) * n, pipeline_mode=pl.Buffered(1)) for op in whole]
+    for op in whole:
+        if op.dtype == jnp.int32:
+            in_specs.append(pl.BlockSpec(memory_space=pltpu.SMEM))
+        else:
+            in_specs.append(pl.BlockSpec(op.shape, lambda s, n=op.ndim: (0,) * n, pipeline_mode=pl.Buffered(1)))
     out_specs, out_shapes = [], []
     for form, dtype in outs:
         if isinstance(form, int):
@@ -366,6 +442,7 @@
         in_specs=in_specs,
         out_specs=out_specs,
         out_shape=out_shapes,
+        scratch_shapes=list(scratch),
         compiler_params=pltpu.CompilerParams(dimension_semantics=("arbitrary",), vmem_limit_bytes=60 * MIB),
         cost_estimate=pl.CostEstimate(flops=flops, bytes_accessed=moved, transcendentals=0),
     )(*tiled, *whole)
@@ -389,9 +466,6 @@
             value = value + lax.ppermute(value, axis, [(s, s ^ step) for s in range(size)])
             step *= 2
         return value
-
-    def along(value, hops):
-        return lax.ppermute(value, 'ty', [(s, (s - 2 * hops) % ty_size) for s in range(ty_size)])
 
     def partner(value):
         return lax.ppermute(value, 'ty', [(s, s ^ 1) for s in range(ty_size)])
@@ -407,18 +481,13 @@
         blocks[antipode] = [shift(low, 1), shift(high, -1)]
         return [piece for r in range(tx_size) for piece in blocks[r]]
 
-    def ring_scatter(make_part, rows):
-        half = rows // 2
-        far = make_part(antipode).astype(jnp.bfloat16)
-        moving_up, moving_down = shift(far[:half], -1), shift(far[half:], 1)
-        moving_up = jnp.pad(moving_up, ((0, rows - half), (0, 0)))
-        moving_down = jnp.pad(moving_down, ((half, 0), (0, 0)))
-        for hops in range(antipode - 1, 0, -1):
-            up = make_part(hops) + moving_up.astype(jnp.float32)
-            down = make_part(tx_size - hops) + moving_down.astype(jnp.float32)
-            up, down = up.astype(jnp.bfloat16), down.astype(jnp.bfloat16)
-            moving_up, moving_down = shift(up, -1), shift(down, 1)
-        return lambda own, low, high: own + moving_up[low:high].astype(jnp.float32) + moving_down[low:high].astype(jnp.float32)
+    def ring_scatter(make_blocks, shape):
+        whole, half = slice(None), shape[0] // 2
+        assert tx_size == 4
+        low, high = grad_call([make_blocks(2)], shape, [[]], [[(slice(0, half), whole), (slice(half, None), whole)]], jnp.bfloat16)
+        low, high = shift(low, -1), shift(high, 1)
+        up, down = grad_call([make_blocks(1), make_blocks(3)], shape, [[(low, 0)], [(high, half)]], [[(whole, whole)], [(whole, whole)]], jnp.bfloat16)
+        return [(shift(up, -1), 0), (shift(down, 1), 0)]
 
     def body(x_act, cot_out, ln1_gain, ln1_bias, ln2_gain, ln2_bias, w_qkv, b_qkv, w_dense, b_dense, w_up, b_up, w_down, b_down):
         batch, seq_len, d_local = x_act.shape
@@ -469,38 +538,48 @@
             [(qkv_width, jnp.bfloat16), (ff_width, jnp.bfloat16), (ff_width, jnp.bfloat16)], (0, n_tok), 2 * n_tok * in_size)
         qkv_seq = qkv_act.reshape(n_seq, seq_len, qkv_width)
         context = attn_fwd(qkv_seq).reshape(n_tok, head)
-        blocks_per_seq = ty_size // 2
-        y_form = ((ty_size, n_seq, own, d_model), (2, 1, own, d_model), lambda s: (lax.rem(s, blocks_per_seq), s // blocks_per_seq, 0, 0))
-        (y_part,) = tile_call(y_kernel, [context, gelu_out], w_back, [(y_form, jnp.bfloat16)], (0, n_tok), 2 * n_tok * back_size, 2 * own)
-        mixed = lax.psum_scatter(y_part.reshape(n_tok, d_model), 'ty', scatter_dimension=0, tiled=True)
-        blocks = to_width(row_call(finish_y_kernel, tx_size, 0, n_seq * own, x_rows, mixed, bias_out.reshape(1, -1)))
-        full = lax.all_gather(blocks.reshape(tx_size * n_seq, own, d_local), 'ty', axis=1, tiled=True)
-        y_out = place_call(place_kernel, place, [full.reshape(tx_size, n_seq * seq_len, d_local)], None, 0, 1, n_seq * seq_len)
+        columns = ty_size // 2
+        same_core = [[2 * x + c for x in range(columns)] for c in range(2)]
+        tile = 2 * PAIRS * own
+        tiles_per_seq = seq_len // tile
+        form = ((columns, n_seq, own, d_model), (PAIRS, 1, own, d_model), lambda s: (lax.rem(s, tiles_per_seq), s // tiles_per_seq, 0, 0))
+        mine, other = tile_call(
+            y_kernel, [context, gelu_out], [place, *w_back], [(form, jnp.bfloat16)] * 2, (0, n_tok), 2 * n_tok * back_size, tile,
+            [pltpu.VMEM((tile, d_model), jnp.bfloat16)])
+
+        def scatter_columns(mine, other):
+            other = partner(other)
+            total = (mine.astype(jnp.float32) + other.astype(jnp.float32)).astype(jnp.bfloat16).reshape(-1, d_model)
+            return lax.psum_scatter(total, 'ty', scatter_dimension=0, axis_index_groups=same_core, tiled=True)
+
+        def gather_columns(block):
+            same = lax.all_gather(block, 'ty', axis=1, axis_index_groups=same_core, tiled=True)
+            other = partner(same)
+            return [half.reshape(-1, columns, own, d_local) for half in (same, other)]
+
+        mixed = scatter_columns(mine, other)
+        block = to_width(row_call(finish_y_kernel, tx_size, 0, n_seq * own, x_rows, mixed, bias_out.reshape(1, -1)))
+        y_out = place_call(place, *gather_columns(block.reshape(tx_size * n_seq, own, d_local)), None, None, n_seq)
 
         d_ctx, d_pre, d_b_up = tile_call(
             d_pre_kernel, [cot_group, pre_act], w_back,
             [(head, jnp.bfloat16), (ff_width, jnp.bfloat16), ((8, ff_width), jnp.float32)], (0, n_tok), 2 * n_tok * back_size)
         d_ctx, d_b_up = d_ctx.reshape(n_seq, seq_len, head), d_b_up.sum(0)
-        d_qkv, d_b_qkv, d_ln, dx_act = [], [], [], None
+        d_b_qkv, d_ln, dx_act = [], [], None
         for s in chunks:
-            d_qkv_seq, d_b_seq = attn_bwd(qkv_seq, d_ctx, s)
-            d_qkv.append(d_qkv_seq.reshape(seq_len, qkv_width))
+            d_qkv, d_b_seq = attn_bwd(qkv_seq, d_ctx, s, (d_qkv, sums) if s else ())
             d_b_qkv.append(d_b_seq.sum((0, 1)))
-            a6_part, sums = tile_call(
-                d_h_kernel, [d_qkv[s], d_pre, x_group], [small, *w_in],
-                [(d_model, jnp.bfloat16), ((4, 8, d_model), jnp.float32)], (s * seq_len, seq_len), 2 * seq_len * in_size)
+            form = ((columns, 1, own, d_model), (PAIRS, 1, own, d_model), lambda t: (t, 0, 0, 0))
+            mine, other, sums = tile_call(
+                d_h_kernel, [d_qkv.reshape(n_tok, qkv_width), d_pre, x_group], [small, place, *w_in],
+                [(form, jnp.bfloat16), (form, jnp.bfloat16), ((4, 8, d_model), jnp.float32)], (s * seq_len, seq_len), 2 * seq_len * in_size, tile,
+                [pltpu.VMEM((tile, d_model), jnp.bfloat16)])
             d_ln.append(sums)
-            value_a6 = lax.psum_scatter(a6_part, 'ty', scatter_dimension=0, tiled=True)
+            value_a6 = scatter_columns(mine, other)
             parts = row_call(finish_dx_kernel, tx_size, s, own, x_rows, value_a6, cot_rows)
-            block = to_width(parts)
-            if s < n_seq - 1:
-                blocks = [block] + [along(block, hops) for hops in range(1, ty_size // 2)]
-                blocks = blocks + [partner(piece) for piece in blocks]
-                dx_act = place_call(place_pieces_kernel, place, blocks, dx_act, s, n_seq, seq_len)
-            else:
-                full = lax.all_gather(block, 'ty', axis=1, tiled=True)
-                dx_act = place_call(place_kernel, place, [full], dx_act, s, n_seq, seq_len)
-        d_qkv = jnp.concatenate(d_qkv, axis=0)
+            dx_act = place_call(place, *gather_columns(to_width(parts)), dx_act, s, n_seq)
+        y_out, dx_act = y_out.reshape(x_act.shape), dx_act.reshape(x_act.shape)
+        d_qkv = d_qkv.reshape(n_tok, qkv_width)
 
         d_ln = sum(d_ln).sum(1).reshape(4, tx_size, d_local)
         d_bias = jnp.concatenate([sum(d_b_qkv), d_b_up]).reshape(4, -1)
@@ -511,16 +590,14 @@
         d_ln = small_sum(got[:, :d_local], 'ty', ty_size)
         d_b_out = cot_out.astype(jnp.float32).sum((0, 1))
 
-        cols = lambda act, r: act[:, r * d_local:(r + 1) * d_local]
-        inner = jnp.concatenate([context, gelu_out], axis=1)
-        add_back = ring_scatter(lambda r: dot(inner, cols(cot_group, r), TN), inner.shape[1])
-        add_up = ring_scatter(lambda r: dot(cols(h_mlp, r), d_pre, TN), d_local)
-        add_qkv = ring_scatter(lambda r: dot(cols(h_attn, r), d_qkv, TN), d_local)
-        d_w_dense = add_back(dot(context, cols(cot_group, 0), TN), 0, head)
-        d_w_down = add_back(dot(gelu_out, cols(cot_group, 0), TN), head, inner.shape[1])
-        d_w_up = add_up(dot(cols(h_mlp, 0), d_pre, TN), 0, d_local)
-        d_w_qkv = add_qkv(dot(cols(h_attn, 0), d_qkv, TN), 0, d_local)
-        y_out = y_out.reshape(batch, seq_len, d_local)
+        in_shape, back_shape = (d_local, qkv_width + ff_width), (head + ff_width, d_local)
+        in_blocks = lambda r: [(h_attn, r, d_local, d_qkv, 0, qkv_width, 0, 0), (h_mlp, r, d_local, d_pre, 0, ff_width, 0, qkv_width)]
+        back_blocks = lambda r: [(context, 0, head, cot_group, r, d_local, 0, 0), (gelu_out, 0, ff_width, cot_group, r, d_local, head, 0)]
+        add_back = ring_scatter(back_blocks, back_shape)
+        add_in = ring_scatter(in_blocks, in_shape)
+        whole = slice(None)
+        d_w_dense, d_w_down = grad_call([back_blocks(0)], back_shape, [add_back], [[(slice(0, head), whole), (slice(head, None), whole)]], jnp.float32)
+        d_w_qkv, d_w_up = grad_call([in_blocks(0)], in_shape, [add_in], [[(whole, slice(0, qkv_width)), (whole, slice(qkv_width, None))]], jnp.float32)
         return (y_out, dx_act, d_ln[0], d_ln[1], d_ln[2], d_ln[3], d_w_qkv.reshape(w_qkv.shape), d_bias[:qkv_width].reshape(b_qkv.shape), d_w_dense, d_b_out, d_w_up, d_bias[qkv_width:], d_w_down, d_b_out)
 
     return jax.shard_map(body, mesh=mesh, in_specs=in_specs, out_specs=out_specs, check_vma=False)

time: 676 us -> 696 us (1.030)
  matrix products: 87.2 us -> 0 us
  Pallas kernels: 213 us -> 299 us
  other arithmetic: 29 us -> 43.1 us
  waiting for transfers between devices: 236 us -> 249 us
  starting transfers between devices: 68.6 us -> 56.8 us
    dot_general x13 -> x0, matrix products: 87.2 us -> none  [dot(): return lax.dot_general(a, b, dims, preferred_element_type=jnp.float32)]
    pallas_call x5 -> x11, Pallas kernels: 49.2 us -> 133 us  [the longest x6 82.4 us: grad_call(): pl.pallas_call(functools.partial(grad_kernel, blocks=terms, moving=adds,...]
    all_gather x2 -> x3, waiting for transfers between devices: 0.04 us -> 56.9 us  [gather_columns(): lax.all_gather(block, 'ty', axis=1, axis_index_groups=same_core, tiled=True)]
    ppermute x41 -> x37, waiting for transfers between devices: 196 us -> 170 us  [shift(): lax.ppermute(value, 'tx', [(s, (s - hops) % tx_size) for s in range(tx_si...]
    ppermute x4 -> x6, waiting for transfers between devices: 0.01 us -> 21.9 us  [partner(): return lax.ppermute(value, 'ty', [(s, s ^ 1) for s in range(ty_size)])]
    ppermute x3 -> x0, waiting for transfers between devices: 18.5 us -> none  [along(): lax.ppermute(value, 'ty', [(s, (s - 2 * hops) % ty_size) for s in range(t...]
    convert_element_type x0 -> x3, other arithmetic: none -> 18.4 us  [scatter_columns(): (mine.astype(jnp.float32) + other.astype(jnp.float32)).astype(jnp.bfloat16)]
    reduce_scatter x3, waiting for transfers between devices: 18.2 us -> 0.06 us  [scatter_columns(): lax.psum_scatter(total, 'ty', scatter_dimension=0, axis_index_groups=same...]
  transfers between devices with their start and end apart: 58 -> 54, of which waited for: 22 -> 23; matrix products, arithmetic and copies ran while one was open for 18% -> 8% of each run, Pallas kernels for 21% -> 42%
where the time goes in v7:
time: 696 us; the launch traced here: 689 us
  Pallas kernels  299 us (43%)
  waiting for transfers between devices  249 us (36%)
  starting transfers between devices  56.8 us (8%)
  other arithmetic  43.1 us (6%)
  local copies, waits for them, and re-layouts  25.5 us (4%)
  between operations  15 us (2%)
    ppermute x37, waiting for transfers between devices, shift(): lax.ppermute(value, 'tx', [(s, (s - hops) % tx_size) for s in range(tx_si...  170 us
    pallas_call x6, Pallas kernels, tile_call(): pl.pallas_call(kernel, grid=(count // rows,), in_specs=in_specs, out_spec...  149 us
    pallas_call x6, Pallas kernels, grad_call(): pl.pallas_call(functools.partial(grad_kernel, blocks=terms, moving=adds,...  82.4 us
    all_gather x3, waiting for transfers between devices, gather_columns(): lax.all_gather(block, 'ty', axis=1, axis_index_groups=same_core, tiled=True)  56.9 us
    ppermute x37, starting transfers between devices, shift(): lax.ppermute(value, 'tx', [(s, (s - hops) % tx_size) for s in range(tx_si...  52.4 us
    pallas_call x2, Pallas kernels, backward(): pl.pallas_call(lambda *refs: kernel(*refs[:5], *refs[5 + len(into):]), gr...  27.8 us
    pallas_call x3, Pallas kernels, place_call(): pl.pallas_call(functools.partial(place_kernel, per=per, chunk=chunk or 0,...  22.3 us
    ppermute x6, waiting for transfers between devices, partner(): return lax.ppermute(value, 'ty', [(s, s ^ 1) for s in range(ty_size)])  21.9 us
  transfers between devices with their start and end apart: 54, of which 23 were waited for; matrix products, arithmetic and copies ran while one was open for 8% of the time, Pallas kernels for 42%

profile of v7, /device:TPU:98, one launch (start us, length us, event | category | flops | bytes accessed | tf_op | source)
XLA Modules:
  0.0 689.2 jit_solution(5309268390819701712)
XLA Ops:
  14.6 15.8 %collective-permute-done = bf16[2,192,512]{2,1,0:T(8,128)(2,1)S(1)} collective-permute-done((bf16[2,192,512]{2,1,0:T(8,128)(2,1)S(1)}, bf16[2,192,512]{2,1,0:T(8,128)(2,1)S(1)}, u32[]{:S(2)}, u32[]{:S(2)}) %collective-permute-start) | collective-permute-done | bytes 393248 | tf_op jit(solution)/shard_map/ppermute | solution.py:461
  39.6 10.0 %collective-permute-done.19 = bf16[2,192,512]{2,1,0:T(8,128)(2,1)S(1)} collective-permute-done((bf16[2,192,512]{2,1,0:T(8,128)(2,1)S(1)}, bf16[2,192,512]{2,1,0:T(8,128)(2,1)S(1)}, u32[]{:S(2)}, u32[]{:S(2)}) %collective-permute-start.19) | collective-permute-done | bytes 393248 | tf_op jit(solution)/shard_map/ppermute | solution.py:461
  52.1 6.4 collective-permute-done.21
  73.0 32.1 %collective-permute-done.6.refs_1_ = bf16[512,1792]{1,0:T(8,128)(2,1)S(1)} collective-permute-done((bf16[512,1792]{1,0:T(8,128)(2,1)S(1)}, bf16[512,1792]{1,0:T(8,128)(2,1)S(1)}, u32[]{:S(2)}, u32[]{:S(2)}) %collective-permute-start.6) | collective-permute-done | bytes 1835040 | tf_op jit(solution)/shard_map/ppermute | solution.py:461
  109.1 24.2 %collective-permute-done.3 = bf16[8,512]{1,0:T(8,128)(2,1)S(1)} collective-permute-done((bf16[8,512]{1,0:T(8,128)(2,1)S(1)}, bf16[8,512]{1,0:T(8,128)(2,1)S(1)}, u32[]{:S(2)}, u32[]{:S(2)}) %collective-permute-start.3) | collective-permute-done | bytes 8224 | tf_op jit(solution)/shard_map/ppermute | solution.py:461
  138.1 14.7 %collective-permute-done.4 = bf16[8,512]{1,0:T(8,128)(2,1)S(1)} collective-permute-done((bf16[8,512]{1,0:T(8,128)(2,1)S(1)}, bf16[8,512]{1,0:T(8,128)(2,1)S(1)}, u32[]{:S(2)}, u32[]{:S(2)}) %collective-permute-start.4) | collective-permute-done | bytes 8224 | tf_op jit(solution)/shard_map/ppermute | solution.py:461
  163.0 18.7 %shard_map.245 = (bf16[3072,2048]{1,0:T(8,128)(2,1)}, bf16[3072,2048]{1,0:T(8,128)(2,1)}) custom-call(bf16[3072,2048]{1,0:T(8,128)(2,1)} %bitcast.101, f32[8,2048]{1,0:T(8,128)} %maximum_convert_fusion.small_ref), custom_call_target="tpu_custom_call" | custom-call | flops 100663296 | bytes 37781504 | tf_op jit(solution)/shard_map/pallas_call | solution.py:439
  181.7 32.9 %shard_map.246 = (bf16[3072,768]{1,0:T(8,128)(2,1)}, bf16[3072,1024]{1,0:T(8,128)(2,1)}, bf16[3072,1024]{1,0:T(8,128)(2,1)}) custom-call(bf16[3072,2048]{1,0:T(8,128)(2,1)} %get-tuple-element.58.h_attn_ref.refs_0_.refs_4_, bf16[3072,2048]{1,0:T(8,128)(2,1)} %get-tuple-element.59.h_mlp_ref.refs_2_.refs_5_, f32[1536,128]{1,0:T(8,128)} %get-tuple-element.136.cos_ref.refs_2_, ...), custom_call_target="tpu_custom_call" | custom-call | flops 22548578304 | bytes 52170240 | tf_op jit(solution)/shard_map/pallas_call | solution.py:439
  214.6 15.6 %af.1 = bf16[2,1536,256]{2,1,0:T(8,128)(2,1)} custom-call(bf16[2,1536,768]{2,1,0:T(8,128)(2,1)} %bitcast.141), custom_call_target="tpu_custom_call" | custom-call | flops 4831838208 | bytes 6291456 | tf_op jit(solution)/shard_map/af/pallas_call | solution.py:119
  230.1 22.8 %shard_map.247 = (bf16[4,2,192,2048]{3,2,1,0:T(8,128)(2,1)}, bf16[4,2,192,2048]{3,2,1,0:T(8,128)(2,1)}) custom-call(bf16[3072,256]{1,0:T(8,128)(2,1)} %bitcast.97, bf16[3072,1024]{1,0:T(8,128)(2,1)} %get-tuple-element.61.gelu_ref.refs_2_, s32[3]{0:T(128)} %pad_add_fusion.place_ref, bf16[1280,512]{1,0:T(8,128)(2,1)} %constant_dynamic-update-slice_fusion.refs_0_, ...), custom_call_target="tpu_custom_call" | custom-call | flops 16106127360 | bytes 25690118 | tf_op jit(solution)/shard_map/pallas_call | solution.py:439
  252.9 10.4 %collective-permute-done.14 = bf16[4,2,192,2048]{3,2,1,0:T(8,128)(2,1)S(1)} collective-permute-done((bf16[4,2,192,2048]{3,2,1,0:T(8,128)(2,1)}, bf16[4,2,192,2048]{3,2,1,0:T(8,128)(2,1)S(1)}, u32[]{:S(2)}, u32[]{:S(2)}) %collective-permute-start.14) | collective-permute-done | bytes 6291488 | tf_op jit(solution)/shard_map/ppermute | solution.py:471
  263.3 8.5 %add_convert_fusion = bf16[4,2,192,2048]{3,2,1,0:T(8,128)(2,1)} fusion(bf16[4,2,192,2048]{3,2,1,0:T(8,128)(2,1)S(1)} %collective-permute-done.14, bf16[4,2,192,2048]{3,2,1,0:T(8,128)(2,1)} %get-tuple-element.62), kind=kLoop, calls=%fused_computation.1 | loop fusion | flops 12582912 | bytes 18874368 | tf_op jit(solution)/shard_map/convert_element_type | solution.py:552
  272.5 27.0 %shard_map.250 = (bf16[3072,256]{1,0:T(8,128)(2,1)}, bf16[3072,1024]{1,0:T(8,128)(2,1)}, f32[8,1024]{1,0:T(8,128)}) custom-call(bf16[3072,2048]{1,0:T(8,128)(2,1)} %bitcast.84, bf16[3072,1024]{1,0:T(8,128)(2,1)} %get-tuple-element.68.pre_ref, bf16[1280,512]{1,0:T(8,128)(2,1)} %constant_dynamic-update-slice_fusion.refs_0_, ...), custom_call_target="tpu_custom_call" | custom-call | flops 16106127360 | bytes 31997952 | tf_op jit(solution)/shard_map/pallas_call | solution.py:439
  299.4 13.9 %ab.2 = (bf16[2,1536,768]{2,1,0:T(8,128)(2,1)}, f32[1,8,768]{2,1,0:T(8,128)}) custom-call(bf16[2,1536,768]{2,1,0:T(8,128)(2,1)} %bitcast.142, bf16[2,1536,256]{2,1,0:T(8,128)(2,1)} %bitcast.144, f32[1536,128]{1,0:T(8,128)} %get-tuple-element.136.cos_ref.refs_2_, f32[1536,128]{1,0:T(8,128)} %get-tuple-element.135.lo_ref.refs_3_, ...), custom_call_target="tpu_custom_call" | custom-call | flops 6039797760 | bytes 5505024 | tf_op jit(solution)/shard_map/ab/pallas_call | solution.py:132
  313.4 23.6 %shard_map.251 = (bf16[4,1,192,2048]{3,2,1,0:T(8,128)(2,1)}, bf16[4,1,192,2048]{3,2,1,0:T(8,128)(2,1)}, f32[4,8,2048]{2,1,0:T(8,128)}) custom-call(bf16[3072,768]{1,0:T(8,128)(2,1)} %bitcast.90, bf16[3072,1024]{1,0:T(8,128)(2,1)} %get-tuple-element.71.d_pre_ref.refs_3_, bf16[3072,2048]{1,0:T(8,128)(2,1)} %bitcast.102, ...), custom_call_target="tpu_custom_call" | custom-call | flops 11274289152 | bytes 25591814 | tf_op jit(solution)/shard_map/pallas_call | solution.py:439
  347.9 13.9 %ab.3 = (bf16[2,1536,768]{2,1,0:T(8,128)(2,1)}, f32[1,8,768]{2,1,0:T(8,128)}) custom-call(bf16[2,1536,768]{2,1,0:T(8,128)(2,1)} %bitcast.143, bf16[2,1536,256]{2,1,0:T(8,128)(2,1)} %bitcast.145, f32[1536,128]{1,0:T(8,128)} %get-tuple-element.136.cos_ref.refs_2_, f32[1536,128]{1,0:T(8,128)} %get-tuple-element.135.lo_ref.refs_3_, ...), custom_call_target="tpu_custom_call", output_to_operand_aliasing={{0}: (5, {})} | custom-call | flops 6039797760 | bytes 5505024 | tf_op jit(solution)/shard_map/ab/pallas_call | solution.py:132
  361.8 23.8 %shard_map.252 = (bf16[4,1,192,2048]{3,2,1,0:T(8,128)(2,1)}, bf16[4,1,192,2048]{3,2,1,0:T(8,128)(2,1)}, f32[4,8,2048]{2,1,0:T(8,128)}) custom-call(bf16[3072,768]{1,0:T(8,128)(2,1)} %bitcast.91, bf16[3072,1024]{1,0:T(8,128)(2,1)} %get-tuple-element.71.d_pre_ref.refs_3_, bf16[3072,2048]{1,0:T(8,128)(2,1)} %bitcast.103, ...), custom_call_target="tpu_custom_call" | custom-call | flops 11274289152 | bytes 25591814 | tf_op jit(solution)/shard_map/pallas_call | solution.py:439
  404.8 9.1 %collective-permute-done.15 = bf16[384,512]{1,0:T(8,128)(2,1)S(1)} collective-permute-done((bf16[384,512]{1,0:T(8,128)(2,1)S(1)}, bf16[384,512]{1,0:T(8,128)(2,1)S(1)}, u32[]{:S(2)}, u32[]{:S(2)}) %collective-permute-start.15) | collective-permute-done | bytes 393248 | tf_op jit(solution)/shard_map/ppermute | solution.py:461
  413.9 8.2 %collective-permute-done.16 = bf16[384,512]{1,0:T(8,128)(2,1)S(1)} collective-permute-done((bf16[384,512]{1,0:T(8,128)(2,1)S(1)}, bf16[384,512]{1,0:T(8,128)(2,1)S(1)}, u32[]{:S(2)}, u32[]{:S(2)}) %collective-permute-start.16) | collective-permute-done | bytes 393248 | tf_op jit(solution)/shard_map/ppermute | solution.py:461
  457.8 39.6 %all-gather.8.cloned.1.call-done = bf16[8,768,512]{2,1,0:T(8,128)(2,1)} async-done(((bf16[8,192,512]{2,1,0:T(8,128)(2,1)}), bf16[8,768,512]{2,1,0:T(8,128)(2,1)}) %all-gather.8.cloned.1.call-update) | async-done | bytes 6291472 | tf_op jit(solution)/shard_map/all_gather | solution.py:556
  507.0 9.7 %shard_map.260 = (bf16[640,512]{1,0:T(8,128)(2,1)}, bf16[640,512]{1,0:T(8,128)(2,1)}) custom-call(bf16[3072,256]{1,0:T(8,128)(2,1)} %bitcast.98, bf16[3072,2048]{1,0:T(8,128)(2,1)} %bitcast.85, bf16[3072,1024]{1,0:T(8,128)(2,1)} %get-tuple-element.61.gelu_ref.refs_2_), custom_call_target="tpu_custom_call" | custom-call | flops 4026531840 | bytes 11010048 | tf_op jit(solution)/shard_map/pallas_call | solution.py:237
  520.9 12.0 %shard_map.257 = (bf16[256,1792]{1,0:T(8,128)(2,1)}, bf16[256,1792]{1,0:T(8,128)(2,1)}) custom-call(bf16[3072,2048]{1,0:T(8,128)(2,1)} %get-tuple-element.58.h_attn_ref.refs_0_.refs_4_, bf16[3072,768]{1,0:T(8,128)(2,1)} %bitcast.92, bf16[3072,2048]{1,0:T(8,128)(2,1)} %get-tuple-element.59.h_mlp_ref.refs_2_.refs_5_, ...), custom_call_target="tpu_custom_call" | custom-call | flops 5637144576 | bytes 17301504 | tf_op jit(solution)/shard_map/pallas_call | solution.py:237
  539.0 14.5 %shard_map.261 = (bf16[1280,512]{1,0:T(8,128)(2,1)}, bf16[1280,512]{1,0:T(8,128)(2,1)}) custom-call(bf16[3072,256]{1,0:T(8,128)(2,1)} %bitcast.99, bf16[3072,2048]{1,0:T(8,128)(2,1)} %bitcast.86, bf16[3072,1024]{1,0:T(8,128)(2,1)} %get-tuple-element.61.gelu_ref.refs_2_, bf16[3072,2048]{1,0:T(8,128)(2,1)} %bitcast.87, bf16[640,512]{1,0:T(8,128)(2,1)} %copy-done.17, ...), custom_call_target="tpu_custom_call" | custom-call | flops 8053063680 | bytes 20447232 | tf_op jit(solution)/shard_map/pallas_call | solution.py:237
  557.6 17.4 %all-gather.12.cloned.1.call-done = bf16[4,768,512]{2,1,0:T(8,128)(2,1)} async-done(((bf16[4,192,512]{2,1,0:T(8,128)(2,1)}), bf16[4,768,512]{2,1,0:T(8,128)(2,1)}) %all-gather.12.cloned.1.call-update) | async-done | bytes 3145744 | tf_op jit(solution)/shard_map/all_gather | solution.py:556
  575.0 19.2 %shard_map.258 = (bf16[512,1792]{1,0:T(8,128)(2,1)}, bf16[512,1792]{1,0:T(8,128)(2,1)}) custom-call(bf16[3072,2048]{1,0:T(8,128)(2,1)} %get-tuple-element.58.h_attn_ref.refs_0_.refs_4_, bf16[3072,768]{1,0:T(8,128)(2,1)} %bitcast.93, bf16[3072,2048]{1,0:T(8,128)(2,1)} %get-tuple-element.59.h_mlp_ref.refs_2_.refs_5_, ...), custom_call_target="tpu_custom_call" | custom-call | flops 11274289152 | bytes 45613056 | tf_op jit(solution)/shard_map/pallas_call | solution.py:237
  597.6 6.3 convert_reduce_fusion
  605.7 11.9 %shard_map.262 = (f32[256,512]{1,0:T(8,128)}, f32[1024,512]{1,0:T(8,128)}) custom-call(bf16[3072,256]{1,0:T(8,128)(2,1)} %bitcast.100, bf16[3072,2048]{1,0:T(8,128)(2,1)} %bitcast.88, bf16[3072,1024]{1,0:T(8,128)(2,1)} %get-tuple-element.61.gelu_ref.refs_2_, bf16[1280,512]{1,0:T(8,128)(2,1)} %collective-permute-done.44.refs_3_, ...), custom_call_target="tpu_custom_call" | custom-call | flops 4026531840 | bytes 17301504 | tf_op jit(solution)/shard_map/pallas_call | solution.py:237
  617.7 20.6 %collective-permute-done.40.refs_4_ = bf16[512,1792]{1,0:T(8,128)(2,1)} collective-permute-done((bf16[512,1792]{1,0:T(8,128)(2,1)}, bf16[512,1792]{1,0:T(8,128)(2,1)}, u32[]{:S(2)}, u32[]{:S(2)}) %collective-permute-start.40) | collective-permute-done | bytes 1835040 | tf_op jit(solution)/shard_map/ppermute | solution.py:461
  638.3 15.0 %shard_map.259 = (f32[512,768]{1,0:T(8,128)}, f32[512,1024]{1,0:T(8,128)}) custom-call(bf16[3072,2048]{1,0:T(8,128)(2,1)} %get-tuple-element.58.h_attn_ref.refs_0_.refs_4_, bf16[3072,768]{1,0:T(8,128)(2,1)} %bitcast.94, bf16[3072,2048]{1,0:T(8,128)(2,1)} %get-tuple-element.59.h_mlp_ref.refs_2_.refs_5_, ...), custom_call_target="tpu_custom_call" | custom-call | flops 5637144576 | bytes 39321600 | tf_op jit(solution)/shard_map/pallas_call | solution.py:237
  657.4 6.2 shard_map.255.rest_0_
  665.3 6.2 shard_map.256
  671.5 10.0 %shard_map.249 = bf16[8,4,2,192,512]{4,3,2,1,0:T(8,128)(2,1)} custom-call(s32[3]{0:T(128)} %pad_add_fusion.place_ref, bf16[8,4,192,512]{3,2,1,0:T(8,128)(2,1)} %bitcast.108, bf16[8,4,192,512]{3,2,1,0:T(8,128)(2,1)} %bitcast.24.other_ref), custom_call_target="tpu_custom_call" | custom-call | flops 6291456 | bytes 25165824 | tf_op jit(solution)/shard_map/pallas_call | solution.py:176
  (232 shorter events, 154.2 us)
Async XLA Ops:
  7.2 155.8 %all-gather.6.cloned.1.call-start = ((), (), s32[]{:S(2)}) async-start(), calls=%async_computation.3 | async-start | bytes 14155776 | tf_op jit(solution)/shard_map/all_gather | solution.py:523
  8.8 21.6 %collective-permute-start = (bf16[2,192,512]{2,1,0:T(8,128)(2,1)S(1)}, bf16[2,192,512]{2,1,0:T(8,128)(2,1)S(1)}, u32[]{:S(2)}, u32[]{:S(2)}) collective-permute-start(bf16[2,192,512]{2,1,0:T(8,128)(2,1)S(1)} %get-tuple-element.123), channel_id=1, source_target_pairs={{0,24},{8,0},{16,8},{24,16},{1,25},{9,1},{17,9},{25,17},{2,26},{10... | collective-permute-start | bytes 1179656 | tf_op jit(solution)/shard_map/ppermute | solution.py:461
  13.5 20.3 %collective-permute-start.2 = (bf16[2,192,512]{2,1,0:T(8,128)(2,1)S(1)}, bf16[2,192,512]{2,1,0:T(8,128)(2,1)S(1)}, u32[]{:S(2)}, u32[]{:S(2)}) collective-permute-start(bf16[2,192,512]{2,1,0:T(8,128)(2,1)S(1)} %get-tuple-element.121), channel_id=1, source_target_pairs={{0,8},{8,16},{16,24},{24,0},{1,9},{9,17},{17,25},{25,1},{2,10},{10... | collective-permute-start | bytes 1179656 | tf_op jit(solution)/shard_map/ppermute | solution.py:461
  36.0 236.5 %all-gather.10.cloned.1.call-start = ((), (), s32[]{:S(2)}) async-start(), calls=%async_computation.6 | async-start | bytes 14155776 | tf_op jit(solution)/shard_map/all_gather | solution.py:524
  38.8 19.6 %collective-permute-start.21 = (bf16[2,192,512]{2,1,0:T(8,128)(2,1)S(1)}, bf16[2,192,512]{2,1,0:T(8,128)(2,1)S(1)}, u32[]{:S(2)}, u32[]{:S(2)}) collective-permute-start(bf16[2,192,512]{2,1,0:T(8,128)(2,1)S(1)} %get-tuple-element.117), channel_id=1, source_target_pairs={{0,8},{8,16},{16,24},{24,0},{1,9},{9,17},{17,25},{25,1},{2,10},{10... | collective-permute-start | bytes 1179656 | tf_op jit(solution)/shard_map/ppermute | solution.py:461
  60.6 338.5 %reduce-scatter.4.cloned.1.call-start = ((), (), s32[]{:S(2)}) async-start(), calls=%async_computation.4 | async-start | bytes 7864320 | tf_op jit(solution)/shard_map/reduce_scatter | solution.py:553
  62.1 43.0 %collective-permute-start.6 = (bf16[512,1792]{1,0:T(8,128)(2,1)S(1)}, bf16[512,1792]{1,0:T(8,128)(2,1)S(1)}, u32[]{:S(2)}, u32[]{:S(2)}) collective-permute-start(bf16[512,1792]{1,0:T(8,128)(2,1)S(1)} %pad_maximum_fusion.refs_0_), channel_id=1, source_target_pairs={{0,24},{8,0},{16,8},{24,16},{1,25},{9,1},{17,9},{25,17},{2,26},{10... | collective-permute-start | bytes 5505032 | tf_op jit(solution)/shard_map/ppermute | solution.py:461
  63.3 44.2 %collective-permute-start.8 = (bf16[512,1792]{1,0:T(8,128)(2,1)S(1)}, bf16[512,1792]{1,0:T(8,128)(2,1)S(1)}, u32[]{:S(2)}, u32[]{:S(2)}) collective-permute-start(bf16[512,1792]{1,0:T(8,128)(2,1)S(1)} %pad_maximum_fusion.refs_0_), channel_id=1, source_target_pairs={{0,8},{8,16},{16,24},{24,0},{1,9},{9,17},{17,25},{25,1},{2,10},{10... | collective-permute-start | bytes 5505032 | tf_op jit(solution)/shard_map/ppermute | solution.py:461
  67.2 91.0 %collective-permute-start.10 = (bf16[1280,512]{1,0:T(8,128)(2,1)}, bf16[1280,512]{1,0:T(8,128)(2,1)}, u32[]{:S(2)}, u32[]{:S(2)}) collective-permute-start(bf16[1280,512]{1,0:T(8,128)(2,1)} %constant_dynamic-update-slice_fusion.refs_0_), channel_id=1, source_target_pairs={{0,24},{8,0},{16,8},{24,16},{1,25},{9,1},{17,9},{25,17},{2,26},{10... | collective-permute-start | bytes 3932168 | tf_op jit(solution)/shard_map/ppermute | solution.py:461
  69.5 90.8 %collective-permute-start.12 = (bf16[1280,512]{1,0:T(8,128)(2,1)}, bf16[1280,512]{1,0:T(8,128)(2,1)}, u32[]{:S(2)}, u32[]{:S(2)}) collective-permute-start(bf16[1280,512]{1,0:T(8,128)(2,1)} %constant_dynamic-update-slice_fusion.refs_0_), channel_id=1, source_target_pairs={{0,8},{8,16},{16,24},{24,0},{1,9},{9,17},{17,25},{25,1},{2,10},{10... | collective-permute-start | bytes 3932168 | tf_op jit(solution)/shard_map/ppermute | solution.py:461
  69.7 63.6 %collective-permute-start.3 = (bf16[8,512]{1,0:T(8,128)(2,1)S(1)}, bf16[8,512]{1,0:T(8,128)(2,1)S(1)}, u32[]{:S(2)}, u32[]{:S(2)}) collective-permute-start(bf16[8,512]{1,0:T(8,128)(2,1)S(1)} %select_select_fusion), channel_id=1, source_target_pairs={{0,24},{8,0},{16,8},{24,16},{1,25},{9,1},{17,9},{25,17},{2,26},{10... | collective-permute-start | bytes 24584 | tf_op jit(solution)/shard_map/ppermute | solution.py:461
  105.1 76.6 %collective-permute-start.7 = (bf16[256,1792]{1,0:T(8,128)(2,1)S(1)}, bf16[256,1792]{1,0:T(8,128)(2,1)}, u32[]{:S(2)}, u32[]{:S(2)}) collective-permute-start(bf16[256,1792]{1,0:T(8,128)(2,1)S(1)} %slice.72), channel_id=1, source_target_pairs={{0,24},{8,0},{16,8},{24,16},{1,25},{9,1},{17,9},{25,17},{2,26},{10... | collective-permute-start | bytes 2752520 | tf_op jit(solution)/shard_map/ppermute | solution.py:461
  108.6 73.1 %collective-permute-start.9 = (bf16[256,1792]{1,0:T(8,128)(2,1)}, bf16[256,1792]{1,0:T(8,128)(2,1)}, u32[]{:S(2)}, u32[]{:S(2)}) collective-permute-start(bf16[256,1792]{1,0:T(8,128)(2,1)} %slice.73), channel_id=1, source_target_pairs={{0,8},{8,16},{16,24},{24,0},{1,9},{9,17},{17,25},{25,1},{2,10},{10... | collective-permute-start | bytes 2752520 | tf_op jit(solution)/shard_map/ppermute | solution.py:461
  159.4 70.8 %collective-permute-start.11 = (bf16[1280,256]{1,0:T(8,128)(2,1)S(1)}, bf16[1280,256]{1,0:T(8,128)(2,1)}, u32[]{:S(2)}, u32[]{:S(2)}) collective-permute-start(bf16[1280,256]{1,0:T(8,128)(2,1)S(1)} %slice.74), channel_id=1, source_target_pairs={{0,24},{8,0},{16,8},{24,16},{1,25},{9,1},{17,9},{25,17},{2,26},{10... | collective-permute-start | bytes 1966088 | tf_op jit(solution)/shard_map/ppermute | solution.py:461
  161.5 68.7 %collective-permute-start.13 = (bf16[1280,256]{1,0:T(8,128)(2,1)S(1)}, bf16[1280,256]{1,0:T(8,128)(2,1)}, u32[]{:S(2)}, u32[]{:S(2)}) collective-permute-start(bf16[1280,256]{1,0:T(8,128)(2,1)S(1)} %slice.75), channel_id=1, source_target_pairs={{0,8},{8,16},{16,24},{24,0},{1,9},{9,17},{17,25},{25,1},{2,10},{10... | collective-permute-start | bytes 1966088 | tf_op jit(solution)/shard_map/ppermute | solution.py:461
  271.9 153.5 %reduce-scatter.8.cloned.1.call-start = ((), (), s32[]{:S(2)}) async-start(), calls=%async_computation.9 | async-start | bytes 3932160 | tf_op jit(solution)/shard_map/reduce_scatter | solution.py:553
  347.8 94.0 %reduce-scatter.6.cloned.1.call-start = ((), (), s32[]{:S(2)}) async-start(), calls=%async_computation.7 | async-start | bytes 3932160 | tf_op jit(solution)/shard_map/reduce_scatter | solution.py:553
  396.6 100.8 %all-gather.8.cloned.1.call-start = ((), (), s32[]{:S(2)}) async-start(), calls=%async_computation.5 | async-start | bytes 7864320 | tf_op jit(solution)/shard_map/all_gather | solution.py:556
  401.1 21.0 %collective-permute-start.16 = (bf16[384,512]{1,0:T(8,128)(2,1)S(1)}, bf16[384,512]{1,0:T(8,128)(2,1)S(1)}, u32[]{:S(2)}, u32[]{:S(2)}) collective-permute-start(bf16[384,512]{1,0:T(8,128)(2,1)S(1)} %get-tuple-element.66), channel_id=1, source_target_pairs={{0,16},{8,24},{16,0},{24,8},{1,17},{9,25},{17,1},{25,9},{2,18},{10... | collective-permute-start | bytes 1179656 | tf_op jit(solution)/shard_map/ppermute | solution.py:461
  423.9 132.8 %all-gather.14.cloned.1.call-start = ((), (), s32[]{:S(2)}) async-start(), calls=%async_computation.10 | async-start | bytes 3932160 | tf_op jit(solution)/shard_map/all_gather | solution.py:556
  441.7 133.3 %all-gather.12.cloned.1.call-start = ((), (), s32[]{:S(2)}) async-start(), calls=%async_computation.8 | async-start | bytes 3932160 | tf_op jit(solution)/shard_map/all_gather | solution.py:556
  497.4 174.1 %collective-permute-start.18 = (bf16[8,768,512]{2,1,0:T(8,128)(2,1)}, bf16[8,768,512]{2,1,0:T(8,128)(2,1)}, u32[]{:S(2)}, u32[]{:S(2)}) collective-permute-start(bf16[8,768,512]{2,1,0:T(8,128)(2,1)} %all-gather.8.cloned.1.call-done), channel_id=1, source_target_pairs={{0,1},{1,0},{2,3},{3,2},{4,5},{5,4},{6,7},{7,6},{8,9},{9,8},{10,11... | collective-permute-start | bytes 18874376 | tf_op jit(solution)/shard_map/ppermute | solution.py:471
  516.7 19.4 %collective-permute-start.42 = (bf16[640,512]{1,0:T(8,128)(2,1)}, bf16[640,512]{1,0:T(8,128)(2,1)S(1)}, u32[]{:S(2)}, u32[]{:S(2)}) collective-permute-start(bf16[640,512]{1,0:T(8,128)(2,1)} %get-tuple-element.95), channel_id=1, source_target_pairs={{0,8},{8,16},{16,24},{24,0},{1,9},{9,17},{17,25},{25,1},{2,10},{10... | collective-permute-start | bytes 1966088 | tf_op jit(solution)/shard_map/ppermute | solution.py:461
  516.7 21.4 %collective-permute-start.43 = (bf16[640,512]{1,0:T(8,128)(2,1)}, bf16[640,512]{1,0:T(8,128)(2,1)S(1)}, u32[]{:S(2)}, u32[]{:S(2)}) collective-permute-start(bf16[640,512]{1,0:T(8,128)(2,1)} %get-tuple-element.96), channel_id=1, source_target_pairs={{0,24},{8,0},{16,8},{24,16},{1,25},{9,1},{17,9},{25,17},{2,26},{10... | collective-permute-start | bytes 1966088 | tf_op jit(solution)/shard_map/ppermute | solution.py:461
  532.9 23.8 %collective-permute-start.38 = (bf16[256,1792]{1,0:T(8,128)(2,1)}, bf16[256,1792]{1,0:T(8,128)(2,1)}, u32[]{:S(2)}, u32[]{:S(2)}) collective-permute-start(bf16[256,1792]{1,0:T(8,128)(2,1)} %get-tuple-element.90), channel_id=1, source_target_pairs={{0,8},{8,16},{16,24},{24,0},{1,9},{9,17},{17,25},{25,1},{2,10},{10... | collective-permute-start | bytes 2752520 | tf_op jit(solution)/shard_map/ppermute | solution.py:461
  532.9 23.8 %collective-permute-start.39 = (bf16[256,1792]{1,0:T(8,128)(2,1)}, bf16[256,1792]{1,0:T(8,128)(2,1)S(1)}, u32[]{:S(2)}, u32[]{:S(2)}) collective-permute-start(bf16[256,1792]{1,0:T(8,128)(2,1)} %get-tuple-element.91), channel_id=1, source_target_pairs={{0,24},{8,0},{16,8},{24,16},{1,25},{9,1},{17,9},{25,17},{2,26},{10... | collective-permute-start | bytes 2752520 | tf_op jit(solution)/shard_map/ppermute | solution.py:461
  553.5 40.8 %collective-permute-start.44 = (bf16[1280,512]{1,0:T(8,128)(2,1)}, bf16[1280,512]{1,0:T(8,128)(2,1)}, u32[]{:S(2)}, u32[]{:S(2)}) collective-permute-start(bf16[1280,512]{1,0:T(8,128)(2,1)} %get-tuple-element.97), channel_id=1, source_target_pairs={{0,8},{8,16},{16,24},{24,0},{1,9},{9,17},{17,25},{25,1},{2,10},{10... | collective-permute-start | bytes 3932168 | tf_op jit(solution)/shard_map/ppermute | solution.py:461
  553.5 42.4 %collective-permute-start.45 = (bf16[1280,512]{1,0:T(8,128)(2,1)}, bf16[1280,512]{1,0:T(8,128)(2,1)}, u32[]{:S(2)}, u32[]{:S(2)}) collective-permute-start(bf16[1280,512]{1,0:T(8,128)(2,1)} %get-tuple-element.98), channel_id=1, source_target_pairs={{0,24},{8,0},{16,8},{24,16},{1,25},{9,1},{17,9},{25,17},{2,26},{10... | collective-permute-start | bytes 3932168 | tf_op jit(solution)/shard_map/ppermute | solution.py:461
  556.7 100.7 %collective-permute-start.31 = (bf16[4,768,512]{2,1,0:T(8,128)(2,1)}, bf16[4,768,512]{2,1,0:T(8,128)(2,1)}, u32[]{:S(2)}, u32[]{:S(2)}) collective-permute-start(bf16[4,768,512]{2,1,0:T(8,128)(2,1)} %all-gather.14.cloned.1.call-done), channel_id=1, source_target_pairs={{0,1},{1,0},{2,3},{3,2},{4,5},{5,4},{6,7},{7,6},{8,9},{9,8},{10,11... | collective-permute-start | bytes 9437192 | tf_op jit(solution)/shard_map/ppermute | solution.py:471
  575.0 88.6 %collective-permute-start.26 = (bf16[4,768,512]{2,1,0:T(8,128)(2,1)}, bf16[4,768,512]{2,1,0:T(8,128)(2,1)S(1)}, u32[]{:S(2)}, u32[]{:S(2)}) collective-permute-start(bf16[4,768,512]{2,1,0:T(8,128)(2,1)} %all-gather.12.cloned.1.call-done), channel_id=1, source_target_pairs={{0,1},{1,0},{2,3},{3,2},{4,5},{5,4},{6,7},{7,6},{8,9},{9,8},{10,11... | collective-permute-start | bytes 9437192 | tf_op jit(solution)/shard_map/ppermute | solution.py:471
  594.2 44.0 %collective-permute-start.40 = (bf16[512,1792]{1,0:T(8,128)(2,1)}, bf16[512,1792]{1,0:T(8,128)(2,1)}, u32[]{:S(2)}, u32[]{:S(2)}) collective-permute-start(bf16[512,1792]{1,0:T(8,128)(2,1)} %get-tuple-element.92), channel_id=1, source_target_pairs={{0,8},{8,16},{16,24},{24,0},{1,9},{9,17},{17,25},{25,1},{2,10},{10... | collective-permute-start | bytes 5505032 | tf_op jit(solution)/shard_map/ppermute | solution.py:461
  595.8 42.5 %collective-permute-start.41 = (bf16[512,1792]{1,0:T(8,128)(2,1)}, bf16[512,1792]{1,0:T(8,128)(2,1)}, u32[]{:S(2)}, u32[]{:S(2)}) collective-permute-start(bf16[512,1792]{1,0:T(8,128)(2,1)} %get-tuple-element.93), channel_id=1, source_target_pairs={{0,24},{8,0},{16,8},{24,16},{1,25},{9,1},{17,9},{25,17},{2,26},{10... | collective-permute-start | bytes 5505032 | tf_op jit(solution)/shard_map/ppermute | solution.py:461
  (57 other events, 907.1 us)
Sparse Core Ops, SparseCore 0:
  36.1 63.3 all-gather.5
  101.1 65.0 all-gather.9
  272.0 60.6 reduce-scatter.3
  347.9 34.9 reduce-scatter.7
  396.7 34.9 reduce-scatter.5
  433.7 63.6 all-gather.7
  499.0 37.0 all-gather.13
  537.7 37.2 all-gather.11

commit v8 on v5

--- a/solution.py
+++ b/solution.py
@@ -60,10 +60,8 @@
 def attn_fwd_kernel(qkv_ref, ctx_ref, *, scale, span):
     seq_len, width = ctx_ref.shape[1:]
     for end in range(span, seq_len + 1, span):
-        @pl.loop(0, span // Q_ROWS)
-        def _(step, end=end):
-            start = pl.multiple_of(end - span + step * Q_ROWS, Q_ROWS)
-            rows = pl.ds(start, Q_ROWS)
+        for start in range(end - span, end, Q_ROWS):
+            rows = slice(start, start + Q_ROWS)
             probs = causal_probs(qkv_ref[0, rows, :width], qkv_ref[0, :end, width:2 * width], start, scale).astype(jnp.bfloat16)
             ctx_ref[0, rows, :] = dot(probs, qkv_ref[0, :end, 2 * width:], NN).astype(jnp.bfloat16)
 
@@ -83,10 +81,8 @@
         db_ref[0, :, col:col + width] += sublane_sum(grad.astype(jnp.float32))
 
     for end in range(span, seq_len + 1, span):
-        @pl.loop(0, span // Q_ROWS)
-        def _(step, end=end):
-            start = pl.multiple_of(end - span + step * Q_ROWS, Q_ROWS)
-            rows = pl.ds(start, Q_ROWS)
+        for start in range(end - span, end, Q_ROWS):
+            rows = slice(start, start + Q_ROWS)
             q_rows, keys = qkv_ref[0, rows, :width], qkv_ref[0, :end, width:2 * width]
             dctx = dctx_ref[0, rows, :]
             probs = causal_probs(q_rows, keys, start, scale)
@@ -126,18 +122,20 @@
             cost_estimate=pl.CostEstimate(flops=8 * n_seq * pairs * width, bytes_accessed=8 * n_seq * seq_len * width, transcendentals=n_seq * pairs),
         )(qkv)
 
-    def backward(qkv, dctx, index):
+    def backward(qkv, dctx, index, into):
+        kernel = functools.partial(attn_bwd_kernel, half=half, scale=scale, span=span)
         return pl.pallas_call(
-            functools.partial(attn_bwd_kernel, half=half, scale=scale, span=span),
+            (lambda *refs: kernel(*refs[:5], *refs[5 + len(into):])),
             grid=(1,),
-            in_specs=[seq_spec(3 * width, index), seq_spec(width, index), tab_spec, tab_spec, tab_spec],
-            out_specs=[seq_spec(3 * width), pl.BlockSpec((1, 8, 3 * width), lambda s: (s, 0, 0))],
-            out_shape=[jax.ShapeDtypeStruct((1, seq_len, 3 * width), jnp.bfloat16), jax.ShapeDtypeStruct((1, 8, 3 * width), jnp.float32)],
+            in_specs=[seq_spec(3 * width, index), seq_spec(width, index), tab_spec, tab_spec, tab_spec] + [pl.BlockSpec(memory_space=pl.ANY)] * len(into),
+            out_specs=[seq_spec(3 * width, index), pl.BlockSpec((1, 8, 3 * width), lambda s: (s, 0, 0))],
+            input_output_aliases={5: 0} if into else {},
+            out_shape=[jax.ShapeDtypeStruct((n_seq, seq_len, 3 * width), jnp.bfloat16), jax.ShapeDtypeStruct((1, 8, 3 * width), jnp.float32)],
             scratch_shapes=[acc_scratch, acc_scratch],
             compiler_params=params,
             name="ab",
             cost_estimate=pl.CostEstimate(flops=20 * pairs * width, bytes_accessed=14 * seq_len * width, transcendentals=pairs),
-        )(qkv, dctx, *tables)
+        )(qkv, dctx, *tables, *into)
 
     return forward, backward
 
@@ -195,6 +193,68 @@
         input_output_aliases={} if out is None else {len(operands) - 1: 0},
         cost_estimate=pl.CostEstimate(flops=groups * tokens * width, bytes_accessed=4 * groups * tokens * width, transcendentals=0),
     )(*operands)
+
+
+def grad_kernel(*refs, blocks, moving, splits):
+    acc_ref = refs[-1]
+    n_out = sum(len(parts) for parts in splits)
+    ins, outs = refs[:-1 - n_out], list(refs[-1 - n_out:-1])
+    step = pl.program_id(0)
+
+    @pl.when(step == 0)
+    def _():
+        acc_ref[...] = jnp.zeros(acc_ref.shape, jnp.float32)
+
+    for index, terms in enumerate(blocks):
+        for lhs, rhs, row, column in terms:
+            part = dot(ins[lhs][...], ins[rhs][...], TN)
+            acc_ref[index, row:row + part.shape[0], column:column + part.shape[1]] += part
+
+    @pl.when(step == pl.num_programs(0) - 1)
+    def _():
+        for index, adds in enumerate(moving):
+            for ref, row in adds:
+                at = slice(row, row + ins[ref].shape[0])
+                acc_ref[index, at, :] += ins[ref][...].astype(jnp.float32)
+        for index, parts in enumerate(splits):
+            for rows, cols in parts:
+                out = outs.pop(0)
+                out[...] = acc_ref[index, rows, cols].astype(out.dtype)
+
+
+def grad_call(blocks, shape, moving, splits, dtype, rows=512):
+    ins, specs, keys = [], [], {}
+
+    def operand(array, block, width):
+        key = (id(array), block, width)
+        if key not in keys:
+            keys[key] = len(ins)
+            ins.append(array)
+            specs.append(pl.BlockSpec((rows, width), lambda s, b=block: (s, b)))
+        return keys[key]
+
+    count = blocks[0][0][0].shape[0]
+    terms = [[(operand(lhs, lb, lw), operand(rhs, rb, rw), row, col) for lhs, lb, lw, rhs, rb, rw, row, col in block] for block in blocks]
+    adds = []
+    for block in moving:
+        found = []
+        for array, row in block:
+            found.append((len(ins), row))
+            ins.append(array)
+            specs.append(pl.BlockSpec(array.shape, lambda s: (0, 0)))
+        adds.append(found)
+    span = lambda at, size: len(range(*at.indices(size)))
+    shapes = [(span(r, shape[0]), span(c, shape[1])) for parts in splits for r, c in parts]
+    return pl.pallas_call(
+        functools.partial(grad_kernel, blocks=terms, moving=adds, splits=splits),
+        grid=(count // rows,),
+        in_specs=specs,
+        out_specs=[pl.BlockSpec(one, lambda s: (0, 0)) for one in shapes],
+        out_shape=[jax.ShapeDtypeStruct(one, dtype) for one in shapes],
+        scratch_shapes=[pltpu.VMEM((len(blocks), *shape), jnp.float32)],
+        compiler_params=pltpu.CompilerParams(dimension_semantics=("arbitrary",), vmem_limit_bytes=60 * MIB),
+        cost_estimate=pl.CostEstimate(flops=2 * len(blocks) * count * shape[0] * shape[1], bytes_accessed=sum(2 * count * spec.block_shape[1] for spec in specs), transcendentals=0),
+    )(*ins)
 
 
 def split_width(value, out_refs):
@@ -407,18 +467,13 @@
         blocks[antipode] = [shift(low, 1), shift(high, -1)]
         return [piece for r in range(tx_size) for piece in blocks[r]]
 
-    def ring_scatter(make_part, rows):
-        half = rows // 2
-        far = make_part(antipode).astype(jnp.bfloat16)
-        moving_up, moving_down = shift(far[:half], -1), shift(far[half:], 1)
-        moving_up = jnp.pad(moving_up, ((0, rows - half), (0, 0)))
-        moving_down = jnp.pad(moving_down, ((half, 0), (0, 0)))
-        for hops in range(antipode - 1, 0, -1):
-            up = make_part(hops) + moving_up.astype(jnp.float32)
-            down = make_part(tx_size - hops) + moving_down.astype(jnp.float32)
-            up, down = up.astype(jnp.bfloat16), down.astype(jnp.bfloat16)
-            moving_up, moving_down = shift(up, -1), shift(down, 1)
-        return lambda own, low, high: own + moving_up[low:high].astype(jnp.float32) + moving_down[low:high].astype(jnp.float32)
+    def ring_scatter(make_blocks, shape):
+        whole, half = slice(None), shape[0] // 2
+        assert tx_size == 4
+        low, high = grad_call([make_blocks(2)], shape, [[]], [[(slice(0, half), whole), (slice(half, None), whole)]], jnp.bfloat16)
+        low, high = shift(low, -1), shift(high, 1)
+        up, down = grad_call([make_blocks(1), make_blocks(3)], shape, [[(low, 0)], [(high, half)]], [[(whole, whole)], [(whole, whole)]], jnp.bfloat16)
+        return [(shift(up, -1), 0), (shift(down, 1), 0)]
 
     def body(x_act, cot_out, ln1_gain, ln1_bias, ln2_gain, ln2_bias, w_qkv, b_qkv, w_dense, b_dense, w_up, b_up, w_down, b_down):
         batch, seq_len, d_local = x_act.shape
@@ -481,26 +536,21 @@
             d_pre_kernel, [cot_group, pre_act], w_back,
             [(head, jnp.bfloat16), (ff_width, jnp.bfloat16), ((8, ff_width), jnp.float32)], (0, n_tok), 2 * n_tok * back_size)
         d_ctx, d_b_up = d_ctx.reshape(n_seq, seq_len, head), d_b_up.sum(0)
-        d_qkv, d_b_qkv, d_ln, dx_act = [], [], [], None
+        d_b_qkv, d_ln, dx_act = [], [], None
         for s in chunks:
-            d_qkv_seq, d_b_seq = attn_bwd(qkv_seq, d_ctx, s)
-            d_qkv.append(d_qkv_seq.reshape(seq_len, qkv_width))
+            d_qkv, d_b_seq = attn_bwd(qkv_seq, d_ctx, s, (d_qkv, sums) if s else ())
             d_b_qkv.append(d_b_seq.sum((0, 1)))
             a6_part, sums = tile_call(
-                d_h_kernel, [d_qkv[s], d_pre, x_group], [small, *w_in],
+                d_h_kernel, [d_qkv.reshape(n_tok, qkv_width), d_pre, x_group], [small, *w_in],
                 [(d_model, jnp.bfloat16), ((4, 8, d_model), jnp.float32)], (s * seq_len, seq_len), 2 * seq_len * in_size)
             d_ln.append(sums)
             value_a6 = lax.psum_scatter(a6_part, 'ty', scatter_dimension=0, tiled=True)
             parts = row_call(finish_dx_kernel, tx_size, s, own, x_rows, value_a6, cot_rows)
             block = to_width(parts)
-            if s < n_seq - 1:
-                blocks = [block] + [along(block, hops) for hops in range(1, ty_size // 2)]
-                blocks = blocks + [partner(piece) for piece in blocks]
-                dx_act = place_call(place_pieces_kernel, place, blocks, dx_act, s, n_seq, seq_len)
-            else:
-                full = lax.all_gather(block, 'ty', axis=1, tiled=True)
-                dx_act = place_call(place_kernel, place, [full], dx_act, s, n_seq, seq_len)
-        d_qkv = jnp.concatenate(d_qkv, axis=0)
+            blocks = [block] + [along(block, hops) for hops in range(1, ty_size // 2)]
+            blocks = blocks + [partner(piece) for piece in blocks]
+            dx_act = place_call(place_pieces_kernel, place, blocks, dx_act, s, n_seq, seq_len)
+        d_qkv = d_qkv.reshape(n_tok, qkv_width)
 
         d_ln = sum(d_ln).sum(1).reshape(4, tx_size, d_local)
         d_bias = jnp.concatenate([sum(d_b_qkv), d_b_up]).reshape(4, -1)
@@ -511,15 +561,14 @@
         d_ln = small_sum(got[:, :d_local], 'ty', ty_size)
         d_b_out = cot_out.astype(jnp.float32).sum((0, 1))
 
-        cols = lambda act, r: act[:, r * d_local:(r + 1) * d_local]
-        inner = jnp.concatenate([context, gelu_out], axis=1)
-        add_back = ring_scatter(lambda r: dot(inner, cols(cot_group, r), TN), inner.shape[1])
-        add_up = ring_scatter(lambda r: dot(cols(h_mlp, r), d_pre, TN), d_local)
-        add_qkv = ring_scatter(lambda r: dot(cols(h_attn, r), d_qkv, TN), d_local)
-        d_w_dense = add_back(dot(context, cols(cot_group, 0), TN), 0, head)
-        d_w_down = add_back(dot(gelu_out, cols(cot_group, 0), TN), head, inner.shape[1])
-        d_w_up = add_up(dot(cols(h_mlp, 0), d_pre, TN), 0, d_local)
-        d_w_qkv = add_qkv(dot(cols(h_attn, 0), d_qkv, TN), 0, d_local)
+        in_shape, back_shape = (d_local, qkv_width + ff_width), (head + ff_width, d_local)
+        in_blocks = lambda r: [(h_attn, r, d_local, d_qkv, 0, qkv_width, 0, 0), (h_mlp, r, d_local, d_pre, 0, ff_width, 0, qkv_width)]
+        back_blocks = lambda r: [(context, 0, head, cot_group, r, d_local, 0, 0), (gelu_out, 0, ff_width, cot_group, r, d_local, head, 0)]
+        add_back = ring_scatter(back_blocks, back_shape)
+        add_in = ring_scatter(in_blocks, in_shape)
+        whole = slice(None)
+        d_w_dense, d_w_down = grad_call([back_blocks(0)], back_shape, [add_back], [[(slice(0, head), whole), (slice(head, None), whole)]], jnp.float32)
+        d_w_qkv, d_w_up = grad_call([in_blocks(0)], in_shape, [add_in], [[(whole, slice(0, qkv_width)), (whole, slice(qkv_width, None))]], jnp.float32)
         y_out = y_out.reshape(batch, seq_len, d_local)
         return (y_out, dx_act, d_ln[0], d_ln[1], d_ln[2], d_ln[3], d_w_qkv.reshape(w_qkv.shape), d_bias[:qkv_width].reshape(b_qkv.shape), d_w_dense, d_b_out, d_w_up, d_bias[qkv_width:], d_w_down, d_b_out)
 

time: 676 us -> 687 us (1.016)
  matrix products: 87.2 us -> 0 us
  Pallas kernels: 213 us -> 288 us
  waiting for transfers between devices: 236 us -> 256 us
    dot_general x13 -> x0, matrix products: 87.2 us -> none  [dot(): return lax.dot_general(a, b, dims, preferred_element_type=jnp.float32)]
    pallas_call x2 -> x8, Pallas kernels: 27.7 us -> 109 us  [the longest x6 83.9 us: grad_call(): pl.pallas_call(functools.partial(grad_kernel, blocks=terms, moving=adds,...]
    ppermute x41 -> x37, waiting for transfers between devices: 196 us -> 217 us  [shift(): lax.ppermute(value, 'tx', [(s, (s - hops) % tx_size) for s in range(tx_si...]
    reduce_scatter x1, waiting for transfers between devices: 18.2 us -> 0.02 us  [body(): lax.psum_scatter(y_part.reshape(n_tok, d_model), 'ty', scatter_dimension=...]
    ppermute x3 -> x6, waiting for transfers between devices: 18.5 us -> 34 us  [along(): lax.ppermute(value, 'ty', [(s, (s - 2 * hops) % ty_size) for s in range(t...]
    ppermute x41 -> x37, starting transfers between devices: 58.4 us -> 49.2 us  [shift(): lax.ppermute(value, 'tx', [(s, (s - hops) % tx_size) for s in range(tx_si...]
    ppermute x3 -> x6, starting transfers between devices: 8.27 us -> 16.7 us  [along(): lax.ppermute(value, 'ty', [(s, (s - 2 * hops) % ty_size) for s in range(t...]
    unnamed x110 -> x82, local copies, waits for them, and re-layouts: 13 us -> 14.7 us
  transfers between devices with their start and end apart: 58 -> 60, of which waited for: 22 -> 23; matrix products, arithmetic and copies ran while one was open for 18% -> 5% of each run, Pallas kernels for 21% -> 41%
where the time goes in v8:
time: 687 us; the launch traced here: 678 us
  Pallas kernels  288 us (42%)
  waiting for transfers between devices  256 us (37%)
  starting transfers between devices  71.9 us (10%)
  other arithmetic  25.9 us (4%)
  local copies, waits for them, and re-layouts  21.8 us (3%)
  between operations  15.2 us (2%)
    ppermute x37, waiting for transfers between devices, shift(): lax.ppermute(value, 'tx', [(s, (s - hops) % tx_size) for s in range(tx_si...  217 us
    pallas_call x6, Pallas kernels, tile_call(): pl.pallas_call(kernel, grid=(count // rows,), in_specs=in_specs, out_spec...  144 us
    pallas_call x6, Pallas kernels, grad_call(): pl.pallas_call(functools.partial(grad_kernel, blocks=terms, moving=adds,...  83.9 us
    ppermute x37, starting transfers between devices, shift(): lax.ppermute(value, 'tx', [(s, (s - hops) % tx_size) for s in range(tx_si...  49.2 us
    ppermute x6, waiting for transfers between devices, along(): lax.ppermute(value, 'ty', [(s, (s - 2 * hops) % ty_size) for s in range(t...  34 us
    pallas_call x2, Pallas kernels, backward(): pl.pallas_call(lambda *refs: kernel(*refs[:5], *refs[5 + len(into):]), gr...  24.8 us
    pallas_call x3, Pallas kernels, place_call(): pl.pallas_call(functools.partial(kernel, chunk=chunk, n_seq=n_seq), in_sp...  21.7 us
    ppermute x6, starting transfers between devices, along(): lax.ppermute(value, 'ty', [(s, (s - 2 * hops) % ty_size) for s in range(t...  16.7 us
  transfers between devices with their start and end apart: 60, of which 23 were waited for; matrix products, arithmetic and copies ran while one was open for 5% of the time, Pallas kernels for 41%

profile of v8, /device:TPU:98, one launch (start us, length us, event | category | flops | bytes accessed | tf_op | source)
XLA Modules:
  0.0 678.2 jit_solution(8216277315126393729)
XLA Ops:
  14.6 15.8 %collective-permute-done = bf16[2,192,512]{2,1,0:T(8,128)(2,1)S(1)} collective-permute-done((bf16[2,192,512]{2,1,0:T(8,128)(2,1)S(1)}, bf16[2,192,512]{2,1,0:T(8,128)(2,1)S(1)}, u32[]{:S(2)}, u32[]{:S(2)}) %collective-permute-start) | collective-permute-done | bytes 393248 | tf_op jit(solution)/shard_map/ppermute | solution.py:444
  38.9 10.1 %collective-permute-done.17 = bf16[2,192,512]{2,1,0:T(8,128)(2,1)} collective-permute-done((bf16[2,192,512]{2,1,0:T(8,128)(2,1)S(1)}, bf16[2,192,512]{2,1,0:T(8,128)(2,1)}, u32[]{:S(2)}, u32[]{:S(2)}) %collective-permute-start.17) | collective-permute-done | bytes 393248 | tf_op jit(solution)/shard_map/ppermute | solution.py:444
  51.4 6.4 collective-permute-done.19
  70.2 34.9 %collective-permute-done.6.refs_1_ = bf16[512,1792]{1,0:T(8,128)(2,1)S(1)} collective-permute-done((bf16[512,1792]{1,0:T(8,128)(2,1)S(1)}, bf16[512,1792]{1,0:T(8,128)(2,1)S(1)}, u32[]{:S(2)}, u32[]{:S(2)}) %collective-permute-start.6) | collective-permute-done | bytes 1835040 | tf_op jit(solution)/shard_map/ppermute | solution.py:444
  108.6 24.7 %collective-permute-done.3 = bf16[8,512]{1,0:T(8,128)(2,1)S(1)} collective-permute-done((bf16[8,512]{1,0:T(8,128)(2,1)S(1)}, bf16[8,512]{1,0:T(8,128)(2,1)S(1)}, u32[]{:S(2)}, u32[]{:S(2)}) %collective-permute-start.3) | collective-permute-done | bytes 8224 | tf_op jit(solution)/shard_map/ppermute | solution.py:444
  134.3 18.5 %collective-permute-done.4 = bf16[8,512]{1,0:T(8,128)(2,1)S(1)} collective-permute-done((bf16[8,512]{1,0:T(8,128)(2,1)S(1)}, bf16[8,512]{1,0:T(8,128)(2,1)S(1)}, u32[]{:S(2)}, u32[]{:S(2)}) %collective-permute-start.4) | collective-permute-done | bytes 8224 | tf_op jit(solution)/shard_map/ppermute | solution.py:444
  164.3 18.7 %shard_map.245 = (bf16[3072,2048]{1,0:T(8,128)(2,1)}, bf16[3072,2048]{1,0:T(8,128)(2,1)}) custom-call(bf16[3072,2048]{1,0:T(8,128)(2,1)} %bitcast.91, f32[8,2048]{1,0:T(8,128)} %maximum_convert_fusion.small_ref), custom_call_target="tpu_custom_call" | custom-call | flops 100663296 | bytes 37781504 | tf_op jit(solution)/shard_map/pallas_call | solution.py:423
  183.0 32.8 %shard_map.246 = (bf16[3072,768]{1,0:T(8,128)(2,1)}, bf16[3072,1024]{1,0:T(8,128)(2,1)}, bf16[3072,1024]{1,0:T(8,128)(2,1)}) custom-call(bf16[3072,2048]{1,0:T(8,128)(2,1)} %get-tuple-element.54.h_attn_ref.refs_0_.refs_4_, bf16[3072,2048]{1,0:T(8,128)(2,1)} %get-tuple-element.55.h_mlp_ref.refs_2_.refs_5_, f32[1536,128]{1,0:T(8,128)} %get-tuple-element.128.cos_ref.refs_2_, ...), custom_call_target="tpu_custom_call" | custom-call | flops 22548578304 | bytes 52170240 | tf_op jit(solution)/shard_map/pallas_call | solution.py:423
  215.9 9.8 %af.1 = bf16[2,1536,256]{2,1,0:T(8,128)(2,1)} custom-call(bf16[2,1536,768]{2,1,0:T(8,128)(2,1)} %bitcast.121), custom_call_target="tpu_custom_call" | custom-call | flops 4831838208 | bytes 6291456 | tf_op jit(solution)/shard_map/af/pallas_call | solution.py:114
  225.7 22.0 %shard_map.247 = bf16[8,2,192,2048]{3,2,1,0:T(8,128)(2,1)} custom-call(bf16[3072,256]{1,0:T(8,128)(2,1)} %bitcast.87, bf16[3072,1024]{1,0:T(8,128)(2,1)} %get-tuple-element.57.gelu_ref.refs_2_, bf16[1280,512]{1,0:T(8,128)(2,1)} %copy-done.26, bf16[1280,512]{1,0:T(8,128)(2,1)} %copy-done.19, bf16[1280,256]{1,0:T(8,128)(2,1)} %collective-permute-done.11.refs_2_, ...), custom_call_target="tpu_custom_call" | custom-call | flops 16106127360 | bytes 25690112 | tf_op jit(solution)/shard_map/pallas_call | solution.py:423
  248.0 26.9 %shard_map.250 = (bf16[3072,256]{1,0:T(8,128)(2,1)}, bf16[3072,1024]{1,0:T(8,128)(2,1)}, f32[8,1024]{1,0:T(8,128)}) custom-call(bf16[3072,2048]{1,0:T(8,128)(2,1)} %bitcast.76, bf16[3072,1024]{1,0:T(8,128)(2,1)} %get-tuple-element.62.pre_ref, bf16[1280,512]{1,0:T(8,128)(2,1)} %copy-done.26, bf16[1280,512]{1,0:T(8,128)(2,1)} %copy-done.19, ...), custom_call_target="tpu_custom_call" | custom-call | flops 16106127360 | bytes 31997952 | tf_op jit(solution)/shard_map/pallas_call | solution.py:423
  274.9 12.3 %ab.2 = (bf16[2,1536,768]{2,1,0:T(8,128)(2,1)}, f32[1,8,768]{2,1,0:T(8,128)}) custom-call(bf16[2,1536,768]{2,1,0:T(8,128)(2,1)} %bitcast.122, bf16[2,1536,256]{2,1,0:T(8,128)(2,1)} %bitcast.124, f32[1536,128]{1,0:T(8,128)} %get-tuple-element.128.cos_ref.refs_2_, f32[1536,128]{1,0:T(8,128)} %get-tuple-element.127.lo_ref.refs_3_, ...), custom_call_target="tpu_custom_call" | custom-call | flops 6039797760 | bytes 5505024 | tf_op jit(solution)/shard_map/ab/pallas_call | solution.py:127
  287.2 22.2 %shard_map.251 = (bf16[1536,2048]{1,0:T(8,128)(2,1)}, f32[4,8,2048]{2,1,0:T(8,128)}) custom-call(bf16[3072,768]{1,0:T(8,128)(2,1)} %bitcast.81, bf16[3072,1024]{1,0:T(8,128)(2,1)} %get-tuple-element.65.d_pre_ref.refs_3_, bf16[3072,2048]{1,0:T(8,128)(2,1)} %bitcast.92, f32[8,2048]{1,0:T(8,128)} %maximum_convert_fusion.small_ref, bf16[512,1792]{1,0:T(8,128)(2,1)} %copy-done.7, ...), custom_call_target="tpu_custom_call" | custom-call | flops 11274289152 | bytes 25591808 | tf_op jit(solution)/shard_map/pallas_call | solution.py:423
  309.6 12.5 %ab.3 = (bf16[2,1536,768]{2,1,0:T(8,128)(2,1)}, f32[1,8,768]{2,1,0:T(8,128)}) custom-call(bf16[2,1536,768]{2,1,0:T(8,128)(2,1)} %bitcast.123, bf16[2,1536,256]{2,1,0:T(8,128)(2,1)} %bitcast.125, f32[1536,128]{1,0:T(8,128)} %get-tuple-element.128.cos_ref.refs_2_, f32[1536,128]{1,0:T(8,128)} %get-tuple-element.127.lo_ref.refs_3_, ...), custom_call_target="tpu_custom_call", output_to_operand_aliasing={{0}: (5, {})} | custom-call | flops 6039797760 | bytes 5505024 | tf_op jit(solution)/shard_map/ab/pallas_call | solution.py:127
  322.1 21.6 %shard_map.252 = (bf16[1536,2048]{1,0:T(8,128)(2,1)}, f32[4,8,2048]{2,1,0:T(8,128)}) custom-call(bf16[3072,768]{1,0:T(8,128)(2,1)} %bitcast.82, bf16[3072,1024]{1,0:T(8,128)(2,1)} %get-tuple-element.65.d_pre_ref.refs_3_, bf16[3072,2048]{1,0:T(8,128)(2,1)} %bitcast.93, f32[8,2048]{1,0:T(8,128)} %maximum_convert_fusion.small_ref, bf16[512,1792]{1,0:T(8,128)(2,1)} %copy-done.7, ...), custom_call_target="tpu_custom_call" | custom-call | flops 11274289152 | bytes 25591808 | tf_op jit(solution)/shard_map/pallas_call | solution.py:423
  352.0 7.8 %collective-permute-done.14 = bf16[384,512]{1,0:T(8,128)(2,1)S(1)} collective-permute-done((bf16[384,512]{1,0:T(8,128)(2,1)S(1)}, bf16[384,512]{1,0:T(8,128)(2,1)S(1)}, u32[]{:S(2)}, u32[]{:S(2)}) %collective-permute-start.14) | collective-permute-done | bytes 393248 | tf_op jit(solution)/shard_map/ppermute | solution.py:444
  359.9 6.8 collective-permute-done.15
  368.0 12.7 %shard_map.257 = (bf16[256,1792]{1,0:T(8,128)(2,1)}, bf16[256,1792]{1,0:T(8,128)(2,1)}) custom-call(bf16[3072,2048]{1,0:T(8,128)(2,1)} %get-tuple-element.54.h_attn_ref.refs_0_.refs_4_, bf16[3072,768]{1,0:T(8,128)(2,1)} %bitcast.83, bf16[3072,2048]{1,0:T(8,128)(2,1)} %get-tuple-element.55.h_mlp_ref.refs_2_.refs_5_, ...), custom_call_target="tpu_custom_call" | custom-call | flops 5637144576 | bytes 17301504 | tf_op jit(solution)/shard_map/pallas_call | solution.py:248
  384.0 9.7 %shard_map.260 = (bf16[640,512]{1,0:T(8,128)(2,1)}, bf16[640,512]{1,0:T(8,128)(2,1)}) custom-call(bf16[3072,256]{1,0:T(8,128)(2,1)} %bitcast.88, bf16[3072,2048]{1,0:T(8,128)(2,1)} %bitcast.77, bf16[3072,1024]{1,0:T(8,128)(2,1)} %get-tuple-element.57.gelu_ref.refs_2_), custom_call_target="tpu_custom_call" | custom-call | flops 4026531840 | bytes 11010048 | tf_op jit(solution)/shard_map/pallas_call | solution.py:248
  396.9 8.5 %collective-permute-done.46.refs_6_ = bf16[256,1792]{1,0:T(8,128)(2,1)S(1)} collective-permute-done((bf16[256,1792]{1,0:T(8,128)(2,1)}, bf16[256,1792]{1,0:T(8,128)(2,1)S(1)}, u32[]{:S(2)}, u32[]{:S(2)}) %collective-permute-start.46) | collective-permute-done | bytes 917536 | tf_op jit(solution)/shard_map/ppermute | solution.py:444
  407.2 20.4 %shard_map.258 = (bf16[512,1792]{1,0:T(8,128)(2,1)}, bf16[512,1792]{1,0:T(8,128)(2,1)}) custom-call(bf16[3072,2048]{1,0:T(8,128)(2,1)} %get-tuple-element.54.h_attn_ref.refs_0_.refs_4_, bf16[3072,768]{1,0:T(8,128)(2,1)} %bitcast.84, bf16[3072,2048]{1,0:T(8,128)(2,1)} %get-tuple-element.55.h_mlp_ref.refs_2_.refs_5_, ...), custom_call_target="tpu_custom_call" | custom-call | flops 11274289152 | bytes 45613056 | tf_op jit(solution)/shard_map/pallas_call | solution.py:248
  427.8 14.5 %shard_map.261 = (bf16[1280,512]{1,0:T(8,128)(2,1)}, bf16[1280,512]{1,0:T(8,128)(2,1)}) custom-call(bf16[3072,256]{1,0:T(8,128)(2,1)} %bitcast.89, bf16[3072,2048]{1,0:T(8,128)(2,1)} %bitcast.78, bf16[3072,1024]{1,0:T(8,128)(2,1)} %get-tuple-element.57.gelu_ref.refs_2_, bf16[3072,2048]{1,0:T(8,128)(2,1)} %bitcast.79, ...), custom_call_target="tpu_custom_call" | custom-call | flops 8053063680 | bytes 20447232 | tf_op jit(solution)/shard_map/pallas_call | solution.py:248
  448.7 48.1 %collective-permute-done.40 = f32[4,960]{1,0:T(4,128)S(1)} collective-permute-done((f32[4,960]{1,0:T(4,128)S(1)}, f32[4,960]{1,0:T(4,128)S(1)}, u32[]{:S(2)}, u32[]{:S(2)}) %collective-permute-start.40) | collective-permute-done | bytes 15392 | tf_op jit(solution)/shard_map/ppermute | solution.py:444
  527.6 19.9 %collective-permute-done.32 = bf16[192,512]{1,0:T(8,128)(2,1)} collective-permute-done((bf16[192,512]{1,0:T(8,128)(2,1)}, bf16[192,512]{1,0:T(8,128)(2,1)}, u32[]{:S(2)}, u32[]{:S(2)}) %collective-permute-start.32) | collective-permute-done | bytes 196640 | tf_op jit(solution)/shard_map/ppermute | solution.py:444
  558.9 22.5 %collective-permute-done.33.refs_1_ = bf16[4,192,512]{2,1,0:T(8,128)(2,1)S(1)} collective-permute-done((bf16[4,192,512]{2,1,0:T(8,128)(2,1)S(1)}, bf16[4,192,512]{2,1,0:T(8,128)(2,1)S(1)}, u32[]{:S(2)}, u32[]{:S(2)}) %collective-permute-start.33) | collective-permute-done | bytes 786464 | tf_op jit(solution)/shard_map/ppermute | solution.py:454
  581.4 11.3 %collective-permute-start.24 = (bf16[4,192,512]{2,1,0:T(8,128)(2,1)S(1)}, bf16[4,192,512]{2,1,0:T(8,128)(2,1)}, u32[]{:S(2)}, u32[]{:S(2)}) collective-permute-start(bf16[4,192,512]{2,1,0:T(8,128)(2,1)S(1)} %pad_maximum_fusion.6.refs_0_), channel_id=1, source_target_pairs={{0,4},{1,5},{2,6},{3,7},{4,0},{5,1},{6,2},{7,3},{8,12},{9,13},{10,... | collective-permute-start | bytes 2359304 | tf_op jit(solution)/shard_map/ppermute | solution.py:454
  593.6 6.3 convert_reduce_fusion
  605.1 8.5 %collective-permute-done.24.refs_2_ = bf16[4,192,512]{2,1,0:T(8,128)(2,1)} collective-permute-done((bf16[4,192,512]{2,1,0:T(8,128)(2,1)S(1)}, bf16[4,192,512]{2,1,0:T(8,128)(2,1)}, u32[]{:S(2)}, u32[]{:S(2)}) %collective-permute-start.24) | collective-permute-done | bytes 786464 | tf_op jit(solution)/shard_map/ppermute | solution.py:454
  615.2 11.7 %shard_map.262 = (f32[256,512]{1,0:T(8,128)}, f32[1024,512]{1,0:T(8,128)}) custom-call(bf16[3072,256]{1,0:T(8,128)(2,1)} %bitcast.90, bf16[3072,2048]{1,0:T(8,128)(2,1)} %bitcast.80, bf16[3072,1024]{1,0:T(8,128)(2,1)} %get-tuple-element.57.gelu_ref.refs_2_, bf16[1280,512]{1,0:T(8,128)(2,1)} %collective-permute-done.52.refs_3_, ...), custom_call_target="tpu_custom_call" | custom-call | flops 4026531840 | bytes 17301504 | tf_op jit(solution)/shard_map/pallas_call | solution.py:248
  626.9 15.0 %shard_map.259 = (f32[512,768]{1,0:T(8,128)}, f32[512,1024]{1,0:T(8,128)}) custom-call(bf16[3072,2048]{1,0:T(8,128)(2,1)} %get-tuple-element.54.h_attn_ref.refs_0_.refs_4_, bf16[3072,768]{1,0:T(8,128)(2,1)} %bitcast.85, bf16[3072,2048]{1,0:T(8,128)(2,1)} %get-tuple-element.55.h_mlp_ref.refs_2_.refs_5_, ...), custom_call_target="tpu_custom_call" | custom-call | flops 5637144576 | bytes 39321600 | tf_op jit(solution)/shard_map/pallas_call | solution.py:248
  647.0 6.1 shard_map.255.refs_8_
  661.1 9.4 %shard_map.249 = bf16[4,3072,512]{2,1,0:T(8,128)(2,1)} custom-call(s32[3]{0:T(128)} %pad_add_fusion.place_ref, bf16[4,3072,512]{2,1,0:T(8,128)(2,1)} %bitcast.95), custom_call_target="tpu_custom_call" | custom-call | flops 6291456 | bytes 25165824 | tf_op jit(solution)/shard_map/pallas_call | solution.py:187
  (247 shorter events, 134.7 us)
Async XLA Ops:
  7.2 157.1 %all-gather.4.cloned.1.call-start = ((), (), s32[]{:S(2)}) async-start(), calls=%async_computation.3 | async-start | bytes 14155776 | tf_op jit(solution)/shard_map/all_gather | solution.py:509
  35.2 212.8 %all-gather.8.cloned.1.call-start = ((), (), s32[]{:S(2)}) async-start(), calls=%async_computation.6 | async-start | bytes 14155776 | tf_op jit(solution)/shard_map/all_gather | solution.py:510
  60.6 284.5 %reduce-scatter.4.cloned.1.call-start = ((), (), s32[]{:S(2)}) async-start(), calls=%async_computation.4 | async-start | bytes 14155776 | tf_op jit(solution)/shard_map/reduce_scatter | solution.py:530
  62.1 43.0 %collective-permute-start.6 = (bf16[512,1792]{1,0:T(8,128)(2,1)S(1)}, bf16[512,1792]{1,0:T(8,128)(2,1)S(1)}, u32[]{:S(2)}, u32[]{:S(2)}) collective-permute-start(bf16[512,1792]{1,0:T(8,128)(2,1)S(1)} %pad_maximum_fusion.refs_0_), channel_id=1, source_target_pairs={{0,24},{8,0},{16,8},{24,16},{1,25},{9,1},{17,9},{25,17},{2,26},{10... | collective-permute-start | bytes 5505032 | tf_op jit(solution)/shard_map/ppermute | solution.py:444
  63.3 44.3 %collective-permute-start.8 = (bf16[512,1792]{1,0:T(8,128)(2,1)S(1)}, bf16[512,1792]{1,0:T(8,128)(2,1)S(1)}, u32[]{:S(2)}, u32[]{:S(2)}) collective-permute-start(bf16[512,1792]{1,0:T(8,128)(2,1)S(1)} %pad_maximum_fusion.refs_0_), channel_id=1, source_target_pairs={{0,8},{8,16},{16,24},{24,0},{1,9},{9,17},{17,25},{25,1},{2,10},{10... | collective-permute-start | bytes 5505032 | tf_op jit(solution)/shard_map/ppermute | solution.py:444
  64.4 94.2 %collective-permute-start.10 = (bf16[1280,512]{1,0:T(8,128)(2,1)S(1)}, bf16[1280,512]{1,0:T(8,128)(2,1)S(1)}, u32[]{:S(2)}, u32[]{:S(2)}) collective-permute-start(bf16[1280,512]{1,0:T(8,128)(2,1)S(1)} %constant_dynamic-update-slice_fusion.refs_0_), channel_id=1, source_target_pairs={{0,24},{8,0},{16,8},{24,16},{1,25},{9,1},{17,9},{25,17},{2,26},{10... | collective-permute-start | bytes 3932168 | tf_op jit(solution)/shard_map/ppermute | solution.py:444
  66.7 95.2 %collective-permute-start.12 = (bf16[1280,512]{1,0:T(8,128)(2,1)S(1)}, bf16[1280,512]{1,0:T(8,128)(2,1)S(1)}, u32[]{:S(2)}, u32[]{:S(2)}) collective-permute-start(bf16[1280,512]{1,0:T(8,128)(2,1)S(1)} %constant_dynamic-update-slice_fusion.refs_0_), channel_id=1, source_target_pairs={{0,8},{8,16},{16,24},{24,0},{1,9},{9,17},{17,25},{25,1},{2,10},{10... | collective-permute-start | bytes 3932168 | tf_op jit(solution)/shard_map/ppermute | solution.py:444
  66.9 66.5 %collective-permute-start.3 = (bf16[8,512]{1,0:T(8,128)(2,1)S(1)}, bf16[8,512]{1,0:T(8,128)(2,1)S(1)}, u32[]{:S(2)}, u32[]{:S(2)}) collective-permute-start(bf16[8,512]{1,0:T(8,128)(2,1)S(1)} %select_select_fusion), channel_id=1, source_target_pairs={{0,24},{8,0},{16,8},{24,16},{1,25},{9,1},{17,9},{25,17},{2,26},{10... | collective-permute-start | bytes 24584 | tf_op jit(solution)/shard_map/ppermute | solution.py:444
  105.2 77.8 %collective-permute-start.7 = (bf16[256,1792]{1,0:T(8,128)(2,1)S(1)}, bf16[256,1792]{1,0:T(8,128)(2,1)}, u32[]{:S(2)}, u32[]{:S(2)}) collective-permute-start(bf16[256,1792]{1,0:T(8,128)(2,1)S(1)} %slice.72), channel_id=1, source_target_pairs={{0,24},{8,0},{16,8},{24,16},{1,25},{9,1},{17,9},{25,17},{2,26},{10... | collective-permute-start | bytes 2752520 | tf_op jit(solution)/shard_map/ppermute | solution.py:444
  108.6 74.4 %collective-permute-start.9 = (bf16[256,1792]{1,0:T(8,128)(2,1)}, bf16[256,1792]{1,0:T(8,128)(2,1)}, u32[]{:S(2)}, u32[]{:S(2)}) collective-permute-start(bf16[256,1792]{1,0:T(8,128)(2,1)} %slice.73), channel_id=1, source_target_pairs={{0,8},{8,16},{16,24},{24,0},{1,9},{9,17},{17,25},{25,1},{2,10},{10... | collective-permute-start | bytes 2752520 | tf_op jit(solution)/shard_map/ppermute | solution.py:444
  158.6 67.1 %collective-permute-start.11 = (bf16[1280,256]{1,0:T(8,128)(2,1)S(1)}, bf16[1280,256]{1,0:T(8,128)(2,1)}, u32[]{:S(2)}, u32[]{:S(2)}) collective-permute-start(bf16[1280,256]{1,0:T(8,128)(2,1)S(1)} %slice.74), channel_id=1, source_target_pairs={{0,24},{8,0},{16,8},{24,16},{1,25},{9,1},{17,9},{25,17},{2,26},{10... | collective-permute-start | bytes 1966088 | tf_op jit(solution)/shard_map/ppermute | solution.py:444
  163.9 61.8 %collective-permute-start.13 = (bf16[1280,256]{1,0:T(8,128)(2,1)}, bf16[1280,256]{1,0:T(8,128)(2,1)}, u32[]{:S(2)}, u32[]{:S(2)}) collective-permute-start(bf16[1280,256]{1,0:T(8,128)(2,1)} %slice.75), channel_id=1, source_target_pairs={{0,8},{8,16},{16,24},{24,0},{1,9},{9,17},{17,25},{25,1},{2,10},{10... | collective-permute-start | bytes 1966088 | tf_op jit(solution)/shard_map/ppermute | solution.py:444
  247.7 263.1 %reduce-scatter.8.cloned.1.call-start = ((), (), s32[]{:S(2)}) async-start(), calls=%async_computation.8 | async-start | bytes 7077888 | tf_op jit(solution)/shard_map/reduce_scatter | solution.py:547
  309.5 207.7 %reduce-scatter.6.cloned.1.call-start = ((), (), s32[]{:S(2)}) async-start(), calls=%async_computation.7 | async-start | bytes 7077888 | tf_op jit(solution)/shard_map/reduce_scatter | solution.py:547
  343.8 317.3 %all-gather.6.cloned.1.call-start = ((), (), s32[]{:S(2)}) async-start(), calls=%async_computation.5 | async-start | bytes 14155776 | tf_op jit(solution)/shard_map/all_gather | solution.py:532
  393.7 34.1 %collective-permute-start.50 = (bf16[640,512]{1,0:T(8,128)(2,1)}, bf16[640,512]{1,0:T(8,128)(2,1)}, u32[]{:S(2)}, u32[]{:S(2)}) collective-permute-start(bf16[640,512]{1,0:T(8,128)(2,1)} %get-tuple-element.87), channel_id=1, source_target_pairs={{0,8},{8,16},{16,24},{24,0},{1,9},{9,17},{17,25},{25,1},{2,10},{10... | collective-permute-start | bytes 1966088 | tf_op jit(solution)/shard_map/ppermute | solution.py:444
  393.8 34.0 %collective-permute-start.51 = (bf16[640,512]{1,0:T(8,128)(2,1)}, bf16[640,512]{1,0:T(8,128)(2,1)}, u32[]{:S(2)}, u32[]{:S(2)}) collective-permute-start(bf16[640,512]{1,0:T(8,128)(2,1)} %get-tuple-element.88), channel_id=1, source_target_pairs={{0,24},{8,0},{16,8},{24,16},{1,25},{9,1},{17,9},{25,17},{2,26},{10... | collective-permute-start | bytes 1966088 | tf_op jit(solution)/shard_map/ppermute | solution.py:444
  427.6 124.3 %collective-permute-start.48 = (bf16[512,1792]{1,0:T(8,128)(2,1)}, bf16[512,1792]{1,0:T(8,128)(2,1)}, u32[]{:S(2)}, u32[]{:S(2)}) collective-permute-start(bf16[512,1792]{1,0:T(8,128)(2,1)} %get-tuple-element.84), channel_id=1, source_target_pairs={{0,8},{8,16},{16,24},{24,0},{1,9},{9,17},{17,25},{25,1},{2,10},{10... | collective-permute-start | bytes 5505032 | tf_op jit(solution)/shard_map/ppermute | solution.py:444
  442.2 71.6 %collective-permute-start.52 = (bf16[1280,512]{1,0:T(8,128)(2,1)}, bf16[1280,512]{1,0:T(8,128)(2,1)}, u32[]{:S(2)}, u32[]{:S(2)}) collective-permute-start(bf16[1280,512]{1,0:T(8,128)(2,1)} %get-tuple-element.89), channel_id=1, source_target_pairs={{0,8},{8,16},{16,24},{24,0},{1,9},{9,17},{17,25},{25,1},{2,10},{10... | collective-permute-start | bytes 3932168 | tf_op jit(solution)/shard_map/ppermute | solution.py:444
  443.3 73.2 %collective-permute-start.53 = (bf16[1280,512]{1,0:T(8,128)(2,1)}, bf16[1280,512]{1,0:T(8,128)(2,1)}, u32[]{:S(2)}, u32[]{:S(2)}) collective-permute-start(bf16[1280,512]{1,0:T(8,128)(2,1)} %get-tuple-element.90), channel_id=1, source_target_pairs={{0,24},{8,0},{16,8},{24,16},{1,25},{9,1},{17,9},{25,17},{2,26},{10... | collective-permute-start | bytes 3932168 | tf_op jit(solution)/shard_map/ppermute | solution.py:444
  445.8 50.9 %collective-permute-start.40 = (f32[4,960]{1,0:T(4,128)S(1)}, f32[4,960]{1,0:T(4,128)S(1)}, u32[]{:S(2)}, u32[]{:S(2)}) collective-permute-start(f32[4,960]{1,0:T(4,128)S(1)} %get-tuple-element.124), channel_id=1, source_target_pairs={{0,16},{8,24},{16,0},{24,8},{1,17},{9,25},{17,1},{25,9},{2,18},{10... | collective-permute-start | bytes 46088 | tf_op jit(solution)/shard_map/ppermute | solution.py:444
  448.0 48.8 %collective-permute-start.41 = (f32[4,960]{1,0:T(4,128)S(1)}, f32[4,960]{1,0:T(4,128)S(1)}, u32[]{:S(2)}, u32[]{:S(2)}) collective-permute-start(f32[4,960]{1,0:T(4,128)S(1)} %get-tuple-element.125), channel_id=1, source_target_pairs={{0,8},{8,16},{16,24},{24,0},{1,9},{9,17},{17,25},{25,1},{2,10},{10... | collective-permute-start | bytes 46088 | tf_op jit(solution)/shard_map/ppermute | solution.py:444
  496.8 61.9 %collective-permute-start.49 = (bf16[512,1792]{1,0:T(8,128)(2,1)}, bf16[512,1792]{1,0:T(8,128)(2,1)}, u32[]{:S(2)}, u32[]{:S(2)}) collective-permute-start(bf16[512,1792]{1,0:T(8,128)(2,1)} %get-tuple-element.85), channel_id=1, source_target_pairs={{0,24},{8,0},{16,8},{24,16},{1,25},{9,1},{17,9},{25,17},{2,26},{10... | collective-permute-start | bytes 5505032 | tf_op jit(solution)/shard_map/ppermute | solution.py:444
  552.1 40.6 %collective-permute-start.34 = (bf16[4,192,512]{2,1,0:T(8,128)(2,1)S(1)}, bf16[4,192,512]{2,1,0:T(8,128)(2,1)S(1)}, u32[]{:S(2)}, u32[]{:S(2)}) collective-permute-start(bf16[4,192,512]{2,1,0:T(8,128)(2,1)S(1)} %pad_maximum_fusion.7.refs_0_), channel_id=1, source_target_pairs={{0,4},{1,5},{2,6},{3,7},{4,0},{5,1},{6,2},{7,3},{8,12},{9,13},{10,... | collective-permute-start | bytes 2359304 | tf_op jit(solution)/shard_map/ppermute | solution.py:454
  555.0 38.0 %collective-permute-start.35 = (bf16[4,192,512]{2,1,0:T(8,128)(2,1)S(1)}, bf16[4,192,512]{2,1,0:T(8,128)(2,1)}, u32[]{:S(2)}, u32[]{:S(2)}) collective-permute-start(bf16[4,192,512]{2,1,0:T(8,128)(2,1)S(1)} %pad_maximum_fusion.7.refs_0_), channel_id=1, source_target_pairs={{0,2},{1,3},{2,4},{3,5},{4,6},{5,7},{6,0},{7,1},{8,10},{9,11},{10,... | collective-permute-start | bytes 2359304 | tf_op jit(solution)/shard_map/ppermute | solution.py:454
  556.9 36.2 %collective-permute-start.36 = (bf16[4,192,512]{2,1,0:T(8,128)(2,1)S(1)}, bf16[4,192,512]{2,1,0:T(8,128)(2,1)}, u32[]{:S(2)}, u32[]{:S(2)}) collective-permute-start(bf16[4,192,512]{2,1,0:T(8,128)(2,1)S(1)} %pad_maximum_fusion.7.refs_0_), channel_id=1, source_target_pairs={{0,1},{1,0},{2,3},{3,2},{4,5},{5,4},{6,7},{7,6},{8,9},{9,8},{10,11... | collective-permute-start | bytes 2359304 | tf_op jit(solution)/shard_map/ppermute | solution.py:457
  558.7 46.4 %collective-permute-start.23 = (bf16[4,192,512]{2,1,0:T(8,128)(2,1)S(1)}, bf16[4,192,512]{2,1,0:T(8,128)(2,1)}, u32[]{:S(2)}, u32[]{:S(2)}) collective-permute-start(bf16[4,192,512]{2,1,0:T(8,128)(2,1)S(1)} %pad_maximum_fusion.6.refs_0_), channel_id=1, source_target_pairs={{0,6},{1,7},{2,0},{3,1},{4,2},{5,3},{6,4},{7,5},{8,14},{9,15},{10,... | collective-permute-start | bytes 2359304 | tf_op jit(solution)/shard_map/ppermute | solution.py:454
  605.1 48.0 %collective-permute-start.26 = (bf16[4,192,512]{2,1,0:T(8,128)(2,1)S(1)}, bf16[4,192,512]{2,1,0:T(8,128)(2,1)}, u32[]{:S(2)}, u32[]{:S(2)}) collective-permute-start(bf16[4,192,512]{2,1,0:T(8,128)(2,1)S(1)} %pad_maximum_fusion.6.refs_0_), channel_id=1, source_target_pairs={{0,1},{1,0},{2,3},{3,2},{4,5},{5,4},{6,7},{7,6},{8,9},{9,8},{10,11... | collective-permute-start | bytes 2359304 | tf_op jit(solution)/shard_map/ppermute | solution.py:457
  613.6 32.5 %collective-permute-start.39 = (bf16[4,192,512]{2,1,0:T(8,128)(2,1)}, bf16[4,192,512]{2,1,0:T(8,128)(2,1)S(1)}, u32[]{:S(2)}, u32[]{:S(2)}) collective-permute-start(bf16[4,192,512]{2,1,0:T(8,128)(2,1)} %collective-permute-done.35.refs_3_), channel_id=1, source_target_pairs={{0,1},{1,0},{2,3},{3,2},{4,5},{5,4},{6,7},{7,6},{8,9},{9,8},{10,11... | collective-permute-start | bytes 2359304 | tf_op jit(solution)/shard_map/ppermute | solution.py:457
  614.6 38.6 %collective-permute-start.27 = (bf16[4,192,512]{2,1,0:T(8,128)(2,1)}, bf16[4,192,512]{2,1,0:T(8,128)(2,1)}, u32[]{:S(2)}, u32[]{:S(2)}) collective-permute-start(bf16[4,192,512]{2,1,0:T(8,128)(2,1)} %collective-permute-done.23.refs_1_), channel_id=1, source_target_pairs={{0,1},{1,0},{2,3},{3,2},{4,5},{5,4},{6,7},{7,6},{8,9},{9,8},{10,11... | collective-permute-start | bytes 2359304 | tf_op jit(solution)/shard_map/ppermute | solution.py:457
  614.6 38.6 %collective-permute-start.28 = (bf16[4,192,512]{2,1,0:T(8,128)(2,1)}, bf16[4,192,512]{2,1,0:T(8,128)(2,1)S(1)}, u32[]{:S(2)}, u32[]{:S(2)}) collective-permute-start(bf16[4,192,512]{2,1,0:T(8,128)(2,1)} %collective-permute-done.24.refs_2_), channel_id=1, source_target_pairs={{0,1},{1,0},{2,3},{3,2},{4,5},{5,4},{6,7},{7,6},{8,9},{9,8},{10,11... | collective-permute-start | bytes 2359304 | tf_op jit(solution)/shard_map/ppermute | solution.py:457
  615.1 38.1 %collective-permute-start.29 = (bf16[4,192,512]{2,1,0:T(8,128)(2,1)}, bf16[4,192,512]{2,1,0:T(8,128)(2,1)S(1)}, u32[]{:S(2)}, u32[]{:S(2)}) collective-permute-start(bf16[4,192,512]{2,1,0:T(8,128)(2,1)} %collective-permute-done.25.refs_3_), channel_id=1, source_target_pairs={{0,1},{1,0},{2,3},{3,2},{4,5},{5,4},{6,7},{7,6},{8,9},{9,8},{10,11... | collective-permute-start | bytes 2359304 | tf_op jit(solution)/shard_map/ppermute | solution.py:457
  (67 other events, 1166.9 us)
Sparse Core Ops, SparseCore 0:
  35.4 63.3 all-gather.3
  100.4 65.0 all-gather.7
  247.8 68.8 reduce-scatter.3
  318.9 39.9 reduce-scatter.7
  361.1 39.6 reduce-scatter.5
  402.2 66.0 all-gather.5

commit v9 on v8

--- a/solution.py
+++ b/solution.py
@@ -12,7 +12,7 @@
 ROTARY_DIVISOR = 4
 LANES = 128
 Q_ROWS = 256
-LN_ROWS = 64
+LN_ROWS = 128
 MIB = 1024 * 1024
 TILE = 256
 SQRT_HALF = 0.5 ** 0.5
@@ -547,9 +547,13 @@
             value_a6 = lax.psum_scatter(a6_part, 'ty', scatter_dimension=0, tiled=True)
             parts = row_call(finish_dx_kernel, tx_size, s, own, x_rows, value_a6, cot_rows)
             block = to_width(parts)
-            blocks = [block] + [along(block, hops) for hops in range(1, ty_size // 2)]
-            blocks = blocks + [partner(piece) for piece in blocks]
-            dx_act = place_call(place_pieces_kernel, place, blocks, dx_act, s, n_seq, seq_len)
+            if s < n_seq - 1:
+                blocks = [block] + [along(block, hops) for hops in range(1, ty_size // 2)]
+                blocks = blocks + [partner(piece) for piece in blocks]
+                dx_act = place_call(place_pieces_kernel, place, blocks, dx_act, s, n_seq, seq_len)
+            else:
+                full = lax.all_gather(block, 'ty', axis=1, tiled=True)
+                dx_act = place_call(place_kernel, place, [full], dx_act, s, n_seq, seq_len)
         d_qkv = d_qkv.reshape(n_tok, qkv_width)
 
         d_ln = sum(d_ln).sum(1).reshape(4, tx_size, d_local)

time: 687 us -> 737 us (1.073)
  waiting for transfers between devices: 256 us -> 322 us
  starting transfers between devices: 71.9 us -> 59.2 us
    reduce_scatter x1, waiting for transfers between devices: 0.02 us -> 52.9 us  [body(): lax.psum_scatter(y_part.reshape(n_tok, d_model), 'ty', scatter_dimension=...]
    ppermute x37, waiting for transfers between devices: 217 us -> 234 us  [shift(): lax.ppermute(value, 'tx', [(s, (s - hops) % tx_size) for s in range(tx_si...]
    ppermute x6 -> x3, starting transfers between devices: 16.7 us -> 3.88 us  [along(): lax.ppermute(value, 'ty', [(s, (s - 2 * hops) % ty_size) for s in range(t...]
    ppermute x6 -> x3, waiting for transfers between devices: 34 us -> 23 us  [along(): lax.ppermute(value, 'ty', [(s, (s - 2 * hops) % ty_size) for s in range(t...]
  transfers between devices with their start and end apart: 60 -> 54, of which waited for: 23 -> 22; matrix products, arithmetic and copies ran while one was open for 5% -> 4% of each run, Pallas kernels for 41% -> 25%
where the time goes in v9:
time: 737 us; the launch traced here: 725 us
  waiting for transfers between devices  322 us (44%)
  Pallas kernels  285 us (39%)
  starting transfers between devices  59.2 us (8%)
  other arithmetic  22.5 us (3%)
  local copies, waits for them, and re-layouts  19.8 us (3%)
  between operations  15.4 us (2%)
    ppermute x37, waiting for transfers between devices, shift(): lax.ppermute(value, 'tx', [(s, (s - hops) % tx_size) for s in range(tx_si...  234 us
    pallas_call x6, Pallas kernels, tile_call(): pl.pallas_call(kernel, grid=(count // rows,), in_specs=in_specs, out_spec...  144 us
    pallas_call x6, Pallas kernels, grad_call(): pl.pallas_call(functools.partial(grad_kernel, blocks=terms, moving=adds,...  83.3 us
    ppermute x37, starting transfers between devices, shift(): lax.ppermute(value, 'tx', [(s, (s - hops) % tx_size) for s in range(tx_si...  53.2 us
    reduce_scatter x1, waiting for transfers between devices, body(): lax.psum_scatter(y_part.reshape(n_tok, d_model), 'ty', scatter_dimension=...  52.9 us
    pallas_call x2, Pallas kernels, backward(): pl.pallas_call(lambda *refs: kernel(*refs[:5], *refs[5 + len(into):]), gr...  24.5 us
    ppermute x3, waiting for transfers between devices, along(): lax.ppermute(value, 'ty', [(s, (s - 2 * hops) % ty_size) for s in range(t...  23 us
    pallas_call x3, Pallas kernels, place_call(): pl.pallas_call(functools.partial(kernel, chunk=chunk, n_seq=n_seq), in_sp...  21.4 us
  transfers between devices with their start and end apart: 54, of which 22 were waited for; matrix products, arithmetic and copies ran while one was open for 4% of the time, Pallas kernels for 25%

profile of v9, /device:TPU:98, one launch (start us, length us, event | category | flops | bytes accessed | tf_op | source)
XLA Modules:
  0.0 724.7 jit_solution(4699923233759699403)
XLA Ops:
  14.6 15.8 %collective-permute-done = bf16[2,192,512]{2,1,0:T(8,128)(2,1)S(1)} collective-permute-done((bf16[2,192,512]{2,1,0:T(8,128)(2,1)S(1)}, bf16[2,192,512]{2,1,0:T(8,128)(2,1)S(1)}, u32[]{:S(2)}, u32[]{:S(2)}) %collective-permute-start) | collective-permute-done | bytes 393248 | tf_op jit(solution)/shard_map/ppermute | solution.py:444
  38.9 10.0 %collective-permute-done.17 = bf16[2,192,512]{2,1,0:T(8,128)(2,1)S(1)} collective-permute-done((bf16[2,192,512]{2,1,0:T(8,128)(2,1)S(1)}, bf16[2,192,512]{2,1,0:T(8,128)(2,1)S(1)}, u32[]{:S(2)}, u32[]{:S(2)}) %collective-permute-start.17) | collective-permute-done | bytes 393248 | tf_op jit(solution)/shard_map/ppermute | solution.py:444
  51.4 6.4 collective-permute-done.19
  68.7 35.1 %collective-permute-done.6.refs_1_ = bf16[512,1792]{1,0:T(8,128)(2,1)S(1)} collective-permute-done((bf16[512,1792]{1,0:T(8,128)(2,1)S(1)}, bf16[512,1792]{1,0:T(8,128)(2,1)S(1)}, u32[]{:S(2)}, u32[]{:S(2)}) %collective-permute-start.6) | collective-permute-done | bytes 1835040 | tf_op jit(solution)/shard_map/ppermute | solution.py:444
  107.2 24.9 %collective-permute-done.3 = bf16[8,512]{1,0:T(8,128)(2,1)S(1)} collective-permute-done((bf16[8,512]{1,0:T(8,128)(2,1)S(1)}, bf16[8,512]{1,0:T(8,128)(2,1)S(1)}, u32[]{:S(2)}, u32[]{:S(2)}) %collective-permute-start.3) | collective-permute-done | bytes 8224 | tf_op jit(solution)/shard_map/ppermute | solution.py:444
  132.8 18.6 %collective-permute-done.4 = bf16[8,512]{1,0:T(8,128)(2,1)S(1)} collective-permute-done((bf16[8,512]{1,0:T(8,128)(2,1)S(1)}, bf16[8,512]{1,0:T(8,128)(2,1)S(1)}, u32[]{:S(2)}, u32[]{:S(2)}) %collective-permute-start.4) | collective-permute-done | bytes 8224 | tf_op jit(solution)/shard_map/ppermute | solution.py:444
  162.8 18.0 %shard_map.245 = (bf16[3072,2048]{1,0:T(8,128)(2,1)}, bf16[3072,2048]{1,0:T(8,128)(2,1)}) custom-call(bf16[3072,2048]{1,0:T(8,128)(2,1)} %bitcast.91, f32[8,2048]{1,0:T(8,128)} %maximum_convert_fusion.small_ref), custom_call_target="tpu_custom_call" | custom-call | flops 100663296 | bytes 37781504 | tf_op jit(solution)/shard_map/pallas_call | solution.py:423
  180.8 32.8 %shard_map.246 = (bf16[3072,768]{1,0:T(8,128)(2,1)}, bf16[3072,1024]{1,0:T(8,128)(2,1)}, bf16[3072,1024]{1,0:T(8,128)(2,1)}) custom-call(bf16[3072,2048]{1,0:T(8,128)(2,1)} %get-tuple-element.54.h_attn_ref.refs_0_.refs_4_, bf16[3072,2048]{1,0:T(8,128)(2,1)} %get-tuple-element.55.h_mlp_ref.refs_2_.refs_5_, f32[1536,128]{1,0:T(8,128)} %get-tuple-element.128.cos_ref.refs_2_, ...), custom_call_target="tpu_custom_call" | custom-call | flops 22548578304 | bytes 52170240 | tf_op jit(solution)/shard_map/pallas_call | solution.py:423
  213.7 27.2 %shard_map.250 = (bf16[3072,256]{1,0:T(8,128)(2,1)}, bf16[3072,1024]{1,0:T(8,128)(2,1)}, f32[8,1024]{1,0:T(8,128)}) custom-call(bf16[3072,2048]{1,0:T(8,128)(2,1)} %bitcast.76, bf16[3072,1024]{1,0:T(8,128)(2,1)} %get-tuple-element.62.pre_ref, bf16[1280,512]{1,0:T(8,128)(2,1)} %copy-done.22, bf16[1280,512]{1,0:T(8,128)(2,1)} %copy-done.17, ...), custom_call_target="tpu_custom_call" | custom-call | flops 16106127360 | bytes 31997952 | tf_op jit(solution)/shard_map/pallas_call | solution.py:423
  240.8 12.2 %ab.2 = (bf16[2,1536,768]{2,1,0:T(8,128)(2,1)}, f32[1,8,768]{2,1,0:T(8,128)}) custom-call(bf16[2,1536,768]{2,1,0:T(8,128)(2,1)} %bitcast.126, bf16[2,1536,256]{2,1,0:T(8,128)(2,1)} %bitcast.129, f32[1536,128]{1,0:T(8,128)} %get-tuple-element.128.cos_ref.refs_2_, f32[1536,128]{1,0:T(8,128)} %get-tuple-element.127.lo_ref.refs_3_, ...), custom_call_target="tpu_custom_call" | custom-call | flops 6039797760 | bytes 5505024 | tf_op jit(solution)/shard_map/ab/pallas_call | solution.py:127
  253.1 22.0 %shard_map.251 = (bf16[1536,2048]{1,0:T(8,128)(2,1)}, f32[4,8,2048]{2,1,0:T(8,128)}) custom-call(bf16[3072,768]{1,0:T(8,128)(2,1)} %bitcast.81, bf16[3072,1024]{1,0:T(8,128)(2,1)} %get-tuple-element.65.d_pre_ref.refs_3_, bf16[3072,2048]{1,0:T(8,128)(2,1)} %bitcast.92, f32[8,2048]{1,0:T(8,128)} %maximum_convert_fusion.small_ref, bf16[512,1792]{1,0:T(8,128)(2,1)} %copy-done.4, ...), custom_call_target="tpu_custom_call" | custom-call | flops 11274289152 | bytes 25591808 | tf_op jit(solution)/shard_map/pallas_call | solution.py:423
  275.1 12.2 %ab.3 = (bf16[2,1536,768]{2,1,0:T(8,128)(2,1)}, f32[1,8,768]{2,1,0:T(8,128)}) custom-call(bf16[2,1536,768]{2,1,0:T(8,128)(2,1)} %bitcast.127, bf16[2,1536,256]{2,1,0:T(8,128)(2,1)} %bitcast.130, f32[1536,128]{1,0:T(8,128)} %get-tuple-element.128.cos_ref.refs_2_, f32[1536,128]{1,0:T(8,128)} %get-tuple-element.127.lo_ref.refs_3_, ...), custom_call_target="tpu_custom_call", output_to_operand_aliasing={{0}: (5, {})} | custom-call | flops 6039797760 | bytes 5505024 | tf_op jit(solution)/shard_map/ab/pallas_call | solution.py:127
  287.3 21.8 %shard_map.252 = (bf16[1536,2048]{1,0:T(8,128)(2,1)}, f32[4,8,2048]{2,1,0:T(8,128)}) custom-call(bf16[3072,768]{1,0:T(8,128)(2,1)} %bitcast.82, bf16[3072,1024]{1,0:T(8,128)(2,1)} %get-tuple-element.65.d_pre_ref.refs_3_, bf16[3072,2048]{1,0:T(8,128)(2,1)} %bitcast.93, f32[8,2048]{1,0:T(8,128)} %maximum_convert_fusion.small_ref, bf16[512,1792]{1,0:T(8,128)(2,1)} %copy-done.4, ...), custom_call_target="tpu_custom_call" | custom-call | flops 11274289152 | bytes 25591808 | tf_op jit(solution)/shard_map/pallas_call | solution.py:423
  309.2 9.8 %af.1 = bf16[2,1536,256]{2,1,0:T(8,128)(2,1)} custom-call(bf16[2,1536,768]{2,1,0:T(8,128)(2,1)} %bitcast.128), custom_call_target="tpu_custom_call" | custom-call | flops 4831838208 | bytes 6291456 | tf_op jit(solution)/shard_map/af/pallas_call | solution.py:114
  319.1 22.1 %shard_map.247 = bf16[8,2,192,2048]{3,2,1,0:T(8,128)(2,1)} custom-call(bf16[3072,256]{1,0:T(8,128)(2,1)} %bitcast.87, bf16[3072,1024]{1,0:T(8,128)(2,1)} %get-tuple-element.57.gelu_ref.refs_2_, bf16[1280,512]{1,0:T(8,128)(2,1)} %copy-done.22, bf16[1280,512]{1,0:T(8,128)(2,1)} %copy-done.17, bf16[1280,256]{1,0:T(8,128)(2,1)} %collective-permute-done.11.refs_2_, ...), custom_call_target="tpu_custom_call" | custom-call | flops 16106127360 | bytes 25690112 | tf_op jit(solution)/shard_map/pallas_call | solution.py:423
  367.3 52.9 %reduce-scatter.4.cloned.1.call-done.mixed_ref = bf16[384,2048]{1,0:T(8,128)(2,1)} async-done(((bf16[3072,2048]{1,0:T(8,128)(2,1)}), bf16[384,2048]{1,0:T(8,128)(2,1)}) %reduce-scatter.4.cloned.1.call-update) | async-done | bytes 1572880 | tf_op jit(solution)/shard_map/reduce_scatter | solution.py:530
  428.1 6.9 collective-permute-done.14
  435.0 9.8 %collective-permute-done.15 = bf16[384,512]{1,0:T(8,128)(2,1)S(1)} collective-permute-done((bf16[384,512]{1,0:T(8,128)(2,1)S(1)}, bf16[384,512]{1,0:T(8,128)(2,1)S(1)}, u32[]{:S(2)}, u32[]{:S(2)}) %collective-permute-start.15) | collective-permute-done | bytes 393248 | tf_op jit(solution)/shard_map/ppermute | solution.py:444
  446.3 9.7 %shard_map.260 = (bf16[640,512]{1,0:T(8,128)(2,1)}, bf16[640,512]{1,0:T(8,128)(2,1)}) custom-call(bf16[3072,256]{1,0:T(8,128)(2,1)} %bitcast.88, bf16[3072,2048]{1,0:T(8,128)(2,1)} %bitcast.77, bf16[3072,1024]{1,0:T(8,128)(2,1)} %get-tuple-element.57.gelu_ref.refs_2_), custom_call_target="tpu_custom_call" | custom-call | flops 4026531840 | bytes 11010048 | tf_op jit(solution)/shard_map/pallas_call | solution.py:248
  464.9 12.3 %shard_map.257 = (bf16[256,1792]{1,0:T(8,128)(2,1)}, bf16[256,1792]{1,0:T(8,128)(2,1)}) custom-call(bf16[3072,2048]{1,0:T(8,128)(2,1)} %get-tuple-element.54.h_attn_ref.refs_0_.refs_4_, bf16[3072,768]{1,0:T(8,128)(2,1)} %bitcast.83, bf16[3072,2048]{1,0:T(8,128)(2,1)} %get-tuple-element.55.h_mlp_ref.refs_2_.refs_5_, ...), custom_call_target="tpu_custom_call" | custom-call | flops 5637144576 | bytes 17301504 | tf_op jit(solution)/shard_map/pallas_call | solution.py:248
  481.0 14.6 %shard_map.261 = (bf16[1280,512]{1,0:T(8,128)(2,1)}, bf16[1280,512]{1,0:T(8,128)(2,1)}) custom-call(bf16[3072,256]{1,0:T(8,128)(2,1)} %bitcast.89, bf16[3072,2048]{1,0:T(8,128)(2,1)} %bitcast.78, bf16[3072,1024]{1,0:T(8,128)(2,1)} %get-tuple-element.57.gelu_ref.refs_2_, bf16[3072,2048]{1,0:T(8,128)(2,1)} %bitcast.79, ...), custom_call_target="tpu_custom_call" | custom-call | flops 8053063680 | bytes 20447232 | tf_op jit(solution)/shard_map/pallas_call | solution.py:248
  499.6 19.7 %shard_map.258 = (bf16[512,1792]{1,0:T(8,128)(2,1)}, bf16[512,1792]{1,0:T(8,128)(2,1)}) custom-call(bf16[3072,2048]{1,0:T(8,128)(2,1)} %get-tuple-element.54.h_attn_ref.refs_0_.refs_4_, bf16[3072,768]{1,0:T(8,128)(2,1)} %bitcast.84, bf16[3072,2048]{1,0:T(8,128)(2,1)} %get-tuple-element.55.h_mlp_ref.refs_2_.refs_5_, ...), custom_call_target="tpu_custom_call" | custom-call | flops 11274289152 | bytes 45613056 | tf_op jit(solution)/shard_map/pallas_call | solution.py:248
  530.9 45.0 %collective-permute-done.23 = bf16[192,512]{1,0:T(8,128)(2,1)S(1)} collective-permute-done((bf16[192,512]{1,0:T(8,128)(2,1)S(1)}, bf16[192,512]{1,0:T(8,128)(2,1)S(1)}, u32[]{:S(2)}, u32[]{:S(2)}) %collective-permute-start.23) | collective-permute-done | bytes 196640 | tf_op jit(solution)/shard_map/ppermute | solution.py:444
  576.0 46.0 %collective-permute-done.25 = bf16[192,512]{1,0:T(8,128)(2,1)} collective-permute-done((bf16[192,512]{1,0:T(8,128)(2,1)S(1)}, bf16[192,512]{1,0:T(8,128)(2,1)}, u32[]{:S(2)}, u32[]{:S(2)}) %collective-permute-start.25) | collective-permute-done | bytes 196640 | tf_op jit(solution)/shard_map/ppermute | solution.py:444
  631.0 6.3 convert_reduce_fusion
  639.9 7.0 collective-permute-done.26.refs_1_
  646.9 14.7 %collective-permute-done.27.refs_2_ = bf16[4,192,512]{2,1,0:T(8,128)(2,1)} collective-permute-done((bf16[4,192,512]{2,1,0:T(8,128)(2,1)S(1)}, bf16[4,192,512]{2,1,0:T(8,128)(2,1)}, u32[]{:S(2)}, u32[]{:S(2)}) %collective-permute-start.27) | collective-permute-done | bytes 786464 | tf_op jit(solution)/shard_map/ppermute | solution.py:454
  662.9 12.0 %shard_map.262 = (f32[256,512]{1,0:T(8,128)}, f32[1024,512]{1,0:T(8,128)}) custom-call(bf16[3072,256]{1,0:T(8,128)(2,1)} %bitcast.90, bf16[3072,2048]{1,0:T(8,128)(2,1)} %bitcast.80, bf16[3072,1024]{1,0:T(8,128)(2,1)} %get-tuple-element.57.gelu_ref.refs_2_, bf16[1280,512]{1,0:T(8,128)(2,1)} %collective-permute-done.45.refs_3_, ...), custom_call_target="tpu_custom_call" | custom-call | flops 4026531840 | bytes 17301504 | tf_op jit(solution)/shard_map/pallas_call | solution.py:248
  676.2 15.0 %shard_map.259 = (f32[512,768]{1,0:T(8,128)}, f32[512,1024]{1,0:T(8,128)}) custom-call(bf16[3072,2048]{1,0:T(8,128)(2,1)} %get-tuple-element.54.h_attn_ref.refs_0_.refs_4_, bf16[3072,768]{1,0:T(8,128)(2,1)} %bitcast.85, bf16[3072,2048]{1,0:T(8,128)(2,1)} %get-tuple-element.55.h_mlp_ref.refs_2_.refs_5_, ...), custom_call_target="tpu_custom_call" | custom-call | flops 5637144576 | bytes 39321600 | tf_op jit(solution)/shard_map/pallas_call | solution.py:248
  695.4 6.1 shard_map.255.rest_0_
  701.5 5.8 shard_map.256
  707.4 9.4 %shard_map.249 = bf16[4,3072,512]{2,1,0:T(8,128)(2,1)} custom-call(s32[3]{0:T(128)} %pad_add_fusion.place_ref, bf16[4,3072,512]{2,1,0:T(8,128)(2,1)} %bitcast.95), custom_call_target="tpu_custom_call" | custom-call | flops 6291456 | bytes 25165824 | tf_op jit(solution)/shard_map/pallas_call | solution.py:187
  (232 shorter events, 127.1 us)
Async XLA Ops:
  7.2 155.6 %all-gather.5.cloned.1.call-start = ((), (), s32[]{:S(2)}) async-start(), calls=%async_computation.3 | async-start | bytes 14155776 | tf_op jit(solution)/shard_map/all_gather | solution.py:509
  35.3 178.4 %all-gather.9.cloned.1.call-start = ((), (), s32[]{:S(2)}) async-start(), calls=%async_computation.6 | async-start | bytes 14155776 | tf_op jit(solution)/shard_map/all_gather | solution.py:510
  59.1 289.7 %reduce-scatter.6.cloned.1.call-start = ((), (), s32[]{:S(2)}) async-start(), calls=%async_computation.7 | async-start | bytes 7077888 | tf_op jit(solution)/shard_map/reduce_scatter | solution.py:547
  60.8 43.0 %collective-permute-start.6 = (bf16[512,1792]{1,0:T(8,128)(2,1)S(1)}, bf16[512,1792]{1,0:T(8,128)(2,1)S(1)}, u32[]{:S(2)}, u32[]{:S(2)}) collective-permute-start(bf16[512,1792]{1,0:T(8,128)(2,1)S(1)} %pad_maximum_fusion.refs_0_), channel_id=1, source_target_pairs={{0,24},{8,0},{16,8},{24,16},{1,25},{9,1},{17,9},{25,17},{2,26},{10... | collective-permute-start | bytes 5505032 | tf_op jit(solution)/shard_map/ppermute | solution.py:444
  61.8 44.3 %collective-permute-start.8 = (bf16[512,1792]{1,0:T(8,128)(2,1)S(1)}, bf16[512,1792]{1,0:T(8,128)(2,1)S(1)}, u32[]{:S(2)}, u32[]{:S(2)}) collective-permute-start(bf16[512,1792]{1,0:T(8,128)(2,1)S(1)} %pad_maximum_fusion.refs_0_), channel_id=1, source_target_pairs={{0,8},{8,16},{16,24},{24,0},{1,9},{9,17},{17,25},{25,1},{2,10},{10... | collective-permute-start | bytes 5505032 | tf_op jit(solution)/shard_map/ppermute | solution.py:444
  63.1 94.2 %collective-permute-start.10 = (bf16[1280,512]{1,0:T(8,128)(2,1)S(1)}, bf16[1280,512]{1,0:T(8,128)(2,1)S(1)}, u32[]{:S(2)}, u32[]{:S(2)}) collective-permute-start(bf16[1280,512]{1,0:T(8,128)(2,1)S(1)} %constant_dynamic-update-slice_fusion.refs_0_), channel_id=1, source_target_pairs={{0,24},{8,0},{16,8},{24,16},{1,25},{9,1},{17,9},{25,17},{2,26},{10... | collective-permute-start | bytes 3932168 | tf_op jit(solution)/shard_map/ppermute | solution.py:444
  65.3 95.4 %collective-permute-start.12 = (bf16[1280,512]{1,0:T(8,128)(2,1)S(1)}, bf16[1280,512]{1,0:T(8,128)(2,1)S(1)}, u32[]{:S(2)}, u32[]{:S(2)}) collective-permute-start(bf16[1280,512]{1,0:T(8,128)(2,1)S(1)} %constant_dynamic-update-slice_fusion.refs_0_), channel_id=1, source_target_pairs={{0,8},{8,16},{16,24},{24,0},{1,9},{9,17},{17,25},{25,1},{2,10},{10... | collective-permute-start | bytes 3932168 | tf_op jit(solution)/shard_map/ppermute | solution.py:444
  65.5 66.6 %collective-permute-start.3 = (bf16[8,512]{1,0:T(8,128)(2,1)S(1)}, bf16[8,512]{1,0:T(8,128)(2,1)S(1)}, u32[]{:S(2)}, u32[]{:S(2)}) collective-permute-start(bf16[8,512]{1,0:T(8,128)(2,1)S(1)} %select_select_fusion), channel_id=1, source_target_pairs={{0,24},{8,0},{16,8},{24,16},{1,25},{9,1},{17,9},{25,17},{2,26},{10... | collective-permute-start | bytes 24584 | tf_op jit(solution)/shard_map/ppermute | solution.py:444
  103.9 76.9 %collective-permute-start.7 = (bf16[256,1792]{1,0:T(8,128)(2,1)S(1)}, bf16[256,1792]{1,0:T(8,128)(2,1)}, u32[]{:S(2)}, u32[]{:S(2)}) collective-permute-start(bf16[256,1792]{1,0:T(8,128)(2,1)S(1)} %slice.72), channel_id=1, source_target_pairs={{0,24},{8,0},{16,8},{24,16},{1,25},{9,1},{17,9},{25,17},{2,26},{10... | collective-permute-start | bytes 2752520 | tf_op jit(solution)/shard_map/ppermute | solution.py:444
  107.2 73.6 %collective-permute-start.9 = (bf16[256,1792]{1,0:T(8,128)(2,1)}, bf16[256,1792]{1,0:T(8,128)(2,1)}, u32[]{:S(2)}, u32[]{:S(2)}) collective-permute-start(bf16[256,1792]{1,0:T(8,128)(2,1)} %slice.73), channel_id=1, source_target_pairs={{0,8},{8,16},{16,24},{24,0},{1,9},{9,17},{17,25},{25,1},{2,10},{10... | collective-permute-start | bytes 2752520 | tf_op jit(solution)/shard_map/ppermute | solution.py:444
  157.3 56.3 %collective-permute-start.11 = (bf16[1280,256]{1,0:T(8,128)(2,1)S(1)}, bf16[1280,256]{1,0:T(8,128)(2,1)}, u32[]{:S(2)}, u32[]{:S(2)}) collective-permute-start(bf16[1280,256]{1,0:T(8,128)(2,1)S(1)} %slice.74), channel_id=1, source_target_pairs={{0,24},{8,0},{16,8},{24,16},{1,25},{9,1},{17,9},{25,17},{2,26},{10... | collective-permute-start | bytes 1966088 | tf_op jit(solution)/shard_map/ppermute | solution.py:444
  162.7 50.9 %collective-permute-start.13 = (bf16[1280,256]{1,0:T(8,128)(2,1)}, bf16[1280,256]{1,0:T(8,128)(2,1)}, u32[]{:S(2)}, u32[]{:S(2)}) collective-permute-start(bf16[1280,256]{1,0:T(8,128)(2,1)} %slice.75), channel_id=1, source_target_pairs={{0,8},{8,16},{16,24},{24,0},{1,9},{9,17},{17,25},{25,1},{2,10},{10... | collective-permute-start | bytes 1966088 | tf_op jit(solution)/shard_map/ppermute | solution.py:444
  309.2 111.1 %reduce-scatter.4.cloned.1.call-start = ((), (), s32[]{:S(2)}) async-start(), calls=%async_computation.4 | async-start | bytes 14155776 | tf_op jit(solution)/shard_map/reduce_scatter | solution.py:530
  341.2 178.1 %reduce-scatter.8.cloned.1.call-start = ((), (), s32[]{:S(2)}) async-start(), calls=%async_computation.9 | async-start | bytes 7077888 | tf_op jit(solution)/shard_map/reduce_scatter | solution.py:547
  341.9 359.6 %all-gather.11.cloned.1.call-start = ((), (), s32[]{:S(2)}) async-start(), calls=%async_computation.8 | async-start | bytes 7077888 | tf_op jit(solution)/shard_map/all_gather | solution.py:555
  366.3 341.1 %all-gather.7.cloned.1.call-start = ((), (), s32[]{:S(2)}) async-start(), calls=%async_computation.5 | async-start | bytes 14155776 | tf_op jit(solution)/shard_map/all_gather | solution.py:532
  456.1 24.9 %collective-permute-start.43 = (bf16[640,512]{1,0:T(8,128)(2,1)}, bf16[640,512]{1,0:T(8,128)(2,1)}, u32[]{:S(2)}, u32[]{:S(2)}) collective-permute-start(bf16[640,512]{1,0:T(8,128)(2,1)} %get-tuple-element.87), channel_id=1, source_target_pairs={{0,8},{8,16},{16,24},{24,0},{1,9},{9,17},{17,25},{25,1},{2,10},{10... | collective-permute-start | bytes 1966088 | tf_op jit(solution)/shard_map/ppermute | solution.py:444
  457.8 23.2 %collective-permute-start.44 = (bf16[640,512]{1,0:T(8,128)(2,1)}, bf16[640,512]{1,0:T(8,128)(2,1)}, u32[]{:S(2)}, u32[]{:S(2)}) collective-permute-start(bf16[640,512]{1,0:T(8,128)(2,1)} %get-tuple-element.88), channel_id=1, source_target_pairs={{0,24},{8,0},{16,8},{24,16},{1,25},{9,1},{17,9},{25,17},{2,26},{10... | collective-permute-start | bytes 1966088 | tf_op jit(solution)/shard_map/ppermute | solution.py:444
  481.0 41.7 %collective-permute-start.36 = (f32[4,512]{1,0:T(4,128)}, f32[4,512]{1,0:T(4,128)}, u32[]{:S(2)}, u32[]{:S(2)}) collective-permute-start(f32[4,512]{1,0:T(4,128)} %slice.82), channel_id=1, source_target_pairs={{0,1},{1,0},{2,3},{3,2},{4,5},{5,4},{6,7},{7,6},{8,9},{9,8},{10,11... | collective-permute-start | bytes 24584 | tf_op jit(solution)/shard_map/ppermute | solution.py:449
  495.6 132.2 %collective-permute-start.45 = (bf16[1280,512]{1,0:T(8,128)(2,1)}, bf16[1280,512]{1,0:T(8,128)(2,1)}, u32[]{:S(2)}, u32[]{:S(2)}) collective-permute-start(bf16[1280,512]{1,0:T(8,128)(2,1)} %get-tuple-element.89), channel_id=1, source_target_pairs={{0,8},{8,16},{16,24},{24,0},{1,9},{9,17},{17,25},{25,1},{2,10},{10... | collective-permute-start | bytes 3932168 | tf_op jit(solution)/shard_map/ppermute | solution.py:444
  495.6 134.1 %collective-permute-start.46 = (bf16[1280,512]{1,0:T(8,128)(2,1)}, bf16[1280,512]{1,0:T(8,128)(2,1)}, u32[]{:S(2)}, u32[]{:S(2)}) collective-permute-start(bf16[1280,512]{1,0:T(8,128)(2,1)} %get-tuple-element.90), channel_id=1, source_target_pairs={{0,24},{8,0},{16,8},{24,16},{1,25},{9,1},{17,9},{25,17},{2,26},{10... | collective-permute-start | bytes 3932168 | tf_op jit(solution)/shard_map/ppermute | solution.py:444
  519.3 120.5 %collective-permute-start.41 = (bf16[512,1792]{1,0:T(8,128)(2,1)}, bf16[512,1792]{1,0:T(8,128)(2,1)}, u32[]{:S(2)}, u32[]{:S(2)}) collective-permute-start(bf16[512,1792]{1,0:T(8,128)(2,1)} %get-tuple-element.84), channel_id=1, source_target_pairs={{0,8},{8,16},{16,24},{24,0},{1,9},{9,17},{17,25},{25,1},{2,10},{10... | collective-permute-start | bytes 5505032 | tf_op jit(solution)/shard_map/ppermute | solution.py:444
  521.4 54.5 %collective-permute-start.23 = (bf16[192,512]{1,0:T(8,128)(2,1)S(1)}, bf16[192,512]{1,0:T(8,128)(2,1)S(1)}, u32[]{:S(2)}, u32[]{:S(2)}) collective-permute-start(bf16[192,512]{1,0:T(8,128)(2,1)S(1)} %get-tuple-element.75), channel_id=1, source_target_pairs={{0,8},{8,16},{16,24},{24,0},{1,9},{9,17},{17,25},{25,1},{2,10},{10... | collective-permute-start | bytes 589832 | tf_op jit(solution)/shard_map/ppermute | solution.py:444
  527.3 48.6 %collective-permute-start.24 = (bf16[192,512]{1,0:T(8,128)(2,1)S(1)}, bf16[192,512]{1,0:T(8,128)(2,1)S(1)}, u32[]{:S(2)}, u32[]{:S(2)}) collective-permute-start(bf16[192,512]{1,0:T(8,128)(2,1)S(1)} %get-tuple-element.76), channel_id=1, source_target_pairs={{0,16},{8,24},{16,0},{24,8},{1,17},{9,25},{17,1},{25,9},{2,18},{10... | collective-permute-start | bytes 589832 | tf_op jit(solution)/shard_map/ppermute | solution.py:444
  575.9 99.0 %collective-permute-start.42 = (bf16[512,1792]{1,0:T(8,128)(2,1)}, bf16[512,1792]{1,0:T(8,128)(2,1)S(1)}, u32[]{:S(2)}, u32[]{:S(2)}) collective-permute-start(bf16[512,1792]{1,0:T(8,128)(2,1)} %get-tuple-element.85), channel_id=1, source_target_pairs={{0,24},{8,0},{16,8},{24,16},{1,25},{9,1},{17,9},{25,17},{2,26},{10... | collective-permute-start | bytes 5505032 | tf_op jit(solution)/shard_map/ppermute | solution.py:444
  575.9 46.0 %collective-permute-start.25 = (bf16[192,512]{1,0:T(8,128)(2,1)S(1)}, bf16[192,512]{1,0:T(8,128)(2,1)}, u32[]{:S(2)}, u32[]{:S(2)}) collective-permute-start(bf16[192,512]{1,0:T(8,128)(2,1)S(1)} %get-tuple-element.77), channel_id=1, source_target_pairs={{0,24},{8,0},{16,8},{24,16},{1,25},{9,1},{17,9},{25,17},{2,26},{10... | collective-permute-start | bytes 589832 | tf_op jit(solution)/shard_map/ppermute | solution.py:444
  627.8 33.8 %collective-permute-start.27 = (bf16[4,192,512]{2,1,0:T(8,128)(2,1)S(1)}, bf16[4,192,512]{2,1,0:T(8,128)(2,1)}, u32[]{:S(2)}, u32[]{:S(2)}) collective-permute-start(bf16[4,192,512]{2,1,0:T(8,128)(2,1)S(1)} %pad_maximum_fusion.7.refs_0_), channel_id=1, source_target_pairs={{0,4},{1,5},{2,6},{3,7},{4,0},{5,1},{6,2},{7,3},{8,12},{9,13},{10,... | collective-permute-start | bytes 2359304 | tf_op jit(solution)/shard_map/ppermute | solution.py:454
  629.7 33.2 %collective-permute-start.28 = (bf16[4,192,512]{2,1,0:T(8,128)(2,1)S(1)}, bf16[4,192,512]{2,1,0:T(8,128)(2,1)}, u32[]{:S(2)}, u32[]{:S(2)}) collective-permute-start(bf16[4,192,512]{2,1,0:T(8,128)(2,1)S(1)} %pad_maximum_fusion.7.refs_0_), channel_id=1, source_target_pairs={{0,2},{1,3},{2,4},{3,5},{4,6},{5,7},{6,0},{7,1},{8,10},{9,11},{10,... | collective-permute-start | bytes 2359304 | tf_op jit(solution)/shard_map/ppermute | solution.py:454
  639.8 55.5 %collective-permute-start.29 = (bf16[4,192,512]{2,1,0:T(8,128)(2,1)S(1)}, bf16[4,192,512]{2,1,0:T(8,128)(2,1)}, u32[]{:S(2)}, u32[]{:S(2)}) collective-permute-start(bf16[4,192,512]{2,1,0:T(8,128)(2,1)S(1)} %pad_maximum_fusion.7.refs_0_), channel_id=1, source_target_pairs={{0,1},{1,0},{2,3},{3,2},{4,5},{5,4},{6,7},{7,6},{8,9},{9,8},{10,11... | collective-permute-start | bytes 2359304 | tf_op jit(solution)/shard_map/ppermute | solution.py:457
  646.9 48.4 %collective-permute-start.30 = (bf16[4,192,512]{2,1,0:T(8,128)(2,1)S(1)}, bf16[4,192,512]{2,1,0:T(8,128)(2,1)}, u32[]{:S(2)}, u32[]{:S(2)}) collective-permute-start(bf16[4,192,512]{2,1,0:T(8,128)(2,1)S(1)} %collective-permute-done.26.refs_1_), channel_id=1, source_target_pairs={{0,1},{1,0},{2,3},{3,2},{4,5},{5,4},{6,7},{7,6},{8,9},{9,8},{10,11... | collective-permute-start | bytes 2359304 | tf_op jit(solution)/shard_map/ppermute | solution.py:457
  661.6 33.7 %collective-permute-start.31 = (bf16[4,192,512]{2,1,0:T(8,128)(2,1)}, bf16[4,192,512]{2,1,0:T(8,128)(2,1)}, u32[]{:S(2)}, u32[]{:S(2)}) collective-permute-start(bf16[4,192,512]{2,1,0:T(8,128)(2,1)} %collective-permute-done.27.refs_2_), channel_id=1, source_target_pairs={{0,1},{1,0},{2,3},{3,2},{4,5},{5,4},{6,7},{7,6},{8,9},{9,8},{10,11... | collective-permute-start | bytes 2359304 | tf_op jit(solution)/shard_map/ppermute | solution.py:457
  662.9 32.5 %collective-permute-start.32 = (bf16[4,192,512]{2,1,0:T(8,128)(2,1)}, bf16[4,192,512]{2,1,0:T(8,128)(2,1)}, u32[]{:S(2)}, u32[]{:S(2)}) collective-permute-start(bf16[4,192,512]{2,1,0:T(8,128)(2,1)} %collective-permute-done.28.refs_3_), channel_id=1, source_target_pairs={{0,1},{1,0},{2,3},{3,2},{4,5},{5,4},{6,7},{7,6},{8,9},{9,8},{10,11... | collective-permute-start | bytes 2359304 | tf_op jit(solution)/shard_map/ppermute | solution.py:457
  (59 other events, 890.5 us)
Sparse Core Ops, SparseCore 0:
  35.4 63.3 all-gather.4
  100.4 65.0 all-gather.8
  309.3 39.5 reduce-scatter.5
  351.0 69.1 reduce-scatter.3
  422.4 39.8 reduce-scatter.7
  463.8 39.2 all-gather.10
  504.7 65.0 all-gather.6

commit v10 on v9

--- a/solution.py
+++ b/solution.py
@@ -524,9 +524,9 @@
             [(qkv_width, jnp.bfloat16), (ff_width, jnp.bfloat16), (ff_width, jnp.bfloat16)], (0, n_tok), 2 * n_tok * in_size)
         qkv_seq = qkv_act.reshape(n_seq, seq_len, qkv_width)
         context = attn_fwd(qkv_seq).reshape(n_tok, head)
-        blocks_per_seq = ty_size // 2
-        y_form = ((ty_size, n_seq, own, d_model), (2, 1, own, d_model), lambda s: (lax.rem(s, blocks_per_seq), s // blocks_per_seq, 0, 0))
-        (y_part,) = tile_call(y_kernel, [context, gelu_out], w_back, [(y_form, jnp.bfloat16)], (0, n_tok), 2 * n_tok * back_size, 2 * own)
+        blocks_per_seq = ty_size // 4
+        y_form = ((ty_size, n_seq, own, d_model), (4, 1, own, d_model), lambda s: (lax.rem(s, blocks_per_seq), s // blocks_per_seq, 0, 0))
+        (y_part,) = tile_call(y_kernel, [context, gelu_out], w_back, [(y_form, jnp.bfloat16)], (0, n_tok), 2 * n_tok * back_size, 4 * own)
         mixed = lax.psum_scatter(y_part.reshape(n_tok, d_model), 'ty', scatter_dimension=0, tiled=True)
         blocks = to_width(row_call(finish_y_kernel, tx_size, 0, n_seq * own, x_rows, mixed, bias_out.reshape(1, -1)))
         full = lax.all_gather(blocks.reshape(tx_size * n_seq, own, d_local), 'ty', axis=1, tiled=True)
@@ -548,7 +548,11 @@
             parts = row_call(finish_dx_kernel, tx_size, s, own, x_rows, value_a6, cot_rows)
             block = to_width(parts)
             if s < n_seq - 1:
-                blocks = [block] + [along(block, hops) for hops in range(1, ty_size // 2)]
+                assert ty_size == 8
+                half = block.shape[0] // 2
+                ahead, behind = along(block, 1), along(block, -1)
+                far = jnp.concatenate([along(ahead[:half], 1), along(behind[half:], -1)], axis=0)
+                blocks = [block, ahead, far, behind]
                 blocks = blocks + [partner(piece) for piece in blocks]
                 dx_act = place_call(place_pieces_kernel, place, blocks, dx_act, s, n_seq, seq_len)
             else:

time: 737 us -> 664 us (0.901)
  waiting for transfers between devices: 322 us -> 238 us
  starting transfers between devices: 59.2 us -> 66.8 us
    ppermute x37, waiting for transfers between devices: 234 us -> 164 us  [shift(): lax.ppermute(value, 'tx', [(s, (s - hops) % tx_size) for s in range(tx_si...]
    ppermute x3 -> x4, waiting for transfers between devices: 23 us -> 13.6 us  [along(): lax.ppermute(value, 'ty', [(s, (s - 2 * hops) % ty_size) for s in range(t...]
  transfers between devices with their start and end apart: 54 -> 55, of which waited for: 22 -> 19; matrix products, arithmetic and copies ran while one was open for 4% -> 6% of each run, Pallas kernels for 25% -> 28%
where the time goes in v10:
time: 664 us; the launch traced here: 652 us
  Pallas kernels  285 us (43%)
  waiting for transfers between devices  238 us (36%)
  starting transfers between devices  66.8 us (10%)
  local copies, waits for them, and re-layouts  24.2 us (4%)
  other arithmetic  22.5 us (3%)
  between operations  15.3 us (2%)
    ppermute x37, waiting for transfers between devices, shift(): lax.ppermute(value, 'tx', [(s, (s - hops) % tx_size) for s in range(tx_si...  164 us
    pallas_call x6, Pallas kernels, tile_call(): pl.pallas_call(kernel, grid=(count // rows,), in_specs=in_specs, out_spec...  144 us
    pallas_call x6, Pallas kernels, grad_call(): pl.pallas_call(functools.partial(grad_kernel, blocks=terms, moving=adds,...  83.3 us
    ppermute x37, starting transfers between devices, shift(): lax.ppermute(value, 'tx', [(s, (s - hops) % tx_size) for s in range(tx_si...  56.6 us
    reduce_scatter x1, waiting for transfers between devices, body(): lax.psum_scatter(y_part.reshape(n_tok, d_model), 'ty', scatter_dimension=...  52.9 us
    pallas_call x2, Pallas kernels, backward(): pl.pallas_call(lambda *refs: kernel(*refs[:5], *refs[5 + len(into):]), gr...  24.6 us
    pallas_call x3, Pallas kernels, place_call(): pl.pallas_call(functools.partial(kernel, chunk=chunk, n_seq=n_seq), in_sp...  21.4 us
    ppermute x4, waiting for transfers between devices, along(): lax.ppermute(value, 'ty', [(s, (s - 2 * hops) % ty_size) for s in range(t...  13.6 us
  transfers between devices with their start and end apart: 55, of which 19 were waited for; matrix products, arithmetic and copies ran while one was open for 6% of the time, Pallas kernels for 28%

profile of v10, /device:TPU:98, one launch (start us, length us, event | category | flops | bytes accessed | tf_op | source)
XLA Modules:
  0.0 652.3 jit_solution(5665449302099673914)
XLA Ops:
  14.6 15.8 %collective-permute-done = bf16[2,192,512]{2,1,0:T(8,128)(2,1)S(1)} collective-permute-done((bf16[2,192,512]{2,1,0:T(8,128)(2,1)S(1)}, bf16[2,192,512]{2,1,0:T(8,128)(2,1)S(1)}, u32[]{:S(2)}, u32[]{:S(2)}) %collective-permute-start) | collective-permute-done | bytes 393248 | tf_op jit(solution)/shard_map/ppermute | solution.py:444
  38.9 10.0 %collective-permute-done.17 = bf16[2,192,512]{2,1,0:T(8,128)(2,1)S(1)} collective-permute-done((bf16[2,192,512]{2,1,0:T(8,128)(2,1)S(1)}, bf16[2,192,512]{2,1,0:T(8,128)(2,1)S(1)}, u32[]{:S(2)}, u32[]{:S(2)}) %collective-permute-start.17) | collective-permute-done | bytes 393248 | tf_op jit(solution)/shard_map/ppermute | solution.py:444
  51.4 6.4 collective-permute-done.19
  68.7 35.1 %collective-permute-done.6.refs_1_ = bf16[512,1792]{1,0:T(8,128)(2,1)S(1)} collective-permute-done((bf16[512,1792]{1,0:T(8,128)(2,1)S(1)}, bf16[512,1792]{1,0:T(8,128)(2,1)S(1)}, u32[]{:S(2)}, u32[]{:S(2)}) %collective-permute-start.6) | collective-permute-done | bytes 1835040 | tf_op jit(solution)/shard_map/ppermute | solution.py:444
  107.2 24.8 %collective-permute-done.3 = bf16[8,512]{1,0:T(8,128)(2,1)S(1)} collective-permute-done((bf16[8,512]{1,0:T(8,128)(2,1)S(1)}, bf16[8,512]{1,0:T(8,128)(2,1)S(1)}, u32[]{:S(2)}, u32[]{:S(2)}) %collective-permute-start.3) | collective-permute-done | bytes 8224 | tf_op jit(solution)/shard_map/ppermute | solution.py:444
  132.8 18.6 %collective-permute-done.4 = bf16[8,512]{1,0:T(8,128)(2,1)S(1)} collective-permute-done((bf16[8,512]{1,0:T(8,128)(2,1)S(1)}, bf16[8,512]{1,0:T(8,128)(2,1)S(1)}, u32[]{:S(2)}, u32[]{:S(2)}) %collective-permute-start.4) | collective-permute-done | bytes 8224 | tf_op jit(solution)/shard_map/ppermute | solution.py:444
  162.7 18.0 %shard_map.245 = (bf16[3072,2048]{1,0:T(8,128)(2,1)}, bf16[3072,2048]{1,0:T(8,128)(2,1)}) custom-call(bf16[3072,2048]{1,0:T(8,128)(2,1)} %bitcast.91, f32[8,2048]{1,0:T(8,128)} %maximum_convert_fusion.small_ref), custom_call_target="tpu_custom_call" | custom-call | flops 100663296 | bytes 37781504 | tf_op jit(solution)/shard_map/pallas_call | solution.py:423
  180.7 32.8 %shard_map.246 = (bf16[3072,768]{1,0:T(8,128)(2,1)}, bf16[3072,1024]{1,0:T(8,128)(2,1)}, bf16[3072,1024]{1,0:T(8,128)(2,1)}) custom-call(bf16[3072,2048]{1,0:T(8,128)(2,1)} %get-tuple-element.54.h_attn_ref.refs_0_.refs_4_, bf16[3072,2048]{1,0:T(8,128)(2,1)} %get-tuple-element.55.h_mlp_ref.refs_2_.refs_5_, f32[1536,128]{1,0:T(8,128)} %get-tuple-element.128.cos_ref.refs_2_, ...), custom_call_target="tpu_custom_call" | custom-call | flops 22548578304 | bytes 52170240 | tf_op jit(solution)/shard_map/pallas_call | solution.py:423
  213.6 27.1 %shard_map.250 = (bf16[3072,256]{1,0:T(8,128)(2,1)}, bf16[3072,1024]{1,0:T(8,128)(2,1)}, f32[8,1024]{1,0:T(8,128)}) custom-call(bf16[3072,2048]{1,0:T(8,128)(2,1)} %bitcast.76, bf16[3072,1024]{1,0:T(8,128)(2,1)} %get-tuple-element.62.pre_ref, bf16[1280,512]{1,0:T(8,128)(2,1)} %copy-done.22, bf16[1280,512]{1,0:T(8,128)(2,1)} %copy-done.18, ...), custom_call_target="tpu_custom_call" | custom-call | flops 16106127360 | bytes 31997952 | tf_op jit(solution)/shard_map/pallas_call | solution.py:423
  240.7 12.3 %ab.2 = (bf16[2,1536,768]{2,1,0:T(8,128)(2,1)}, f32[1,8,768]{2,1,0:T(8,128)}) custom-call(bf16[2,1536,768]{2,1,0:T(8,128)(2,1)} %bitcast.127, bf16[2,1536,256]{2,1,0:T(8,128)(2,1)} %bitcast.130, f32[1536,128]{1,0:T(8,128)} %get-tuple-element.128.cos_ref.refs_2_, f32[1536,128]{1,0:T(8,128)} %get-tuple-element.127.lo_ref.refs_3_, ...), custom_call_target="tpu_custom_call" | custom-call | flops 6039797760 | bytes 5505024 | tf_op jit(solution)/shard_map/ab/pallas_call | solution.py:127
  252.9 22.0 %shard_map.251 = (bf16[1536,2048]{1,0:T(8,128)(2,1)}, f32[4,8,2048]{2,1,0:T(8,128)}) custom-call(bf16[3072,768]{1,0:T(8,128)(2,1)} %bitcast.81, bf16[3072,1024]{1,0:T(8,128)(2,1)} %get-tuple-element.65.d_pre_ref.refs_3_, bf16[3072,2048]{1,0:T(8,128)(2,1)} %bitcast.92, f32[8,2048]{1,0:T(8,128)} %maximum_convert_fusion.small_ref, bf16[512,1792]{1,0:T(8,128)(2,1)} %copy-done.4, ...), custom_call_target="tpu_custom_call" | custom-call | flops 11274289152 | bytes 25591808 | tf_op jit(solution)/shard_map/pallas_call | solution.py:423
  274.9 12.3 %ab.3 = (bf16[2,1536,768]{2,1,0:T(8,128)(2,1)}, f32[1,8,768]{2,1,0:T(8,128)}) custom-call(bf16[2,1536,768]{2,1,0:T(8,128)(2,1)} %bitcast.128, bf16[2,1536,256]{2,1,0:T(8,128)(2,1)} %bitcast.131, f32[1536,128]{1,0:T(8,128)} %get-tuple-element.128.cos_ref.refs_2_, f32[1536,128]{1,0:T(8,128)} %get-tuple-element.127.lo_ref.refs_3_, ...), custom_call_target="tpu_custom_call", output_to_operand_aliasing={{0}: (5, {})} | custom-call | flops 6039797760 | bytes 5505024 | tf_op jit(solution)/shard_map/ab/pallas_call | solution.py:127
  287.2 21.7 %shard_map.252 = (bf16[1536,2048]{1,0:T(8,128)(2,1)}, f32[4,8,2048]{2,1,0:T(8,128)}) custom-call(bf16[3072,768]{1,0:T(8,128)(2,1)} %bitcast.82, bf16[3072,1024]{1,0:T(8,128)(2,1)} %get-tuple-element.65.d_pre_ref.refs_3_, bf16[3072,2048]{1,0:T(8,128)(2,1)} %bitcast.93, f32[8,2048]{1,0:T(8,128)} %maximum_convert_fusion.small_ref, bf16[512,1792]{1,0:T(8,128)(2,1)} %copy-done.4, ...), custom_call_target="tpu_custom_call" | custom-call | flops 11274289152 | bytes 25591808 | tf_op jit(solution)/shard_map/pallas_call | solution.py:423
  309.1 9.9 %af.1 = bf16[2,1536,256]{2,1,0:T(8,128)(2,1)} custom-call(bf16[2,1536,768]{2,1,0:T(8,128)(2,1)} %bitcast.129), custom_call_target="tpu_custom_call" | custom-call | flops 4831838208 | bytes 6291456 | tf_op jit(solution)/shard_map/af/pallas_call | solution.py:114
  319.0 22.0 %shard_map.247 = bf16[8,2,192,2048]{3,2,1,0:T(8,128)(2,1)} custom-call(bf16[3072,256]{1,0:T(8,128)(2,1)} %bitcast.87, bf16[3072,1024]{1,0:T(8,128)(2,1)} %get-tuple-element.57.gelu_ref.refs_2_, bf16[1280,512]{1,0:T(8,128)(2,1)} %copy-done.22, bf16[1280,512]{1,0:T(8,128)(2,1)} %copy-done.18, bf16[1280,256]{1,0:T(8,128)(2,1)} %collective-permute-done.11.refs_2_, ...), custom_call_target="tpu_custom_call" | custom-call | flops 16106127360 | bytes 25690112 | tf_op jit(solution)/shard_map/pallas_call | solution.py:423
  367.1 52.9 %reduce-scatter.4.cloned.1.call-done.mixed_ref = bf16[384,2048]{1,0:T(8,128)(2,1)} async-done(((bf16[3072,2048]{1,0:T(8,128)(2,1)}), bf16[384,2048]{1,0:T(8,128)(2,1)}) %reduce-scatter.4.cloned.1.call-update) | async-done | bytes 1572880 | tf_op jit(solution)/shard_map/reduce_scatter | solution.py:530
  427.9 7.0 %collective-permute-done.14 = bf16[384,512]{1,0:T(8,128)(2,1)S(1)} collective-permute-done((bf16[384,512]{1,0:T(8,128)(2,1)S(1)}, bf16[384,512]{1,0:T(8,128)(2,1)S(1)}, u32[]{:S(2)}, u32[]{:S(2)}) %collective-permute-start.14) | collective-permute-done | bytes 393248 | tf_op jit(solution)/shard_map/ppermute | solution.py:444
  434.9 9.8 %collective-permute-done.15 = bf16[384,512]{1,0:T(8,128)(2,1)S(1)} collective-permute-done((bf16[384,512]{1,0:T(8,128)(2,1)S(1)}, bf16[384,512]{1,0:T(8,128)(2,1)S(1)}, u32[]{:S(2)}, u32[]{:S(2)}) %collective-permute-start.15) | collective-permute-done | bytes 393248 | tf_op jit(solution)/shard_map/ppermute | solution.py:444
  454.5 12.1 %shard_map.257 = (bf16[256,1792]{1,0:T(8,128)(2,1)}, bf16[256,1792]{1,0:T(8,128)(2,1)}) custom-call(bf16[3072,2048]{1,0:T(8,128)(2,1)} %get-tuple-element.54.h_attn_ref.refs_0_.refs_4_, bf16[3072,768]{1,0:T(8,128)(2,1)} %bitcast.83, bf16[3072,2048]{1,0:T(8,128)(2,1)} %get-tuple-element.55.h_mlp_ref.refs_2_.refs_5_, ...), custom_call_target="tpu_custom_call" | custom-call | flops 5637144576 | bytes 17301504 | tf_op jit(solution)/shard_map/pallas_call | solution.py:248
  477.8 9.7 %shard_map.260 = (bf16[640,512]{1,0:T(8,128)(2,1)}, bf16[640,512]{1,0:T(8,128)(2,1)}) custom-call(bf16[3072,256]{1,0:T(8,128)(2,1)} %bitcast.88, bf16[3072,2048]{1,0:T(8,128)(2,1)} %bitcast.77, bf16[3072,1024]{1,0:T(8,128)(2,1)} %get-tuple-element.57.gelu_ref.refs_2_), custom_call_target="tpu_custom_call" | custom-call | flops 4026531840 | bytes 11010048 | tf_op jit(solution)/shard_map/pallas_call | solution.py:248
  487.5 10.7 %collective-permute-done.23 = bf16[192,512]{1,0:T(8,128)(2,1)S(1)} collective-permute-done((bf16[192,512]{1,0:T(8,128)(2,1)S(1)}, bf16[192,512]{1,0:T(8,128)(2,1)S(1)}, u32[]{:S(2)}, u32[]{:S(2)}) %collective-permute-start.23) | collective-permute-done | bytes 196640 | tf_op jit(solution)/shard_map/ppermute | solution.py:444
  504.4 19.9 %shard_map.258 = (bf16[512,1792]{1,0:T(8,128)(2,1)}, bf16[512,1792]{1,0:T(8,128)(2,1)}) custom-call(bf16[3072,2048]{1,0:T(8,128)(2,1)} %get-tuple-element.54.h_attn_ref.refs_0_.refs_4_, bf16[3072,768]{1,0:T(8,128)(2,1)} %bitcast.84, bf16[3072,2048]{1,0:T(8,128)(2,1)} %get-tuple-element.55.h_mlp_ref.refs_2_.refs_5_, ...), custom_call_target="tpu_custom_call" | custom-call | flops 11274289152 | bytes 45613056 | tf_op jit(solution)/shard_map/pallas_call | solution.py:248
  528.4 14.3 %shard_map.261 = (bf16[1280,512]{1,0:T(8,128)(2,1)}, bf16[1280,512]{1,0:T(8,128)(2,1)}) custom-call(bf16[3072,256]{1,0:T(8,128)(2,1)} %bitcast.89, bf16[3072,2048]{1,0:T(8,128)(2,1)} %bitcast.78, bf16[3072,1024]{1,0:T(8,128)(2,1)} %get-tuple-element.57.gelu_ref.refs_2_, bf16[3072,2048]{1,0:T(8,128)(2,1)} %bitcast.79, bf16[640,512]{1,0:T(8,128)(2,1)} %copy-done.15, ...), custom_call_target="tpu_custom_call" | custom-call | flops 8053063680 | bytes 20447232 | tf_op jit(solution)/shard_map/pallas_call | solution.py:248
  548.5 6.3 convert_reduce_fusion
  556.7 7.5 %collective-permute-done.27 = bf16[2,192,512]{2,1,0:T(8,128)(2,1)} collective-permute-done((bf16[2,192,512]{2,1,0:T(8,128)(2,1)S(1)}, bf16[2,192,512]{2,1,0:T(8,128)(2,1)}, u32[]{:S(2)}, u32[]{:S(2)}) %collective-permute-start.27) | collective-permute-done | bytes 393248 | tf_op jit(solution)/shard_map/ppermute | solution.py:454
  571.4 6.1 collective-permute-done.29
  579.3 11.5 %collective-permute-done.46.refs_3_ = bf16[1280,512]{1,0:T(8,128)(2,1)} collective-permute-done((bf16[1280,512]{1,0:T(8,128)(2,1)}, bf16[1280,512]{1,0:T(8,128)(2,1)}, u32[]{:S(2)}, u32[]{:S(2)}) %collective-permute-start.46) | collective-permute-done | bytes 1310752 | tf_op jit(solution)/shard_map/ppermute | solution.py:444
  591.4 12.3 %shard_map.262 = (f32[256,512]{1,0:T(8,128)}, f32[1024,512]{1,0:T(8,128)}) custom-call(bf16[3072,256]{1,0:T(8,128)(2,1)} %bitcast.90, bf16[3072,2048]{1,0:T(8,128)(2,1)} %bitcast.80, bf16[3072,1024]{1,0:T(8,128)(2,1)} %get-tuple-element.57.gelu_ref.refs_2_, bf16[1280,512]{1,0:T(8,128)(2,1)} %collective-permute-done.46.refs_3_, ...), custom_call_target="tpu_custom_call" | custom-call | flops 4026531840 | bytes 17301504 | tf_op jit(solution)/shard_map/pallas_call | solution.py:248
  603.7 15.0 %shard_map.259 = (f32[512,768]{1,0:T(8,128)}, f32[512,1024]{1,0:T(8,128)}) custom-call(bf16[3072,2048]{1,0:T(8,128)(2,1)} %get-tuple-element.54.h_attn_ref.refs_0_.refs_4_, bf16[3072,768]{1,0:T(8,128)(2,1)} %bitcast.85, bf16[3072,2048]{1,0:T(8,128)(2,1)} %get-tuple-element.55.h_mlp_ref.refs_2_.refs_5_, ...), custom_call_target="tpu_custom_call" | custom-call | flops 5637144576 | bytes 39321600 | tf_op jit(solution)/shard_map/pallas_call | solution.py:248
  622.9 6.1 shard_map.255.rest_0_
  629.1 5.8 shard_map.256
  635.0 9.4 %shard_map.249 = bf16[4,3072,512]{2,1,0:T(8,128)(2,1)} custom-call(s32[3]{0:T(128)} %pad_add_fusion.place_ref, bf16[4,3072,512]{2,1,0:T(8,128)(2,1)} %bitcast.95), custom_call_target="tpu_custom_call" | custom-call | flops 6291456 | bytes 25165824 | tf_op jit(solution)/shard_map/pallas_call | solution.py:187
  (232 shorter events, 131.8 us)
Async XLA Ops:
  7.2 155.5 %all-gather.5.cloned.1.call-start = ((), (), s32[]{:S(2)}) async-start(), calls=%async_computation.3 | async-start | bytes 14155776 | tf_op jit(solution)/shard_map/all_gather | solution.py:509
  35.3 178.3 %all-gather.9.cloned.1.call-start = ((), (), s32[]{:S(2)}) async-start(), calls=%async_computation.6 | async-start | bytes 14155776 | tf_op jit(solution)/shard_map/all_gather | solution.py:510
  59.1 289.5 %reduce-scatter.6.cloned.1.call-start = ((), (), s32[]{:S(2)}) async-start(), calls=%async_computation.7 | async-start | bytes 7077888 | tf_op jit(solution)/shard_map/reduce_scatter | solution.py:547
  60.8 43.0 %collective-permute-start.6 = (bf16[512,1792]{1,0:T(8,128)(2,1)S(1)}, bf16[512,1792]{1,0:T(8,128)(2,1)S(1)}, u32[]{:S(2)}, u32[]{:S(2)}) collective-permute-start(bf16[512,1792]{1,0:T(8,128)(2,1)S(1)} %pad_maximum_fusion.refs_0_), channel_id=1, source_target_pairs={{0,24},{8,0},{16,8},{24,16},{1,25},{9,1},{17,9},{25,17},{2,26},{10... | collective-permute-start | bytes 5505032 | tf_op jit(solution)/shard_map/ppermute | solution.py:444
  61.8 44.3 %collective-permute-start.8 = (bf16[512,1792]{1,0:T(8,128)(2,1)S(1)}, bf16[512,1792]{1,0:T(8,128)(2,1)S(1)}, u32[]{:S(2)}, u32[]{:S(2)}) collective-permute-start(bf16[512,1792]{1,0:T(8,128)(2,1)S(1)} %pad_maximum_fusion.refs_0_), channel_id=1, source_target_pairs={{0,8},{8,16},{16,24},{24,0},{1,9},{9,17},{17,25},{25,1},{2,10},{10... | collective-permute-start | bytes 5505032 | tf_op jit(solution)/shard_map/ppermute | solution.py:444
  63.1 94.2 %collective-permute-start.10 = (bf16[1280,512]{1,0:T(8,128)(2,1)S(1)}, bf16[1280,512]{1,0:T(8,128)(2,1)S(1)}, u32[]{:S(2)}, u32[]{:S(2)}) collective-permute-start(bf16[1280,512]{1,0:T(8,128)(2,1)S(1)} %constant_dynamic-update-slice_fusion.refs_0_), channel_id=1, source_target_pairs={{0,24},{8,0},{16,8},{24,16},{1,25},{9,1},{17,9},{25,17},{2,26},{10... | collective-permute-start | bytes 3932168 | tf_op jit(solution)/shard_map/ppermute | solution.py:444
  65.3 95.4 %collective-permute-start.12 = (bf16[1280,512]{1,0:T(8,128)(2,1)S(1)}, bf16[1280,512]{1,0:T(8,128)(2,1)S(1)}, u32[]{:S(2)}, u32[]{:S(2)}) collective-permute-start(bf16[1280,512]{1,0:T(8,128)(2,1)S(1)} %constant_dynamic-update-slice_fusion.refs_0_), channel_id=1, source_target_pairs={{0,8},{8,16},{16,24},{24,0},{1,9},{9,17},{17,25},{25,1},{2,10},{10... | collective-permute-start | bytes 3932168 | tf_op jit(solution)/shard_map/ppermute | solution.py:444
  65.4 66.6 %collective-permute-start.3 = (bf16[8,512]{1,0:T(8,128)(2,1)S(1)}, bf16[8,512]{1,0:T(8,128)(2,1)S(1)}, u32[]{:S(2)}, u32[]{:S(2)}) collective-permute-start(bf16[8,512]{1,0:T(8,128)(2,1)S(1)} %select_select_fusion), channel_id=1, source_target_pairs={{0,24},{8,0},{16,8},{24,16},{1,25},{9,1},{17,9},{25,17},{2,26},{10... | collective-permute-start | bytes 24584 | tf_op jit(solution)/shard_map/ppermute | solution.py:444
  103.9 76.8 %collective-permute-start.7 = (bf16[256,1792]{1,0:T(8,128)(2,1)S(1)}, bf16[256,1792]{1,0:T(8,128)(2,1)}, u32[]{:S(2)}, u32[]{:S(2)}) collective-permute-start(bf16[256,1792]{1,0:T(8,128)(2,1)S(1)} %slice.80), channel_id=1, source_target_pairs={{0,24},{8,0},{16,8},{24,16},{1,25},{9,1},{17,9},{25,17},{2,26},{10... | collective-permute-start | bytes 2752520 | tf_op jit(solution)/shard_map/ppermute | solution.py:444
  107.2 73.5 %collective-permute-start.9 = (bf16[256,1792]{1,0:T(8,128)(2,1)}, bf16[256,1792]{1,0:T(8,128)(2,1)}, u32[]{:S(2)}, u32[]{:S(2)}) collective-permute-start(bf16[256,1792]{1,0:T(8,128)(2,1)} %slice.81), channel_id=1, source_target_pairs={{0,8},{8,16},{16,24},{24,0},{1,9},{9,17},{17,25},{25,1},{2,10},{10... | collective-permute-start | bytes 2752520 | tf_op jit(solution)/shard_map/ppermute | solution.py:444
  157.3 56.2 %collective-permute-start.11 = (bf16[1280,256]{1,0:T(8,128)(2,1)S(1)}, bf16[1280,256]{1,0:T(8,128)(2,1)}, u32[]{:S(2)}, u32[]{:S(2)}) collective-permute-start(bf16[1280,256]{1,0:T(8,128)(2,1)S(1)} %slice.82), channel_id=1, source_target_pairs={{0,24},{8,0},{16,8},{24,16},{1,25},{9,1},{17,9},{25,17},{2,26},{10... | collective-permute-start | bytes 1966088 | tf_op jit(solution)/shard_map/ppermute | solution.py:444
  162.6 50.9 %collective-permute-start.13 = (bf16[1280,256]{1,0:T(8,128)(2,1)}, bf16[1280,256]{1,0:T(8,128)(2,1)}, u32[]{:S(2)}, u32[]{:S(2)}) collective-permute-start(bf16[1280,256]{1,0:T(8,128)(2,1)} %slice.83), channel_id=1, source_target_pairs={{0,8},{8,16},{16,24},{24,0},{1,9},{9,17},{17,25},{25,1},{2,10},{10... | collective-permute-start | bytes 1966088 | tf_op jit(solution)/shard_map/ppermute | solution.py:444
  309.0 111.0 %reduce-scatter.4.cloned.1.call-start = ((), (), s32[]{:S(2)}) async-start(), calls=%async_computation.4 | async-start | bytes 14155776 | tf_op jit(solution)/shard_map/reduce_scatter | solution.py:530
  341.0 131.3 %reduce-scatter.8.cloned.1.call-start = ((), (), s32[]{:S(2)}) async-start(), calls=%async_computation.9 | async-start | bytes 7077888 | tf_op jit(solution)/shard_map/reduce_scatter | solution.py:547
  341.7 287.4 %all-gather.11.cloned.1.call-start = ((), (), s32[]{:S(2)}) async-start(), calls=%async_computation.8 | async-start | bytes 7077888 | tf_op jit(solution)/shard_map/all_gather | solution.py:559
  366.1 268.9 %all-gather.7.cloned.1.call-start = ((), (), s32[]{:S(2)}) async-start(), calls=%async_computation.5 | async-start | bytes 14155776 | tf_op jit(solution)/shard_map/all_gather | solution.py:532
  466.6 34.9 %collective-permute-start.40 = (bf16[256,1792]{1,0:T(8,128)(2,1)}, bf16[256,1792]{1,0:T(8,128)(2,1)}, u32[]{:S(2)}, u32[]{:S(2)}) collective-permute-start(bf16[256,1792]{1,0:T(8,128)(2,1)} %get-tuple-element.82), channel_id=1, source_target_pairs={{0,8},{8,16},{16,24},{24,0},{1,9},{9,17},{17,25},{25,1},{2,10},{10... | collective-permute-start | bytes 2752520 | tf_op jit(solution)/shard_map/ppermute | solution.py:444
  466.6 37.8 %collective-permute-start.41 = (bf16[256,1792]{1,0:T(8,128)(2,1)}, bf16[256,1792]{1,0:T(8,128)(2,1)}, u32[]{:S(2)}, u32[]{:S(2)}) collective-permute-start(bf16[256,1792]{1,0:T(8,128)(2,1)} %get-tuple-element.83), channel_id=1, source_target_pairs={{0,24},{8,0},{16,8},{24,16},{1,25},{9,1},{17,9},{25,17},{2,26},{10... | collective-permute-start | bytes 2752520 | tf_op jit(solution)/shard_map/ppermute | solution.py:444
  476.0 25.4 %collective-permute-start.25 = (bf16[192,512]{1,0:T(8,128)(2,1)S(1)}, bf16[192,512]{1,0:T(8,128)(2,1)S(1)}, u32[]{:S(2)}, u32[]{:S(2)}) collective-permute-start(bf16[192,512]{1,0:T(8,128)(2,1)S(1)} %get-tuple-element.77), channel_id=1, source_target_pairs={{0,24},{8,0},{16,8},{24,16},{1,25},{9,1},{17,9},{25,17},{2,26},{10... | collective-permute-start | bytes 589832 | tf_op jit(solution)/shard_map/ppermute | solution.py:444
  498.2 26.1 %collective-permute-start.44 = (bf16[640,512]{1,0:T(8,128)(2,1)}, bf16[640,512]{1,0:T(8,128)(2,1)S(1)}, u32[]{:S(2)}, u32[]{:S(2)}) collective-permute-start(bf16[640,512]{1,0:T(8,128)(2,1)} %get-tuple-element.87), channel_id=1, source_target_pairs={{0,8},{8,16},{16,24},{24,0},{1,9},{9,17},{17,25},{25,1},{2,10},{10... | collective-permute-start | bytes 1966088 | tf_op jit(solution)/shard_map/ppermute | solution.py:444
  498.2 26.9 %collective-permute-start.45 = (bf16[640,512]{1,0:T(8,128)(2,1)}, bf16[640,512]{1,0:T(8,128)(2,1)}, u32[]{:S(2)}, u32[]{:S(2)}) collective-permute-start(bf16[640,512]{1,0:T(8,128)(2,1)} %get-tuple-element.88), channel_id=1, source_target_pairs={{0,24},{8,0},{16,8},{24,16},{1,25},{9,1},{17,9},{25,17},{2,26},{10... | collective-permute-start | bytes 1966088 | tf_op jit(solution)/shard_map/ppermute | solution.py:444
  501.4 41.4 %collective-permute-start.39 = (f32[4,512]{1,0:T(4,128)S(1)}, f32[4,512]{1,0:T(4,128)S(1)}, u32[]{:S(2)}, u32[]{:S(2)}) collective-permute-start(f32[4,512]{1,0:T(4,128)S(1)} %add.101), channel_id=1, source_target_pairs={{0,4},{1,5},{2,6},{3,7},{4,0},{5,1},{6,2},{7,3},{8,12},{9,13},{10,... | collective-permute-start | bytes 24584 | tf_op jit(solution)/shard_map/ppermute | solution.py:449
  501.6 41.2 %collective-permute-start.26 = (bf16[4,192,512]{2,1,0:T(8,128)(2,1)S(1)}, bf16[4,192,512]{2,1,0:T(8,128)(2,1)S(1)}, u32[]{:S(2)}, u32[]{:S(2)}) collective-permute-start(bf16[4,192,512]{2,1,0:T(8,128)(2,1)S(1)} %pad_maximum_fusion.7.refs_0_), channel_id=1, source_target_pairs={{0,6},{1,7},{2,0},{3,1},{4,2},{5,3},{6,4},{7,5},{8,14},{9,15},{10,... | collective-permute-start | bytes 2359304 | tf_op jit(solution)/shard_map/ppermute | solution.py:454
  504.4 41.8 %collective-permute-start.28 = (bf16[4,192,512]{2,1,0:T(8,128)(2,1)S(1)}, bf16[4,192,512]{2,1,0:T(8,128)(2,1)}, u32[]{:S(2)}, u32[]{:S(2)}) collective-permute-start(bf16[4,192,512]{2,1,0:T(8,128)(2,1)S(1)} %pad_maximum_fusion.7.refs_0_), channel_id=1, source_target_pairs={{0,2},{1,3},{2,4},{3,5},{4,6},{5,7},{6,0},{7,1},{8,10},{9,11},{10,... | collective-permute-start | bytes 2359304 | tf_op jit(solution)/shard_map/ppermute | solution.py:454
  525.1 66.2 %collective-permute-start.42 = (bf16[512,1792]{1,0:T(8,128)(2,1)}, bf16[512,1792]{1,0:T(8,128)(2,1)S(1)}, u32[]{:S(2)}, u32[]{:S(2)}) collective-permute-start(bf16[512,1792]{1,0:T(8,128)(2,1)} %get-tuple-element.84), channel_id=1, source_target_pairs={{0,8},{8,16},{16,24},{24,0},{1,9},{9,17},{17,25},{25,1},{2,10},{10... | collective-permute-start | bytes 5505032 | tf_op jit(solution)/shard_map/ppermute | solution.py:444
  525.1 78.6 %collective-permute-start.43 = (bf16[512,1792]{1,0:T(8,128)(2,1)}, bf16[512,1792]{1,0:T(8,128)(2,1)}, u32[]{:S(2)}, u32[]{:S(2)}) collective-permute-start(bf16[512,1792]{1,0:T(8,128)(2,1)} %get-tuple-element.85), channel_id=1, source_target_pairs={{0,24},{8,0},{16,8},{24,16},{1,25},{9,1},{17,9},{25,17},{2,26},{10... | collective-permute-start | bytes 5505032 | tf_op jit(solution)/shard_map/ppermute | solution.py:444
  542.7 48.1 %collective-permute-start.46 = (bf16[1280,512]{1,0:T(8,128)(2,1)}, bf16[1280,512]{1,0:T(8,128)(2,1)}, u32[]{:S(2)}, u32[]{:S(2)}) collective-permute-start(bf16[1280,512]{1,0:T(8,128)(2,1)} %get-tuple-element.89), channel_id=1, source_target_pairs={{0,8},{8,16},{16,24},{24,0},{1,9},{9,17},{17,25},{25,1},{2,10},{10... | collective-permute-start | bytes 3932168 | tf_op jit(solution)/shard_map/ppermute | solution.py:444
  542.9 47.9 %collective-permute-start.47 = (bf16[1280,512]{1,0:T(8,128)(2,1)}, bf16[1280,512]{1,0:T(8,128)(2,1)}, u32[]{:S(2)}, u32[]{:S(2)}) collective-permute-start(bf16[1280,512]{1,0:T(8,128)(2,1)} %get-tuple-element.90), channel_id=1, source_target_pairs={{0,24},{8,0},{16,8},{24,16},{1,25},{9,1},{17,9},{25,17},{2,26},{10... | collective-permute-start | bytes 3932168 | tf_op jit(solution)/shard_map/ppermute | solution.py:444
  577.5 45.4 %collective-permute-start.30 = (bf16[4,192,512]{2,1,0:T(8,128)(2,1)S(1)}, bf16[4,192,512]{2,1,0:T(8,128)(2,1)}, u32[]{:S(2)}, u32[]{:S(2)}) collective-permute-start(bf16[4,192,512]{2,1,0:T(8,128)(2,1)S(1)} %pad_maximum_fusion.7.refs_0_), channel_id=1, source_target_pairs={{0,1},{1,0},{2,3},{3,2},{4,5},{5,4},{6,7},{7,6},{8,9},{9,8},{10,11... | collective-permute-start | bytes 2359304 | tf_op jit(solution)/shard_map/ppermute | solution.py:457
  590.8 32.1 %collective-permute-start.31 = (bf16[4,192,512]{2,1,0:T(8,128)(2,1)S(1)}, bf16[4,192,512]{2,1,0:T(8,128)(2,1)}, u32[]{:S(2)}, u32[]{:S(2)}) collective-permute-start(bf16[4,192,512]{2,1,0:T(8,128)(2,1)S(1)} %collective-permute-done.26.refs_1_), channel_id=1, source_target_pairs={{0,1},{1,0},{2,3},{3,2},{4,5},{5,4},{6,7},{7,6},{8,9},{9,8},{10,11... | collective-permute-start | bytes 2359304 | tf_op jit(solution)/shard_map/ppermute | solution.py:457
  590.8 32.1 %collective-permute-start.33 = (bf16[4,192,512]{2,1,0:T(8,128)(2,1)}, bf16[4,192,512]{2,1,0:T(8,128)(2,1)}, u32[]{:S(2)}, u32[]{:S(2)}) collective-permute-start(bf16[4,192,512]{2,1,0:T(8,128)(2,1)} %collective-permute-done.28.refs_3_), channel_id=1, source_target_pairs={{0,1},{1,0},{2,3},{3,2},{4,5},{5,4},{6,7},{7,6},{8,9},{9,8},{10,11... | collective-permute-start | bytes 2359304 | tf_op jit(solution)/shard_map/ppermute | solution.py:457
  591.3 31.6 %collective-permute-start.32 = (bf16[4,192,512]{2,1,0:T(8,128)(2,1)}, bf16[4,192,512]{2,1,0:T(8,128)(2,1)}, u32[]{:S(2)}, u32[]{:S(2)}) collective-permute-start(bf16[4,192,512]{2,1,0:T(8,128)(2,1)} %constant_dynamic-update-slice_fusion.2.refs_2_), channel_id=1, source_target_pairs={{0,1},{1,0},{2,3},{3,2},{4,5},{5,4},{6,7},{7,6},{8,9},{9,8},{10,11... | collective-permute-start | bytes 2359304 | tf_op jit(solution)/shard_map/ppermute | solution.py:457
  (57 other events, 890.7 us)
Sparse Core Ops, SparseCore 0:
  35.4 63.3 all-gather.4
  100.4 65.0 all-gather.8
  309.1 39.4 reduce-scatter.5
  350.8 69.1 reduce-scatter.3
  422.2 39.8 reduce-scatter.7
  463.6 40.2 all-gather.10
  505.5 74.2 all-gather.6

commit v11 on v10

--- a/solution.py
+++ b/solution.py
@@ -255,6 +255,12 @@
         compiler_params=pltpu.CompilerParams(dimension_semantics=("arbitrary",), vmem_limit_bytes=60 * MIB),
         cost_estimate=pl.CostEstimate(flops=2 * len(blocks) * count * shape[0] * shape[1], bytes_accessed=sum(2 * count * spec.block_shape[1] for spec in specs), transcendentals=0),
     )(*ins)
+
+
+def join_kernel(low_ref, high_ref, out_ref):
+    half = low_ref.shape[0]
+    out_ref[:half] = low_ref[...]
+    out_ref[half:] = high_ref[...]
 
 
 def split_width(value, out_refs):
@@ -551,7 +557,14 @@
                 assert ty_size == 8
                 half = block.shape[0] // 2
                 ahead, behind = along(block, 1), along(block, -1)
-                far = jnp.concatenate([along(ahead[:half], 1), along(behind[half:], -1)], axis=0)
+                halves = [along(ahead[:half], 1), along(behind[half:], -1)]
+                far = pl.pallas_call(
+                    join_kernel,
+                    out_shape=jax.ShapeDtypeStruct(block.shape, block.dtype),
+                    compiler_params=pltpu.CompilerParams(vmem_limit_bytes=16 * MIB),
+                    name="cat",
+                    cost_estimate=pl.CostEstimate(flops=block.size, bytes_accessed=4 * block.size, transcendentals=0),
+                )(*halves)
                 blocks = [block, ahead, far, behind]
                 blocks = blocks + [partner(piece) for piece in blocks]
                 dx_act = place_call(place_pieces_kernel, place, blocks, dx_act, s, n_seq, seq_len)

time: 664 us -> 664 us (level)
  waiting for transfers between devices: 238 us -> 245 us
    ppermute x37, waiting for transfers between devices: 164 us -> 176 us  [shift(): lax.ppermute(value, 'tx', [(s, (s - hops) % tx_size) for s in range(tx_si...]
    unnamed x73 -> x76, local copies, waits for them, and re-layouts: 13.5 us -> 11.8 us
  transfers between devices with their start and end apart: 55 -> 55, of which waited for: 19 -> 18; matrix products, arithmetic and copies ran while one was open for 6% -> 5% of each run, Pallas kernels for 28% -> 28%
where the time goes in v11:
time: 664 us; the launch traced here: 652 us
  Pallas kernels  285 us (43%)
  waiting for transfers between devices  245 us (37%)
  starting transfers between devices  64.8 us (10%)
  other arithmetic  22.7 us (3%)
  local copies, waits for them, and re-layouts  18.9 us (3%)
  between operations  15.4 us (2%)
    ppermute x37, waiting for transfers between devices, shift(): lax.ppermute(value, 'tx', [(s, (s - hops) % tx_size) for s in range(tx_si...  176 us
    pallas_call x6, Pallas kernels, tile_call(): pl.pallas_call(kernel, grid=(count // rows,), in_specs=in_specs, out_spec...  144 us
    pallas_call x6, Pallas kernels, grad_call(): pl.pallas_call(functools.partial(grad_kernel, blocks=terms, moving=adds,...  82.7 us
    ppermute x37, starting transfers between devices, shift(): lax.ppermute(value, 'tx', [(s, (s - hops) % tx_size) for s in range(tx_si...  56.7 us
    reduce_scatter x1, waiting for transfers between devices, body(): lax.psum_scatter(y_part.reshape(n_tok, d_model), 'ty', scatter_dimension=...  52.9 us
    pallas_call x2, Pallas kernels, backward(): pl.pallas_call(lambda *refs: kernel(*refs[:5], *refs[5 + len(into):]), gr...  24.6 us
    pallas_call x3, Pallas kernels, place_call(): pl.pallas_call(functools.partial(kernel, chunk=chunk, n_seq=n_seq), in_sp...  21.4 us
  transfers between devices with their start and end apart: 55, of which 18 were waited for; matrix products, arithmetic and copies ran while one was open for 5% of the time, Pallas kernels for 28%

profile of v11, /device:TPU:98, one launch (start us, length us, event | category | flops | bytes accessed | tf_op | source)
XLA Modules:
  0.0 651.9 jit_solution(15218558649868485151)
XLA Ops:
  14.6 15.8 %collective-permute-done = bf16[2,192,512]{2,1,0:T(8,128)(2,1)S(1)} collective-permute-done((bf16[2,192,512]{2,1,0:T(8,128)(2,1)S(1)}, bf16[2,192,512]{2,1,0:T(8,128)(2,1)S(1)}, u32[]{:S(2)}, u32[]{:S(2)}) %collective-permute-start) | collective-permute-done | bytes 393248 | tf_op jit(solution)/shard_map/ppermute | solution.py:450
  38.9 10.0 %collective-permute-done.17 = bf16[2,192,512]{2,1,0:T(8,128)(2,1)S(1)} collective-permute-done((bf16[2,192,512]{2,1,0:T(8,128)(2,1)S(1)}, bf16[2,192,512]{2,1,0:T(8,128)(2,1)S(1)}, u32[]{:S(2)}, u32[]{:S(2)}) %collective-permute-start.17) | collective-permute-done | bytes 393248 | tf_op jit(solution)/shard_map/ppermute | solution.py:450
  51.3 6.4 collective-permute-done.19
  68.7 35.1 %collective-permute-done.6.refs_1_ = bf16[512,1792]{1,0:T(8,128)(2,1)S(1)} collective-permute-done((bf16[512,1792]{1,0:T(8,128)(2,1)S(1)}, bf16[512,1792]{1,0:T(8,128)(2,1)S(1)}, u32[]{:S(2)}, u32[]{:S(2)}) %collective-permute-start.6) | collective-permute-done | bytes 1835040 | tf_op jit(solution)/shard_map/ppermute | solution.py:450
  107.2 24.8 %collective-permute-done.3 = bf16[8,512]{1,0:T(8,128)(2,1)S(1)} collective-permute-done((bf16[8,512]{1,0:T(8,128)(2,1)S(1)}, bf16[8,512]{1,0:T(8,128)(2,1)S(1)}, u32[]{:S(2)}, u32[]{:S(2)}) %collective-permute-start.3) | collective-permute-done | bytes 8224 | tf_op jit(solution)/shard_map/ppermute | solution.py:450
  132.8 18.6 %collective-permute-done.4 = bf16[8,512]{1,0:T(8,128)(2,1)S(1)} collective-permute-done((bf16[8,512]{1,0:T(8,128)(2,1)S(1)}, bf16[8,512]{1,0:T(8,128)(2,1)S(1)}, u32[]{:S(2)}, u32[]{:S(2)}) %collective-permute-start.4) | collective-permute-done | bytes 8224 | tf_op jit(solution)/shard_map/ppermute | solution.py:450
  162.7 18.0 %shard_map.245 = (bf16[3072,2048]{1,0:T(8,128)(2,1)}, bf16[3072,2048]{1,0:T(8,128)(2,1)}) custom-call(bf16[3072,2048]{1,0:T(8,128)(2,1)} %bitcast.91, f32[8,2048]{1,0:T(8,128)} %maximum_convert_fusion.small_ref), custom_call_target="tpu_custom_call" | custom-call | flops 100663296 | bytes 37781504 | tf_op jit(solution)/shard_map/pallas_call | solution.py:429
  180.7 32.8 %shard_map.246 = (bf16[3072,768]{1,0:T(8,128)(2,1)}, bf16[3072,1024]{1,0:T(8,128)(2,1)}, bf16[3072,1024]{1,0:T(8,128)(2,1)}) custom-call(bf16[3072,2048]{1,0:T(8,128)(2,1)} %get-tuple-element.54.h_attn_ref.refs_0_.refs_4_, bf16[3072,2048]{1,0:T(8,128)(2,1)} %get-tuple-element.55.h_mlp_ref.refs_2_.refs_5_, f32[1536,128]{1,0:T(8,128)} %get-tuple-element.128.cos_ref.refs_2_, ...), custom_call_target="tpu_custom_call" | custom-call | flops 22548578304 | bytes 52170240 | tf_op jit(solution)/shard_map/pallas_call | solution.py:429
  213.6 27.1 %shard_map.250 = (bf16[3072,256]{1,0:T(8,128)(2,1)}, bf16[3072,1024]{1,0:T(8,128)(2,1)}, f32[8,1024]{1,0:T(8,128)}) custom-call(bf16[3072,2048]{1,0:T(8,128)(2,1)} %bitcast.76, bf16[3072,1024]{1,0:T(8,128)(2,1)} %get-tuple-element.62.pre_ref, bf16[1280,512]{1,0:T(8,128)(2,1)} %copy-done.24, bf16[1280,512]{1,0:T(8,128)(2,1)} %copy-done.20, ...), custom_call_target="tpu_custom_call" | custom-call | flops 16106127360 | bytes 31997952 | tf_op jit(solution)/shard_map/pallas_call | solution.py:429
  240.7 12.3 %ab.2 = (bf16[2,1536,768]{2,1,0:T(8,128)(2,1)}, f32[1,8,768]{2,1,0:T(8,128)}) custom-call(bf16[2,1536,768]{2,1,0:T(8,128)(2,1)} %bitcast.127, bf16[2,1536,256]{2,1,0:T(8,128)(2,1)} %bitcast.130, f32[1536,128]{1,0:T(8,128)} %get-tuple-element.128.cos_ref.refs_2_, f32[1536,128]{1,0:T(8,128)} %get-tuple-element.127.lo_ref.refs_3_, ...), custom_call_target="tpu_custom_call" | custom-call | flops 6039797760 | bytes 5505024 | tf_op jit(solution)/shard_map/ab/pallas_call | solution.py:127
  253.0 21.9 %shard_map.251 = (bf16[1536,2048]{1,0:T(8,128)(2,1)}, f32[4,8,2048]{2,1,0:T(8,128)}) custom-call(bf16[3072,768]{1,0:T(8,128)(2,1)} %bitcast.81, bf16[3072,1024]{1,0:T(8,128)(2,1)} %get-tuple-element.65.d_pre_ref.refs_3_, bf16[3072,2048]{1,0:T(8,128)(2,1)} %bitcast.92, f32[8,2048]{1,0:T(8,128)} %maximum_convert_fusion.small_ref, bf16[512,1792]{1,0:T(8,128)(2,1)} %copy-done.5, ...), custom_call_target="tpu_custom_call" | custom-call | flops 11274289152 | bytes 25591808 | tf_op jit(solution)/shard_map/pallas_call | solution.py:429
  274.9 12.3 %ab.3 = (bf16[2,1536,768]{2,1,0:T(8,128)(2,1)}, f32[1,8,768]{2,1,0:T(8,128)}) custom-call(bf16[2,1536,768]{2,1,0:T(8,128)(2,1)} %bitcast.128, bf16[2,1536,256]{2,1,0:T(8,128)(2,1)} %bitcast.131, f32[1536,128]{1,0:T(8,128)} %get-tuple-element.128.cos_ref.refs_2_, f32[1536,128]{1,0:T(8,128)} %get-tuple-element.127.lo_ref.refs_3_, ...), custom_call_target="tpu_custom_call", output_to_operand_aliasing={{0}: (5, {})} | custom-call | flops 6039797760 | bytes 5505024 | tf_op jit(solution)/shard_map/ab/pallas_call | solution.py:127
  287.2 21.7 %shard_map.252 = (bf16[1536,2048]{1,0:T(8,128)(2,1)}, f32[4,8,2048]{2,1,0:T(8,128)}) custom-call(bf16[3072,768]{1,0:T(8,128)(2,1)} %bitcast.82, bf16[3072,1024]{1,0:T(8,128)(2,1)} %get-tuple-element.65.d_pre_ref.refs_3_, bf16[3072,2048]{1,0:T(8,128)(2,1)} %bitcast.93, f32[8,2048]{1,0:T(8,128)} %maximum_convert_fusion.small_ref, bf16[512,1792]{1,0:T(8,128)(2,1)} %copy-done.5, ...), custom_call_target="tpu_custom_call" | custom-call | flops 11274289152 | bytes 25591808 | tf_op jit(solution)/shard_map/pallas_call | solution.py:429
  309.1 9.8 %af.1 = bf16[2,1536,256]{2,1,0:T(8,128)(2,1)} custom-call(bf16[2,1536,768]{2,1,0:T(8,128)(2,1)} %bitcast.129), custom_call_target="tpu_custom_call" | custom-call | flops 4831838208 | bytes 6291456 | tf_op jit(solution)/shard_map/af/pallas_call | solution.py:114
  318.9 22.0 %shard_map.247 = bf16[8,2,192,2048]{3,2,1,0:T(8,128)(2,1)} custom-call(bf16[3072,256]{1,0:T(8,128)(2,1)} %bitcast.87, bf16[3072,1024]{1,0:T(8,128)(2,1)} %get-tuple-element.57.gelu_ref.refs_2_, bf16[1280,512]{1,0:T(8,128)(2,1)} %copy-done.24, bf16[1280,512]{1,0:T(8,128)(2,1)} %copy-done.20, bf16[1280,256]{1,0:T(8,128)(2,1)} %collective-permute-done.11.refs_2_, ...), custom_call_target="tpu_custom_call" | custom-call | flops 16106127360 | bytes 25690112 | tf_op jit(solution)/shard_map/pallas_call | solution.py:429
  343.2 5.5 reduce-scatter.6.cloned.1.call-done.a6_ref
  367.1 52.9 %reduce-scatter.4.cloned.1.call-done.mixed_ref = bf16[384,2048]{1,0:T(8,128)(2,1)} async-done(((bf16[3072,2048]{1,0:T(8,128)(2,1)}), bf16[384,2048]{1,0:T(8,128)(2,1)}) %reduce-scatter.4.cloned.1.call-update) | async-done | bytes 1572880 | tf_op jit(solution)/shard_map/reduce_scatter | solution.py:536
  427.9 6.9 %collective-permute-done.14 = bf16[384,512]{1,0:T(8,128)(2,1)S(1)} collective-permute-done((bf16[384,512]{1,0:T(8,128)(2,1)S(1)}, bf16[384,512]{1,0:T(8,128)(2,1)S(1)}, u32[]{:S(2)}, u32[]{:S(2)}) %collective-permute-start.14) | collective-permute-done | bytes 393248 | tf_op jit(solution)/shard_map/ppermute | solution.py:450
  434.8 9.8 %collective-permute-done.15 = bf16[384,512]{1,0:T(8,128)(2,1)S(1)} collective-permute-done((bf16[384,512]{1,0:T(8,128)(2,1)S(1)}, bf16[384,512]{1,0:T(8,128)(2,1)S(1)}, u32[]{:S(2)}, u32[]{:S(2)}) %collective-permute-start.15) | collective-permute-done | bytes 393248 | tf_op jit(solution)/shard_map/ppermute | solution.py:450
  454.5 12.1 %shard_map.257 = (bf16[256,1792]{1,0:T(8,128)(2,1)}, bf16[256,1792]{1,0:T(8,128)(2,1)}) custom-call(bf16[3072,2048]{1,0:T(8,128)(2,1)} %get-tuple-element.54.h_attn_ref.refs_0_.refs_4_, bf16[3072,768]{1,0:T(8,128)(2,1)} %bitcast.83, bf16[3072,2048]{1,0:T(8,128)(2,1)} %get-tuple-element.55.h_mlp_ref.refs_2_.refs_5_, ...), custom_call_target="tpu_custom_call" | custom-call | flops 5637144576 | bytes 17301504 | tf_op jit(solution)/shard_map/pallas_call | solution.py:248
  477.8 9.6 %shard_map.260 = (bf16[640,512]{1,0:T(8,128)(2,1)}, bf16[640,512]{1,0:T(8,128)(2,1)}) custom-call(bf16[3072,256]{1,0:T(8,128)(2,1)} %bitcast.88, bf16[3072,2048]{1,0:T(8,128)(2,1)} %bitcast.77, bf16[3072,1024]{1,0:T(8,128)(2,1)} %get-tuple-element.57.gelu_ref.refs_2_), custom_call_target="tpu_custom_call" | custom-call | flops 4026531840 | bytes 11010048 | tf_op jit(solution)/shard_map/pallas_call | solution.py:248
  487.5 10.7 %collective-permute-done.23 = bf16[192,512]{1,0:T(8,128)(2,1)S(1)} collective-permute-done((bf16[192,512]{1,0:T(8,128)(2,1)S(1)}, bf16[192,512]{1,0:T(8,128)(2,1)S(1)}, u32[]{:S(2)}, u32[]{:S(2)}) %collective-permute-start.23) | collective-permute-done | bytes 196640 | tf_op jit(solution)/shard_map/ppermute | solution.py:450
  504.4 19.9 %shard_map.258 = (bf16[512,1792]{1,0:T(8,128)(2,1)}, bf16[512,1792]{1,0:T(8,128)(2,1)}) custom-call(bf16[3072,2048]{1,0:T(8,128)(2,1)} %get-tuple-element.54.h_attn_ref.refs_0_.refs_4_, bf16[3072,768]{1,0:T(8,128)(2,1)} %bitcast.84, bf16[3072,2048]{1,0:T(8,128)(2,1)} %get-tuple-element.55.h_mlp_ref.refs_2_.refs_5_, ...), custom_call_target="tpu_custom_call" | custom-call | flops 11274289152 | bytes 45613056 | tf_op jit(solution)/shard_map/pallas_call | solution.py:248
  530.2 14.3 %shard_map.261 = (bf16[1280,512]{1,0:T(8,128)(2,1)}, bf16[1280,512]{1,0:T(8,128)(2,1)}) custom-call(bf16[3072,256]{1,0:T(8,128)(2,1)} %bitcast.89, bf16[3072,2048]{1,0:T(8,128)(2,1)} %bitcast.78, bf16[3072,1024]{1,0:T(8,128)(2,1)} %get-tuple-element.57.gelu_ref.refs_2_, bf16[3072,2048]{1,0:T(8,128)(2,1)} %bitcast.79, bf16[640,512]{1,0:T(8,128)(2,1)} %copy-done.17, ...), custom_call_target="tpu_custom_call" | custom-call | flops 8053063680 | bytes 20447232 | tf_op jit(solution)/shard_map/pallas_call | solution.py:248
  548.7 6.5 %convert_reduce_fusion = f32[512]{0:T(512)S(1)} fusion(bf16[8,1536,512]{2,1,0:T(8,128)(2,1)} %param.15), kind=kLoop, calls=%fused_computation | loop fusion | flops 12582400 | bytes 12584960 | tf_op jit(solution)/shard_map/reduce_sum | solution.py:583
  557.8 9.0 %collective-permute-done.29.high_ref = bf16[2,192,512]{2,1,0:T(8,128)(2,1)S(1)} collective-permute-done((bf16[2,192,512]{2,1,0:T(8,128)(2,1)S(1)}, bf16[2,192,512]{2,1,0:T(8,128)(2,1)S(1)}, u32[]{:S(2)}, u32[]{:S(2)}) %collective-permute-start.29) | collective-permute-done | bytes 393248 | tf_op jit(solution)/shard_map/ppermute | solution.py:460
  566.9 23.2 %collective-permute-done.46.refs_3_ = bf16[1280,512]{1,0:T(8,128)(2,1)} collective-permute-done((bf16[1280,512]{1,0:T(8,128)(2,1)}, bf16[1280,512]{1,0:T(8,128)(2,1)}, u32[]{:S(2)}, u32[]{:S(2)}) %collective-permute-start.46) | collective-permute-done | bytes 1310752 | tf_op jit(solution)/shard_map/ppermute | solution.py:450
  590.7 11.7 %shard_map.262 = (f32[256,512]{1,0:T(8,128)}, f32[1024,512]{1,0:T(8,128)}) custom-call(bf16[3072,256]{1,0:T(8,128)(2,1)} %bitcast.90, bf16[3072,2048]{1,0:T(8,128)(2,1)} %bitcast.80, bf16[3072,1024]{1,0:T(8,128)(2,1)} %get-tuple-element.57.gelu_ref.refs_2_, bf16[1280,512]{1,0:T(8,128)(2,1)} %collective-permute-done.46.refs_3_, ...), custom_call_target="tpu_custom_call" | custom-call | flops 4026531840 | bytes 17301504 | tf_op jit(solution)/shard_map/pallas_call | solution.py:248
  602.4 15.0 %shard_map.259 = (f32[512,768]{1,0:T(8,128)}, f32[512,1024]{1,0:T(8,128)}) custom-call(bf16[3072,2048]{1,0:T(8,128)(2,1)} %get-tuple-element.54.h_attn_ref.refs_0_.refs_4_, bf16[3072,768]{1,0:T(8,128)(2,1)} %bitcast.85, bf16[3072,2048]{1,0:T(8,128)(2,1)} %get-tuple-element.55.h_mlp_ref.refs_2_.refs_5_, ...), custom_call_target="tpu_custom_call" | custom-call | flops 5637144576 | bytes 39321600 | tf_op jit(solution)/shard_map/pallas_call | solution.py:248
  622.5 6.1 shard_map.255.rest_0_
  628.7 5.8 shard_map.256
  634.5 9.4 %shard_map.249 = bf16[4,3072,512]{2,1,0:T(8,128)(2,1)} custom-call(s32[3]{0:T(128)} %pad_add_fusion.place_ref, bf16[4,3072,512]{2,1,0:T(8,128)(2,1)} %bitcast.95), custom_call_target="tpu_custom_call" | custom-call | flops 6291456 | bytes 25165824 | tf_op jit(solution)/shard_map/pallas_call | solution.py:187
  (235 shorter events, 119.1 us)
Async XLA Ops:
  7.2 155.5 %all-gather.5.cloned.1.call-start = ((), (), s32[]{:S(2)}) async-start(), calls=%async_computation.3 | async-start | bytes 14155776 | tf_op jit(solution)/shard_map/all_gather | solution.py:515
  35.3 178.3 %all-gather.9.cloned.1.call-start = ((), (), s32[]{:S(2)}) async-start(), calls=%async_computation.6 | async-start | bytes 14155776 | tf_op jit(solution)/shard_map/all_gather | solution.py:516
  59.1 289.5 %reduce-scatter.6.cloned.1.call-start = ((), (), s32[]{:S(2)}) async-start(), calls=%async_computation.7 | async-start | bytes 7077888 | tf_op jit(solution)/shard_map/reduce_scatter | solution.py:553
  60.8 43.0 %collective-permute-start.6 = (bf16[512,1792]{1,0:T(8,128)(2,1)S(1)}, bf16[512,1792]{1,0:T(8,128)(2,1)S(1)}, u32[]{:S(2)}, u32[]{:S(2)}) collective-permute-start(bf16[512,1792]{1,0:T(8,128)(2,1)S(1)} %pad_maximum_fusion.refs_0_), channel_id=1, source_target_pairs={{0,24},{8,0},{16,8},{24,16},{1,25},{9,1},{17,9},{25,17},{2,26},{10... | collective-permute-start | bytes 5505032 | tf_op jit(solution)/shard_map/ppermute | solution.py:450
  61.8 44.3 %collective-permute-start.8 = (bf16[512,1792]{1,0:T(8,128)(2,1)S(1)}, bf16[512,1792]{1,0:T(8,128)(2,1)S(1)}, u32[]{:S(2)}, u32[]{:S(2)}) collective-permute-start(bf16[512,1792]{1,0:T(8,128)(2,1)S(1)} %pad_maximum_fusion.refs_0_), channel_id=1, source_target_pairs={{0,8},{8,16},{16,24},{24,0},{1,9},{9,17},{17,25},{25,1},{2,10},{10... | collective-permute-start | bytes 5505032 | tf_op jit(solution)/shard_map/ppermute | solution.py:450
  63.1 94.2 %collective-permute-start.10 = (bf16[1280,512]{1,0:T(8,128)(2,1)S(1)}, bf16[1280,512]{1,0:T(8,128)(2,1)S(1)}, u32[]{:S(2)}, u32[]{:S(2)}) collective-permute-start(bf16[1280,512]{1,0:T(8,128)(2,1)S(1)} %constant_dynamic-update-slice_fusion.refs_0_), channel_id=1, source_target_pairs={{0,24},{8,0},{16,8},{24,16},{1,25},{9,1},{17,9},{25,17},{2,26},{10... | collective-permute-start | bytes 3932168 | tf_op jit(solution)/shard_map/ppermute | solution.py:450
  65.3 95.4 %collective-permute-start.12 = (bf16[1280,512]{1,0:T(8,128)(2,1)S(1)}, bf16[1280,512]{1,0:T(8,128)(2,1)S(1)}, u32[]{:S(2)}, u32[]{:S(2)}) collective-permute-start(bf16[1280,512]{1,0:T(8,128)(2,1)S(1)} %constant_dynamic-update-slice_fusion.refs_0_), channel_id=1, source_target_pairs={{0,8},{8,16},{16,24},{24,0},{1,9},{9,17},{17,25},{25,1},{2,10},{10... | collective-permute-start | bytes 3932168 | tf_op jit(solution)/shard_map/ppermute | solution.py:450
  65.4 66.6 %collective-permute-start.3 = (bf16[8,512]{1,0:T(8,128)(2,1)S(1)}, bf16[8,512]{1,0:T(8,128)(2,1)S(1)}, u32[]{:S(2)}, u32[]{:S(2)}) collective-permute-start(bf16[8,512]{1,0:T(8,128)(2,1)S(1)} %select_select_fusion), channel_id=1, source_target_pairs={{0,24},{8,0},{16,8},{24,16},{1,25},{9,1},{17,9},{25,17},{2,26},{10... | collective-permute-start | bytes 24584 | tf_op jit(solution)/shard_map/ppermute | solution.py:450
  103.9 76.8 %collective-permute-start.7 = (bf16[256,1792]{1,0:T(8,128)(2,1)S(1)}, bf16[256,1792]{1,0:T(8,128)(2,1)}, u32[]{:S(2)}, u32[]{:S(2)}) collective-permute-start(bf16[256,1792]{1,0:T(8,128)(2,1)S(1)} %slice.80), channel_id=1, source_target_pairs={{0,24},{8,0},{16,8},{24,16},{1,25},{9,1},{17,9},{25,17},{2,26},{10... | collective-permute-start | bytes 2752520 | tf_op jit(solution)/shard_map/ppermute | solution.py:450
  107.2 73.5 %collective-permute-start.9 = (bf16[256,1792]{1,0:T(8,128)(2,1)}, bf16[256,1792]{1,0:T(8,128)(2,1)}, u32[]{:S(2)}, u32[]{:S(2)}) collective-permute-start(bf16[256,1792]{1,0:T(8,128)(2,1)} %slice.81), channel_id=1, source_target_pairs={{0,8},{8,16},{16,24},{24,0},{1,9},{9,17},{17,25},{25,1},{2,10},{10... | collective-permute-start | bytes 2752520 | tf_op jit(solution)/shard_map/ppermute | solution.py:450
  157.3 56.2 %collective-permute-start.11 = (bf16[1280,256]{1,0:T(8,128)(2,1)S(1)}, bf16[1280,256]{1,0:T(8,128)(2,1)}, u32[]{:S(2)}, u32[]{:S(2)}) collective-permute-start(bf16[1280,256]{1,0:T(8,128)(2,1)S(1)} %slice.82), channel_id=1, source_target_pairs={{0,24},{8,0},{16,8},{24,16},{1,25},{9,1},{17,9},{25,17},{2,26},{10... | collective-permute-start | bytes 1966088 | tf_op jit(solution)/shard_map/ppermute | solution.py:450
  162.6 51.0 %collective-permute-start.13 = (bf16[1280,256]{1,0:T(8,128)(2,1)}, bf16[1280,256]{1,0:T(8,128)(2,1)}, u32[]{:S(2)}, u32[]{:S(2)}) collective-permute-start(bf16[1280,256]{1,0:T(8,128)(2,1)} %slice.83), channel_id=1, source_target_pairs={{0,8},{8,16},{16,24},{24,0},{1,9},{9,17},{17,25},{25,1},{2,10},{10... | collective-permute-start | bytes 1966088 | tf_op jit(solution)/shard_map/ppermute | solution.py:450
  309.0 111.0 %reduce-scatter.4.cloned.1.call-start = ((), (), s32[]{:S(2)}) async-start(), calls=%async_computation.4 | async-start | bytes 14155776 | tf_op jit(solution)/shard_map/reduce_scatter | solution.py:536
  341.0 131.3 %reduce-scatter.8.cloned.1.call-start = ((), (), s32[]{:S(2)}) async-start(), calls=%async_computation.9 | async-start | bytes 7077888 | tf_op jit(solution)/shard_map/reduce_scatter | solution.py:553
  341.6 287.0 %all-gather.11.cloned.1.call-start = ((), (), s32[]{:S(2)}) async-start(), calls=%async_computation.8 | async-start | bytes 7077888 | tf_op jit(solution)/shard_map/all_gather | solution.py:572
  366.1 268.4 %all-gather.7.cloned.1.call-start = ((), (), s32[]{:S(2)}) async-start(), calls=%async_computation.5 | async-start | bytes 14155776 | tf_op jit(solution)/shard_map/all_gather | solution.py:538
  466.7 34.9 %collective-permute-start.40 = (bf16[256,1792]{1,0:T(8,128)(2,1)}, bf16[256,1792]{1,0:T(8,128)(2,1)}, u32[]{:S(2)}, u32[]{:S(2)}) collective-permute-start(bf16[256,1792]{1,0:T(8,128)(2,1)} %get-tuple-element.82), channel_id=1, source_target_pairs={{0,8},{8,16},{16,24},{24,0},{1,9},{9,17},{17,25},{25,1},{2,10},{10... | collective-permute-start | bytes 2752520 | tf_op jit(solution)/shard_map/ppermute | solution.py:450
  466.7 37.8 %collective-permute-start.41 = (bf16[256,1792]{1,0:T(8,128)(2,1)}, bf16[256,1792]{1,0:T(8,128)(2,1)}, u32[]{:S(2)}, u32[]{:S(2)}) collective-permute-start(bf16[256,1792]{1,0:T(8,128)(2,1)} %get-tuple-element.83), channel_id=1, source_target_pairs={{0,24},{8,0},{16,8},{24,16},{1,25},{9,1},{17,9},{25,17},{2,26},{10... | collective-permute-start | bytes 2752520 | tf_op jit(solution)/shard_map/ppermute | solution.py:450
  474.5 23.7 %collective-permute-start.23 = (bf16[192,512]{1,0:T(8,128)(2,1)S(1)}, bf16[192,512]{1,0:T(8,128)(2,1)S(1)}, u32[]{:S(2)}, u32[]{:S(2)}) collective-permute-start(bf16[192,512]{1,0:T(8,128)(2,1)S(1)} %get-tuple-element.75), channel_id=1, source_target_pairs={{0,8},{8,16},{16,24},{24,0},{1,9},{9,17},{17,25},{25,1},{2,10},{10... | collective-permute-start | bytes 589832 | tf_op jit(solution)/shard_map/ppermute | solution.py:450
  476.0 25.4 %collective-permute-start.25 = (bf16[192,512]{1,0:T(8,128)(2,1)S(1)}, bf16[192,512]{1,0:T(8,128)(2,1)S(1)}, u32[]{:S(2)}, u32[]{:S(2)}) collective-permute-start(bf16[192,512]{1,0:T(8,128)(2,1)S(1)} %get-tuple-element.77), channel_id=1, source_target_pairs={{0,24},{8,0},{16,8},{24,16},{1,25},{9,1},{17,9},{25,17},{2,26},{10... | collective-permute-start | bytes 589832 | tf_op jit(solution)/shard_map/ppermute | solution.py:450
  498.2 26.3 %collective-permute-start.44 = (bf16[640,512]{1,0:T(8,128)(2,1)}, bf16[640,512]{1,0:T(8,128)(2,1)S(1)}, u32[]{:S(2)}, u32[]{:S(2)}) collective-permute-start(bf16[640,512]{1,0:T(8,128)(2,1)} %get-tuple-element.87), channel_id=1, source_target_pairs={{0,8},{8,16},{16,24},{24,0},{1,9},{9,17},{17,25},{25,1},{2,10},{10... | collective-permute-start | bytes 1966088 | tf_op jit(solution)/shard_map/ppermute | solution.py:450
  498.2 29.6 %collective-permute-start.45 = (bf16[640,512]{1,0:T(8,128)(2,1)}, bf16[640,512]{1,0:T(8,128)(2,1)}, u32[]{:S(2)}, u32[]{:S(2)}) collective-permute-start(bf16[640,512]{1,0:T(8,128)(2,1)} %get-tuple-element.88), channel_id=1, source_target_pairs={{0,24},{8,0},{16,8},{24,16},{1,25},{9,1},{17,9},{25,17},{2,26},{10... | collective-permute-start | bytes 1966088 | tf_op jit(solution)/shard_map/ppermute | solution.py:450
  501.5 43.1 %collective-permute-start.39 = (f32[4,512]{1,0:T(4,128)S(1)}, f32[4,512]{1,0:T(4,128)S(1)}, u32[]{:S(2)}, u32[]{:S(2)}) collective-permute-start(f32[4,512]{1,0:T(4,128)S(1)} %add.101), channel_id=1, source_target_pairs={{0,4},{1,5},{2,6},{3,7},{4,0},{5,1},{6,2},{7,3},{8,12},{9,13},{10,... | collective-permute-start | bytes 24584 | tf_op jit(solution)/shard_map/ppermute | solution.py:455
  504.4 40.2 %collective-permute-start.28 = (bf16[4,192,512]{2,1,0:T(8,128)(2,1)S(1)}, bf16[4,192,512]{2,1,0:T(8,128)(2,1)S(1)}, u32[]{:S(2)}, u32[]{:S(2)}) collective-permute-start(bf16[4,192,512]{2,1,0:T(8,128)(2,1)S(1)} %pad_maximum_fusion.7.refs_0_), channel_id=1, source_target_pairs={{0,2},{1,3},{2,4},{3,5},{4,6},{5,7},{6,0},{7,1},{8,10},{9,11},{10,... | collective-permute-start | bytes 2359304 | tf_op jit(solution)/shard_map/ppermute | solution.py:460
  524.4 66.2 %collective-permute-start.42 = (bf16[512,1792]{1,0:T(8,128)(2,1)}, bf16[512,1792]{1,0:T(8,128)(2,1)}, u32[]{:S(2)}, u32[]{:S(2)}) collective-permute-start(bf16[512,1792]{1,0:T(8,128)(2,1)} %get-tuple-element.84), channel_id=1, source_target_pairs={{0,8},{8,16},{16,24},{24,0},{1,9},{9,17},{17,25},{25,1},{2,10},{10... | collective-permute-start | bytes 5505032 | tf_op jit(solution)/shard_map/ppermute | solution.py:450
  524.5 77.9 %collective-permute-start.43 = (bf16[512,1792]{1,0:T(8,128)(2,1)}, bf16[512,1792]{1,0:T(8,128)(2,1)}, u32[]{:S(2)}, u32[]{:S(2)}) collective-permute-start(bf16[512,1792]{1,0:T(8,128)(2,1)} %get-tuple-element.85), channel_id=1, source_target_pairs={{0,24},{8,0},{16,8},{24,16},{1,25},{9,1},{17,9},{25,17},{2,26},{10... | collective-permute-start | bytes 5505032 | tf_op jit(solution)/shard_map/ppermute | solution.py:450
  544.5 45.5 %collective-permute-start.46 = (bf16[1280,512]{1,0:T(8,128)(2,1)}, bf16[1280,512]{1,0:T(8,128)(2,1)}, u32[]{:S(2)}, u32[]{:S(2)}) collective-permute-start(bf16[1280,512]{1,0:T(8,128)(2,1)} %get-tuple-element.89), channel_id=1, source_target_pairs={{0,8},{8,16},{16,24},{24,0},{1,9},{9,17},{17,25},{25,1},{2,10},{10... | collective-permute-start | bytes 3932168 | tf_op jit(solution)/shard_map/ppermute | solution.py:450
  544.7 45.4 %collective-permute-start.47 = (bf16[1280,512]{1,0:T(8,128)(2,1)}, bf16[1280,512]{1,0:T(8,128)(2,1)}, u32[]{:S(2)}, u32[]{:S(2)}) collective-permute-start(bf16[1280,512]{1,0:T(8,128)(2,1)} %get-tuple-element.90), channel_id=1, source_target_pairs={{0,24},{8,0},{16,8},{24,16},{1,25},{9,1},{17,9},{25,17},{2,26},{10... | collective-permute-start | bytes 3932168 | tf_op jit(solution)/shard_map/ppermute | solution.py:450
  566.8 54.8 %collective-permute-start.30 = (bf16[4,192,512]{2,1,0:T(8,128)(2,1)S(1)}, bf16[4,192,512]{2,1,0:T(8,128)(2,1)}, u32[]{:S(2)}, u32[]{:S(2)}) collective-permute-start(bf16[4,192,512]{2,1,0:T(8,128)(2,1)S(1)} %pad_maximum_fusion.7.refs_0_), channel_id=1, source_target_pairs={{0,1},{1,0},{2,3},{3,2},{4,5},{5,4},{6,7},{7,6},{8,9},{9,8},{10,11... | collective-permute-start | bytes 2359304 | tf_op jit(solution)/shard_map/ppermute | solution.py:463
  590.1 31.6 %collective-permute-start.31 = (bf16[4,192,512]{2,1,0:T(8,128)(2,1)S(1)}, bf16[4,192,512]{2,1,0:T(8,128)(2,1)S(1)}, u32[]{:S(2)}, u32[]{:S(2)}) collective-permute-start(bf16[4,192,512]{2,1,0:T(8,128)(2,1)S(1)} %collective-permute-done.26.refs_1_), channel_id=1, source_target_pairs={{0,1},{1,0},{2,3},{3,2},{4,5},{5,4},{6,7},{7,6},{8,9},{9,8},{10,11... | collective-permute-start | bytes 2359304 | tf_op jit(solution)/shard_map/ppermute | solution.py:463
  590.1 31.6 %collective-permute-start.33 = (bf16[4,192,512]{2,1,0:T(8,128)(2,1)}, bf16[4,192,512]{2,1,0:T(8,128)(2,1)}, u32[]{:S(2)}, u32[]{:S(2)}) collective-permute-start(bf16[4,192,512]{2,1,0:T(8,128)(2,1)} %copy-done.7), channel_id=1, source_target_pairs={{0,1},{1,0},{2,3},{3,2},{4,5},{5,4},{6,7},{7,6},{8,9},{9,8},{10,11... | collective-permute-start | bytes 2359304 | tf_op jit(solution)/shard_map/ppermute | solution.py:463
  590.6 31.1 %collective-permute-start.32 = (bf16[4,192,512]{2,1,0:T(8,128)(2,1)S(1)}, bf16[4,192,512]{2,1,0:T(8,128)(2,1)}, u32[]{:S(2)}, u32[]{:S(2)}) collective-permute-start(bf16[4,192,512]{2,1,0:T(8,128)(2,1)S(1)} %cat.1.refs_2_), channel_id=1, source_target_pairs={{0,1},{1,0},{2,3},{3,2},{4,5},{5,4},{6,7},{7,6},{8,9},{9,8},{10,11... | collective-permute-start | bytes 2359304 | tf_op jit(solution)/shard_map/ppermute | solution.py:463
  (59 other events, 935.5 us)
Sparse Core Ops, SparseCore 0:
  35.4 63.3 all-gather.4
  100.4 65.0 all-gather.8
  309.1 39.4 reduce-scatter.5
  350.8 69.1 reduce-scatter.3
  422.2 39.9 reduce-scatter.7
  463.6 40.3 all-gather.10
  505.6 74.0 all-gather.6
